TPU v7x, 32 devices: a whole 2x2x4 slice. The times are simulated.
32 devices in a mesh: wide: 16 (over z, y, core), narrow: 2 (over x).
Axes of the slice: x: 2, y: 2, z: 4, core: 2. Of those that a mesh axis runs over, the one named last changes fastest.
Arguments:
- examples: bfloat16 [80, 8192], P('wide', 'narrow'), may hold values from -6 to 6
- references: bfloat16 [128, 8192], P('wide', 'narrow'), may hold values from -6 to 6
- gate_weight: bfloat16 [8192, 28672], P('narrow', 'wide'), may hold values from -0.0625 to 0.0625
- up_weight: bfloat16 [8192, 28672], P('narrow', 'wide'), may hold values from -0.0625 to 0.0625
- down_weight: bfloat16 [28672, 8192], P('wide', 'narrow'), may hold values from -0.03125 to 0.03125
- cotangent: bfloat16 [80, 8192], P('wide', 'narrow'), may hold values from -6 to 6
- pair_ref: int32 [80, 4], replicated, may hold values from 0 to 127
- points: int32 [8], replicated, may hold values from 1 to 8
Outputs:
- expected: bfloat16 [80, 8192], P('wide', 'narrow')
All inputs are finite; a program needn't handle non-finite values.
Results may differ from a plain program's by a relative error of at most 0.005.
Values may be sent and summed in bfloat16 or wider, within the bound.
No kernel may reach another device: no remote copies, remote signals or barrier semaphores. Data moves between devices by JAX's collectives and lax.ppermute only.
A program may use at most 128 MiB of HBM per device.

v0:
```python
import jax
import jax.numpy as jnp
from jax import lax
from jax.experimental import pallas as pl
from jax.experimental.pallas import tpu as pltpu
from jax.sharding import PartitionSpec as P


VMEM = pl.BlockSpec(memory_space=pltpu.VMEM)
SMEM = pl.BlockSpec(memory_space=pltpu.SMEM)
ANY = pl.BlockSpec(memory_space=pl.ANY)


def factors(size):
    pair = 2 if size % 2 == 0 else 1
    near = 2 if (size // pair) % 2 == 0 else 1
    return size // (pair * near), near, pair


def rounded(rows, unit):
    return -(-rows // unit) * unit


def shift_permute(array, axis, dims, digit, amount):
    below = 1
    for size in dims[digit + 1:]:
        below *= size
    size = dims[digit]
    total = below * size
    for d in dims[:digit]:
        total *= d
    pairs = []
    for at in range(total):
        own = (at // below) % size
        to = (own + amount) % size
        pairs.append((at, at + (to - own) * below))
    return lax.ppermute(array, axis, pairs)


def pack(arrays):
    rows = jnp.concatenate(arrays)
    count, width = rows.shape
    whole = count // 8 * 8
    rest = count - whole
    if rest == 0:
        return rows, whole, 1
    pieces = whole // rest if whole else 0
    if not pieces or whole % rest or width % (pieces * 128):
        return jnp.pad(rows, ((0, 8 - rest), (0, 0))), whole + 8, 1
    cut = rows[whole:].reshape(rest * pieces, width // pieces)
    return jnp.concatenate([rows[:whole], cut], axis=1), whole, pieces


def assemble(own, whole, pieces, counts, width):
    blocks = len(own)
    packed = own[0].shape
    total = blocks * sum(counts)
    across_lanes = width // pieces

    def body(*refs):
        out, stack = refs[-2], refs[-1]
        for b in range(blocks):
            stack[pl.ds(b * packed[0], packed[0]), :] = refs[b][...]
        row = lax.broadcasted_iota(jnp.int32, (total, blocks * packed[0]), 0)
        col = lax.broadcasted_iota(jnp.int32, (total, blocks * packed[0]), 1)
        held = jnp.zeros_like(row)
        block = jnp.zeros_like(row)
        at = first = 0
        for count in counts:
            for b in range(blocks):
                inside = (row >= at) & (row < at + count)
                held = jnp.where(inside, row - at + first, held)
                block = jnp.where(inside, b, block)
                at += count
            first += count

        def pick(wanted, valid):
            return (valid & (col == wanted)).astype(jnp.float32).astype(jnp.bfloat16)

        base = block * packed[0]
        uncut = pick(base + held, held < whole)
        for j in range(pieces):
            lanes = pl.ds(j * across_lanes, across_lanes)
            value = jnp.dot(uncut, stack[:, lanes], preferred_element_type=jnp.float32)
            if packed[1] > width:
                value = value + jnp.dot(
                    pick(base + (held - whole) * pieces + j, held >= whole),
                    stack[:, pl.ds(width, across_lanes)],
                    preferred_element_type=jnp.float32,
                )
            out[:, lanes] = value.astype(jnp.bfloat16)

    dtype = own[0].dtype
    return pl.pallas_call(
        body,
        out_shape=jax.ShapeDtypeStruct((total, width), dtype),
        in_specs=[VMEM] * blocks,
        out_specs=VMEM,
        scratch_shapes=[pltpu.VMEM((blocks * packed[0], packed[1]), dtype)],
        compiler_params=pltpu.CompilerParams(vmem_limit_bytes=6 * 1024 * 1024),
        cost_estimate=pl.CostEstimate(flops=10**9, bytes_accessed=10**6, transcendentals=0),
        name="assemble",
    )(*own)


def join(halves, layout):
    width = halves[0].shape[1]
    blocks = halves[0].shape[0] // sum(layout)
    e, r, k = (blocks * rows for rows in layout)
    count = len(halves)

    def body(*refs):
        main, side = refs[-2:]
        for h in range(count):
            main[pl.ds(h * e, e), :] = refs[h][pl.ds(0, e), :]
            main[pl.ds(count * e + h * r, r), :] = refs[h][pl.ds(e, r), :]
            side[pl.ds(h * k, k), :] = refs[h][pl.ds(e + r, k), :]

    dtype = halves[0].dtype
    return pl.pallas_call(
        body,
        out_shape=(
            jax.ShapeDtypeStruct((count * (e + r), width), dtype),
            jax.ShapeDtypeStruct((count * k, width), dtype),
        ),
        in_specs=[VMEM] * count,
        out_specs=(VMEM, VMEM),
        compiler_params=pltpu.CompilerParams(vmem_limit_bytes=4 * 1024 * 1024),
        cost_estimate=pl.CostEstimate(flops=10**9, bytes_accessed=10**6, transcendentals=0),
        name="join",
    )(*halves)


def across(left, right):
    return lax.dot_general(left, right, (((1,), (1,)), ((), ())), preferred_element_type=jnp.float32)


def parts_of(size, unit):
    for count in (4, 2):
        if size % (count * unit) == 0:
            return [(i * (size // count), size // count) for i in range(count)]
    return [(0, size)]


def first_of(place):
    if place is None:
        return 0
    steps, peers, share, offset = place
    return pl.multiple_of((lax.axis_index("narrow") + steps) % peers * share + offset, 128)


def streams(weights, buffers, sems, first, width, by_depth, by_unit):
    gate, up, down = weights
    both, below = buffers
    units, depths = [], []
    for i, (row, count) in enumerate(by_unit):
        units.append(
            pltpu.make_async_copy(
                down.at[pl.ds(first + row, count)], below.at[pl.ds(row, count)], sems.at[2, i]
            )
        )
    for i, (row, count) in enumerate(by_depth):
        some = pl.ds(row, count)
        depths.append(
            [
                pltpu.make_async_copy(
                    source.at[some, pl.ds(first, width)],
                    both.at[some, pl.ds(w * width, width)],
                    sems.at[w, i],
                )
                for w, source in enumerate((gate, up))
            ]
        )
    return units, depths


def fetch(weights, place, width):
    depth = weights[0].shape[0]
    by_depth, by_unit = parts_of(depth, 128), parts_of(width, 32)

    def body(gate, up, down, both, below, sems):
        first = first_of(place)
        units, depths = streams((gate, up, down), (both, below), sems, first, width, by_depth, by_unit)
        copies = units + [copy for pair in depths for copy in pair]
        for copy in copies:
            copy.start()
        for copy in copies:
            copy.wait()

    return pl.pallas_call(
        body,
        out_shape=(
            pltpu.VMEM((depth, 2 * width), jnp.bfloat16),
            pltpu.VMEM((width, depth), jnp.bfloat16),
        ),
        in_specs=[ANY, ANY, ANY],
        out_specs=(VMEM, VMEM),
        scratch_shapes=[pltpu.SemaphoreType.DMA((3, 4))],
        compiler_params=pltpu.CompilerParams(vmem_limit_bytes=1024 * 1024),
        cost_estimate=pl.CostEstimate(
            flops=4 * 10**9, bytes_accessed=6 * depth * width, transcendentals=0
        ),
        name="fetch",
    )(*weights)


def forward(main, side, weights, place, width, dtype, next_one=None):
    rows, half = main.shape[0], side.shape[0] // 2
    depth = main.shape[1]
    by_depth, by_unit = parts_of(depth, 128), parts_of(width, 32)
    ready = len(weights) == 2

    def put_side(out, value):
        out[pl.ds(rows, half), pl.ds(0, width)] = value[:half].astype(dtype)
        out[pl.ds(rows, half), pl.ds(width, width)] = value[half:].astype(dtype)

    def body_ready(main_ref, side_ref, both, below, *refs):
        copies = []
        if next_one is not None:
            *refs, next_both, next_below, sems = refs
            *more, out = refs
            units, depths = streams(
                more, (next_both, next_below), sems, first_of(next_one[1]), next_one[2],
                parts_of(depth, 128), parts_of(next_one[2], 32),
            )
            copies = units + [copy for pair in depths for copy in pair]
        else:
            (out,) = refs
        for copy in copies:
            copy.start()
        out[pl.ds(0, rows), :] = jnp.dot(
            main_ref[...], both[...], preferred_element_type=jnp.float32
        ).astype(dtype)
        put_side(out, across(side_ref[...], below[...]))
        for copy in copies:
            copy.wait()

    def body(main_ref, side_ref, gate, up, down, out, both, below, total, sems):
        first = first_of(place)
        units, depths = streams((gate, up, down), (both, below), sems, first, width, by_depth, by_unit)
        for copy in units + [copy for pair in depths for copy in pair]:
            copy.start()
        for copy in units:
            copy.wait()
        put_side(out, across(side_ref[...], below[...]))
        for i, (row, count) in enumerate(by_depth):
            for copy in depths[i]:
                copy.wait()
            some = pl.ds(row, count)
            part = jnp.dot(main_ref[:, some], both[some, :], preferred_element_type=jnp.float32)
            if i > 0:
                part = total[...] + part
            if i == len(by_depth) - 1:
                out[pl.ds(0, rows), :] = part.astype(dtype)
            else:
                total[...] = part

    out_shape = [jax.ShapeDtypeStruct((rows + half, 2 * width), dtype)]
    operands = [main, side, *weights]
    specs = [VMEM] * 2 + [VMEM if ready else ANY] * len(weights)
    if ready:
        scratch = []
        if next_one is not None:
            operands += next_one[0]
            specs += [ANY] * 3
            out_shape += [
                pltpu.VMEM((depth, 2 * next_one[2]), jnp.bfloat16),
                pltpu.VMEM((next_one[2], depth), jnp.bfloat16),
            ]
            scratch = [pltpu.SemaphoreType.DMA((3, 4))]
    else:
        scratch = [
            pltpu.VMEM((depth, 2 * width), jnp.bfloat16),
            pltpu.VMEM((width, depth), jnp.bfloat16),
            pltpu.VMEM((rows, 2 * width), jnp.float32),
            pltpu.SemaphoreType.DMA((3, 4)),
        ]
    return pl.pallas_call(
        body_ready if ready else body,
        out_shape=out_shape,
        in_specs=specs,
        out_specs=[VMEM] * len(out_shape),
        scratch_shapes=scratch,
        compiler_params=pltpu.CompilerParams(vmem_limit_bytes=(4 if ready else 20) * 1024 * 1024),
        cost_estimate=pl.CostEstimate(
            flops=4 * depth * width * (rows + half), bytes_accessed=6 * depth * width, transcendentals=0
        ),
        name="forward",
    )(*operands)


def coefficients(kept, received, picks, points, examples):
    width = kept.shape[1] // 2
    pairs, references = picks.shape[0] // examples, picks.shape[1]
    rows = examples + references
    count = points.shape[0]
    lanes = 128 if width % 128 == 0 else width
    piece = 16 if examples % 32 == 16 else examples // 2
    scale = 1.0 / (pairs * count)

    def body(points_ref, picks_ref, kept_ref, *refs):
        got, out, base_gate, base_up = refs[:-3], refs[-3], refs[-2], refs[-1]
        picks = picks_ref[...]
        steps = [points_ref[m].astype(jnp.float32) * 0.125 for m in range(count)]

        def block(j, _):
            if lanes == width:
                of = [pl.ds(w * width, width) for w in range(2)]
            else:
                of = [pl.ds(pl.multiple_of(w * width + j * lanes, 128), lanes) for w in range(2)]

            def total(start, size, w):
                value = kept_ref[pl.ds(start, size), of[w]]
                for ref in got:
                    value = value + ref[pl.ds(start, size), of[w]].astype(jnp.float32)
                return value

            for w, target in enumerate((base_gate, base_up)):
                value = total(0, references, w)
                high = value.astype(jnp.bfloat16)
                low = (value - high.astype(jnp.float32)).astype(jnp.bfloat16)
                target[...] = jnp.dot(picks, high, preferred_element_type=jnp.float32) + jnp.dot(
                    picks, low, preferred_element_type=jnp.float32
                )
            upstream = [total(rows, examples // 2, w) for w in range(2)]
            for first in range(0, examples, piece):
                gate = total(references + first, piece, 0) * 0.5
                up = total(references + first, piece, 1)
                coef_gate = jnp.zeros_like(gate)
                coef_up = jnp.zeros_like(gate)
                for p in range(pairs):
                    start = base_gate[pl.ds(p * examples + first, piece), :] * 0.5
                    span = gate - start
                    flat = jnp.zeros_like(gate)
                    tilted = jnp.zeros_like(gate)
                    for t in steps:
                        half = start + t * span
                        two_s = 1.0 + jnp.tanh(half)
                        silu = half * two_s
                        slope = two_s + silu * (2.0 - two_s)
                        coef_up = coef_up + silu
                        flat = flat + slope
                        tilted = tilted + t * slope
                    start_up = base_up[pl.ds(p * examples + first, piece), :]
                    coef_gate = coef_gate + (start_up * flat + (up - start_up) * tilted)
                base_gate[pl.ds(first, piece), :] = coef_gate * (0.5 * scale)
                base_up[pl.ds(first, piece), :] = coef_up * scale
            for w, source in enumerate((base_gate, base_up)):
                for h in range(2):
                    some = pl.ds(h * (examples // 2), examples // 2)
                    out[some, of[w]] = (upstream[h] * source[some, :]).astype(jnp.bfloat16)
            return 0

        lax.fori_loop(0, width // lanes, block, 0)

    return pl.pallas_call(
        body,
        out_shape=jax.ShapeDtypeStruct((examples, 2 * width), jnp.bfloat16),
        in_specs=[SMEM, VMEM, VMEM] + [VMEM] * len(received),
        out_specs=VMEM,
        scratch_shapes=[pltpu.VMEM((pairs * examples, lanes), jnp.float32)] * 2,
        compiler_params=pltpu.CompilerParams(vmem_limit_bytes=4 * 1024 * 1024),
        cost_estimate=pl.CostEstimate(flops=5 * 10**9, bytes_accessed=10**6, transcendentals=0),
        name="coefficients",
    )(points, picks, kept, *received)


def backward(grads, weights, place, total, final):
    rows = grads.shape[0]
    width = grads.shape[1] // 2
    depth = weights[0].shape[0]
    by_depth = parts_of(depth, 128)
    ready = len(weights) == 1

    def body(grads_ref, *refs):
        if ready:
            both, *outs = refs
        else:
            gate, up, *outs, both, sems = refs
            _, depths = streams((gate, up, None), (both, None), sems, first_of(place), width, by_depth, [])
            for pair in depths:
                for copy in pair:
                    copy.start()
        for i, (row, count) in enumerate(by_depth):
            some = pl.ds(row, count)
            if not ready:
                for copy in depths[i]:
                    copy.wait()
            value = across(grads_ref[...], both[some, :])
            if total is not None:
                value = value + outs[0][:, some]
            if final:
                outs[-2][:, some] = value[rows // 2:, :].astype(jnp.bfloat16)
                outs[-1][:, some] = value[:rows // 2, :]
            else:
                outs[-1][:, some] = value

    operands = [grads, *weights]
    specs = [VMEM] + [VMEM if ready else ANY] * len(weights)
    if total is not None:
        operands.append(total)
        specs.append(VMEM)
    if final:
        out_shape = (
            jax.ShapeDtypeStruct((rows // 2, depth), jnp.bfloat16),
            jax.ShapeDtypeStruct((rows // 2, depth), jnp.float32),
        )
        out_specs = (VMEM, VMEM)
    else:
        out_shape, out_specs = jax.ShapeDtypeStruct((rows, depth), jnp.float32), VMEM
    scratch = [pltpu.VMEM((depth, 2 * width), jnp.bfloat16), pltpu.SemaphoreType.DMA((2, 4))]
    return pl.pallas_call(
        body,
        out_shape=out_shape,
        in_specs=specs,
        out_specs=out_specs,
        scratch_shapes=[] if ready else scratch,
        compiler_params=pltpu.CompilerParams(vmem_limit_bytes=(4 if ready else 12) * 1024 * 1024),
        cost_estimate=pl.CostEstimate(
            flops=4 * rows * width * depth, bytes_accessed=4 * width * depth, transcendentals=0
        ),
        name="backward",
    )(*operands)


def choices(pair_ref, dims, e, r):
    far, near, pair = dims
    blocks = far * near * pair
    examples, pairs = pair_ref.shape

    def body(pair_ref, out, rows):
        at = lax.axis_index("wide")
        z, y, c = at // (near * pair), at // pair % near, at % pair
        col = lax.broadcasted_iota(jnp.int32, (examples, blocks * r), 1)
        name = jnp.zeros_like(col)
        for q in range(blocks):
            s, b, p = q % far, q // far % near, q // (far * near)
            owner = ((z + far - s) % far * near + (y + near - b) % near) * pair + (c + pair - p) % pair
            rows[pl.ds(q * e, e), :] = pair_ref[pl.ds(owner * e, e), :]
            name = jnp.where((col >= q * r) & (col < (q + 1) * r), owner * r + col - q * r, name)
        for p in range(pairs):
            out[pl.ds(p * examples, examples), :] = (
                (rows[:, pl.ds(p, 1)] == name).astype(jnp.float32).astype(jnp.bfloat16)
            )

    return pl.pallas_call(
        body,
        out_shape=jax.ShapeDtypeStruct((pairs * examples, blocks * r), jnp.bfloat16),
        in_specs=[VMEM],
        out_specs=VMEM,
        scratch_shapes=[pltpu.VMEM((examples, pairs), jnp.int32)],
        compiler_params=pltpu.CompilerParams(vmem_limit_bytes=2 * 1024 * 1024),
        cost_estimate=pl.CostEstimate(flops=10**9, bytes_accessed=10**6, transcendentals=0),
        name="choices",
    )(pair_ref)


def chunks_of(width):
    if width % 128 or width < 512:
        return [(0, rounded(width, 128))]
    first = rounded(width // 2, 256)
    return [(0, first), (first, width - first)]


def on_device(
    examples, references, gate_weight, up_weight, down_weight, cotangent, pair_ref, points
):
    dims = factors(lax.axis_size("wide"))
    far, near, pair = dims
    peers = lax.axis_size("narrow")
    e, r, k = examples.shape[0], references.shape[0], cotangent.shape[0]
    depth, hidden = gate_weight.shape
    blocks = far * near * pair

    share = hidden // peers
    whole_weights = [gate_weight, up_weight, down_weight]
    aligned = share % 128 == 0
    ahead = aligned and peers == 2
    if aligned:
        whole_weights = [
            pltpu.with_memory_space_constraint(w, pltpu.MemorySpace.HBM) for w in whole_weights
        ]
    chunks = chunks_of(share)
    picks = choices(pair_ref, dims, e, r)

    def at_peer(steps, offset, width):
        if aligned:
            return whole_weights, (steps % peers, peers, share, offset)
        start = (lax.axis_index("narrow") + steps) % peers * share
        more = width - share

        def cut(weight, axis):
            piece = lax.dynamic_slice_in_dim(weight, start, share, axis)
            return jnp.pad(piece, [(0, more if d == axis else 0) for d in range(2)])

        return [cut(gate_weight, 1), cut(up_weight, 1), cut(down_weight, 0)], None

    own, whole, pieces = pack([references, examples, cotangent])
    column = [own]
    for s in range(1, far):
        column.append(shift_permute(own, "wide", dims, 0, s))
    plane = list(column)
    for b in range(1, near):
        for block in column:
            plane.append(shift_permute(block, "wide", dims, 1, b))
    half = assemble(plane, whole, pieces, (r, e, k), depth)
    halves = [half] + [shift_permute(half, "wide", dims, 2, b) for b in range(1, pair)]
    main, side = join(halves, (r, e, k))

    blocks_of_weights = {}
    later = None
    if ahead:
        wanted = [(s, chunk) for s in (1, 0) for chunk in chunks]
        for s, chunk in wanted:
            if len(chunks) == 2 and (s, chunk) == (0, chunks[0]):
                later = (s, chunk)
                continue
            blocks_of_weights[s, chunk[0]] = fetch(*at_peer(s, *chunk), chunk[1])

    parts = []
    for i, (offset, width) in enumerate(chunks):
        received = []
        for s in range(1, peers):
            weights, place = at_peer(s, offset, width)
            next_one = None
            if ahead:
                weights = blocks_of_weights[s, offset]
                if later is not None and i == 1:
                    next_one = (*at_peer(later[0], *later[1]), later[1][1])
            sent, *more = forward(main, side, weights, place, width, jnp.bfloat16, next_one)
            if more:
                blocks_of_weights[later[0], later[1][0]] = more
            received.append(shift_permute(sent, "narrow", (peers,), 0, s))
        parts.append((offset, width, received))

    jobs = []
    for offset, width, received in parts:
        weights, place = at_peer(0, offset, width)
        if ahead:
            weights = blocks_of_weights[0, offset]
        (kept,) = forward(main, side, weights, place, width, jnp.float32)
        grads = coefficients(kept, received, picks, points, blocks * e)
        jobs.append((grads, offset, width, 0))
        jobs += [
            (shift_permute(grads, "narrow", (peers,), 0, s), offset, width, s) for s in range(1, peers)
        ]
    jobs.sort(key=lambda job: job[3])
    total = None
    for i, (grads, offset, width, s) in enumerate(jobs):
        weights, place = at_peer(peers - s, offset, width)
        weights = blocks_of_weights[s, offset][:1] if ahead else weights[:2]
        total = backward(grads, weights, place, total, i == len(jobs) - 1 and pair == 2)

    if pair == 2:
        sent, kept = total
        total = kept + shift_permute(sent, "wide", dims, 2, 1).astype(jnp.float32)
    if near == 2:
        half = total.shape[0] // 2
        sent = total[half:].astype(jnp.bfloat16)
        total = total[:half] + shift_permute(sent, "wide", dims, 1, 1).astype(jnp.float32)
    result = total[:e]
    got = [
        shift_permute(total[s * e:(s + 1) * e].astype(jnp.bfloat16), "wide", dims, 0, far - s)
        for s in range(1, far)
    ]
    for piece in got:
        result = result + piece.astype(jnp.float32)
    return result.astype(jnp.bfloat16)


def solution(mesh):
    in_specs = (
        P("wide", "narrow"),
        P("wide", "narrow"),
        P("narrow", "wide"),
        P("narrow", "wide"),
        P("wide", "narrow"),
        P("wide", "narrow"),
        P(),
        P(),
    )
    out_specs = P("wide", "narrow")
    return jax.shard_map(on_device, mesh=mesh, in_specs=in_specs, out_specs=out_specs, check_vma=False)
```

profile of v0, /device:TPU:0, one launch (start us, length us, event | category | flops | bytes accessed | tf_op | source)
XLA Modules:
  0.0 99.9 jit_solution(11688562838580854396)
XLA Ops:
  0.0 0.9 slice.29
  0.9 0.9 fusion.refs_0_
  1.8 3.1 %collective-permute-start = (bf16[16,4608]{1,0:T(8,128)(2,1)S(1)}, bf16[16,4608]{1,0:T(8,128)(2,1)S(1)}, u32[]{:S(2)}, u32[]{:S(2)}) collective-permute-start(bf16[16,4608]{1,0:T(8,128)(2,1)S(1)} %fusion.refs_0_), channel_id=1, source_target_pairs={{0,8},{2,10},{4,12},{6,14},{8,16},{10,18},{12,20},{14,22},{16,24},... | collective-permute-start | bytes 442376 | tf_op jit(solution)/shard_map/ppermute | solution.py:37
  4.9 2.6 %collective-permute-start.1 = (bf16[16,4608]{1,0:T(8,128)(2,1)S(1)}, bf16[16,4608]{1,0:T(8,128)(2,1)S(1)}, u32[]{:S(2)}, u32[]{:S(2)}) collective-permute-start(bf16[16,4608]{1,0:T(8,128)(2,1)S(1)} %fusion.refs_0_), channel_id=1, source_target_pairs={{0,16},{2,18},{4,20},{6,22},{8,24},{10,26},{12,28},{14,30},{16,0},... | collective-permute-start | bytes 442376 | tf_op jit(solution)/shard_map/ppermute | solution.py:37
  7.5 1.3 %collective-permute-start.2 = (bf16[16,4608]{1,0:T(8,128)(2,1)S(1)}, bf16[16,4608]{1,0:T(8,128)(2,1)S(1)}, u32[]{:S(2)}, u32[]{:S(2)}) collective-permute-start(bf16[16,4608]{1,0:T(8,128)(2,1)S(1)} %fusion.refs_0_), channel_id=1, source_target_pairs={{0,24},{2,26},{4,28},{6,30},{8,0},{10,2},{12,4},{14,6},{16,8},{18,... | collective-permute-start | bytes 442376 | tf_op jit(solution)/shard_map/ppermute | solution.py:37
  8.9 1.5 %collective-permute-start.3 = (bf16[16,4608]{1,0:T(8,128)(2,1)S(1)}, bf16[16,4608]{1,0:T(8,128)(2,1)S(1)}, u32[]{:S(2)}, u32[]{:S(2)}) collective-permute-start(bf16[16,4608]{1,0:T(8,128)(2,1)S(1)} %fusion.refs_0_), channel_id=1, source_target_pairs={{0,4},{2,6},{4,0},{6,2},{8,12},{10,14},{12,8},{14,10},{16,20},{18,... | collective-permute-start | bytes 442376 | tf_op jit(solution)/shard_map/ppermute | solution.py:37
  10.4 1.4 %collective-permute-done.refs_1_ = bf16[16,4608]{1,0:T(8,128)(2,1)S(1)} collective-permute-done((bf16[16,4608]{1,0:T(8,128)(2,1)S(1)}, bf16[16,4608]{1,0:T(8,128)(2,1)S(1)}, u32[]{:S(2)}, u32[]{:S(2)}) %collective-permute-start) | collective-permute-done | bytes 147488 | tf_op jit(solution)/shard_map/ppermute | solution.py:37
  11.8 1.7 %collective-permute-start.4 = (bf16[16,4608]{1,0:T(8,128)(2,1)S(1)}, bf16[16,4608]{1,0:T(8,128)(2,1)S(1)}, u32[]{:S(2)}, u32[]{:S(2)}) collective-permute-start(bf16[16,4608]{1,0:T(8,128)(2,1)S(1)} %collective-permute-done.refs_1_), channel_id=1, source_target_pairs={{0,4},{2,6},{4,0},{6,2},{8,12},{10,14},{12,8},{14,10},{16,20},{18,... | collective-permute-start | bytes 442376 | tf_op jit(solution)/shard_map/ppermute | solution.py:37
  13.5 3.7 %collective-permute-done.1.refs_2_ = bf16[16,4608]{1,0:T(8,128)(2,1)S(1)} collective-permute-done((bf16[16,4608]{1,0:T(8,128)(2,1)S(1)}, bf16[16,4608]{1,0:T(8,128)(2,1)S(1)}, u32[]{:S(2)}, u32[]{:S(2)}) %collective-permute-start.1) | collective-permute-done | bytes 147488 | tf_op jit(solution)/shard_map/ppermute | solution.py:37
  17.2 1.5 %collective-permute-start.5 = (bf16[16,4608]{1,0:T(8,128)(2,1)S(1)}, bf16[16,4608]{1,0:T(8,128)(2,1)S(1)}, u32[]{:S(2)}, u32[]{:S(2)}) collective-permute-start(bf16[16,4608]{1,0:T(8,128)(2,1)S(1)} %collective-permute-done.1.refs_2_), channel_id=1, source_target_pairs={{0,4},{2,6},{4,0},{6,2},{8,12},{10,14},{12,8},{14,10},{16,20},{18,... | collective-permute-start | bytes 442376 | tf_op jit(solution)/shard_map/ppermute | solution.py:37
  18.7 0.5 collective-permute-start.6
  19.3 4.7 %collective-permute-done.5.refs_6_ = bf16[16,4608]{1,0:T(8,128)(2,1)S(1)} collective-permute-done((bf16[16,4608]{1,0:T(8,128)(2,1)S(1)}, bf16[16,4608]{1,0:T(8,128)(2,1)S(1)}, u32[]{:S(2)}, u32[]{:S(2)}) %collective-permute-start.5) | collective-permute-done | bytes 147488 | tf_op jit(solution)/shard_map/ppermute | solution.py:37
  23.9 2.1 %collective-permute-done.6.refs_7_ = bf16[16,4608]{1,0:T(8,128)(2,1)S(1)} collective-permute-done((bf16[16,4608]{1,0:T(8,128)(2,1)S(1)}, bf16[16,4608]{1,0:T(8,128)(2,1)S(1)}, u32[]{:S(2)}, u32[]{:S(2)}) %collective-permute-start.6) | collective-permute-done | bytes 147488 | tf_op jit(solution)/shard_map/ppermute | solution.py:37
  26.1 0.8 assemble.1.refs_0_
  26.8 0.1 collective-permute-start.7
  26.9 0.8 copy.9.pair_ref
  27.7 3.9 %fetch.4 = (bf16[4096,768]{1,0:T(8,128)(2,1)S(1)}, bf16[384,4096]{1,0:T(8,128)(2,1)S(1)}) custom-call(bf16[4096,1792]{1,0:T(8,128)(2,1)} %gate.5, bf16[4096,1792]{1,0:T(8,128)(2,1)} %up.5, bf16[1792,4096]{1,0:T(8,128)(2,1)} %down.5), custom_call_target="tpu_custom_call" | custom-call | flops 4000000000 | bytes 9437184 | tf_op jit(solution)/shard_map/fetch/pallas_call | solution.py:190
  31.6 4.8 %fetch.5 = (bf16[4096,1024]{1,0:T(8,128)(2,1)S(1)}, bf16[512,4096]{1,0:T(8,128)(2,1)S(1)}) custom-call(bf16[4096,1792]{1,0:T(8,128)(2,1)} %gate.5, bf16[4096,1792]{1,0:T(8,128)(2,1)} %up.5, bf16[1792,4096]{1,0:T(8,128)(2,1)} %down.5), custom_call_target="tpu_custom_call" | custom-call | flops 4000000000 | bytes 12582912 | tf_op jit(solution)/shard_map/fetch/pallas_call | solution.py:190
  36.3 3.9 %fetch.3 = (bf16[4096,768]{1,0:T(8,128)(2,1)S(1)}, bf16[384,4096]{1,0:T(8,128)(2,1)S(1)}) custom-call(bf16[4096,1792]{1,0:T(8,128)(2,1)} %gate.5, bf16[4096,1792]{1,0:T(8,128)(2,1)} %up.5, bf16[1792,4096]{1,0:T(8,128)(2,1)} %down.5), custom_call_target="tpu_custom_call" | custom-call | flops 4000000000 | bytes 9437184 | tf_op jit(solution)/shard_map/fetch/pallas_call | solution.py:190
  40.2 0.2 join.1
  40.4 3.2 %forward.7 = bf16[248,1024]{1,0:T(8,128)(2,1)S(1)} custom-call(bf16[208,4096]{1,0:T(8,128)(2,1)S(1)} %get-tuple-element.18.main_ref, bf16[80,4096]{1,0:T(8,128)(2,1)S(1)} %get-tuple-element.19.side_ref, bf16[4096,1024]{1,0:T(8,128)(2,1)S(1)} %get-tuple-element.27.both.refs_0_, bf16[512,4096]{1,0:T(8,128)(2,1)S(1)} %get-tuple-element.28.below), custom_call_target="tpu_custom_call" | custom-call | flops 2080374784 | bytes 12582912 | tf_op jit(solution)/shard_map/forward/pallas_call | solution.py:278
  43.6 1.6 %collective-permute-start.10 = (bf16[248,1024]{1,0:T(8,128)(2,1)S(1)}, bf16[248,1024]{1,0:T(8,128)(2,1)S(1)}, u32[]{:S(2)}, u32[]{:S(2)}) collective-permute-start(bf16[248,1024]{1,0:T(8,128)(2,1)S(1)} %forward.7), channel_id=1, source_target_pairs={{0,1},{1,0},{2,3},{3,2},{4,5},{5,4},{6,7},{7,6},{8,9},{9,8},{10,11... | collective-permute-start | bytes 1523720 | tf_op jit(solution)/shard_map/ppermute | solution.py:37
  45.2 0.1 choices.1.picks_ref
  45.4 7.1 %forward.5 = (bf16[248,768]{1,0:T(8,128)(2,1)S(1)}, bf16[4096,1024]{1,0:T(8,128)(2,1)S(1)}, bf16[512,4096]{1,0:T(8,128)(2,1)S(1)}) custom-call(bf16[208,4096]{1,0:T(8,128)(2,1)S(1)} %get-tuple-element.18.main_ref, bf16[80,4096]{1,0:T(8,128)(2,1)S(1)} %get-tuple-element.19.side_ref, bf16[4096,768]{1,0:T(8,128)(2,1)S(1)} %get-tuple-element.22.both.refs_0_, ...), custom_call_target="tpu_custom_call" | custom-call | flops 1560281088 | bytes 9437184 | tf_op jit(solution)/shard_map/forward/pallas_call | solution.py:278
  52.5 0.5 collective-permute-start.8
  53.0 2.4 %forward.4.kept_ref = f32[248,768]{1,0:T(8,128)S(1)} custom-call(bf16[208,4096]{1,0:T(8,128)(2,1)S(1)} %get-tuple-element.18.main_ref, bf16[80,4096]{1,0:T(8,128)(2,1)S(1)} %get-tuple-element.19.side_ref, bf16[4096,768]{1,0:T(8,128)(2,1)S(1)} %get-tuple-element.20.both.refs_0_, bf16[384,4096]{1,0:T(8,128)(2,1)S(1)} %get-tuple-element.21.below), custom_call_target="tpu_custom_call" | custom-call | flops 1560281088 | bytes 9437184 | tf_op jit(solution)/shard_map/forward/pallas_call | solution.py:278
  55.4 3.2 %forward.6.kept_ref = f32[248,1024]{1,0:T(8,128)S(1)} custom-call(bf16[208,4096]{1,0:T(8,128)(2,1)S(1)} %get-tuple-element.18.main_ref, bf16[80,4096]{1,0:T(8,128)(2,1)S(1)} %get-tuple-element.19.side_ref, bf16[4096,1024]{1,0:T(8,128)(2,1)S(1)} %get-tuple-element.25.both.refs_0_, bf16[512,4096]{1,0:T(8,128)(2,1)S(1)} %get-tuple-element.26.below), custom_call_target="tpu_custom_call" | custom-call | flops 2080374784 | bytes 12582912 | tf_op jit(solution)/shard_map/forward/pallas_call | solution.py:278
  58.6 4.0 %coefficients.3.grads_ref = bf16[80,1024]{1,0:T(8,128)(2,1)S(1)} custom-call(s32[8]{0:T(128)S(1)} %copy-done, bf16[320,128]{1,0:T(8,128)(2,1)S(1)} %choices.1.picks_ref, f32[248,1024]{1,0:T(8,128)S(1)} %forward.6.kept_ref, bf16[248,1024]{1,0:T(8,128)(2,1)S(1)} %collective-permute-done.10.refs_0_), custom_call_target="tpu_custom_call" | custom-call | flops 5000000000 | bytes 1000000 | tf_op jit(solution)/shard_map/coefficients/pallas_call | solution.py:356
  62.6 1.7 %collective-permute-start.11 = (bf16[80,1024]{1,0:T(8,128)(2,1)S(1)}, bf16[80,1024]{1,0:T(8,128)(2,1)S(1)}, u32[]{:S(2)}, u32[]{:S(2)}) collective-permute-start(bf16[80,1024]{1,0:T(8,128)(2,1)S(1)} %coefficients.3.grads_ref), channel_id=1, source_target_pairs={{0,1},{1,0},{2,3},{3,2},{4,5},{5,4},{6,7},{7,6},{8,9},{9,8},{10,11... | collective-permute-start | bytes 491528 | tf_op jit(solution)/shard_map/ppermute | solution.py:37
  64.3 2.0 %collective-permute-done.8.refs_0_ = bf16[248,768]{1,0:T(8,128)(2,1)S(1)} collective-permute-done((bf16[248,768]{1,0:T(8,128)(2,1)S(1)}, bf16[248,768]{1,0:T(8,128)(2,1)S(1)}, u32[]{:S(2)}, u32[]{:S(2)}) %collective-permute-start.8) | collective-permute-done | bytes 380960 | tf_op jit(solution)/shard_map/ppermute | solution.py:37
  66.3 3.0 %coefficients.2.grads_ref = bf16[80,768]{1,0:T(8,128)(2,1)S(1)} custom-call(s32[8]{0:T(128)S(1)} %copy-done, bf16[320,128]{1,0:T(8,128)(2,1)S(1)} %choices.1.picks_ref, f32[248,768]{1,0:T(8,128)S(1)} %forward.4.kept_ref, bf16[248,768]{1,0:T(8,128)(2,1)S(1)} %collective-permute-done.8.refs_0_), custom_call_target="tpu_custom_call" | custom-call | flops 5000000000 | bytes 1000000 | tf_op jit(solution)/shard_map/coefficients/pallas_call | solution.py:356
  69.2 1.6 %collective-permute-start.9 = (bf16[80,768]{1,0:T(8,128)(2,1)S(1)}, bf16[80,768]{1,0:T(8,128)(2,1)S(1)}, u32[]{:S(2)}, u32[]{:S(2)}) collective-permute-start(bf16[80,768]{1,0:T(8,128)(2,1)S(1)} %coefficients.2.grads_ref), channel_id=1, source_target_pairs={{0,1},{1,0},{2,3},{3,2},{4,5},{5,4},{6,7},{7,6},{8,9},{9,8},{10,11... | collective-permute-start | bytes 368648 | tf_op jit(solution)/shard_map/ppermute | solution.py:37
  70.9 2.7 %backward.4.refs_1_ = f32[80,4096]{1,0:T(8,128)S(1)} custom-call(bf16[80,1024]{1,0:T(8,128)(2,1)S(1)} %coefficients.3.grads_ref, bf16[4096,1024]{1,0:T(8,128)(2,1)S(1)} %get-tuple-element.25.both.refs_0_), custom_call_target="tpu_custom_call" | custom-call | flops 671088640 | bytes 8388608 | tf_op jit(solution)/shard_map/backward/pallas_call | solution.py:412
  73.5 2.0 %backward.5.refs_1_ = f32[80,4096]{1,0:T(8,128)S(1)} custom-call(bf16[80,768]{1,0:T(8,128)(2,1)S(1)} %coefficients.2.grads_ref, bf16[4096,768]{1,0:T(8,128)(2,1)S(1)} %get-tuple-element.20.both.refs_0_, f32[80,4096]{1,0:T(8,128)S(1)} %backward.4.refs_1_), custom_call_target="tpu_custom_call" | custom-call | flops 503316480 | bytes 6291456 | tf_op jit(solution)/shard_map/backward/pallas_call | solution.py:412
  75.5 2.7 %backward.6.refs_1_ = f32[80,4096]{1,0:T(8,128)S(1)} custom-call(bf16[80,1024]{1,0:T(8,128)(2,1)S(1)} %collective-permute-done.11.grads_ref, bf16[4096,1024]{1,0:T(8,128)(2,1)S(1)} %get-tuple-element.27.both.refs_0_, f32[80,4096]{1,0:T(8,128)S(1)} %backward.5.refs_1_), custom_call_target="tpu_custom_call" | custom-call | flops 671088640 | bytes 8388608 | tf_op jit(solution)/shard_map/backward/pallas_call | solution.py:412
  78.2 2.0 %backward.7 = (bf16[40,4096]{1,0:T(8,128)(2,1)S(1)}, f32[40,4096]{1,0:T(8,128)S(1)}) custom-call(bf16[80,768]{1,0:T(8,128)(2,1)S(1)} %collective-permute-done.9.grads_ref, bf16[4096,768]{1,0:T(8,128)(2,1)S(1)} %get-tuple-element.22.both.refs_0_, f32[80,4096]{1,0:T(8,128)S(1)} %backward.6.refs_1_), custom_call_target="tpu_custom_call" | custom-call | flops 503316480 | bytes 6291456 | tf_op jit(solution)/shard_map/backward/pallas_call | solution.py:412
  80.3 0.1 collective-permute-start.12
  80.3 1.6 %collective-permute-done.12 = bf16[40,4096]{1,0:T(8,128)(2,1)S(1)} collective-permute-done((bf16[40,4096]{1,0:T(8,128)(2,1)S(1)}, bf16[40,4096]{1,0:T(8,128)(2,1)S(1)}, u32[]{:S(2)}, u32[]{:S(2)}) %collective-permute-start.12) | collective-permute-done | bytes 327712 | tf_op jit(solution)/shard_map/ppermute | solution.py:37
  82.0 0.1 convert_add_fusion
  82.1 1.6 %collective-permute-start.13 = (bf16[20,4096]{1,0:T(8,128)(2,1)S(1)}, bf16[20,4096]{1,0:T(8,128)(2,1)S(1)}, u32[]{:S(2)}, u32[]{:S(2)}) collective-permute-start(bf16[20,4096]{1,0:T(8,128)(2,1)S(1)} %slice.51), channel_id=1, source_target_pairs={{0,4},{2,6},{4,0},{6,2},{8,12},{10,14},{12,8},{14,10},{16,20},{18,... | collective-permute-start | bytes 491528 | tf_op jit(solution)/shard_map/ppermute | solution.py:37
  83.7 5.4 %collective-permute-done.13 = bf16[20,4096]{1,0:T(8,128)(2,1)S(1)} collective-permute-done((bf16[20,4096]{1,0:T(8,128)(2,1)S(1)}, bf16[20,4096]{1,0:T(8,128)(2,1)S(1)}, u32[]{:S(2)}, u32[]{:S(2)}) %collective-permute-start.13) | collective-permute-done | bytes 163872 | tf_op jit(solution)/shard_map/ppermute | solution.py:37
  89.2 3.8 %collective-permute-start.14 = (bf16[5,4096]{1,0:T(8,128)(2,1)S(1)}, bf16[5,4096]{1,0:T(8,128)(2,1)S(1)}, u32[]{:S(2)}, u32[]{:S(2)}) collective-permute-start(bf16[5,4096]{1,0:T(8,128)(2,1)S(1)} %get-tuple-element.33), channel_id=1, source_target_pairs={{0,24},{2,26},{4,28},{6,30},{8,0},{10,2},{12,4},{14,6},{16,8},{18,... | collective-permute-start | bytes 122888 | tf_op jit(solution)/shard_map/ppermute | solution.py:37
  93.0 0.2 collective-permute-start.15
  93.2 0.8 collective-permute-start.16
  94.0 1.2 %collective-permute-done.14 = bf16[5,4096]{1,0:T(8,128)(2,1)S(1)} collective-permute-done((bf16[5,4096]{1,0:T(8,128)(2,1)S(1)}, bf16[5,4096]{1,0:T(8,128)(2,1)S(1)}, u32[]{:S(2)}, u32[]{:S(2)}) %collective-permute-start.14) | collective-permute-done | bytes 40992 | tf_op jit(solution)/shard_map/ppermute | solution.py:37
  95.2 3.1 %collective-permute-done.15 = bf16[5,4096]{1,0:T(8,128)(2,1)S(1)} collective-permute-done((bf16[5,4096]{1,0:T(8,128)(2,1)S(1)}, bf16[5,4096]{1,0:T(8,128)(2,1)S(1)}, u32[]{:S(2)}, u32[]{:S(2)}) %collective-permute-start.15) | collective-permute-done | bytes 40992 | tf_op jit(solution)/shard_map/ppermute | solution.py:37
  98.3 0.9 collective-permute-done.16
  99.2 0.7 fusion.3
  (13 shorter events, 0.2 us)
Async XLA Ops:
  1.8 9.9 %collective-permute-start = (bf16[16,4608]{1,0:T(8,128)(2,1)S(1)}, bf16[16,4608]{1,0:T(8,128)(2,1)S(1)}, u32[]{:S(2)}, u32[]{:S(2)}) collective-permute-start(bf16[16,4608]{1,0:T(8,128)(2,1)S(1)} %fusion.refs_0_), channel_id=1, source_target_pairs={{0,8},{2,10},{4,12},{6,14},{8,16},{10,18},{12,20},{14,22},{16,24},... | collective-permute-start | bytes 442376 | tf_op jit(solution)/shard_map/ppermute | solution.py:37
  4.9 12.3 %collective-permute-start.1 = (bf16[16,4608]{1,0:T(8,128)(2,1)S(1)}, bf16[16,4608]{1,0:T(8,128)(2,1)S(1)}, u32[]{:S(2)}, u32[]{:S(2)}) collective-permute-start(bf16[16,4608]{1,0:T(8,128)(2,1)S(1)} %fusion.refs_0_), channel_id=1, source_target_pairs={{0,16},{2,18},{4,20},{6,22},{8,24},{10,26},{12,28},{14,30},{16,0},... | collective-permute-start | bytes 442376 | tf_op jit(solution)/shard_map/ppermute | solution.py:37
  7.5 11.2 %collective-permute-start.2 = (bf16[16,4608]{1,0:T(8,128)(2,1)S(1)}, bf16[16,4608]{1,0:T(8,128)(2,1)S(1)}, u32[]{:S(2)}, u32[]{:S(2)}) collective-permute-start(bf16[16,4608]{1,0:T(8,128)(2,1)S(1)} %fusion.refs_0_), channel_id=1, source_target_pairs={{0,24},{2,26},{4,28},{6,30},{8,0},{10,2},{12,4},{14,6},{16,8},{18,... | collective-permute-start | bytes 442376 | tf_op jit(solution)/shard_map/ppermute | solution.py:37
  8.9 10.4 %collective-permute-start.3 = (bf16[16,4608]{1,0:T(8,128)(2,1)S(1)}, bf16[16,4608]{1,0:T(8,128)(2,1)S(1)}, u32[]{:S(2)}, u32[]{:S(2)}) collective-permute-start(bf16[16,4608]{1,0:T(8,128)(2,1)S(1)} %fusion.refs_0_), channel_id=1, source_target_pairs={{0,4},{2,6},{4,0},{6,2},{8,12},{10,14},{12,8},{14,10},{16,20},{18,... | collective-permute-start | bytes 442376 | tf_op jit(solution)/shard_map/ppermute | solution.py:37
  11.8 7.5 %collective-permute-start.4 = (bf16[16,4608]{1,0:T(8,128)(2,1)S(1)}, bf16[16,4608]{1,0:T(8,128)(2,1)S(1)}, u32[]{:S(2)}, u32[]{:S(2)}) collective-permute-start(bf16[16,4608]{1,0:T(8,128)(2,1)S(1)} %collective-permute-done.refs_1_), channel_id=1, source_target_pairs={{0,4},{2,6},{4,0},{6,2},{8,12},{10,14},{12,8},{14,10},{16,20},{18,... | collective-permute-start | bytes 442376 | tf_op jit(solution)/shard_map/ppermute | solution.py:37
  17.2 6.7 %collective-permute-start.5 = (bf16[16,4608]{1,0:T(8,128)(2,1)S(1)}, bf16[16,4608]{1,0:T(8,128)(2,1)S(1)}, u32[]{:S(2)}, u32[]{:S(2)}) collective-permute-start(bf16[16,4608]{1,0:T(8,128)(2,1)S(1)} %collective-permute-done.1.refs_2_), channel_id=1, source_target_pairs={{0,4},{2,6},{4,0},{6,2},{8,12},{10,14},{12,8},{14,10},{16,20},{18,... | collective-permute-start | bytes 442376 | tf_op jit(solution)/shard_map/ppermute | solution.py:37
  18.7 7.3 %collective-permute-start.6 = (bf16[16,4608]{1,0:T(8,128)(2,1)S(1)}, bf16[16,4608]{1,0:T(8,128)(2,1)S(1)}, u32[]{:S(2)}, u32[]{:S(2)}) collective-permute-start(bf16[16,4608]{1,0:T(8,128)(2,1)S(1)} %collective-permute-done.2.refs_3_), channel_id=1, source_target_pairs={{0,4},{2,6},{4,0},{6,2},{8,12},{10,14},{12,8},{14,10},{16,20},{18,... | collective-permute-start | bytes 442376 | tf_op jit(solution)/shard_map/ppermute | solution.py:37
  26.8 13.4 %collective-permute-start.7 = (bf16[144,4096]{1,0:T(8,128)(2,1)S(1)}, bf16[144,4096]{1,0:T(8,128)(2,1)S(1)}, u32[]{:S(2)}, u32[]{:S(2)}) collective-permute-start(bf16[144,4096]{1,0:T(8,128)(2,1)S(1)} %assemble.1.refs_0_), channel_id=1, source_target_pairs={{0,2},{2,0},{4,6},{6,4},{8,10},{10,8},{12,14},{14,12},{16,18},{18,... | collective-permute-start | bytes 3538952 | tf_op jit(solution)/shard_map/ppermute | solution.py:37
  43.6 15.0 %collective-permute-start.10 = (bf16[248,1024]{1,0:T(8,128)(2,1)S(1)}, bf16[248,1024]{1,0:T(8,128)(2,1)S(1)}, u32[]{:S(2)}, u32[]{:S(2)}) collective-permute-start(bf16[248,1024]{1,0:T(8,128)(2,1)S(1)} %forward.7), channel_id=1, source_target_pairs={{0,1},{1,0},{2,3},{3,2},{4,5},{5,4},{6,7},{7,6},{8,9},{9,8},{10,11... | collective-permute-start | bytes 1523720 | tf_op jit(solution)/shard_map/ppermute | solution.py:37
  52.5 13.8 %collective-permute-start.8 = (bf16[248,768]{1,0:T(8,128)(2,1)S(1)}, bf16[248,768]{1,0:T(8,128)(2,1)S(1)}, u32[]{:S(2)}, u32[]{:S(2)}) collective-permute-start(bf16[248,768]{1,0:T(8,128)(2,1)S(1)} %get-tuple-element.24), channel_id=1, source_target_pairs={{0,1},{1,0},{2,3},{3,2},{4,5},{5,4},{6,7},{7,6},{8,9},{9,8},{10,11... | collective-permute-start | bytes 1142792 | tf_op jit(solution)/shard_map/ppermute | solution.py:37
  55.4 3.2 %copy-start = (s32[8]{0:T(128)S(1)}, s32[8]{0:T(128)}, u32[]{:S(2)}) copy-start(s32[8]{0:T(128)} %points_ref.3) | copy-start | bytes 100
  62.6 12.9 %collective-permute-start.11 = (bf16[80,1024]{1,0:T(8,128)(2,1)S(1)}, bf16[80,1024]{1,0:T(8,128)(2,1)S(1)}, u32[]{:S(2)}, u32[]{:S(2)}) collective-permute-start(bf16[80,1024]{1,0:T(8,128)(2,1)S(1)} %coefficients.3.grads_ref), channel_id=1, source_target_pairs={{0,1},{1,0},{2,3},{3,2},{4,5},{5,4},{6,7},{7,6},{8,9},{9,8},{10,11... | collective-permute-start | bytes 491528 | tf_op jit(solution)/shard_map/ppermute | solution.py:37
  69.2 9.0 %collective-permute-start.9 = (bf16[80,768]{1,0:T(8,128)(2,1)S(1)}, bf16[80,768]{1,0:T(8,128)(2,1)S(1)}, u32[]{:S(2)}, u32[]{:S(2)}) collective-permute-start(bf16[80,768]{1,0:T(8,128)(2,1)S(1)} %coefficients.2.grads_ref), channel_id=1, source_target_pairs={{0,1},{1,0},{2,3},{3,2},{4,5},{5,4},{6,7},{7,6},{8,9},{9,8},{10,11... | collective-permute-start | bytes 368648 | tf_op jit(solution)/shard_map/ppermute | solution.py:37
  80.3 1.7 %collective-permute-start.12 = (bf16[40,4096]{1,0:T(8,128)(2,1)S(1)}, bf16[40,4096]{1,0:T(8,128)(2,1)S(1)}, u32[]{:S(2)}, u32[]{:S(2)}) collective-permute-start(bf16[40,4096]{1,0:T(8,128)(2,1)S(1)} %get-tuple-element.30), channel_id=1, source_target_pairs={{0,2},{2,0},{4,6},{6,4},{8,10},{10,8},{12,14},{14,12},{16,18},{18,... | collective-permute-start | bytes 983048 | tf_op jit(solution)/shard_map/ppermute | solution.py:37
  82.1 7.0 %collective-permute-start.13 = (bf16[20,4096]{1,0:T(8,128)(2,1)S(1)}, bf16[20,4096]{1,0:T(8,128)(2,1)S(1)}, u32[]{:S(2)}, u32[]{:S(2)}) collective-permute-start(bf16[20,4096]{1,0:T(8,128)(2,1)S(1)} %slice.51), channel_id=1, source_target_pairs={{0,4},{2,6},{4,0},{6,2},{8,12},{10,14},{12,8},{14,10},{16,20},{18,... | collective-permute-start | bytes 491528 | tf_op jit(solution)/shard_map/ppermute | solution.py:37
  89.2 6.0 %collective-permute-start.14 = (bf16[5,4096]{1,0:T(8,128)(2,1)S(1)}, bf16[5,4096]{1,0:T(8,128)(2,1)S(1)}, u32[]{:S(2)}, u32[]{:S(2)}) collective-permute-start(bf16[5,4096]{1,0:T(8,128)(2,1)S(1)} %get-tuple-element.33), channel_id=1, source_target_pairs={{0,24},{2,26},{4,28},{6,30},{8,0},{10,2},{12,4},{14,6},{16,8},{18,... | collective-permute-start | bytes 122888 | tf_op jit(solution)/shard_map/ppermute | solution.py:37
  93.0 5.3 %collective-permute-start.15 = (bf16[5,4096]{1,0:T(8,128)(2,1)S(1)}, bf16[5,4096]{1,0:T(8,128)(2,1)S(1)}, u32[]{:S(2)}, u32[]{:S(2)}) collective-permute-start(bf16[5,4096]{1,0:T(8,128)(2,1)S(1)} %get-tuple-element.35), channel_id=1, source_target_pairs={{0,16},{2,18},{4,20},{6,22},{8,24},{10,26},{12,28},{14,30},{16,0},... | collective-permute-start | bytes 122888 | tf_op jit(solution)/shard_map/ppermute | solution.py:37
  93.2 6.1 %collective-permute-start.16 = (bf16[5,4096]{1,0:T(8,128)(2,1)S(1)}, bf16[5,4096]{1,0:T(8,128)(2,1)S(1)}, u32[]{:S(2)}, u32[]{:S(2)}) collective-permute-start(bf16[5,4096]{1,0:T(8,128)(2,1)S(1)} %get-tuple-element.34), channel_id=1, source_target_pairs={{0,8},{2,10},{4,12},{6,14},{8,16},{10,18},{12,20},{14,22},{16,24},... | collective-permute-start | bytes 122888 | tf_op jit(solution)/shard_map/ppermute | solution.py:37
where the time goes:
time: 100 us; the launch traced here: 99.9 us
  Pallas kernels  45.8 us (46%)
  waiting for transfers between devices  26.2 us (26%)
  starting transfers between devices  24.3 us (24%)
  local copies, waits for them, and re-layouts  1.74 us (2%)
  other arithmetic  1.71 us (2%)
    ppermute x17, waiting for transfers between devices, shift_permute(): return lax.ppermute(array, axis, pairs)  26.2 us
    ppermute x17, starting transfers between devices, shift_permute(): return lax.ppermute(array, axis, pairs)  24.3 us
    pallas_call x4, Pallas kernels, forward(): pl.pallas_call(body_ready if ready else body, out_shape=out_shape, in_spe...  15.9 us
    pallas_call x3, Pallas kernels, fetch(): pl.pallas_call(body, out_shape=(pltpu.VMEM((depth, 2 * width), jnp.bfloat...  12.5 us
    pallas_call x4, Pallas kernels, backward(): pl.pallas_call(body, out_shape=out_shape, in_specs=specs, out_specs=out_s...  9.39 us
    pallas_call x2, Pallas kernels, coefficients(): pl.pallas_call(body, out_shape=jax.ShapeDtypeStruct((examples, 2 * width)...  6.94 us
  transfers between devices with their start and end apart: 17, of which 10 were waited for; matrix products, arithmetic and copies ran while one was open for 1% of the time, Pallas kernels for 40%

commit v1 on v0

--- a/solution.py
+++ b/solution.py
@@ -21,34 +21,75 @@
     return -(-rows // unit) * unit
 
 
-def shift_permute(array, axis, dims, digit, amount):
+def permute(array, axis, dims, digit, amount):
     below = 1
     for size in dims[digit + 1:]:
         below *= size
-    size = dims[digit]
-    total = below * size
-    for d in dims[:digit]:
-        total *= d
-    pairs = []
-    for at in range(total):
-        own = (at // below) % size
-        to = (own + amount) % size
-        pairs.append((at, at + (to - own) * below))
+    total = below
+    for size in dims[:digit + 1]:
+        total *= size
+    pairs = [
+        (at, at + (((at // below) % dims[digit] ^ amount) - (at // below) % dims[digit]) * below)
+        for at in range(total)
+    ]
     return lax.ppermute(array, axis, pairs)
 
 
+def shift(array, size, amount):
+    return lax.ppermute(array, "narrow", [(at, (at + amount) % size) for at in range(size)])
+
+
+def halvings(size):
+    if size == 1:
+        return [0]
+    return [2 * v for v in halvings(size // 2)] + [2 * v + 1 for v in halvings(size // 2)]
+
+
 def pack(arrays):
-    rows = jnp.concatenate(arrays)
-    count, width = rows.shape
+    count, width = sum(a.shape[0] for a in arrays), arrays[0].shape[1]
     whole = count // 8 * 8
     rest = count - whole
-    if rest == 0:
-        return rows, whole, 1
-    pieces = whole // rest if whole else 0
-    if not pieces or whole % rest or width % (pieces * 128):
-        return jnp.pad(rows, ((0, 8 - rest), (0, 0))), whole + 8, 1
-    cut = rows[whole:].reshape(rest * pieces, width // pieces)
-    return jnp.concatenate([rows[:whole], cut], axis=1), whole, pieces
+    pieces = whole // rest if rest and whole else 1
+    cut = rest > 0 and whole > 0 and whole % rest == 0 and width % (pieces * 128) == 0
+    if not cut:
+        whole, pieces = rounded(count, 8), 1
+    lanes = width // pieces
+
+    def body(*refs):
+        sources, (out, *held, sems) = refs[:len(arrays)], refs[len(arrays):]
+        copies = [
+            pltpu.make_async_copy(source, target, sems.at[i])
+            for i, (source, target) in enumerate(zip(sources, held))
+        ]
+        for copy in copies:
+            copy.start()
+        for copy in copies:
+            copy.wait()
+        rows = jnp.concatenate([ref[...].astype(jnp.float32) for ref in held])
+        if not cut:
+            if whole > count:
+                rows = jnp.concatenate([rows, jnp.zeros((whole - count, width), jnp.float32)])
+            out[...] = rows.astype(out.dtype)
+            return
+        out[:, pl.ds(0, width)] = rows[:whole].astype(out.dtype)
+        beside = [
+            rows[whole + i:whole + i + 1, j * lanes:(j + 1) * lanes]
+            for i in range(rest)
+            for j in range(pieces)
+        ]
+        out[:, pl.ds(width, lanes)] = jnp.concatenate(beside).astype(out.dtype)
+
+    packed = pl.pallas_call(
+        body,
+        out_shape=jax.ShapeDtypeStruct((whole, width + lanes if cut else width), arrays[0].dtype),
+        in_specs=[ANY] * len(arrays),
+        out_specs=VMEM,
+        scratch_shapes=[pltpu.VMEM(a.shape, a.dtype) for a in arrays]
+        + [pltpu.SemaphoreType.DMA((len(arrays),))],
+        compiler_params=pltpu.CompilerParams(vmem_limit_bytes=4 * 1024 * 1024),
+        name="pack",
+    )(*(pltpu.with_memory_space_constraint(a, pltpu.MemorySpace.HBM) for a in arrays))
+    return packed, whole, pieces
 
 
 def assemble(own, whole, pieces, counts, width):
@@ -365,11 +406,12 @@
     )(points, picks, kept, *received)
 
 
-def backward(grads, weights, place, total, final):
+def backward(grads, weights, place, total, final, span=None):
     rows = grads.shape[0]
     width = grads.shape[1] // 2
     depth = weights[0].shape[0]
-    by_depth = parts_of(depth, 128)
+    low, columns = span or (0, depth)
+    by_depth = [(low + row, count) for row, count in parts_of(columns, 128)]
     ready = len(weights) == 1
 
     def body(grads_ref, *refs):
@@ -382,7 +424,7 @@
                 for copy in pair:
                     copy.start()
         for i, (row, count) in enumerate(by_depth):
-            some = pl.ds(row, count)
+            some, own = pl.ds(row, count), pl.ds(row - low, count)
             if not ready:
                 for copy in depths[i]:
                     copy.wait()
@@ -390,10 +432,10 @@
             if total is not None:
                 value = value + outs[0][:, some]
             if final:
-                outs[-2][:, some] = value[rows // 2:, :].astype(jnp.bfloat16)
-                outs[-1][:, some] = value[:rows // 2, :]
+                outs[-2][:, own] = value[rows // 2:, :].astype(jnp.bfloat16)
+                outs[-1][:, own] = value[:rows // 2, :]
             else:
-                outs[-1][:, some] = value
+                outs[-1][:, own] = value
 
     operands = [grads, *weights]
     specs = [VMEM] + [VMEM if ready else ANY] * len(weights)
@@ -402,12 +444,12 @@
         specs.append(VMEM)
     if final:
         out_shape = (
-            jax.ShapeDtypeStruct((rows // 2, depth), jnp.bfloat16),
-            jax.ShapeDtypeStruct((rows // 2, depth), jnp.float32),
+            jax.ShapeDtypeStruct((rows // 2, columns), jnp.bfloat16),
+            jax.ShapeDtypeStruct((rows // 2, columns), jnp.float32),
         )
         out_specs = (VMEM, VMEM)
     else:
-        out_shape, out_specs = jax.ShapeDtypeStruct((rows, depth), jnp.float32), VMEM
+        out_shape, out_specs = jax.ShapeDtypeStruct((rows, columns), jnp.float32), VMEM
     scratch = [pltpu.VMEM((depth, 2 * width), jnp.bfloat16), pltpu.SemaphoreType.DMA((2, 4))]
     return pl.pallas_call(
         body,
@@ -417,7 +459,7 @@
         scratch_shapes=[] if ready else scratch,
         compiler_params=pltpu.CompilerParams(vmem_limit_bytes=(4 if ready else 12) * 1024 * 1024),
         cost_estimate=pl.CostEstimate(
-            flops=4 * rows * width * depth, bytes_accessed=4 * width * depth, transcendentals=0
+            flops=4 * rows * width * columns, bytes_accessed=4 * width * columns, transcendentals=0
         ),
         name="backward",
     )(*operands)
@@ -434,8 +476,8 @@
         col = lax.broadcasted_iota(jnp.int32, (examples, blocks * r), 1)
         name = jnp.zeros_like(col)
         for q in range(blocks):
-            s, b, p = q % far, q // far % near, q // (far * near)
-            owner = ((z + far - s) % far * near + (y + near - b) % near) * pair + (c + pair - p) % pair
+            s, b, p = halvings(far)[q % far], q // far % near, q // (far * near)
+            owner = ((z ^ s) * near + (y ^ b)) * pair + (c ^ p)
             rows[pl.ds(q * e, e), :] = pair_ref[pl.ds(owner * e, e), :]
             name = jnp.where((col >= q * r) & (col < (q + 1) * r), owner * r + col - q * r, name)
         for p in range(pairs):
@@ -458,8 +500,8 @@
 def chunks_of(width):
     if width % 128 or width < 512:
         return [(0, rounded(width, 128))]
-    first = rounded(width // 2, 256)
-    return [(0, first), (first, width - first)]
+    last = max(256, width // 4 // 256 * 256)
+    return [(0, width - last), (width - last, last)]
 
 
 def on_device(
@@ -496,15 +538,22 @@
         return [cut(gate_weight, 1), cut(up_weight, 1), cut(down_weight, 0)], None
 
     own, whole, pieces = pack([references, examples, cotangent])
-    column = [own]
-    for s in range(1, far):
-        column.append(shift_permute(own, "wide", dims, 0, s))
-    plane = list(column)
-    for b in range(1, near):
-        for block in column:
-            plane.append(shift_permute(block, "wide", dims, 1, b))
+    column = {0: own}
+    step = far // 2
+    while step:
+        for s in sorted(column):
+            column[s + step] = permute(column[s], "wide", dims, 0, step)
+        step //= 2
+    beside = {}
+    if near == 2:
+        for s, block in column.items():
+            beside[s] = permute(block, "wide", dims, 1, 1)
+    order = halvings(far)
+    plane = [column[s] for s in order] + [beside[s] for s in order if near == 2]
     half = assemble(plane, whole, pieces, (r, e, k), depth)
-    halves = [half] + [shift_permute(half, "wide", dims, 2, b) for b in range(1, pair)]
+    halves = [half]
+    if pair == 2:
+        halves.append(permute(half, "wide", dims, 2, 1))
     main, side = join(halves, (r, e, k))
 
     blocks_of_weights = {}
@@ -530,7 +579,7 @@
             sent, *more = forward(main, side, weights, place, width, jnp.bfloat16, next_one)
             if more:
                 blocks_of_weights[later[0], later[1][0]] = more
-            received.append(shift_permute(sent, "narrow", (peers,), 0, s))
+            received.append(shift(sent, peers, s))
         parts.append((offset, width, received))
 
     jobs = []
@@ -541,31 +590,31 @@
         (kept,) = forward(main, side, weights, place, width, jnp.float32)
         grads = coefficients(kept, received, picks, points, blocks * e)
         jobs.append((grads, offset, width, 0))
-        jobs += [
-            (shift_permute(grads, "narrow", (peers,), 0, s), offset, width, s) for s in range(1, peers)
-        ]
+        jobs += [(shift(grads, peers, s), offset, width, s) for s in range(1, peers)]
     jobs.sort(key=lambda job: job[3])
     total = None
+    last = []
     for i, (grads, offset, width, s) in enumerate(jobs):
         weights, place = at_peer(peers - s, offset, width)
         weights = blocks_of_weights[s, offset][:1] if ahead else weights[:2]
-        total = backward(grads, weights, place, total, i == len(jobs) - 1 and pair == 2)
-
-    if pair == 2:
-        sent, kept = total
-        total = kept + shift_permute(sent, "wide", dims, 2, 1).astype(jnp.float32)
-    if near == 2:
-        half = total.shape[0] // 2
-        sent = total[half:].astype(jnp.bfloat16)
-        total = total[:half] + shift_permute(sent, "wide", dims, 1, 1).astype(jnp.float32)
-    result = total[:e]
-    got = [
-        shift_permute(total[s * e:(s + 1) * e].astype(jnp.bfloat16), "wide", dims, 0, far - s)
-        for s in range(1, far)
-    ]
-    for piece in got:
-        result = result + piece.astype(jnp.float32)
-    return result.astype(jnp.bfloat16)
+        if i < len(jobs) - 1:
+            total = backward(grads, weights, place, total, False)
+        else:
+            spans = [(0, depth // 2), (depth // 2, depth // 2)] if depth % 256 == 0 else [(0, depth)]
+            last = [backward(grads, weights, place, total, pair == 2, span) for span in spans]
+
+    results = []
+    for value in last:
+        if pair == 2:
+            sent, kept = value
+            value = kept + permute(sent, "wide", dims, 2, 1).astype(jnp.float32)
+        steps = [(1, 1)] * (near == 2) + [(0, 1 << i) for i in range(far.bit_length() - 1)]
+        for digit, amount in steps:
+            middle = value.shape[0] // 2
+            got = permute(value[middle:].astype(jnp.bfloat16), "wide", dims, digit, amount)
+            value = value[:middle] + got.astype(jnp.float32)
+        results.append(value.astype(jnp.bfloat16))
+    return results[0] if len(results) == 1 else jnp.concatenate(results, axis=1)
 
 
 def solution(mesh):

time: 100 us -> 114 us (1.14)
  local copies, waits for them, and re-layouts: 1.74 us -> 10.6 us
  Pallas kernels: 45.8 us -> 51.2 us
    unnamed x3 -> x31, local copies, waits for them, and re-layouts: 0.78 us -> 10.5 us
    pallas_call x3, Pallas kernels: 12.5 us -> 15.3 us  [fetch(): pl.pallas_call(body, out_shape=(pltpu.VMEM((depth, 2 * width), jnp.bfloat...]
    ppermute x17 -> x20, starting transfers between devices: 24.3 us -> 25 us  [the longest x16 20.6 us: permute(): return lax.ppermute(array, axis, pairs)]
    ppermute x17 -> x20, waiting for transfers between devices: 26.2 us -> 25.8 us  [the longest x16 25.8 us: permute(): return lax.ppermute(array, axis, pairs)]
    pallas_call x4 -> x5, Pallas kernels: 9.39 us -> 9.42 us  [backward(): pl.pallas_call(body, out_shape=out_shape, in_specs=specs, out_specs=out_s...]
  transfers between devices with their start and end apart: 17 -> 20, of which waited for: 10 -> 12; matrix products, arithmetic and copies ran while one was open for 1% -> 0% of each run, Pallas kernels for 40% -> 39%
where the time goes in v1:
time: 114 us
  Pallas kernels  51.2 us (45%)
  waiting for transfers between devices  25.8 us (23%)
  starting transfers between devices  25 us (22%)
  local copies, waits for them, and re-layouts  10.6 us (9%)
    ppermute x16, waiting for transfers between devices, permute(): return lax.ppermute(array, axis, pairs)  25.8 us
    ppermute x16, starting transfers between devices, permute(): return lax.ppermute(array, axis, pairs)  20.6 us
    pallas_call x4, Pallas kernels, forward(): pl.pallas_call(body_ready if ready else body, out_shape=out_shape, in_spe...  17 us
    pallas_call x3, Pallas kernels, fetch(): pl.pallas_call(body, out_shape=(pltpu.VMEM((depth, 2 * width), jnp.bfloat...  15.3 us
    unnamed x31, local copies, waits for them, and re-layouts  10.5 us
    pallas_call x5, Pallas kernels, backward(): pl.pallas_call(body, out_shape=out_shape, in_specs=specs, out_specs=out_s...  9.42 us
    pallas_call x2, Pallas kernels, coefficients(): pl.pallas_call(body, out_shape=jax.ShapeDtypeStruct((examples, 2 * width)...  7.46 us
    ppermute x4, starting transfers between devices, shift(): lax.ppermute(array, 'narrow', [(at, (at + amount) % size) for at in range...  4.33 us
  transfers between devices with their start and end apart: 20, of which 12 were waited for; matrix products, arithmetic and copies ran while one was open for 0% of the time, Pallas kernels for 39%

profile of v1, /device:TPU:0, one launch (start us, length us, event | category | flops | bytes accessed | tf_op | source)
XLA Modules:
  0.0 113.7 jit_solution(8544154677658781900)
XLA Ops:
  0.0 1.0 pack.1.refs_0_
  1.0 4.1 %collective-permute-start = (bf16[16,4608]{1,0:T(8,128)(2,1)S(1)}, bf16[16,4608]{1,0:T(8,128)(2,1)S(1)}, u32[]{:S(2)}, u32[]{:S(2)}) collective-permute-start(bf16[16,4608]{1,0:T(8,128)(2,1)S(1)} %pack.1.refs_0_), channel_id=1, source_target_pairs={{0,16},{2,18},{4,20},{6,22},{8,24},{10,26},{12,28},{14,30},{16,0},... | collective-permute-start | bytes 442376 | tf_op jit(solution)/shard_map/ppermute | solution.py:35
  5.1 1.6 %collective-permute-start.1 = (bf16[16,4608]{1,0:T(8,128)(2,1)S(1)}, bf16[16,4608]{1,0:T(8,128)(2,1)S(1)}, u32[]{:S(2)}, u32[]{:S(2)}) collective-permute-start(bf16[16,4608]{1,0:T(8,128)(2,1)S(1)} %pack.1.refs_0_), channel_id=1, source_target_pairs={{0,8},{2,10},{4,12},{6,14},{8,0},{10,2},{12,4},{14,6},{16,24},{18,... | collective-permute-start | bytes 442376 | tf_op jit(solution)/shard_map/ppermute | solution.py:35
  6.7 5.5 %collective-permute-done.refs_1_ = bf16[16,4608]{1,0:T(8,128)(2,1)S(1)} collective-permute-done((bf16[16,4608]{1,0:T(8,128)(2,1)S(1)}, bf16[16,4608]{1,0:T(8,128)(2,1)S(1)}, u32[]{:S(2)}, u32[]{:S(2)}) %collective-permute-start) | collective-permute-done | bytes 147488 | tf_op jit(solution)/shard_map/ppermute | solution.py:35
  12.2 0.6 collective-permute-start.2
  12.8 1.5 %collective-permute-start.3 = (bf16[16,4608]{1,0:T(8,128)(2,1)S(1)}, bf16[16,4608]{1,0:T(8,128)(2,1)S(1)}, u32[]{:S(2)}, u32[]{:S(2)}) collective-permute-start(bf16[16,4608]{1,0:T(8,128)(2,1)S(1)} %pack.1.refs_0_), channel_id=1, source_target_pairs={{0,4},{2,6},{4,0},{6,2},{8,12},{10,14},{12,8},{14,10},{16,20},{18,... | collective-permute-start | bytes 442376 | tf_op jit(solution)/shard_map/ppermute | solution.py:35
  14.9 1.5 %collective-permute-start.5 = (bf16[16,4608]{1,0:T(8,128)(2,1)S(1)}, bf16[16,4608]{1,0:T(8,128)(2,1)S(1)}, u32[]{:S(2)}, u32[]{:S(2)}) collective-permute-start(bf16[16,4608]{1,0:T(8,128)(2,1)S(1)} %collective-permute-done.1.refs_2_), channel_id=1, source_target_pairs={{0,4},{2,6},{4,0},{6,2},{8,12},{10,14},{12,8},{14,10},{16,20},{18,... | collective-permute-start | bytes 442376 | tf_op jit(solution)/shard_map/ppermute | solution.py:35
  16.4 1.0 collective-permute-done.2.refs_3_
  17.4 1.6 %collective-permute-start.6 = (bf16[16,4608]{1,0:T(8,128)(2,1)S(1)}, bf16[16,4608]{1,0:T(8,128)(2,1)S(1)}, u32[]{:S(2)}, u32[]{:S(2)}) collective-permute-start(bf16[16,4608]{1,0:T(8,128)(2,1)S(1)} %collective-permute-done.2.refs_3_), channel_id=1, source_target_pairs={{0,4},{2,6},{4,0},{6,2},{8,12},{10,14},{12,8},{14,10},{16,20},{18,... | collective-permute-start | bytes 442376 | tf_op jit(solution)/shard_map/ppermute | solution.py:35
  18.9 0.6 collective-permute-done.3.refs_4_
  19.6 3.2 %collective-permute-done.4.refs_5_ = bf16[16,4608]{1,0:T(8,128)(2,1)S(1)} collective-permute-done((bf16[16,4608]{1,0:T(8,128)(2,1)S(1)}, bf16[16,4608]{1,0:T(8,128)(2,1)S(1)}, u32[]{:S(2)}, u32[]{:S(2)}) %collective-permute-start.4) | collective-permute-done | bytes 147488 | tf_op jit(solution)/shard_map/ppermute | solution.py:35
  22.7 3.2 %collective-permute-done.5.refs_6_ = bf16[16,4608]{1,0:T(8,128)(2,1)S(1)} collective-permute-done((bf16[16,4608]{1,0:T(8,128)(2,1)S(1)}, bf16[16,4608]{1,0:T(8,128)(2,1)S(1)}, u32[]{:S(2)}, u32[]{:S(2)}) %collective-permute-start.5) | collective-permute-done | bytes 147488 | tf_op jit(solution)/shard_map/ppermute | solution.py:35
  25.9 1.9 %collective-permute-done.6.refs_7_ = bf16[16,4608]{1,0:T(8,128)(2,1)S(1)} collective-permute-done((bf16[16,4608]{1,0:T(8,128)(2,1)S(1)}, bf16[16,4608]{1,0:T(8,128)(2,1)S(1)}, u32[]{:S(2)}, u32[]{:S(2)}) %collective-permute-start.6) | collective-permute-done | bytes 147488 | tf_op jit(solution)/shard_map/ppermute | solution.py:35
  27.8 0.8 assemble.1.refs_0_
  28.6 5.7 %fetch.5 = (bf16[4096,1280]{1,0:T(8,128)(2,1)S(1)}, bf16[640,4096]{1,0:T(8,128)(2,1)S(1)}) custom-call(bf16[4096,1792]{1,0:T(8,128)(2,1)} %gate.5, bf16[4096,1792]{1,0:T(8,128)(2,1)} %up.5, bf16[1792,4096]{1,0:T(8,128)(2,1)} %down.5), custom_call_target="tpu_custom_call" | custom-call | flops 4000000000 | bytes 15728640 | tf_op jit(solution)/shard_map/fetch/pallas_call | solution.py:231
  34.3 6.7 %fetch.4 = (bf16[4096,512]{1,0:T(8,128)(2,1)S(1)}, bf16[256,4096]{1,0:T(8,128)(2,1)S(1)}) custom-call(bf16[4096,1792]{1,0:T(8,128)(2,1)} %gate.5, bf16[4096,1792]{1,0:T(8,128)(2,1)} %up.5, bf16[1792,4096]{1,0:T(8,128)(2,1)} %down.5), custom_call_target="tpu_custom_call" | custom-call | flops 4000000000 | bytes 6291456 | tf_op jit(solution)/shard_map/fetch/pallas_call | solution.py:231
  41.1 2.0 %copy-done.1 = bf16[4096,512]{1,0:T(8,128)(2,1)} copy-done((bf16[4096,512]{1,0:T(8,128)(2,1)}, bf16[4096,512]{1,0:T(8,128)(2,1)S(1)}, u32[]{:S(2)}) %copy-start.1) | copy-done | bytes 4194328
  43.1 1.3 %copy-done.6 = bf16[256,4096]{1,0:T(8,128)(2,1)} copy-done((bf16[256,4096]{1,0:T(8,128)(2,1)}, bf16[256,4096]{1,0:T(8,128)(2,1)S(1)}, u32[]{:S(2)}) %copy-start.6) | copy-done | bytes 2097176
  44.6 3.9 %forward.7 = bf16[248,1280]{1,0:T(8,128)(2,1)S(1)} custom-call(bf16[208,4096]{1,0:T(8,128)(2,1)S(1)} %get-tuple-element.20.main_ref, bf16[80,4096]{1,0:T(8,128)(2,1)S(1)} %get-tuple-element.21.side_ref, bf16[4096,1280]{1,0:T(8,128)(2,1)S(1)} %get-tuple-element.29.both.refs_0_, bf16[640,4096]{1,0:T(8,128)(2,1)S(1)} %get-tuple-element.30.below), custom_call_target="tpu_custom_call" | custom-call | flops 2600468480 | bytes 15728640 | tf_op jit(solution)/shard_map/forward/pallas_call | solution.py:319
  48.5 1.6 %collective-permute-start.10 = (bf16[248,1280]{1,0:T(8,128)(2,1)S(1)}, bf16[248,1280]{1,0:T(8,128)(2,1)}, u32[]{:S(2)}, u32[]{:S(2)}) collective-permute-start(bf16[248,1280]{1,0:T(8,128)(2,1)S(1)} %forward.7), channel_id=1, source_target_pairs={{0,1},{1,0},{2,3},{3,2},{4,5},{5,4},{6,7},{7,6},{8,9},{9,8},{10,11... | collective-permute-start | bytes 1904648 | tf_op jit(solution)/shard_map/ppermute | solution.py:39
  50.1 2.9 %fetch.3 = (bf16[4096,512]{1,0:T(8,128)(2,1)S(1)}, bf16[256,4096]{1,0:T(8,128)(2,1)S(1)}) custom-call(bf16[4096,1792]{1,0:T(8,128)(2,1)} %gate.5, bf16[4096,1792]{1,0:T(8,128)(2,1)} %up.5, bf16[1792,4096]{1,0:T(8,128)(2,1)} %down.5), custom_call_target="tpu_custom_call" | custom-call | flops 4000000000 | bytes 6291456 | tf_op jit(solution)/shard_map/fetch/pallas_call | solution.py:231
  53.0 2.0 %copy-done.4 = bf16[4096,512]{1,0:T(8,128)(2,1)} copy-done((bf16[4096,512]{1,0:T(8,128)(2,1)}, bf16[4096,512]{1,0:T(8,128)(2,1)S(1)}, u32[]{:S(2)}) %copy-start.4) | copy-done | bytes 4194328
  55.0 1.4 %copy-done.8 = bf16[256,4096]{1,0:T(8,128)(2,1)} copy-done((bf16[256,4096]{1,0:T(8,128)(2,1)}, bf16[256,4096]{1,0:T(8,128)(2,1)S(1)}, u32[]{:S(2)}) %copy-start.8) | copy-done | bytes 2097176
  56.7 1.4 %copy-done.7 = bf16[256,4096]{1,0:T(8,128)(2,1)S(1)} copy-done((bf16[256,4096]{1,0:T(8,128)(2,1)S(1)}, bf16[256,4096]{1,0:T(8,128)(2,1)}, u32[]{:S(2)}) %copy-start.7) | copy-done | bytes 2097176
  58.1 2.2 %copy-done.2 = bf16[4096,512]{1,0:T(8,128)(2,1)S(1)} copy-done((bf16[4096,512]{1,0:T(8,128)(2,1)S(1)}, bf16[4096,512]{1,0:T(8,128)(2,1)}, u32[]{:S(2)}) %copy-start.2) | copy-done | bytes 4194328
  60.3 7.5 %forward.5 = (bf16[248,512]{1,0:T(8,128)(2,1)S(1)}, bf16[4096,1280]{1,0:T(8,128)(2,1)S(1)}, bf16[640,4096]{1,0:T(8,128)(2,1)S(1)}) custom-call(bf16[208,4096]{1,0:T(8,128)(2,1)S(1)} %get-tuple-element.20.main_ref, bf16[80,4096]{1,0:T(8,128)(2,1)S(1)} %get-tuple-element.21.side_ref, bf16[4096,512]{1,0:T(8,128)(2,1)S(1)} %copy-done.2, ...), custom_call_target="tpu_custom_call" | custom-call | flops 1040187392 | bytes 6291456 | tf_op jit(solution)/shard_map/forward/pallas_call | solution.py:319
  68.4 1.6 %forward.4.kept_ref = f32[248,512]{1,0:T(8,128)S(1)} custom-call(bf16[208,4096]{1,0:T(8,128)(2,1)S(1)} %get-tuple-element.20.main_ref, bf16[80,4096]{1,0:T(8,128)(2,1)S(1)} %get-tuple-element.21.side_ref, bf16[4096,512]{1,0:T(8,128)(2,1)S(1)} %copy-done.5, bf16[256,4096]{1,0:T(8,128)(2,1)S(1)} %copy-done.9), custom_call_target="tpu_custom_call" | custom-call | flops 1040187392 | bytes 6291456 | tf_op jit(solution)/shard_map/forward/pallas_call | solution.py:319
  70.1 3.9 %forward.6.kept_ref = f32[248,1280]{1,0:T(8,128)S(1)} custom-call(bf16[208,4096]{1,0:T(8,128)(2,1)S(1)} %get-tuple-element.20.main_ref, bf16[80,4096]{1,0:T(8,128)(2,1)S(1)} %get-tuple-element.21.side_ref, bf16[4096,1280]{1,0:T(8,128)(2,1)S(1)} %get-tuple-element.27.both.refs_0_, bf16[640,4096]{1,0:T(8,128)(2,1)S(1)} %get-tuple-element.28.below), custom_call_target="tpu_custom_call" | custom-call | flops 2600468480 | bytes 15728640 | tf_op jit(solution)/shard_map/forward/pallas_call | solution.py:319
  74.0 5.3 %coefficients.3.grads_ref = bf16[80,1280]{1,0:T(8,128)(2,1)S(1)} custom-call(s32[8]{0:T(128)S(1)} %copy-done.10, bf16[320,128]{1,0:T(8,128)(2,1)S(1)} %choices.1.picks_ref, f32[248,1280]{1,0:T(8,128)S(1)} %forward.6.kept_ref, bf16[248,1280]{1,0:T(8,128)(2,1)} %collective-permute-done.10.refs_0_), custom_call_target="tpu_custom_call" | custom-call | flops 5000000000 | bytes 1000000 | tf_op jit(solution)/shard_map/coefficients/pallas_call | solution.py:397
  79.3 1.5 %collective-permute-start.11 = (bf16[80,1280]{1,0:T(8,128)(2,1)S(1)}, bf16[80,1280]{1,0:T(8,128)(2,1)S(1)}, u32[]{:S(2)}, u32[]{:S(2)}) collective-permute-start(bf16[80,1280]{1,0:T(8,128)(2,1)S(1)} %coefficients.3.grads_ref), channel_id=1, source_target_pairs={{0,1},{1,0},{2,3},{3,2},{4,5},{5,4},{6,7},{7,6},{8,9},{9,8},{10,11... | collective-permute-start | bytes 614408 | tf_op jit(solution)/shard_map/ppermute | solution.py:39
  80.9 2.2 %coefficients.2.grads_ref = bf16[80,512]{1,0:T(8,128)(2,1)S(1)} custom-call(s32[8]{0:T(128)S(1)} %copy-done.10, bf16[320,128]{1,0:T(8,128)(2,1)S(1)} %choices.1.picks_ref, f32[248,512]{1,0:T(8,128)S(1)} %forward.4.kept_ref, bf16[248,512]{1,0:T(8,128)(2,1)S(1)} %collective-permute-done.8.refs_0_), custom_call_target="tpu_custom_call" | custom-call | flops 5000000000 | bytes 1000000 | tf_op jit(solution)/shard_map/coefficients/pallas_call | solution.py:397
  83.7 3.2 %backward.5.refs_1_ = f32[80,4096]{1,0:T(8,128)S(1)} custom-call(bf16[80,1280]{1,0:T(8,128)(2,1)S(1)} %coefficients.3.grads_ref, bf16[4096,1280]{1,0:T(8,128)(2,1)S(1)} %get-tuple-element.27.both.refs_0_), custom_call_target="tpu_custom_call" | custom-call | flops 838860800 | bytes 10485760 | tf_op jit(solution)/shard_map/backward/pallas_call | solution.py:454
  86.9 1.4 %backward.6.refs_1_ = f32[80,4096]{1,0:T(8,128)S(1)} custom-call(bf16[80,512]{1,0:T(8,128)(2,1)S(1)} %coefficients.2.grads_ref, bf16[4096,512]{1,0:T(8,128)(2,1)S(1)} %copy-done.5, f32[80,4096]{1,0:T(8,128)S(1)} %backward.5.refs_1_), custom_call_target="tpu_custom_call" | custom-call | flops 335544320 | bytes 4194304 | tf_op jit(solution)/shard_map/backward/pallas_call | solution.py:454
  88.4 3.3 %backward.7.refs_1_ = f32[80,4096]{1,0:T(8,128)S(1)} custom-call(bf16[80,1280]{1,0:T(8,128)(2,1)S(1)} %collective-permute-done.11.grads_ref, bf16[4096,1280]{1,0:T(8,128)(2,1)S(1)} %bitcast.1, f32[80,4096]{1,0:T(8,128)S(1)} %backward.6.refs_1_), custom_call_target="tpu_custom_call" | custom-call | flops 838860800 | bytes 10485760 | tf_op jit(solution)/shard_map/backward/pallas_call | solution.py:454
  91.6 0.8 backward.8
  92.5 0.8 backward.9
  93.9 1.6 %collective-permute-start.13 = (bf16[20,2048]{1,0:T(8,128)(2,1)S(1)}, bf16[20,2048]{1,0:T(8,128)(2,1)S(1)}, u32[]{:S(2)}, u32[]{:S(2)}) collective-permute-start(bf16[20,2048]{1,0:T(8,128)(2,1)S(1)} %slice.83), channel_id=1, source_target_pairs={{0,4},{2,6},{4,0},{6,2},{8,12},{10,14},{12,8},{14,10},{16,20},{18,... | collective-permute-start | bytes 245768 | tf_op jit(solution)/shard_map/ppermute | solution.py:35
  95.6 0.9 collective-permute-start.17
  96.5 3.1 %collective-permute-done.13 = bf16[20,2048]{1,0:T(8,128)(2,1)S(1)} collective-permute-done((bf16[20,2048]{1,0:T(8,128)(2,1)S(1)}, bf16[20,2048]{1,0:T(8,128)(2,1)S(1)}, u32[]{:S(2)}, u32[]{:S(2)}) %collective-permute-start.13) | collective-permute-done | bytes 81952 | tf_op jit(solution)/shard_map/ppermute | solution.py:35
  99.6 0.7 collective-permute-start.14
  100.3 0.6 collective-permute-done.17
  101.0 0.8 collective-permute-start.18
  101.8 2.6 %collective-permute-done.14 = bf16[10,2048]{1,0:T(8,128)(2,1)S(1)} collective-permute-done((bf16[10,2048]{1,0:T(8,128)(2,1)S(1)}, bf16[10,2048]{1,0:T(8,128)(2,1)S(1)}, u32[]{:S(2)}, u32[]{:S(2)}) %collective-permute-start.14) | collective-permute-done | bytes 40992 | tf_op jit(solution)/shard_map/ppermute | solution.py:35
  104.5 3.7 %collective-permute-start.15 = (bf16[5,2048]{1,0:T(8,128)(2,1)S(1)}, bf16[5,2048]{1,0:T(8,128)(2,1)S(1)}, u32[]{:S(2)}, u32[]{:S(2)}) collective-permute-start(bf16[5,2048]{1,0:T(8,128)(2,1)S(1)} %slice.87), channel_id=1, source_target_pairs={{0,16},{2,18},{4,20},{6,22},{8,24},{10,26},{12,28},{14,30},{16,0},... | collective-permute-start | bytes 61448 | tf_op jit(solution)/shard_map/ppermute | solution.py:35
  108.2 0.8 collective-permute-start.19
  109.0 1.1 collective-permute-done.15
  110.0 3.0 %collective-permute-done.19 = bf16[5,2048]{1,0:T(8,128)(2,1)S(1)} collective-permute-done((bf16[5,2048]{1,0:T(8,128)(2,1)S(1)}, bf16[5,2048]{1,0:T(8,128)(2,1)S(1)}, u32[]{:S(2)}, u32[]{:S(2)}) %collective-permute-start.19) | collective-permute-done | bytes 20512 | tf_op jit(solution)/shard_map/ppermute | solution.py:35
  113.1 0.6 pad_maximum_fusion
  (57 shorter events, 3.2 us)
Async XLA Ops:
  1.0 11.2 %collective-permute-start = (bf16[16,4608]{1,0:T(8,128)(2,1)S(1)}, bf16[16,4608]{1,0:T(8,128)(2,1)S(1)}, u32[]{:S(2)}, u32[]{:S(2)}) collective-permute-start(bf16[16,4608]{1,0:T(8,128)(2,1)S(1)} %pack.1.refs_0_), channel_id=1, source_target_pairs={{0,16},{2,18},{4,20},{6,22},{8,24},{10,26},{12,28},{14,30},{16,0},... | collective-permute-start | bytes 442376 | tf_op jit(solution)/shard_map/ppermute | solution.py:35
  5.1 9.8 %collective-permute-start.1 = (bf16[16,4608]{1,0:T(8,128)(2,1)S(1)}, bf16[16,4608]{1,0:T(8,128)(2,1)S(1)}, u32[]{:S(2)}, u32[]{:S(2)}) collective-permute-start(bf16[16,4608]{1,0:T(8,128)(2,1)S(1)} %pack.1.refs_0_), channel_id=1, source_target_pairs={{0,8},{2,10},{4,12},{6,14},{8,0},{10,2},{12,4},{14,6},{16,24},{18,... | collective-permute-start | bytes 442376 | tf_op jit(solution)/shard_map/ppermute | solution.py:35
  12.2 5.1 %collective-permute-start.2 = (bf16[16,4608]{1,0:T(8,128)(2,1)S(1)}, bf16[16,4608]{1,0:T(8,128)(2,1)S(1)}, u32[]{:S(2)}, u32[]{:S(2)}) collective-permute-start(bf16[16,4608]{1,0:T(8,128)(2,1)S(1)} %collective-permute-done.refs_1_), channel_id=1, source_target_pairs={{0,8},{2,10},{4,12},{6,14},{8,0},{10,2},{12,4},{14,6},{16,24},{18,... | collective-permute-start | bytes 442376 | tf_op jit(solution)/shard_map/ppermute | solution.py:35
  12.8 6.7 %collective-permute-start.3 = (bf16[16,4608]{1,0:T(8,128)(2,1)S(1)}, bf16[16,4608]{1,0:T(8,128)(2,1)S(1)}, u32[]{:S(2)}, u32[]{:S(2)}) collective-permute-start(bf16[16,4608]{1,0:T(8,128)(2,1)S(1)} %pack.1.refs_0_), channel_id=1, source_target_pairs={{0,4},{2,6},{4,0},{6,2},{8,12},{10,14},{12,8},{14,10},{16,20},{18,... | collective-permute-start | bytes 442376 | tf_op jit(solution)/shard_map/ppermute | solution.py:35
  14.4 8.4 %collective-permute-start.4 = (bf16[16,4608]{1,0:T(8,128)(2,1)S(1)}, bf16[16,4608]{1,0:T(8,128)(2,1)S(1)}, u32[]{:S(2)}, u32[]{:S(2)}) collective-permute-start(bf16[16,4608]{1,0:T(8,128)(2,1)S(1)} %collective-permute-done.refs_1_), channel_id=1, source_target_pairs={{0,4},{2,6},{4,0},{6,2},{8,12},{10,14},{12,8},{14,10},{16,20},{18,... | collective-permute-start | bytes 442376 | tf_op jit(solution)/shard_map/ppermute | solution.py:35
  14.9 11.0 %collective-permute-start.5 = (bf16[16,4608]{1,0:T(8,128)(2,1)S(1)}, bf16[16,4608]{1,0:T(8,128)(2,1)S(1)}, u32[]{:S(2)}, u32[]{:S(2)}) collective-permute-start(bf16[16,4608]{1,0:T(8,128)(2,1)S(1)} %collective-permute-done.1.refs_2_), channel_id=1, source_target_pairs={{0,4},{2,6},{4,0},{6,2},{8,12},{10,14},{12,8},{14,10},{16,20},{18,... | collective-permute-start | bytes 442376 | tf_op jit(solution)/shard_map/ppermute | solution.py:35
  17.4 10.4 %collective-permute-start.6 = (bf16[16,4608]{1,0:T(8,128)(2,1)S(1)}, bf16[16,4608]{1,0:T(8,128)(2,1)S(1)}, u32[]{:S(2)}, u32[]{:S(2)}) collective-permute-start(bf16[16,4608]{1,0:T(8,128)(2,1)S(1)} %collective-permute-done.2.refs_3_), channel_id=1, source_target_pairs={{0,4},{2,6},{4,0},{6,2},{8,12},{10,14},{12,8},{14,10},{16,20},{18,... | collective-permute-start | bytes 442376 | tf_op jit(solution)/shard_map/ppermute | solution.py:35
  28.6 15.9 %collective-permute-start.7 = (bf16[144,4096]{1,0:T(8,128)(2,1)S(1)}, bf16[144,4096]{1,0:T(8,128)(2,1)S(1)}, u32[]{:S(2)}, u32[]{:S(2)}) collective-permute-start(bf16[144,4096]{1,0:T(8,128)(2,1)S(1)} %assemble.1.refs_0_), channel_id=1, source_target_pairs={{0,2},{2,0},{4,6},{6,4},{8,10},{10,8},{12,14},{14,12},{16,18},{18,... | collective-permute-start | bytes 3538952 | tf_op jit(solution)/shard_map/ppermute | solution.py:35
  34.3 10.3 %copy-start = (bf16[4096,1280]{1,0:T(8,128)(2,1)}, bf16[4096,1280]{1,0:T(8,128)(2,1)S(1)}, u32[]{:S(2)}) copy-start(bf16[4096,1280]{1,0:T(8,128)(2,1)S(1)} %get-tuple-element.29.both.refs_0_) | copy-start | bytes 31457284
  41.1 2.1 %copy-start.1 = (bf16[4096,512]{1,0:T(8,128)(2,1)}, bf16[4096,512]{1,0:T(8,128)(2,1)S(1)}, u32[]{:S(2)}) copy-start(bf16[4096,512]{1,0:T(8,128)(2,1)S(1)} %get-tuple-element.24.both.refs_0_) | copy-start | bytes 12582916
  43.1 1.3 %copy-start.6 = (bf16[256,4096]{1,0:T(8,128)(2,1)}, bf16[256,4096]{1,0:T(8,128)(2,1)S(1)}, u32[]{:S(2)}) copy-start(bf16[256,4096]{1,0:T(8,128)(2,1)S(1)} %get-tuple-element.25.below) | copy-start | bytes 6291460
  48.5 7.9 %copy-start.11 = (s32[80,4]{0,1:T(4,128)S(1)}, s32[80,4]{0,1:T(4,128)}, u32[]{:S(2)}) copy-start(s32[80,4]{0,1:T(4,128)} %param.14) | copy-start | bytes 3844
  48.5 25.5 %collective-permute-start.10 = (bf16[248,1280]{1,0:T(8,128)(2,1)S(1)}, bf16[248,1280]{1,0:T(8,128)(2,1)}, u32[]{:S(2)}, u32[]{:S(2)}) collective-permute-start(bf16[248,1280]{1,0:T(8,128)(2,1)S(1)} %forward.7), channel_id=1, source_target_pairs={{0,1},{1,0},{2,3},{3,2},{4,5},{5,4},{6,7},{7,6},{8,9},{9,8},{10,11... | collective-permute-start | bytes 1904648 | tf_op jit(solution)/shard_map/ppermute | solution.py:39
  53.0 2.0 %copy-start.4 = (bf16[4096,512]{1,0:T(8,128)(2,1)}, bf16[4096,512]{1,0:T(8,128)(2,1)S(1)}, u32[]{:S(2)}) copy-start(bf16[4096,512]{1,0:T(8,128)(2,1)S(1)} %get-tuple-element.22.both.refs_0_) | copy-start | bytes 12582916
  55.0 1.4 %copy-start.8 = (bf16[256,4096]{1,0:T(8,128)(2,1)}, bf16[256,4096]{1,0:T(8,128)(2,1)S(1)}, u32[]{:S(2)}) copy-start(bf16[256,4096]{1,0:T(8,128)(2,1)S(1)} %get-tuple-element.23.below) | copy-start | bytes 6291460
  56.5 1.6 %copy-start.7 = (bf16[256,4096]{1,0:T(8,128)(2,1)S(1)}, bf16[256,4096]{1,0:T(8,128)(2,1)}, u32[]{:S(2)}) copy-start(bf16[256,4096]{1,0:T(8,128)(2,1)} %copy-done.6) | copy-start | bytes 6291460
  58.1 2.2 %copy-start.2 = (bf16[4096,512]{1,0:T(8,128)(2,1)S(1)}, bf16[4096,512]{1,0:T(8,128)(2,1)}, u32[]{:S(2)}) copy-start(bf16[4096,512]{1,0:T(8,128)(2,1)} %copy-done.1) | copy-start | bytes 12582916
  60.3 8.1 %copy-start.5 = (bf16[4096,512]{1,0:T(8,128)(2,1)S(1)}, bf16[4096,512]{1,0:T(8,128)(2,1)}, u32[]{:S(2)}) copy-start(bf16[4096,512]{1,0:T(8,128)(2,1)} %copy-done.4) | copy-start | bytes 12582916
  60.3 8.1 %copy-start.9 = (bf16[256,4096]{1,0:T(8,128)(2,1)S(1)}, bf16[256,4096]{1,0:T(8,128)(2,1)}, u32[]{:S(2)}) copy-start(bf16[256,4096]{1,0:T(8,128)(2,1)} %copy-done.8) | copy-start | bytes 6291460
  67.8 13.1 %collective-permute-start.8 = (bf16[248,512]{1,0:T(8,128)(2,1)S(1)}, bf16[248,512]{1,0:T(8,128)(2,1)S(1)}, u32[]{:S(2)}, u32[]{:S(2)}) collective-permute-start(bf16[248,512]{1,0:T(8,128)(2,1)S(1)} %get-tuple-element.26), channel_id=1, source_target_pairs={{0,1},{1,0},{2,3},{3,2},{4,5},{5,4},{6,7},{7,6},{8,9},{9,8},{10,11... | collective-permute-start | bytes 761864 | tf_op jit(solution)/shard_map/ppermute | solution.py:39
  70.0 4.0 %copy-start.10 = (s32[8]{0:T(128)S(1)}, s32[8]{0:T(128)}, u32[]{:S(2)}) copy-start(s32[8]{0:T(128)} %points_ref.3) | copy-start | bytes 100
  79.3 9.0 %collective-permute-start.11 = (bf16[80,1280]{1,0:T(8,128)(2,1)S(1)}, bf16[80,1280]{1,0:T(8,128)(2,1)S(1)}, u32[]{:S(2)}, u32[]{:S(2)}) collective-permute-start(bf16[80,1280]{1,0:T(8,128)(2,1)S(1)} %coefficients.3.grads_ref), channel_id=1, source_target_pairs={{0,1},{1,0},{2,3},{3,2},{4,5},{5,4},{6,7},{7,6},{8,9},{9,8},{10,11... | collective-permute-start | bytes 614408 | tf_op jit(solution)/shard_map/ppermute | solution.py:39
  80.9 7.5 %slice-start = ((s8[10485760]{0:T(1024)(128)(4,1)}), s8[4194304]{0:T(1024)(128)(4,1)S(1)}, s32[]{:S(2)}) async-start(s8[10485760]{0:T(1024)(128)(4,1)} %bitcast), calls=%async_computation | async-start | bytes 8388608
  80.9 7.5 %slice-start.1 = ((s8[10485760]{0:T(1024)(128)(4,1)}), s8[4194304]{0:T(1024)(128)(4,1)S(1)}, s32[]{:S(2)}) async-start(s8[10485760]{0:T(1024)(128)(4,1)} %bitcast), calls=%async_computation.1 | async-start | bytes 8388608
  83.0 5.3 %slice-start.2 = ((s8[10485760]{0:T(1024)(128)(4,1)}), s8[2097152]{0:T(1024)(128)(4,1)S(1)}, s32[]{:S(2)}) async-start(s8[10485760]{0:T(1024)(128)(4,1)} %bitcast), calls=%async_computation.2 | async-start | bytes 4194304
  83.0 8.6 %collective-permute-start.9 = (bf16[80,512]{1,0:T(8,128)(2,1)S(1)}, bf16[80,512]{1,0:T(8,128)(2,1)S(1)}, u32[]{:S(2)}, u32[]{:S(2)}) collective-permute-start(bf16[80,512]{1,0:T(8,128)(2,1)S(1)} %coefficients.2.grads_ref), channel_id=1, source_target_pairs={{0,1},{1,0},{2,3},{3,2},{4,5},{5,4},{6,7},{7,6},{8,9},{9,8},{10,11... | collective-permute-start | bytes 245768 | tf_op jit(solution)/shard_map/ppermute | solution.py:39
  88.3 3.3 %copy-start.3 = (bf16[4096,512]{1,0:T(8,128)(2,1)S(1)}, bf16[4096,512]{1,0:T(8,128)(2,1)}, u32[]{:S(2)}) copy-start(bf16[4096,512]{1,0:T(8,128)(2,1)} %copy-done.1) | copy-start | bytes 12582916
  92.4 1.5 %collective-permute-start.12 = (bf16[40,2048]{1,0:T(8,128)(2,1)S(1)}, bf16[40,2048]{1,0:T(8,128)(2,1)S(1)}, u32[]{:S(2)}, u32[]{:S(2)}) collective-permute-start(bf16[40,2048]{1,0:T(8,128)(2,1)S(1)} %get-tuple-element.32), channel_id=1, source_target_pairs={{0,2},{2,0},{4,6},{6,4},{8,10},{10,8},{12,14},{14,12},{16,18},{18,... | collective-permute-start | bytes 491528 | tf_op jit(solution)/shard_map/ppermute | solution.py:35
  93.2 2.3 %collective-permute-start.16 = (bf16[40,2048]{1,0:T(8,128)(2,1)S(1)}, bf16[40,2048]{1,0:T(8,128)(2,1)S(1)}, u32[]{:S(2)}, u32[]{:S(2)}) collective-permute-start(bf16[40,2048]{1,0:T(8,128)(2,1)S(1)} %get-tuple-element.34), channel_id=1, source_target_pairs={{0,2},{2,0},{4,6},{6,4},{8,10},{10,8},{12,14},{14,12},{16,18},{18,... | collective-permute-start | bytes 491528 | tf_op jit(solution)/shard_map/ppermute | solution.py:35
  93.9 5.6 %collective-permute-start.13 = (bf16[20,2048]{1,0:T(8,128)(2,1)S(1)}, bf16[20,2048]{1,0:T(8,128)(2,1)S(1)}, u32[]{:S(2)}, u32[]{:S(2)}) collective-permute-start(bf16[20,2048]{1,0:T(8,128)(2,1)S(1)} %slice.83), channel_id=1, source_target_pairs={{0,4},{2,6},{4,0},{6,2},{8,12},{10,14},{12,8},{14,10},{16,20},{18,... | collective-permute-start | bytes 245768 | tf_op jit(solution)/shard_map/ppermute | solution.py:35
  95.6 5.4 %collective-permute-start.17 = (bf16[20,2048]{1,0:T(8,128)(2,1)S(1)}, bf16[20,2048]{1,0:T(8,128)(2,1)S(1)}, u32[]{:S(2)}, u32[]{:S(2)}) collective-permute-start(bf16[20,2048]{1,0:T(8,128)(2,1)S(1)} %slice.82), channel_id=1, source_target_pairs={{0,4},{2,6},{4,0},{6,2},{8,12},{10,14},{12,8},{14,10},{16,20},{18,... | collective-permute-start | bytes 245768 | tf_op jit(solution)/shard_map/ppermute | solution.py:35
  99.6 4.8 %collective-permute-start.14 = (bf16[10,2048]{1,0:T(8,128)(2,1)S(1)}, bf16[10,2048]{1,0:T(8,128)(2,1)S(1)}, u32[]{:S(2)}, u32[]{:S(2)}) collective-permute-start(bf16[10,2048]{1,0:T(8,128)(2,1)S(1)} %slice.85), channel_id=1, source_target_pairs={{0,8},{2,10},{4,12},{6,14},{8,0},{10,2},{12,4},{14,6},{16,24},{18,... | collective-permute-start | bytes 122888 | tf_op jit(solution)/shard_map/ppermute | solution.py:35
  101.0 7.1 %collective-permute-start.18 = (bf16[10,2048]{1,0:T(8,128)(2,1)S(1)}, bf16[10,2048]{1,0:T(8,128)(2,1)S(1)}, u32[]{:S(2)}, u32[]{:S(2)}) collective-permute-start(bf16[10,2048]{1,0:T(8,128)(2,1)S(1)} %slice.84), channel_id=1, source_target_pairs={{0,8},{2,10},{4,12},{6,14},{8,0},{10,2},{12,4},{14,6},{16,24},{18,... | collective-permute-start | bytes 122888 | tf_op jit(solution)/shard_map/ppermute | solution.py:35
  104.5 5.6 %collective-permute-start.15 = (bf16[5,2048]{1,0:T(8,128)(2,1)S(1)}, bf16[5,2048]{1,0:T(8,128)(2,1)S(1)}, u32[]{:S(2)}, u32[]{:S(2)}) collective-permute-start(bf16[5,2048]{1,0:T(8,128)(2,1)S(1)} %slice.87), channel_id=1, source_target_pairs={{0,16},{2,18},{4,20},{6,22},{8,24},{10,26},{12,28},{14,30},{16,0},... | collective-permute-start | bytes 61448 | tf_op jit(solution)/shard_map/ppermute | solution.py:35
  108.2 4.9 %collective-permute-start.19 = (bf16[5,2048]{1,0:T(8,128)(2,1)S(1)}, bf16[5,2048]{1,0:T(8,128)(2,1)S(1)}, u32[]{:S(2)}, u32[]{:S(2)}) collective-permute-start(bf16[5,2048]{1,0:T(8,128)(2,1)S(1)} %slice.86), channel_id=1, source_target_pairs={{0,16},{2,18},{4,20},{6,22},{8,24},{10,26},{12,28},{14,30},{16,0},... | collective-permute-start | bytes 61448 | tf_op jit(solution)/shard_map/ppermute | solution.py:35

commit v2 on v1

--- a/solution.py
+++ b/solution.py
@@ -343,6 +343,8 @@
         got, out, base_gate, base_up = refs[:-3], refs[-3], refs[-2], refs[-1]
         picks = picks_ref[...]
         steps = [points_ref[m].astype(jnp.float32) * 0.125 for m in range(count)]
+        steps_1 = sum(steps[1:], steps[0])
+        steps_2 = sum((t * t for t in steps[1:]), steps[0] * steps[0])
 
         def block(j, _):
             if lanes == width:
@@ -372,16 +374,17 @@
                 for p in range(pairs):
                     start = base_gate[pl.ds(p * examples + first, piece), :] * 0.5
                     span = gate - start
-                    flat = jnp.zeros_like(gate)
-                    tilted = jnp.zeros_like(gate)
+                    flat = count + (count * start + steps_1 * span)
+                    tilted = steps_1 + (steps_1 * start + steps_2 * span)
+                    coef_up = coef_up + (count * start + steps_1 * span)
                     for t in steps:
                         half = start + t * span
-                        two_s = 1.0 + jnp.tanh(half)
-                        silu = half * two_s
-                        slope = two_s + silu * (2.0 - two_s)
-                        coef_up = coef_up + silu
-                        flat = flat + slope
-                        tilted = tilted + t * slope
+                        v = jnp.tanh(half)
+                        bent = half * v
+                        turn = v - v * bent
+                        coef_up = coef_up + bent
+                        flat = flat + turn
+                        tilted = tilted + t * turn
                     start_up = base_up[pl.ds(p * examples + first, piece), :]
                     coef_gate = coef_gate + (start_up * flat + (up - start_up) * tilted)
                 base_gate[pl.ds(first, piece), :] = coef_gate * (0.5 * scale)
@@ -406,19 +409,20 @@
     )(points, picks, kept, *received)
 
 
-def backward(grads, weights, place, total, final, span=None):
-    rows = grads.shape[0]
-    width = grads.shape[1] // 2
-    depth = weights[0].shape[0]
+def backward(items, total, final, span=None):
+    grads, weights, place = items[0]
+    rows, width, depth = grads.shape[0], grads.shape[1] // 2, weights[0].shape[0]
     low, columns = span or (0, depth)
     by_depth = [(low + row, count) for row, count in parts_of(columns, 128)]
     ready = len(weights) == 1
 
-    def body(grads_ref, *refs):
+    def body(*refs):
+        grads_refs, refs = refs[:len(items)], refs[len(items):]
         if ready:
-            both, *outs = refs
+            boths, outs = refs[:len(items)], refs[len(items):]
         else:
             gate, up, *outs, both, sems = refs
+            boths = [both]
             _, depths = streams((gate, up, None), (both, None), sems, first_of(place), width, by_depth, [])
             for pair in depths:
                 for copy in pair:
@@ -428,17 +432,18 @@
             if not ready:
                 for copy in depths[i]:
                     copy.wait()
-            value = across(grads_ref[...], both[some, :])
-            if total is not None:
-                value = value + outs[0][:, some]
+            value = None if total is None else outs[0][:, some]
+            for grads_ref, both in zip(grads_refs, boths):
+                part = across(grads_ref[...], both[some, :])
+                value = part if value is None else value + part
             if final:
                 outs[-2][:, own] = value[rows // 2:, :].astype(jnp.bfloat16)
                 outs[-1][:, own] = value[:rows // 2, :]
             else:
                 outs[-1][:, own] = value
 
-    operands = [grads, *weights]
-    specs = [VMEM] + [VMEM if ready else ANY] * len(weights)
+    operands = [item[0] for item in items] + [w for item in items for w in item[1]]
+    specs = [VMEM] * len(items) + [VMEM if ready else ANY] * (len(operands) - len(items))
     if total is not None:
         operands.append(total)
         specs.append(VMEM)
@@ -459,7 +464,9 @@
         scratch_shapes=[] if ready else scratch,
         compiler_params=pltpu.CompilerParams(vmem_limit_bytes=(4 if ready else 12) * 1024 * 1024),
         cost_estimate=pl.CostEstimate(
-            flops=4 * rows * width * columns, bytes_accessed=4 * width * columns, transcendentals=0
+            flops=2 * rows * columns * sum(item[0].shape[1] for item in items),
+            bytes_accessed=4 * width * columns,
+            transcendentals=0,
         ),
         name="backward",
     )(*operands)
@@ -500,8 +507,8 @@
 def chunks_of(width):
     if width % 128 or width < 512:
         return [(0, rounded(width, 128))]
-    last = max(256, width // 4 // 256 * 256)
-    return [(0, width - last), (width - last, last)]
+    first = rounded(width // 2, 256)
+    return [(0, first), (first, width - first)]
 
 
 def on_device(
@@ -557,14 +564,9 @@
     main, side = join(halves, (r, e, k))
 
     blocks_of_weights = {}
-    later = None
     if ahead:
-        wanted = [(s, chunk) for s in (1, 0) for chunk in chunks]
-        for s, chunk in wanted:
-            if len(chunks) == 2 and (s, chunk) == (0, chunks[0]):
-                later = (s, chunk)
-                continue
-            blocks_of_weights[s, chunk[0]] = fetch(*at_peer(s, *chunk), chunk[1])
+        for chunk in chunks:
+            blocks_of_weights[1, chunk[0]] = fetch(*at_peer(1, *chunk), chunk[1])
 
     parts = []
     for i, (offset, width) in enumerate(chunks):
@@ -574,11 +576,11 @@
             next_one = None
             if ahead:
                 weights = blocks_of_weights[s, offset]
-                if later is not None and i == 1:
-                    next_one = (*at_peer(later[0], *later[1]), later[1][1])
+                later = chunks[-1 - i]
+                next_one = (*at_peer(0, *later), later[1])
             sent, *more = forward(main, side, weights, place, width, jnp.bfloat16, next_one)
             if more:
-                blocks_of_weights[later[0], later[1][0]] = more
+                blocks_of_weights[0, later[0]] = more
             received.append(shift(sent, peers, s))
         parts.append((offset, width, received))
 
@@ -591,17 +593,20 @@
         grads = coefficients(kept, received, picks, points, blocks * e)
         jobs.append((grads, offset, width, 0))
         jobs += [(shift(grads, peers, s), offset, width, s) for s in range(1, peers)]
-    jobs.sort(key=lambda job: job[3])
-    total = None
-    last = []
-    for i, (grads, offset, width, s) in enumerate(jobs):
+    items = []
+    for grads, offset, width, s in jobs:
         weights, place = at_peer(peers - s, offset, width)
         weights = blocks_of_weights[s, offset][:1] if ahead else weights[:2]
-        if i < len(jobs) - 1:
-            total = backward(grads, weights, place, total, False)
-        else:
-            spans = [(0, depth // 2), (depth // 2, depth // 2)] if depth % 256 == 0 else [(0, depth)]
-            last = [backward(grads, weights, place, total, pair == 2, span) for span in spans]
+        items.append((grads, weights, place))
+    if ahead and len(items) == 4:
+        groups = [items[:1], items[1:3], items[3:]]
+    else:
+        groups = [[item] for item in items]
+    total = None
+    for group in groups[:-1]:
+        total = backward(group, total, False)
+    spans = [(0, depth // 2), (depth // 2, depth // 2)] if depth % 256 == 0 else [(0, depth)]
+    last = [backward(groups[-1], total, pair == 2, span) for span in spans]
 
     results = []
     for value in last:

time: 114 us -> 102 us (0.89)
  local copies, waits for them, and re-layouts: 10.6 us -> 0.88 us
  Pallas kernels: 51.2 us -> 46.3 us
  waiting for transfers between devices: 25.8 us -> 28.2 us
    unnamed x31 -> x3, local copies, waits for them, and re-layouts: 10.5 us -> 0.78 us
    pallas_call x3 -> x2, Pallas kernels: 15.3 us -> 8.66 us  [fetch(): pl.pallas_call(body, out_shape=(pltpu.VMEM((depth, 2 * width), jnp.bfloat...]
    pallas_call x4, Pallas kernels: 17 us -> 19.4 us  [forward(): pl.pallas_call(body_ready if ready else body, out_shape=out_shape, in_spe...]
    ppermute x4, waiting for transfers between devices: 0.01 us -> 2.25 us  [shift(): lax.ppermute(array, 'narrow', [(at, (at + amount) % size) for at in range...]
    pallas_call x5 -> x4, Pallas kernels: 9.42 us -> 9.35 us  [backward(): pl.pallas_call(body, out_shape=out_shape, in_specs=specs, out_specs=out_s...]
  transfers between devices with their start and end apart: 20 -> 20, of which waited for: 12 -> 12; matrix products, arithmetic and copies ran while one was open for 0% -> 1% of each run, Pallas kernels for 39% -> 36%
where the time goes in v2:
time: 102 us
  Pallas kernels  46.3 us (45%)
  waiting for transfers between devices  28.2 us (28%)
  starting transfers between devices  25.7 us (25%)
    ppermute x16, waiting for transfers between devices, permute(): return lax.ppermute(array, axis, pairs)  26 us
    ppermute x16, starting transfers between devices, permute(): return lax.ppermute(array, axis, pairs)  20.3 us
    pallas_call x4, Pallas kernels, forward(): pl.pallas_call(body_ready if ready else body, out_shape=out_shape, in_spe...  19.4 us
    pallas_call x4, Pallas kernels, backward(): pl.pallas_call(body, out_shape=out_shape, in_specs=specs, out_specs=out_s...  9.35 us
    pallas_call x2, Pallas kernels, fetch(): pl.pallas_call(body, out_shape=(pltpu.VMEM((depth, 2 * width), jnp.bfloat...  8.66 us
    pallas_call x2, Pallas kernels, coefficients(): pl.pallas_call(body, out_shape=jax.ShapeDtypeStruct((examples, 2 * width)...  6.82 us
    ppermute x4, starting transfers between devices, shift(): lax.ppermute(array, 'narrow', [(at, (at + amount) % size) for at in range...  5.39 us
    ppermute x4, waiting for transfers between devices, shift(): lax.ppermute(array, 'narrow', [(at, (at + amount) % size) for at in range...  2.25 us
  transfers between devices with their start and end apart: 20, of which 12 were waited for; matrix products, arithmetic and copies ran while one was open for 1% of the time, Pallas kernels for 36%

profile of v2, /device:TPU:0, one launch (start us, length us, event | category | flops | bytes accessed | tf_op | source)
XLA Modules:
  0.0 102.1 jit_solution(2361355824538667885)
XLA Ops:
  0.0 1.0 pack.1.refs_0_
  1.0 4.1 %collective-permute-start = (bf16[16,4608]{1,0:T(8,128)(2,1)S(1)}, bf16[16,4608]{1,0:T(8,128)(2,1)S(1)}, u32[]{:S(2)}, u32[]{:S(2)}) collective-permute-start(bf16[16,4608]{1,0:T(8,128)(2,1)S(1)} %pack.1.refs_0_), channel_id=1, source_target_pairs={{0,16},{2,18},{4,20},{6,22},{8,24},{10,26},{12,28},{14,30},{16,0},... | collective-permute-start | bytes 442376 | tf_op jit(solution)/shard_map/ppermute | solution.py:35
  5.1 1.6 %collective-permute-start.1 = (bf16[16,4608]{1,0:T(8,128)(2,1)S(1)}, bf16[16,4608]{1,0:T(8,128)(2,1)S(1)}, u32[]{:S(2)}, u32[]{:S(2)}) collective-permute-start(bf16[16,4608]{1,0:T(8,128)(2,1)S(1)} %pack.1.refs_0_), channel_id=1, source_target_pairs={{0,8},{2,10},{4,12},{6,14},{8,0},{10,2},{12,4},{14,6},{16,24},{18,... | collective-permute-start | bytes 442376 | tf_op jit(solution)/shard_map/ppermute | solution.py:35
  6.7 5.5 %collective-permute-done.refs_1_ = bf16[16,4608]{1,0:T(8,128)(2,1)S(1)} collective-permute-done((bf16[16,4608]{1,0:T(8,128)(2,1)S(1)}, bf16[16,4608]{1,0:T(8,128)(2,1)S(1)}, u32[]{:S(2)}, u32[]{:S(2)}) %collective-permute-start) | collective-permute-done | bytes 147488 | tf_op jit(solution)/shard_map/ppermute | solution.py:35
  12.2 0.6 collective-permute-start.2
  12.8 1.5 %collective-permute-start.3 = (bf16[16,4608]{1,0:T(8,128)(2,1)S(1)}, bf16[16,4608]{1,0:T(8,128)(2,1)S(1)}, u32[]{:S(2)}, u32[]{:S(2)}) collective-permute-start(bf16[16,4608]{1,0:T(8,128)(2,1)S(1)} %pack.1.refs_0_), channel_id=1, source_target_pairs={{0,4},{2,6},{4,0},{6,2},{8,12},{10,14},{12,8},{14,10},{16,20},{18,... | collective-permute-start | bytes 442376 | tf_op jit(solution)/shard_map/ppermute | solution.py:35
  14.4 0.5 collective-permute-start.4
  14.9 1.5 %collective-permute-start.5 = (bf16[16,4608]{1,0:T(8,128)(2,1)S(1)}, bf16[16,4608]{1,0:T(8,128)(2,1)S(1)}, u32[]{:S(2)}, u32[]{:S(2)}) collective-permute-start(bf16[16,4608]{1,0:T(8,128)(2,1)S(1)} %collective-permute-done.1.refs_2_), channel_id=1, source_target_pairs={{0,4},{2,6},{4,0},{6,2},{8,12},{10,14},{12,8},{14,10},{16,20},{18,... | collective-permute-start | bytes 442376 | tf_op jit(solution)/shard_map/ppermute | solution.py:35
  16.4 1.0 collective-permute-done.2.refs_3_
  17.4 1.6 %collective-permute-start.6 = (bf16[16,4608]{1,0:T(8,128)(2,1)S(1)}, bf16[16,4608]{1,0:T(8,128)(2,1)S(1)}, u32[]{:S(2)}, u32[]{:S(2)}) collective-permute-start(bf16[16,4608]{1,0:T(8,128)(2,1)S(1)} %collective-permute-done.2.refs_3_), channel_id=1, source_target_pairs={{0,4},{2,6},{4,0},{6,2},{8,12},{10,14},{12,8},{14,10},{16,20},{18,... | collective-permute-start | bytes 442376 | tf_op jit(solution)/shard_map/ppermute | solution.py:35
  18.9 0.6 collective-permute-done.3.refs_4_
  19.6 3.2 %collective-permute-done.4.refs_5_ = bf16[16,4608]{1,0:T(8,128)(2,1)S(1)} collective-permute-done((bf16[16,4608]{1,0:T(8,128)(2,1)S(1)}, bf16[16,4608]{1,0:T(8,128)(2,1)S(1)}, u32[]{:S(2)}, u32[]{:S(2)}) %collective-permute-start.4) | collective-permute-done | bytes 147488 | tf_op jit(solution)/shard_map/ppermute | solution.py:35
  22.7 3.2 %collective-permute-done.5.refs_6_ = bf16[16,4608]{1,0:T(8,128)(2,1)S(1)} collective-permute-done((bf16[16,4608]{1,0:T(8,128)(2,1)S(1)}, bf16[16,4608]{1,0:T(8,128)(2,1)S(1)}, u32[]{:S(2)}, u32[]{:S(2)}) %collective-permute-start.5) | collective-permute-done | bytes 147488 | tf_op jit(solution)/shard_map/ppermute | solution.py:35
  25.9 1.9 %collective-permute-done.6.refs_7_ = bf16[16,4608]{1,0:T(8,128)(2,1)S(1)} collective-permute-done((bf16[16,4608]{1,0:T(8,128)(2,1)S(1)}, bf16[16,4608]{1,0:T(8,128)(2,1)S(1)}, u32[]{:S(2)}, u32[]{:S(2)}) %collective-permute-start.6) | collective-permute-done | bytes 147488 | tf_op jit(solution)/shard_map/ppermute | solution.py:35
  27.8 0.8 assemble.1.refs_0_
  28.6 0.8 copy.9.pair_ref
  29.4 4.8 %fetch.2 = (bf16[4096,1024]{1,0:T(8,128)(2,1)S(1)}, bf16[512,4096]{1,0:T(8,128)(2,1)S(1)}) custom-call(bf16[4096,1792]{1,0:T(8,128)(2,1)} %refs_0_.5, bf16[4096,1792]{1,0:T(8,128)(2,1)} %refs_1_.5, bf16[1792,4096]{1,0:T(8,128)(2,1)} %refs_2_.5), custom_call_target="tpu_custom_call" | custom-call | flops 4000000000 | bytes 12582912 | tf_op jit(solution)/shard_map/fetch/pallas_call | solution.py:231
  34.2 3.9 %fetch.3 = (bf16[4096,768]{1,0:T(8,128)(2,1)S(1)}, bf16[384,4096]{1,0:T(8,128)(2,1)S(1)}) custom-call(bf16[4096,1792]{1,0:T(8,128)(2,1)} %refs_0_.5, bf16[4096,1792]{1,0:T(8,128)(2,1)} %refs_1_.5, bf16[1792,4096]{1,0:T(8,128)(2,1)} %refs_2_.5), custom_call_target="tpu_custom_call" | custom-call | flops 4000000000 | bytes 9437184 | tf_op jit(solution)/shard_map/fetch/pallas_call | solution.py:231
  38.1 0.2 join.1
  38.3 6.9 %forward.4 = (bf16[248,1024]{1,0:T(8,128)(2,1)S(1)}, bf16[4096,768]{1,0:T(8,128)(2,1)S(1)}, bf16[384,4096]{1,0:T(8,128)(2,1)S(1)}) custom-call(bf16[208,4096]{1,0:T(8,128)(2,1)S(1)} %get-tuple-element.21.main_ref, bf16[80,4096]{1,0:T(8,128)(2,1)S(1)} %get-tuple-element.22.side_ref, bf16[4096,1024]{1,0:T(8,128)(2,1)S(1)} %get-tuple-element.23.both.refs_2_, ...), custom_call_target="tpu_custom_call" | custom-call | flops 2080374784 | bytes 12582912 | tf_op jit(solution)/shard_map/forward/pallas_call | solution.py:319
  45.1 1.6 %collective-permute-start.10 = (bf16[248,1024]{1,0:T(8,128)(2,1)S(1)}, bf16[248,1024]{1,0:T(8,128)(2,1)S(1)}, u32[]{:S(2)}, u32[]{:S(2)}) collective-permute-start(bf16[248,1024]{1,0:T(8,128)(2,1)S(1)} %get-tuple-element.32), channel_id=1, source_target_pairs={{0,1},{1,0},{2,3},{3,2},{4,5},{5,4},{6,7},{7,6},{8,9},{9,8},{10,11... | collective-permute-start | bytes 1523720 | tf_op jit(solution)/shard_map/ppermute | solution.py:39
  46.8 0.1 choices.1.picks_ref
  46.9 7.1 %forward.6 = (bf16[248,768]{1,0:T(8,128)(2,1)S(1)}, bf16[4096,1024]{1,0:T(8,128)(2,1)S(1)}, bf16[512,4096]{1,0:T(8,128)(2,1)S(1)}) custom-call(bf16[208,4096]{1,0:T(8,128)(2,1)S(1)} %get-tuple-element.21.main_ref, bf16[80,4096]{1,0:T(8,128)(2,1)S(1)} %get-tuple-element.22.side_ref, bf16[4096,768]{1,0:T(8,128)(2,1)S(1)} %get-tuple-element.27.both.refs_1_, ...), custom_call_target="tpu_custom_call" | custom-call | flops 1560281088 | bytes 9437184 | tf_op jit(solution)/shard_map/forward/pallas_call | solution.py:319
  54.0 0.5 collective-permute-start.8
  54.5 2.4 %forward.5.kept_ref = f32[248,768]{1,0:T(8,128)S(1)} custom-call(bf16[208,4096]{1,0:T(8,128)(2,1)S(1)} %get-tuple-element.21.main_ref, bf16[80,4096]{1,0:T(8,128)(2,1)S(1)} %get-tuple-element.22.side_ref, bf16[4096,768]{1,0:T(8,128)(2,1)S(1)} %get-tuple-element.25.both.refs_3_, bf16[384,4096]{1,0:T(8,128)(2,1)S(1)} %get-tuple-element.26.below), custom_call_target="tpu_custom_call" | custom-call | flops 1560281088 | bytes 9437184 | tf_op jit(solution)/shard_map/forward/pallas_call | solution.py:319
  56.8 3.1 %forward.7.kept_ref = f32[248,1024]{1,0:T(8,128)S(1)} custom-call(bf16[208,4096]{1,0:T(8,128)(2,1)S(1)} %get-tuple-element.21.main_ref, bf16[80,4096]{1,0:T(8,128)(2,1)S(1)} %get-tuple-element.22.side_ref, bf16[4096,1024]{1,0:T(8,128)(2,1)S(1)} %get-tuple-element.30.both.refs_1_, bf16[512,4096]{1,0:T(8,128)(2,1)S(1)} %get-tuple-element.31.below), custom_call_target="tpu_custom_call" | custom-call | flops 2080374784 | bytes 12582912 | tf_op jit(solution)/shard_map/forward/pallas_call | solution.py:319
  60.0 3.9 %coefficients.3.refs_0_ = bf16[80,1024]{1,0:T(8,128)(2,1)S(1)} custom-call(s32[8]{0:T(128)S(1)} %copy-done, bf16[320,128]{1,0:T(8,128)(2,1)S(1)} %choices.1.picks_ref, f32[248,1024]{1,0:T(8,128)S(1)} %forward.7.kept_ref, bf16[248,1024]{1,0:T(8,128)(2,1)S(1)} %collective-permute-done.10.refs_0_), custom_call_target="tpu_custom_call" | custom-call | flops 5000000000 | bytes 1000000 | tf_op jit(solution)/shard_map/coefficients/pallas_call | solution.py:400
  63.9 1.7 %collective-permute-start.11 = (bf16[80,1024]{1,0:T(8,128)(2,1)S(1)}, bf16[80,1024]{1,0:T(8,128)(2,1)S(1)}, u32[]{:S(2)}, u32[]{:S(2)}) collective-permute-start(bf16[80,1024]{1,0:T(8,128)(2,1)S(1)} %coefficients.3.refs_0_), channel_id=1, source_target_pairs={{0,1},{1,0},{2,3},{3,2},{4,5},{5,4},{6,7},{7,6},{8,9},{9,8},{10,11... | collective-permute-start | bytes 491528 | tf_op jit(solution)/shard_map/ppermute | solution.py:39
  65.6 2.2 %collective-permute-done.8.refs_0_ = bf16[248,768]{1,0:T(8,128)(2,1)S(1)} collective-permute-done((bf16[248,768]{1,0:T(8,128)(2,1)S(1)}, bf16[248,768]{1,0:T(8,128)(2,1)S(1)}, u32[]{:S(2)}, u32[]{:S(2)}) %collective-permute-start.8) | collective-permute-done | bytes 380960 | tf_op jit(solution)/shard_map/ppermute | solution.py:39
  67.8 2.9 %coefficients.2.refs_1_ = bf16[80,768]{1,0:T(8,128)(2,1)S(1)} custom-call(s32[8]{0:T(128)S(1)} %copy-done, bf16[320,128]{1,0:T(8,128)(2,1)S(1)} %choices.1.picks_ref, f32[248,768]{1,0:T(8,128)S(1)} %forward.5.kept_ref, bf16[248,768]{1,0:T(8,128)(2,1)S(1)} %collective-permute-done.8.refs_0_), custom_call_target="tpu_custom_call" | custom-call | flops 5000000000 | bytes 1000000 | tf_op jit(solution)/shard_map/coefficients/pallas_call | solution.py:400
  70.7 1.6 %collective-permute-start.9 = (bf16[80,768]{1,0:T(8,128)(2,1)S(1)}, bf16[80,768]{1,0:T(8,128)(2,1)S(1)}, u32[]{:S(2)}, u32[]{:S(2)}) collective-permute-start(bf16[80,768]{1,0:T(8,128)(2,1)S(1)} %coefficients.2.refs_1_), channel_id=1, source_target_pairs={{0,1},{1,0},{2,3},{3,2},{4,5},{5,4},{6,7},{7,6},{8,9},{9,8},{10,11... | collective-permute-start | bytes 368648 | tf_op jit(solution)/shard_map/ppermute | solution.py:39
  72.4 2.7 %backward.4.refs_4_ = f32[80,4096]{1,0:T(8,128)S(1)} custom-call(bf16[80,1024]{1,0:T(8,128)(2,1)S(1)} %coefficients.3.refs_0_, bf16[4096,1024]{1,0:T(8,128)(2,1)S(1)} %get-tuple-element.30.both.refs_1_), custom_call_target="tpu_custom_call" | custom-call | flops 671088640 | bytes 8388608 | tf_op jit(solution)/shard_map/backward/pallas_call | solution.py:459
  75.0 4.5 %backward.5.refs_2_ = f32[80,4096]{1,0:T(8,128)S(1)} custom-call(bf16[80,1024]{1,0:T(8,128)(2,1)S(1)} %collective-permute-done.11.refs_0_, bf16[80,768]{1,0:T(8,128)(2,1)S(1)} %coefficients.2.refs_1_, bf16[4096,1024]{1,0:T(8,128)(2,1)S(1)} %get-tuple-element.23.both.refs_2_, bf16[4096,768]{1,0:T(8,128)(2,1)S(1)} %get-tuple-element.25.both.refs_3_, ...), custom_call_target="tpu_custom_call" | custom-call | flops 1174405120 | bytes 8388608 | tf_op jit(solution)/shard_map/backward/pallas_call | solution.py:459
  79.6 1.1 %backward.7 = (bf16[40,2048]{1,0:T(8,128)(2,1)S(1)}, f32[40,2048]{1,0:T(8,128)S(1)}) custom-call(bf16[80,768]{1,0:T(8,128)(2,1)S(1)} %collective-permute-done.9.refs_0_, bf16[4096,768]{1,0:T(8,128)(2,1)S(1)} %get-tuple-element.27.both.refs_1_, f32[80,4096]{1,0:T(8,128)S(1)} %backward.5.refs_2_), custom_call_target="tpu_custom_call" | custom-call | flops 251658240 | bytes 3145728 | tf_op jit(solution)/shard_map/backward/pallas_call | solution.py:459
  80.7 1.1 %backward.6 = (bf16[40,2048]{1,0:T(8,128)(2,1)S(1)}, f32[40,2048]{1,0:T(8,128)S(1)}) custom-call(bf16[80,768]{1,0:T(8,128)(2,1)S(1)} %collective-permute-done.9.refs_0_, bf16[4096,768]{1,0:T(8,128)(2,1)S(1)} %get-tuple-element.27.both.refs_1_, f32[80,4096]{1,0:T(8,128)S(1)} %backward.5.refs_2_), custom_call_target="tpu_custom_call" | custom-call | flops 251658240 | bytes 3145728 | tf_op jit(solution)/shard_map/backward/pallas_call | solution.py:459
  81.8 0.6 collective-permute-start.12
  82.4 1.6 %collective-permute-start.17 = (bf16[20,2048]{1,0:T(8,128)(2,1)S(1)}, bf16[20,2048]{1,0:T(8,128)(2,1)S(1)}, u32[]{:S(2)}, u32[]{:S(2)}) collective-permute-start(bf16[20,2048]{1,0:T(8,128)(2,1)S(1)} %slice.82), channel_id=1, source_target_pairs={{0,4},{2,6},{4,0},{6,2},{8,12},{10,14},{12,8},{14,10},{16,20},{18,... | collective-permute-start | bytes 245768 | tf_op jit(solution)/shard_map/ppermute | solution.py:35
  84.1 1.0 collective-permute-start.13
  85.0 2.9 %collective-permute-done.17 = bf16[20,2048]{1,0:T(8,128)(2,1)S(1)} collective-permute-done((bf16[20,2048]{1,0:T(8,128)(2,1)S(1)}, bf16[20,2048]{1,0:T(8,128)(2,1)S(1)}, u32[]{:S(2)}, u32[]{:S(2)}) %collective-permute-start.17) | collective-permute-done | bytes 81952 | tf_op jit(solution)/shard_map/ppermute | solution.py:35
  88.0 0.4 collective-permute-start.18
  88.4 1.0 collective-permute-done.13
  89.4 0.8 collective-permute-start.14
  90.2 2.6 %collective-permute-done.18 = bf16[10,2048]{1,0:T(8,128)(2,1)S(1)} collective-permute-done((bf16[10,2048]{1,0:T(8,128)(2,1)S(1)}, bf16[10,2048]{1,0:T(8,128)(2,1)S(1)}, u32[]{:S(2)}, u32[]{:S(2)}) %collective-permute-start.18) | collective-permute-done | bytes 40992 | tf_op jit(solution)/shard_map/ppermute | solution.py:35
  92.9 3.7 %collective-permute-start.19 = (bf16[5,2048]{1,0:T(8,128)(2,1)S(1)}, bf16[5,2048]{1,0:T(8,128)(2,1)S(1)}, u32[]{:S(2)}, u32[]{:S(2)}) collective-permute-start(bf16[5,2048]{1,0:T(8,128)(2,1)S(1)} %slice.86), channel_id=1, source_target_pairs={{0,16},{2,18},{4,20},{6,22},{8,24},{10,26},{12,28},{14,30},{16,0},... | collective-permute-start | bytes 61448 | tf_op jit(solution)/shard_map/ppermute | solution.py:35
  96.6 0.8 collective-permute-start.15
  97.4 1.1 %collective-permute-done.19 = bf16[5,2048]{1,0:T(8,128)(2,1)S(1)} collective-permute-done((bf16[5,2048]{1,0:T(8,128)(2,1)S(1)}, bf16[5,2048]{1,0:T(8,128)(2,1)S(1)}, u32[]{:S(2)}, u32[]{:S(2)}) %collective-permute-start.19) | collective-permute-done | bytes 20512 | tf_op jit(solution)/shard_map/ppermute | solution.py:35
  98.4 3.0 %collective-permute-done.15 = bf16[5,2048]{1,0:T(8,128)(2,1)S(1)} collective-permute-done((bf16[5,2048]{1,0:T(8,128)(2,1)S(1)}, bf16[5,2048]{1,0:T(8,128)(2,1)S(1)}, u32[]{:S(2)}, u32[]{:S(2)}) %collective-permute-start.15) | collective-permute-done | bytes 20512 | tf_op jit(solution)/shard_map/ppermute | solution.py:35
  101.5 0.6 pad_maximum_fusion
  (26 shorter events, 0.4 us)
Async XLA Ops:
  1.0 11.2 %collective-permute-start = (bf16[16,4608]{1,0:T(8,128)(2,1)S(1)}, bf16[16,4608]{1,0:T(8,128)(2,1)S(1)}, u32[]{:S(2)}, u32[]{:S(2)}) collective-permute-start(bf16[16,4608]{1,0:T(8,128)(2,1)S(1)} %pack.1.refs_0_), channel_id=1, source_target_pairs={{0,16},{2,18},{4,20},{6,22},{8,24},{10,26},{12,28},{14,30},{16,0},... | collective-permute-start | bytes 442376 | tf_op jit(solution)/shard_map/ppermute | solution.py:35
  5.1 9.8 %collective-permute-start.1 = (bf16[16,4608]{1,0:T(8,128)(2,1)S(1)}, bf16[16,4608]{1,0:T(8,128)(2,1)S(1)}, u32[]{:S(2)}, u32[]{:S(2)}) collective-permute-start(bf16[16,4608]{1,0:T(8,128)(2,1)S(1)} %pack.1.refs_0_), channel_id=1, source_target_pairs={{0,8},{2,10},{4,12},{6,14},{8,0},{10,2},{12,4},{14,6},{16,24},{18,... | collective-permute-start | bytes 442376 | tf_op jit(solution)/shard_map/ppermute | solution.py:35
  12.2 5.1 %collective-permute-start.2 = (bf16[16,4608]{1,0:T(8,128)(2,1)S(1)}, bf16[16,4608]{1,0:T(8,128)(2,1)S(1)}, u32[]{:S(2)}, u32[]{:S(2)}) collective-permute-start(bf16[16,4608]{1,0:T(8,128)(2,1)S(1)} %collective-permute-done.refs_1_), channel_id=1, source_target_pairs={{0,8},{2,10},{4,12},{6,14},{8,0},{10,2},{12,4},{14,6},{16,24},{18,... | collective-permute-start | bytes 442376 | tf_op jit(solution)/shard_map/ppermute | solution.py:35
  12.8 6.7 %collective-permute-start.3 = (bf16[16,4608]{1,0:T(8,128)(2,1)S(1)}, bf16[16,4608]{1,0:T(8,128)(2,1)S(1)}, u32[]{:S(2)}, u32[]{:S(2)}) collective-permute-start(bf16[16,4608]{1,0:T(8,128)(2,1)S(1)} %pack.1.refs_0_), channel_id=1, source_target_pairs={{0,4},{2,6},{4,0},{6,2},{8,12},{10,14},{12,8},{14,10},{16,20},{18,... | collective-permute-start | bytes 442376 | tf_op jit(solution)/shard_map/ppermute | solution.py:35
  14.4 8.4 %collective-permute-start.4 = (bf16[16,4608]{1,0:T(8,128)(2,1)S(1)}, bf16[16,4608]{1,0:T(8,128)(2,1)S(1)}, u32[]{:S(2)}, u32[]{:S(2)}) collective-permute-start(bf16[16,4608]{1,0:T(8,128)(2,1)S(1)} %collective-permute-done.refs_1_), channel_id=1, source_target_pairs={{0,4},{2,6},{4,0},{6,2},{8,12},{10,14},{12,8},{14,10},{16,20},{18,... | collective-permute-start | bytes 442376 | tf_op jit(solution)/shard_map/ppermute | solution.py:35
  14.9 11.0 %collective-permute-start.5 = (bf16[16,4608]{1,0:T(8,128)(2,1)S(1)}, bf16[16,4608]{1,0:T(8,128)(2,1)S(1)}, u32[]{:S(2)}, u32[]{:S(2)}) collective-permute-start(bf16[16,4608]{1,0:T(8,128)(2,1)S(1)} %collective-permute-done.1.refs_2_), channel_id=1, source_target_pairs={{0,4},{2,6},{4,0},{6,2},{8,12},{10,14},{12,8},{14,10},{16,20},{18,... | collective-permute-start | bytes 442376 | tf_op jit(solution)/shard_map/ppermute | solution.py:35
  17.4 10.4 %collective-permute-start.6 = (bf16[16,4608]{1,0:T(8,128)(2,1)S(1)}, bf16[16,4608]{1,0:T(8,128)(2,1)S(1)}, u32[]{:S(2)}, u32[]{:S(2)}) collective-permute-start(bf16[16,4608]{1,0:T(8,128)(2,1)S(1)} %collective-permute-done.2.refs_3_), channel_id=1, source_target_pairs={{0,4},{2,6},{4,0},{6,2},{8,12},{10,14},{12,8},{14,10},{16,20},{18,... | collective-permute-start | bytes 442376 | tf_op jit(solution)/shard_map/ppermute | solution.py:35
  28.6 9.5 %collective-permute-start.7 = (bf16[144,4096]{1,0:T(8,128)(2,1)S(1)}, bf16[144,4096]{1,0:T(8,128)(2,1)S(1)}, u32[]{:S(2)}, u32[]{:S(2)}) collective-permute-start(bf16[144,4096]{1,0:T(8,128)(2,1)S(1)} %assemble.1.refs_0_), channel_id=1, source_target_pairs={{0,2},{2,0},{4,6},{6,4},{8,10},{10,8},{12,14},{14,12},{16,18},{18,... | collective-permute-start | bytes 3538952 | tf_op jit(solution)/shard_map/ppermute | solution.py:35
  45.1 14.8 %collective-permute-start.10 = (bf16[248,1024]{1,0:T(8,128)(2,1)S(1)}, bf16[248,1024]{1,0:T(8,128)(2,1)S(1)}, u32[]{:S(2)}, u32[]{:S(2)}) collective-permute-start(bf16[248,1024]{1,0:T(8,128)(2,1)S(1)} %get-tuple-element.32), channel_id=1, source_target_pairs={{0,1},{1,0},{2,3},{3,2},{4,5},{5,4},{6,7},{7,6},{8,9},{9,8},{10,11... | collective-permute-start | bytes 1523720 | tf_op jit(solution)/shard_map/ppermute | solution.py:39
  54.0 13.8 %collective-permute-start.8 = (bf16[248,768]{1,0:T(8,128)(2,1)S(1)}, bf16[248,768]{1,0:T(8,128)(2,1)S(1)}, u32[]{:S(2)}, u32[]{:S(2)}) collective-permute-start(bf16[248,768]{1,0:T(8,128)(2,1)S(1)} %get-tuple-element.29), channel_id=1, source_target_pairs={{0,1},{1,0},{2,3},{3,2},{4,5},{5,4},{6,7},{7,6},{8,9},{9,8},{10,11... | collective-permute-start | bytes 1142792 | tf_op jit(solution)/shard_map/ppermute | solution.py:39
  56.8 3.2 %copy-start = (s32[8]{0:T(128)S(1)}, s32[8]{0:T(128)}, u32[]{:S(2)}) copy-start(s32[8]{0:T(128)} %points_ref.3) | copy-start | bytes 100
  63.9 11.1 %collective-permute-start.11 = (bf16[80,1024]{1,0:T(8,128)(2,1)S(1)}, bf16[80,1024]{1,0:T(8,128)(2,1)S(1)}, u32[]{:S(2)}, u32[]{:S(2)}) collective-permute-start(bf16[80,1024]{1,0:T(8,128)(2,1)S(1)} %coefficients.3.refs_0_), channel_id=1, source_target_pairs={{0,1},{1,0},{2,3},{3,2},{4,5},{5,4},{6,7},{7,6},{8,9},{9,8},{10,11... | collective-permute-start | bytes 491528 | tf_op jit(solution)/shard_map/ppermute | solution.py:39
  70.7 8.8 %collective-permute-start.9 = (bf16[80,768]{1,0:T(8,128)(2,1)S(1)}, bf16[80,768]{1,0:T(8,128)(2,1)S(1)}, u32[]{:S(2)}, u32[]{:S(2)}) collective-permute-start(bf16[80,768]{1,0:T(8,128)(2,1)S(1)} %coefficients.2.refs_1_), channel_id=1, source_target_pairs={{0,1},{1,0},{2,3},{3,2},{4,5},{5,4},{6,7},{7,6},{8,9},{9,8},{10,11... | collective-permute-start | bytes 368648 | tf_op jit(solution)/shard_map/ppermute | solution.py:39
  80.7 1.7 %collective-permute-start.16 = (bf16[40,2048]{1,0:T(8,128)(2,1)S(1)}, bf16[40,2048]{1,0:T(8,128)(2,1)S(1)}, u32[]{:S(2)}, u32[]{:S(2)}) collective-permute-start(bf16[40,2048]{1,0:T(8,128)(2,1)S(1)} %get-tuple-element.36), channel_id=1, source_target_pairs={{0,2},{2,0},{4,6},{6,4},{8,10},{10,8},{12,14},{14,12},{16,18},{18,... | collective-permute-start | bytes 491528 | tf_op jit(solution)/shard_map/ppermute | solution.py:35
  81.8 2.2 %collective-permute-start.12 = (bf16[40,2048]{1,0:T(8,128)(2,1)S(1)}, bf16[40,2048]{1,0:T(8,128)(2,1)S(1)}, u32[]{:S(2)}, u32[]{:S(2)}) collective-permute-start(bf16[40,2048]{1,0:T(8,128)(2,1)S(1)} %get-tuple-element.34), channel_id=1, source_target_pairs={{0,2},{2,0},{4,6},{6,4},{8,10},{10,8},{12,14},{14,12},{16,18},{18,... | collective-permute-start | bytes 491528 | tf_op jit(solution)/shard_map/ppermute | solution.py:35
  82.4 5.5 %collective-permute-start.17 = (bf16[20,2048]{1,0:T(8,128)(2,1)S(1)}, bf16[20,2048]{1,0:T(8,128)(2,1)S(1)}, u32[]{:S(2)}, u32[]{:S(2)}) collective-permute-start(bf16[20,2048]{1,0:T(8,128)(2,1)S(1)} %slice.82), channel_id=1, source_target_pairs={{0,4},{2,6},{4,0},{6,2},{8,12},{10,14},{12,8},{14,10},{16,20},{18,... | collective-permute-start | bytes 245768 | tf_op jit(solution)/shard_map/ppermute | solution.py:35
  84.1 5.2 %collective-permute-start.13 = (bf16[20,2048]{1,0:T(8,128)(2,1)S(1)}, bf16[20,2048]{1,0:T(8,128)(2,1)S(1)}, u32[]{:S(2)}, u32[]{:S(2)}) collective-permute-start(bf16[20,2048]{1,0:T(8,128)(2,1)S(1)} %slice.83), channel_id=1, source_target_pairs={{0,4},{2,6},{4,0},{6,2},{8,12},{10,14},{12,8},{14,10},{16,20},{18,... | collective-permute-start | bytes 245768 | tf_op jit(solution)/shard_map/ppermute | solution.py:35
  88.0 4.8 %collective-permute-start.18 = (bf16[10,2048]{1,0:T(8,128)(2,1)S(1)}, bf16[10,2048]{1,0:T(8,128)(2,1)S(1)}, u32[]{:S(2)}, u32[]{:S(2)}) collective-permute-start(bf16[10,2048]{1,0:T(8,128)(2,1)S(1)} %slice.84), channel_id=1, source_target_pairs={{0,8},{2,10},{4,12},{6,14},{8,0},{10,2},{12,4},{14,6},{16,24},{18,... | collective-permute-start | bytes 122888 | tf_op jit(solution)/shard_map/ppermute | solution.py:35
  89.4 7.2 %collective-permute-start.14 = (bf16[10,2048]{1,0:T(8,128)(2,1)S(1)}, bf16[10,2048]{1,0:T(8,128)(2,1)S(1)}, u32[]{:S(2)}, u32[]{:S(2)}) collective-permute-start(bf16[10,2048]{1,0:T(8,128)(2,1)S(1)} %slice.85), channel_id=1, source_target_pairs={{0,8},{2,10},{4,12},{6,14},{8,0},{10,2},{12,4},{14,6},{16,24},{18,... | collective-permute-start | bytes 122888 | tf_op jit(solution)/shard_map/ppermute | solution.py:35
  92.9 5.6 %collective-permute-start.19 = (bf16[5,2048]{1,0:T(8,128)(2,1)S(1)}, bf16[5,2048]{1,0:T(8,128)(2,1)S(1)}, u32[]{:S(2)}, u32[]{:S(2)}) collective-permute-start(bf16[5,2048]{1,0:T(8,128)(2,1)S(1)} %slice.86), channel_id=1, source_target_pairs={{0,16},{2,18},{4,20},{6,22},{8,24},{10,26},{12,28},{14,30},{16,0},... | collective-permute-start | bytes 61448 | tf_op jit(solution)/shard_map/ppermute | solution.py:35
  96.6 4.9 %collective-permute-start.15 = (bf16[5,2048]{1,0:T(8,128)(2,1)S(1)}, bf16[5,2048]{1,0:T(8,128)(2,1)S(1)}, u32[]{:S(2)}, u32[]{:S(2)}) collective-permute-start(bf16[5,2048]{1,0:T(8,128)(2,1)S(1)} %slice.87), channel_id=1, source_target_pairs={{0,16},{2,18},{4,20},{6,22},{8,24},{10,26},{12,28},{14,30},{16,0},... | collective-permute-start | bytes 61448 | tf_op jit(solution)/shard_map/ppermute | solution.py:35

commit v3 on v2

--- a/solution.py
+++ b/solution.py
@@ -269,10 +269,14 @@
             (out,) = refs
         for copy in copies:
             copy.start()
-        out[pl.ds(0, rows), :] = jnp.dot(
-            main_ref[...], both[...], preferred_element_type=jnp.float32
-        ).astype(dtype)
-        put_side(out, across(side_ref[...], below[...]))
+
+        @pl.when(lax.axis_index("narrow") >= 0)
+        def _():
+            out[pl.ds(0, rows), :] = jnp.dot(
+                main_ref[...], both[...], preferred_element_type=jnp.float32
+            ).astype(dtype)
+            put_side(out, across(side_ref[...], below[...]))
+
         for copy in copies:
             copy.wait()
 
@@ -609,15 +613,25 @@
     last = [backward(groups[-1], total, pair == 2, span) for span in spans]
 
     results = []
-    for value in last:
+    for i, value in enumerate(last):
         if pair == 2:
             sent, kept = value
             value = kept + permute(sent, "wide", dims, 2, 1).astype(jnp.float32)
-        steps = [(1, 1)] * (near == 2) + [(0, 1 << i) for i in range(far.bit_length() - 1)]
-        for digit, amount in steps:
-            middle = value.shape[0] // 2
-            got = permute(value[middle:].astype(jnp.bfloat16), "wide", dims, digit, amount)
-            value = value[:middle] + got.astype(jnp.float32)
+        digits = [(1, 1)] * (near == 2) + [(0, 1 << bit) for bit in range(far.bit_length() - 1)]
+        steps = list(digits)
+        if i % 2 and len(steps) > 1:
+            steps[:2] = steps[1::-1]
+        for step in steps:
+            at = digits.index(step)
+            outer, inner = 1 << at, value.shape[0] >> (at + 1)
+            digits.remove(step)
+
+            def half(which):
+                rows = [value[(2 * o + which) * inner:(2 * o + which + 1) * inner] for o in range(outer)]
+                return rows[0] if outer == 1 else jnp.concatenate(rows)
+
+            got = permute(half(1).astype(jnp.bfloat16), "wide", dims, *step)
+            value = half(0) + got.astype(jnp.float32)
         results.append(value.astype(jnp.bfloat16))
     return results[0] if len(results) == 1 else jnp.concatenate(results, axis=1)
 

time: 102 us -> 98 us (0.961)
  Pallas kernels: 46.3 us -> 41 us
    pallas_call x4, Pallas kernels: 19.4 us -> 14.4 us  [forward(): pl.pallas_call(body_ready if ready else body, out_shape=out_shape, in_spe...]
    ppermute x4, waiting for transfers between devices: 2.25 us -> 4.54 us  [shift(): lax.ppermute(array, 'narrow', [(at, (at + amount) % size) for at in range...]
    ppermute x16, waiting for transfers between devices: 26 us -> 23.7 us  [permute(): return lax.ppermute(array, axis, pairs)]
  transfers between devices with their start and end apart: 20 -> 20, of which waited for: 12 -> 13; matrix products, arithmetic and copies ran while one was open for 1% -> 1% of each run, Pallas kernels for 36% -> 35%
where the time goes in v3:
time: 98 us; the launch traced here: 97.8 us
  Pallas kernels  41 us (42%)
  waiting for transfers between devices  28.2 us (29%)
  starting transfers between devices  26.5 us (27%)
    ppermute x16, waiting for transfers between devices, permute(): return lax.ppermute(array, axis, pairs)  23.7 us
    ppermute x16, starting transfers between devices, permute(): return lax.ppermute(array, axis, pairs)  21.2 us
    pallas_call x4, Pallas kernels, forward(): pl.pallas_call(body_ready if ready else body, out_shape=out_shape, in_spe...  14.4 us
    pallas_call x4, Pallas kernels, backward(): pl.pallas_call(body, out_shape=out_shape, in_specs=specs, out_specs=out_s...  9.35 us
    pallas_call x2, Pallas kernels, fetch(): pl.pallas_call(body, out_shape=(pltpu.VMEM((depth, 2 * width), jnp.bfloat...  8.66 us
    pallas_call x2, Pallas kernels, coefficients(): pl.pallas_call(body, out_shape=jax.ShapeDtypeStruct((examples, 2 * width)...  6.63 us
    ppermute x4, starting transfers between devices, shift(): lax.ppermute(array, 'narrow', [(at, (at + amount) % size) for at in range...  5.34 us
    ppermute x4, waiting for transfers between devices, shift(): lax.ppermute(array, 'narrow', [(at, (at + amount) % size) for at in range...  4.54 us
  transfers between devices with their start and end apart: 20, of which 13 were waited for; matrix products, arithmetic and copies ran while one was open for 1% of the time, Pallas kernels for 35%

profile of v3, /device:TPU:0, one launch (start us, length us, event | category | flops | bytes accessed | tf_op | source)
XLA Modules:
  0.0 97.8 jit_solution(13252083483394360634)
XLA Ops:
  0.0 1.0 pack.1.refs_0_
  1.0 4.1 %collective-permute-start = (bf16[16,4608]{1,0:T(8,128)(2,1)S(1)}, bf16[16,4608]{1,0:T(8,128)(2,1)S(1)}, u32[]{:S(2)}, u32[]{:S(2)}) collective-permute-start(bf16[16,4608]{1,0:T(8,128)(2,1)S(1)} %pack.1.refs_0_), channel_id=1, source_target_pairs={{0,16},{2,18},{4,20},{6,22},{8,24},{10,26},{12,28},{14,30},{16,0},... | collective-permute-start | bytes 442376 | tf_op jit(solution)/shard_map/ppermute | solution.py:35
  5.1 1.6 %collective-permute-start.1 = (bf16[16,4608]{1,0:T(8,128)(2,1)S(1)}, bf16[16,4608]{1,0:T(8,128)(2,1)S(1)}, u32[]{:S(2)}, u32[]{:S(2)}) collective-permute-start(bf16[16,4608]{1,0:T(8,128)(2,1)S(1)} %pack.1.refs_0_), channel_id=1, source_target_pairs={{0,8},{2,10},{4,12},{6,14},{8,0},{10,2},{12,4},{14,6},{16,24},{18,... | collective-permute-start | bytes 442376 | tf_op jit(solution)/shard_map/ppermute | solution.py:35
  6.7 5.5 %collective-permute-done.refs_1_ = bf16[16,4608]{1,0:T(8,128)(2,1)S(1)} collective-permute-done((bf16[16,4608]{1,0:T(8,128)(2,1)S(1)}, bf16[16,4608]{1,0:T(8,128)(2,1)S(1)}, u32[]{:S(2)}, u32[]{:S(2)}) %collective-permute-start) | collective-permute-done | bytes 147488 | tf_op jit(solution)/shard_map/ppermute | solution.py:35
  12.2 0.6 collective-permute-start.2
  12.8 1.5 %collective-permute-start.3 = (bf16[16,4608]{1,0:T(8,128)(2,1)S(1)}, bf16[16,4608]{1,0:T(8,128)(2,1)S(1)}, u32[]{:S(2)}, u32[]{:S(2)}) collective-permute-start(bf16[16,4608]{1,0:T(8,128)(2,1)S(1)} %pack.1.refs_0_), channel_id=1, source_target_pairs={{0,4},{2,6},{4,0},{6,2},{8,12},{10,14},{12,8},{14,10},{16,20},{18,... | collective-permute-start | bytes 442376 | tf_op jit(solution)/shard_map/ppermute | solution.py:35
  14.4 0.5 collective-permute-start.4
  14.9 1.5 %collective-permute-start.5 = (bf16[16,4608]{1,0:T(8,128)(2,1)S(1)}, bf16[16,4608]{1,0:T(8,128)(2,1)S(1)}, u32[]{:S(2)}, u32[]{:S(2)}) collective-permute-start(bf16[16,4608]{1,0:T(8,128)(2,1)S(1)} %collective-permute-done.1.refs_2_), channel_id=1, source_target_pairs={{0,4},{2,6},{4,0},{6,2},{8,12},{10,14},{12,8},{14,10},{16,20},{18,... | collective-permute-start | bytes 442376 | tf_op jit(solution)/shard_map/ppermute | solution.py:35
  16.4 1.0 collective-permute-done.2.refs_3_
  17.4 1.6 %collective-permute-start.6 = (bf16[16,4608]{1,0:T(8,128)(2,1)S(1)}, bf16[16,4608]{1,0:T(8,128)(2,1)S(1)}, u32[]{:S(2)}, u32[]{:S(2)}) collective-permute-start(bf16[16,4608]{1,0:T(8,128)(2,1)S(1)} %collective-permute-done.2.refs_3_), channel_id=1, source_target_pairs={{0,4},{2,6},{4,0},{6,2},{8,12},{10,14},{12,8},{14,10},{16,20},{18,... | collective-permute-start | bytes 442376 | tf_op jit(solution)/shard_map/ppermute | solution.py:35
  18.9 0.6 collective-permute-done.3.refs_4_
  19.6 3.2 %collective-permute-done.4.refs_5_ = bf16[16,4608]{1,0:T(8,128)(2,1)S(1)} collective-permute-done((bf16[16,4608]{1,0:T(8,128)(2,1)S(1)}, bf16[16,4608]{1,0:T(8,128)(2,1)S(1)}, u32[]{:S(2)}, u32[]{:S(2)}) %collective-permute-start.4) | collective-permute-done | bytes 147488 | tf_op jit(solution)/shard_map/ppermute | solution.py:35
  22.7 3.2 %collective-permute-done.5.refs_6_ = bf16[16,4608]{1,0:T(8,128)(2,1)S(1)} collective-permute-done((bf16[16,4608]{1,0:T(8,128)(2,1)S(1)}, bf16[16,4608]{1,0:T(8,128)(2,1)S(1)}, u32[]{:S(2)}, u32[]{:S(2)}) %collective-permute-start.5) | collective-permute-done | bytes 147488 | tf_op jit(solution)/shard_map/ppermute | solution.py:35
  25.9 1.9 %collective-permute-done.6.refs_7_ = bf16[16,4608]{1,0:T(8,128)(2,1)S(1)} collective-permute-done((bf16[16,4608]{1,0:T(8,128)(2,1)S(1)}, bf16[16,4608]{1,0:T(8,128)(2,1)S(1)}, u32[]{:S(2)}, u32[]{:S(2)}) %collective-permute-start.6) | collective-permute-done | bytes 147488 | tf_op jit(solution)/shard_map/ppermute | solution.py:35
  27.8 0.8 assemble.1.refs_0_
  28.6 0.8 copy.9.pair_ref
  29.4 4.8 %fetch.2 = (bf16[4096,1024]{1,0:T(8,128)(2,1)S(1)}, bf16[512,4096]{1,0:T(8,128)(2,1)S(1)}) custom-call(bf16[4096,1792]{1,0:T(8,128)(2,1)} %refs_0_.5, bf16[4096,1792]{1,0:T(8,128)(2,1)} %refs_1_.5, bf16[1792,4096]{1,0:T(8,128)(2,1)} %refs_2_.5), custom_call_target="tpu_custom_call" | custom-call | flops 4000000000 | bytes 12582912 | tf_op jit(solution)/shard_map/fetch/pallas_call | solution.py:231
  34.2 3.9 %fetch.3 = (bf16[4096,768]{1,0:T(8,128)(2,1)S(1)}, bf16[384,4096]{1,0:T(8,128)(2,1)S(1)}) custom-call(bf16[4096,1792]{1,0:T(8,128)(2,1)} %refs_0_.5, bf16[4096,1792]{1,0:T(8,128)(2,1)} %refs_1_.5, bf16[1792,4096]{1,0:T(8,128)(2,1)} %refs_2_.5), custom_call_target="tpu_custom_call" | custom-call | flops 4000000000 | bytes 9437184 | tf_op jit(solution)/shard_map/fetch/pallas_call | solution.py:231
  38.1 0.2 join.1
  38.3 3.9 %forward.4 = (bf16[248,1024]{1,0:T(8,128)(2,1)S(1)}, bf16[4096,768]{1,0:T(8,128)(2,1)S(1)}, bf16[384,4096]{1,0:T(8,128)(2,1)S(1)}) custom-call(bf16[208,4096]{1,0:T(8,128)(2,1)S(1)} %get-tuple-element.21.main_ref, bf16[80,4096]{1,0:T(8,128)(2,1)S(1)} %get-tuple-element.22.side_ref, bf16[4096,1024]{1,0:T(8,128)(2,1)S(1)} %get-tuple-element.23.both.refs_2_, ...), custom_call_target="tpu_custom_call" | custom-call | flops 2080374784 | bytes 12582912 | tf_op jit(solution)/shard_map/forward/pallas_call | solution.py:323
  42.1 1.6 %collective-permute-start.10 = (bf16[248,1024]{1,0:T(8,128)(2,1)S(1)}, bf16[248,1024]{1,0:T(8,128)(2,1)S(1)}, u32[]{:S(2)}, u32[]{:S(2)}) collective-permute-start(bf16[248,1024]{1,0:T(8,128)(2,1)S(1)} %get-tuple-element.32), channel_id=1, source_target_pairs={{0,1},{1,0},{2,3},{3,2},{4,5},{5,4},{6,7},{7,6},{8,9},{9,8},{10,11... | collective-permute-start | bytes 1523720 | tf_op jit(solution)/shard_map/ppermute | solution.py:39
  43.9 4.8 %forward.6 = (bf16[248,768]{1,0:T(8,128)(2,1)S(1)}, bf16[4096,1024]{1,0:T(8,128)(2,1)S(1)}, bf16[512,4096]{1,0:T(8,128)(2,1)S(1)}) custom-call(bf16[208,4096]{1,0:T(8,128)(2,1)S(1)} %get-tuple-element.21.main_ref, bf16[80,4096]{1,0:T(8,128)(2,1)S(1)} %get-tuple-element.22.side_ref, bf16[4096,768]{1,0:T(8,128)(2,1)S(1)} %get-tuple-element.27.both.refs_1_, ...), custom_call_target="tpu_custom_call" | custom-call | flops 1560281088 | bytes 9437184 | tf_op jit(solution)/shard_map/forward/pallas_call | solution.py:323
  48.8 0.5 collective-permute-start.8
  49.2 2.4 %forward.5.kept_ref = f32[248,768]{1,0:T(8,128)S(1)} custom-call(bf16[208,4096]{1,0:T(8,128)(2,1)S(1)} %get-tuple-element.21.main_ref, bf16[80,4096]{1,0:T(8,128)(2,1)S(1)} %get-tuple-element.22.side_ref, bf16[4096,768]{1,0:T(8,128)(2,1)S(1)} %get-tuple-element.25.both.refs_3_, bf16[384,4096]{1,0:T(8,128)(2,1)S(1)} %get-tuple-element.26.below), custom_call_target="tpu_custom_call" | custom-call | flops 1560281088 | bytes 9437184 | tf_op jit(solution)/shard_map/forward/pallas_call | solution.py:323
  51.6 3.3 %forward.7.kept_ref = f32[248,1024]{1,0:T(8,128)S(1)} custom-call(bf16[208,4096]{1,0:T(8,128)(2,1)S(1)} %get-tuple-element.21.main_ref, bf16[80,4096]{1,0:T(8,128)(2,1)S(1)} %get-tuple-element.22.side_ref, bf16[4096,1024]{1,0:T(8,128)(2,1)S(1)} %get-tuple-element.30.both.refs_1_, bf16[512,4096]{1,0:T(8,128)(2,1)S(1)} %get-tuple-element.31.below), custom_call_target="tpu_custom_call" | custom-call | flops 2080374784 | bytes 12582912 | tf_op jit(solution)/shard_map/forward/pallas_call | solution.py:323
  54.9 1.7 %collective-permute-done.10.refs_0_ = bf16[248,1024]{1,0:T(8,128)(2,1)S(1)} collective-permute-done((bf16[248,1024]{1,0:T(8,128)(2,1)S(1)}, bf16[248,1024]{1,0:T(8,128)(2,1)S(1)}, u32[]{:S(2)}, u32[]{:S(2)}) %collective-permute-start.10) | collective-permute-done | bytes 507936 | tf_op jit(solution)/shard_map/ppermute | solution.py:39
  56.7 3.7 %coefficients.3.refs_0_ = bf16[80,1024]{1,0:T(8,128)(2,1)S(1)} custom-call(s32[8]{0:T(128)S(1)} %copy-done, bf16[320,128]{1,0:T(8,128)(2,1)S(1)} %choices.1.picks_ref, f32[248,1024]{1,0:T(8,128)S(1)} %forward.7.kept_ref, bf16[248,1024]{1,0:T(8,128)(2,1)S(1)} %collective-permute-done.10.refs_0_), custom_call_target="tpu_custom_call" | custom-call | flops 5000000000 | bytes 1000000 | tf_op jit(solution)/shard_map/coefficients/pallas_call | solution.py:404
  60.4 1.6 %collective-permute-start.11 = (bf16[80,1024]{1,0:T(8,128)(2,1)S(1)}, bf16[80,1024]{1,0:T(8,128)(2,1)S(1)}, u32[]{:S(2)}, u32[]{:S(2)}) collective-permute-start(bf16[80,1024]{1,0:T(8,128)(2,1)S(1)} %coefficients.3.refs_0_), channel_id=1, source_target_pairs={{0,1},{1,0},{2,3},{3,2},{4,5},{5,4},{6,7},{7,6},{8,9},{9,8},{10,11... | collective-permute-start | bytes 491528 | tf_op jit(solution)/shard_map/ppermute | solution.py:39
  62.0 2.8 %collective-permute-done.8.refs_0_ = bf16[248,768]{1,0:T(8,128)(2,1)S(1)} collective-permute-done((bf16[248,768]{1,0:T(8,128)(2,1)S(1)}, bf16[248,768]{1,0:T(8,128)(2,1)S(1)}, u32[]{:S(2)}, u32[]{:S(2)}) %collective-permute-start.8) | collective-permute-done | bytes 380960 | tf_op jit(solution)/shard_map/ppermute | solution.py:39
  64.8 2.9 %coefficients.2.refs_1_ = bf16[80,768]{1,0:T(8,128)(2,1)S(1)} custom-call(s32[8]{0:T(128)S(1)} %copy-done, bf16[320,128]{1,0:T(8,128)(2,1)S(1)} %choices.1.picks_ref, f32[248,768]{1,0:T(8,128)S(1)} %forward.5.kept_ref, bf16[248,768]{1,0:T(8,128)(2,1)S(1)} %collective-permute-done.8.refs_0_), custom_call_target="tpu_custom_call" | custom-call | flops 5000000000 | bytes 1000000 | tf_op jit(solution)/shard_map/coefficients/pallas_call | solution.py:404
  67.7 1.6 %collective-permute-start.9 = (bf16[80,768]{1,0:T(8,128)(2,1)S(1)}, bf16[80,768]{1,0:T(8,128)(2,1)S(1)}, u32[]{:S(2)}, u32[]{:S(2)}) collective-permute-start(bf16[80,768]{1,0:T(8,128)(2,1)S(1)} %coefficients.2.refs_1_), channel_id=1, source_target_pairs={{0,1},{1,0},{2,3},{3,2},{4,5},{5,4},{6,7},{7,6},{8,9},{9,8},{10,11... | collective-permute-start | bytes 368648 | tf_op jit(solution)/shard_map/ppermute | solution.py:39
  69.4 2.7 %backward.4.refs_4_ = f32[80,4096]{1,0:T(8,128)S(1)} custom-call(bf16[80,1024]{1,0:T(8,128)(2,1)S(1)} %coefficients.3.refs_0_, bf16[4096,1024]{1,0:T(8,128)(2,1)S(1)} %get-tuple-element.30.both.refs_1_), custom_call_target="tpu_custom_call" | custom-call | flops 671088640 | bytes 8388608 | tf_op jit(solution)/shard_map/backward/pallas_call | solution.py:463
  72.0 4.5 %backward.5.refs_2_ = f32[80,4096]{1,0:T(8,128)S(1)} custom-call(bf16[80,1024]{1,0:T(8,128)(2,1)S(1)} %collective-permute-done.11.refs_0_, bf16[80,768]{1,0:T(8,128)(2,1)S(1)} %coefficients.2.refs_1_, bf16[4096,1024]{1,0:T(8,128)(2,1)S(1)} %get-tuple-element.23.both.refs_2_, bf16[4096,768]{1,0:T(8,128)(2,1)S(1)} %get-tuple-element.25.both.refs_3_, ...), custom_call_target="tpu_custom_call" | custom-call | flops 1174405120 | bytes 8388608 | tf_op jit(solution)/shard_map/backward/pallas_call | solution.py:463
  76.6 1.1 %backward.7 = (bf16[40,2048]{1,0:T(8,128)(2,1)S(1)}, f32[40,2048]{1,0:T(8,128)S(1)}) custom-call(bf16[80,768]{1,0:T(8,128)(2,1)S(1)} %collective-permute-done.9.refs_0_, bf16[4096,768]{1,0:T(8,128)(2,1)S(1)} %get-tuple-element.27.both.refs_1_, f32[80,4096]{1,0:T(8,128)S(1)} %backward.5.refs_2_), custom_call_target="tpu_custom_call" | custom-call | flops 251658240 | bytes 3145728 | tf_op jit(solution)/shard_map/backward/pallas_call | solution.py:463
  77.7 1.1 %backward.6 = (bf16[40,2048]{1,0:T(8,128)(2,1)S(1)}, f32[40,2048]{1,0:T(8,128)S(1)}) custom-call(bf16[80,768]{1,0:T(8,128)(2,1)S(1)} %collective-permute-done.9.refs_0_, bf16[4096,768]{1,0:T(8,128)(2,1)S(1)} %get-tuple-element.27.both.refs_1_, f32[80,4096]{1,0:T(8,128)S(1)} %backward.5.refs_2_), custom_call_target="tpu_custom_call" | custom-call | flops 251658240 | bytes 3145728 | tf_op jit(solution)/shard_map/backward/pallas_call | solution.py:463
  78.8 0.6 collective-permute-start.12
  79.5 0.3 collective-permute-start.17
  79.8 0.6 collective-permute-done.12
  80.5 1.6 %collective-permute-start.13 = (bf16[20,2048]{1,0:T(8,128)(2,1)S(1)}, bf16[20,2048]{1,0:T(8,128)(2,1)S(1)}, u32[]{:S(2)}, u32[]{:S(2)}) collective-permute-start(bf16[20,2048]{1,0:T(8,128)(2,1)S(1)} %slice.91), channel_id=1, source_target_pairs={{0,4},{2,6},{4,0},{6,2},{8,12},{10,14},{12,8},{14,10},{16,20},{18,... | collective-permute-start | bytes 245768 | tf_op jit(solution)/shard_map/ppermute | solution.py:35
  82.1 2.2 %collective-permute-done.17 = bf16[20,2048]{1,0:T(8,128)(2,1)S(1)} collective-permute-done((bf16[20,2048]{1,0:T(8,128)(2,1)S(1)}, bf16[20,2048]{1,0:T(8,128)(2,1)S(1)}, u32[]{:S(2)}, u32[]{:S(2)}) %collective-permute-start.17) | collective-permute-done | bytes 81952 | tf_op jit(solution)/shard_map/ppermute | solution.py:35
  84.3 1.6 %collective-permute-start.18 = (bf16[10,2048]{1,0:T(8,128)(2,1)S(1)}, bf16[10,2048]{1,0:T(8,128)(2,1)S(1)}, u32[]{:S(2)}, u32[]{:S(2)}) collective-permute-start(bf16[10,2048]{1,0:T(8,128)(2,1)S(1)} %slice.92), channel_id=1, source_target_pairs={{0,4},{2,6},{4,0},{6,2},{8,12},{10,14},{12,8},{14,10},{16,20},{18,... | collective-permute-start | bytes 122888 | tf_op jit(solution)/shard_map/ppermute | solution.py:35
  86.0 0.5 collective-permute-start.14
  86.5 2.2 %collective-permute-done.18 = bf16[10,2048]{1,0:T(8,128)(2,1)S(1)} collective-permute-done((bf16[10,2048]{1,0:T(8,128)(2,1)S(1)}, bf16[10,2048]{1,0:T(8,128)(2,1)S(1)}, u32[]{:S(2)}, u32[]{:S(2)}) %collective-permute-start.18) | collective-permute-done | bytes 40992 | tf_op jit(solution)/shard_map/ppermute | solution.py:35
  88.7 3.4 %collective-permute-start.19 = (bf16[5,2048]{1,0:T(8,128)(2,1)S(1)}, bf16[5,2048]{1,0:T(8,128)(2,1)S(1)}, u32[]{:S(2)}, u32[]{:S(2)}) collective-permute-start(bf16[5,2048]{1,0:T(8,128)(2,1)S(1)} %slice.94), channel_id=1, source_target_pairs={{0,16},{2,18},{4,20},{6,22},{8,24},{10,26},{12,28},{14,30},{16,0},... | collective-permute-start | bytes 61448 | tf_op jit(solution)/shard_map/ppermute | solution.py:35
  92.2 1.6 %collective-permute-start.15 = (bf16[5,2048]{1,0:T(8,128)(2,1)S(1)}, bf16[5,2048]{1,0:T(8,128)(2,1)S(1)}, u32[]{:S(2)}, u32[]{:S(2)}) collective-permute-start(bf16[5,2048]{1,0:T(8,128)(2,1)S(1)} %slice.95), channel_id=1, source_target_pairs={{0,16},{2,18},{4,20},{6,22},{8,24},{10,26},{12,28},{14,30},{16,0},... | collective-permute-start | bytes 61448 | tf_op jit(solution)/shard_map/ppermute | solution.py:35
  93.8 0.8 collective-permute-done.19
  94.7 2.5 %collective-permute-done.15 = bf16[5,2048]{1,0:T(8,128)(2,1)S(1)} collective-permute-done((bf16[5,2048]{1,0:T(8,128)(2,1)S(1)}, bf16[5,2048]{1,0:T(8,128)(2,1)S(1)}, u32[]{:S(2)}, u32[]{:S(2)}) %collective-permute-start.15) | collective-permute-done | bytes 20512 | tf_op jit(solution)/shard_map/ppermute | solution.py:35
  97.2 0.6 pad_maximum_fusion.1
  (28 shorter events, 0.6 us)
Async XLA Ops:
  1.0 11.2 %collective-permute-start = (bf16[16,4608]{1,0:T(8,128)(2,1)S(1)}, bf16[16,4608]{1,0:T(8,128)(2,1)S(1)}, u32[]{:S(2)}, u32[]{:S(2)}) collective-permute-start(bf16[16,4608]{1,0:T(8,128)(2,1)S(1)} %pack.1.refs_0_), channel_id=1, source_target_pairs={{0,16},{2,18},{4,20},{6,22},{8,24},{10,26},{12,28},{14,30},{16,0},... | collective-permute-start | bytes 442376 | tf_op jit(solution)/shard_map/ppermute | solution.py:35
  5.1 9.8 %collective-permute-start.1 = (bf16[16,4608]{1,0:T(8,128)(2,1)S(1)}, bf16[16,4608]{1,0:T(8,128)(2,1)S(1)}, u32[]{:S(2)}, u32[]{:S(2)}) collective-permute-start(bf16[16,4608]{1,0:T(8,128)(2,1)S(1)} %pack.1.refs_0_), channel_id=1, source_target_pairs={{0,8},{2,10},{4,12},{6,14},{8,0},{10,2},{12,4},{14,6},{16,24},{18,... | collective-permute-start | bytes 442376 | tf_op jit(solution)/shard_map/ppermute | solution.py:35
  12.2 5.1 %collective-permute-start.2 = (bf16[16,4608]{1,0:T(8,128)(2,1)S(1)}, bf16[16,4608]{1,0:T(8,128)(2,1)S(1)}, u32[]{:S(2)}, u32[]{:S(2)}) collective-permute-start(bf16[16,4608]{1,0:T(8,128)(2,1)S(1)} %collective-permute-done.refs_1_), channel_id=1, source_target_pairs={{0,8},{2,10},{4,12},{6,14},{8,0},{10,2},{12,4},{14,6},{16,24},{18,... | collective-permute-start | bytes 442376 | tf_op jit(solution)/shard_map/ppermute | solution.py:35
  12.8 6.7 %collective-permute-start.3 = (bf16[16,4608]{1,0:T(8,128)(2,1)S(1)}, bf16[16,4608]{1,0:T(8,128)(2,1)S(1)}, u32[]{:S(2)}, u32[]{:S(2)}) collective-permute-start(bf16[16,4608]{1,0:T(8,128)(2,1)S(1)} %pack.1.refs_0_), channel_id=1, source_target_pairs={{0,4},{2,6},{4,0},{6,2},{8,12},{10,14},{12,8},{14,10},{16,20},{18,... | collective-permute-start | bytes 442376 | tf_op jit(solution)/shard_map/ppermute | solution.py:35
  14.4 8.4 %collective-permute-start.4 = (bf16[16,4608]{1,0:T(8,128)(2,1)S(1)}, bf16[16,4608]{1,0:T(8,128)(2,1)S(1)}, u32[]{:S(2)}, u32[]{:S(2)}) collective-permute-start(bf16[16,4608]{1,0:T(8,128)(2,1)S(1)} %collective-permute-done.refs_1_), channel_id=1, source_target_pairs={{0,4},{2,6},{4,0},{6,2},{8,12},{10,14},{12,8},{14,10},{16,20},{18,... | collective-permute-start | bytes 442376 | tf_op jit(solution)/shard_map/ppermute | solution.py:35
  14.9 11.0 %collective-permute-start.5 = (bf16[16,4608]{1,0:T(8,128)(2,1)S(1)}, bf16[16,4608]{1,0:T(8,128)(2,1)S(1)}, u32[]{:S(2)}, u32[]{:S(2)}) collective-permute-start(bf16[16,4608]{1,0:T(8,128)(2,1)S(1)} %collective-permute-done.1.refs_2_), channel_id=1, source_target_pairs={{0,4},{2,6},{4,0},{6,2},{8,12},{10,14},{12,8},{14,10},{16,20},{18,... | collective-permute-start | bytes 442376 | tf_op jit(solution)/shard_map/ppermute | solution.py:35
  17.4 10.4 %collective-permute-start.6 = (bf16[16,4608]{1,0:T(8,128)(2,1)S(1)}, bf16[16,4608]{1,0:T(8,128)(2,1)S(1)}, u32[]{:S(2)}, u32[]{:S(2)}) collective-permute-start(bf16[16,4608]{1,0:T(8,128)(2,1)S(1)} %collective-permute-done.2.refs_3_), channel_id=1, source_target_pairs={{0,4},{2,6},{4,0},{6,2},{8,12},{10,14},{12,8},{14,10},{16,20},{18,... | collective-permute-start | bytes 442376 | tf_op jit(solution)/shard_map/ppermute | solution.py:35
  28.6 9.5 %collective-permute-start.7 = (bf16[144,4096]{1,0:T(8,128)(2,1)S(1)}, bf16[144,4096]{1,0:T(8,128)(2,1)S(1)}, u32[]{:S(2)}, u32[]{:S(2)}) collective-permute-start(bf16[144,4096]{1,0:T(8,128)(2,1)S(1)} %assemble.1.refs_0_), channel_id=1, source_target_pairs={{0,2},{2,0},{4,6},{6,4},{8,10},{10,8},{12,14},{14,12},{16,18},{18,... | collective-permute-start | bytes 3538952 | tf_op jit(solution)/shard_map/ppermute | solution.py:35
  42.1 14.5 %collective-permute-start.10 = (bf16[248,1024]{1,0:T(8,128)(2,1)S(1)}, bf16[248,1024]{1,0:T(8,128)(2,1)S(1)}, u32[]{:S(2)}, u32[]{:S(2)}) collective-permute-start(bf16[248,1024]{1,0:T(8,128)(2,1)S(1)} %get-tuple-element.32), channel_id=1, source_target_pairs={{0,1},{1,0},{2,3},{3,2},{4,5},{5,4},{6,7},{7,6},{8,9},{9,8},{10,11... | collective-permute-start | bytes 1523720 | tf_op jit(solution)/shard_map/ppermute | solution.py:39
  48.8 16.0 %collective-permute-start.8 = (bf16[248,768]{1,0:T(8,128)(2,1)S(1)}, bf16[248,768]{1,0:T(8,128)(2,1)S(1)}, u32[]{:S(2)}, u32[]{:S(2)}) collective-permute-start(bf16[248,768]{1,0:T(8,128)(2,1)S(1)} %get-tuple-element.29), channel_id=1, source_target_pairs={{0,1},{1,0},{2,3},{3,2},{4,5},{5,4},{6,7},{7,6},{8,9},{9,8},{10,11... | collective-permute-start | bytes 1142792 | tf_op jit(solution)/shard_map/ppermute | solution.py:39
  51.6 5.1 %copy-start = (s32[8]{0:T(128)S(1)}, s32[8]{0:T(128)}, u32[]{:S(2)}) copy-start(s32[8]{0:T(128)} %points_ref.3) | copy-start | bytes 100
  60.4 11.6 %collective-permute-start.11 = (bf16[80,1024]{1,0:T(8,128)(2,1)S(1)}, bf16[80,1024]{1,0:T(8,128)(2,1)S(1)}, u32[]{:S(2)}, u32[]{:S(2)}) collective-permute-start(bf16[80,1024]{1,0:T(8,128)(2,1)S(1)} %coefficients.3.refs_0_), channel_id=1, source_target_pairs={{0,1},{1,0},{2,3},{3,2},{4,5},{5,4},{6,7},{7,6},{8,9},{9,8},{10,11... | collective-permute-start | bytes 491528 | tf_op jit(solution)/shard_map/ppermute | solution.py:39
  67.7 8.8 %collective-permute-start.9 = (bf16[80,768]{1,0:T(8,128)(2,1)S(1)}, bf16[80,768]{1,0:T(8,128)(2,1)S(1)}, u32[]{:S(2)}, u32[]{:S(2)}) collective-permute-start(bf16[80,768]{1,0:T(8,128)(2,1)S(1)} %coefficients.2.refs_1_), channel_id=1, source_target_pairs={{0,1},{1,0},{2,3},{3,2},{4,5},{5,4},{6,7},{7,6},{8,9},{9,8},{10,11... | collective-permute-start | bytes 368648 | tf_op jit(solution)/shard_map/ppermute | solution.py:39
  77.7 1.7 %collective-permute-start.16 = (bf16[40,2048]{1,0:T(8,128)(2,1)S(1)}, bf16[40,2048]{1,0:T(8,128)(2,1)S(1)}, u32[]{:S(2)}, u32[]{:S(2)}) collective-permute-start(bf16[40,2048]{1,0:T(8,128)(2,1)S(1)} %get-tuple-element.36), channel_id=1, source_target_pairs={{0,2},{2,0},{4,6},{6,4},{8,10},{10,8},{12,14},{14,12},{16,18},{18,... | collective-permute-start | bytes 491528 | tf_op jit(solution)/shard_map/ppermute | solution.py:35
  78.8 1.6 %collective-permute-start.12 = (bf16[40,2048]{1,0:T(8,128)(2,1)S(1)}, bf16[40,2048]{1,0:T(8,128)(2,1)S(1)}, u32[]{:S(2)}, u32[]{:S(2)}) collective-permute-start(bf16[40,2048]{1,0:T(8,128)(2,1)S(1)} %get-tuple-element.34), channel_id=1, source_target_pairs={{0,2},{2,0},{4,6},{6,4},{8,10},{10,8},{12,14},{14,12},{16,18},{18,... | collective-permute-start | bytes 491528 | tf_op jit(solution)/shard_map/ppermute | solution.py:35
  79.5 4.8 %collective-permute-start.17 = (bf16[20,2048]{1,0:T(8,128)(2,1)S(1)}, bf16[20,2048]{1,0:T(8,128)(2,1)S(1)}, u32[]{:S(2)}, u32[]{:S(2)}) collective-permute-start(bf16[20,2048]{1,0:T(8,128)(2,1)S(1)} %pad_maximum_fusion), channel_id=1, source_target_pairs={{0,8},{2,10},{4,12},{6,14},{8,0},{10,2},{12,4},{14,6},{16,24},{18,... | collective-permute-start | bytes 245768 | tf_op jit(solution)/shard_map/ppermute | solution.py:35
  80.5 5.4 %collective-permute-start.13 = (bf16[20,2048]{1,0:T(8,128)(2,1)S(1)}, bf16[20,2048]{1,0:T(8,128)(2,1)S(1)}, u32[]{:S(2)}, u32[]{:S(2)}) collective-permute-start(bf16[20,2048]{1,0:T(8,128)(2,1)S(1)} %slice.91), channel_id=1, source_target_pairs={{0,4},{2,6},{4,0},{6,2},{8,12},{10,14},{12,8},{14,10},{16,20},{18,... | collective-permute-start | bytes 245768 | tf_op jit(solution)/shard_map/ppermute | solution.py:35
  84.3 4.3 %collective-permute-start.18 = (bf16[10,2048]{1,0:T(8,128)(2,1)S(1)}, bf16[10,2048]{1,0:T(8,128)(2,1)S(1)}, u32[]{:S(2)}, u32[]{:S(2)}) collective-permute-start(bf16[10,2048]{1,0:T(8,128)(2,1)S(1)} %slice.92), channel_id=1, source_target_pairs={{0,4},{2,6},{4,0},{6,2},{8,12},{10,14},{12,8},{14,10},{16,20},{18,... | collective-permute-start | bytes 122888 | tf_op jit(solution)/shard_map/ppermute | solution.py:35
  86.0 6.2 %collective-permute-start.14 = (bf16[10,2048]{1,0:T(8,128)(2,1)S(1)}, bf16[10,2048]{1,0:T(8,128)(2,1)S(1)}, u32[]{:S(2)}, u32[]{:S(2)}) collective-permute-start(bf16[10,2048]{1,0:T(8,128)(2,1)S(1)} %slice.93), channel_id=1, source_target_pairs={{0,8},{2,10},{4,12},{6,14},{8,0},{10,2},{12,4},{14,6},{16,24},{18,... | collective-permute-start | bytes 122888 | tf_op jit(solution)/shard_map/ppermute | solution.py:35
  88.7 5.9 %collective-permute-start.19 = (bf16[5,2048]{1,0:T(8,128)(2,1)S(1)}, bf16[5,2048]{1,0:T(8,128)(2,1)S(1)}, u32[]{:S(2)}, u32[]{:S(2)}) collective-permute-start(bf16[5,2048]{1,0:T(8,128)(2,1)S(1)} %slice.94), channel_id=1, source_target_pairs={{0,16},{2,18},{4,20},{6,22},{8,24},{10,26},{12,28},{14,30},{16,0},... | collective-permute-start | bytes 61448 | tf_op jit(solution)/shard_map/ppermute | solution.py:35
  92.2 5.0 %collective-permute-start.15 = (bf16[5,2048]{1,0:T(8,128)(2,1)S(1)}, bf16[5,2048]{1,0:T(8,128)(2,1)S(1)}, u32[]{:S(2)}, u32[]{:S(2)}) collective-permute-start(bf16[5,2048]{1,0:T(8,128)(2,1)S(1)} %slice.95), channel_id=1, source_target_pairs={{0,16},{2,18},{4,20},{6,22},{8,24},{10,26},{12,28},{14,30},{16,0},... | collective-permute-start | bytes 61448 | tf_op jit(solution)/shard_map/ppermute | solution.py:35

commit v4 on v3

--- a/solution.py
+++ b/solution.py
@@ -194,13 +194,13 @@
     gate, up, down = weights
     both, below = buffers
     units, depths = [], []
-    for i, (row, count) in enumerate(by_unit):
+    for i, (row, count) in enumerate(by_unit if below is not None else ()):
         units.append(
             pltpu.make_async_copy(
                 down.at[pl.ds(first + row, count)], below.at[pl.ds(row, count)], sems.at[2, i]
             )
         )
-    for i, (row, count) in enumerate(by_depth):
+    for i, (row, count) in enumerate(by_depth if both is not None else ()):
         some = pl.ds(row, count)
         depths.append(
             [
@@ -245,6 +245,69 @@
     )(*weights)
 
 
+def arriving(next_one, depth):
+    _, _, width, both, below = next_one
+    return [pltpu.VMEM((depth, 2 * width), jnp.bfloat16)] * both + [
+        pltpu.VMEM((width, depth), jnp.bfloat16)
+    ] * below
+
+
+def while_arriving(next_one, depth, sources, targets, sems, work):
+    if next_one is None:
+        return work()
+    _, place, width, both, below = next_one
+    targets = list(targets)
+    buffers = (targets.pop(0) if both else None, targets.pop(0) if below else None)
+    units, depths = streams(
+        sources, buffers, sems, first_of(place), width, parts_of(depth, 128), parts_of(width, 32)
+    )
+    copies = units + [copy for pair in depths for copy in pair]
+    for copy in copies:
+        copy.start()
+    pl.when(lax.axis_index("narrow") >= 0)(work)
+    for copy in copies:
+        copy.wait()
+
+
+def forward_half(half, side_rows, weights, width, next_one=None):
+    depth = half.shape[1]
+    rows = half.shape[0] - side_rows
+    top = rounded(-(-side_rows // 2), 8)
+    rest = side_rows - top
+
+    def body(half_ref, both, below, *refs):
+        sources, (out, *targets) = (refs[:3], refs[3:]) if next_one else ((), refs)
+        sems = targets.pop() if next_one else None
+
+        def work():
+            out[pl.ds(0, rows), :] = jnp.dot(
+                half_ref[pl.ds(0, rows), :], both[...], preferred_element_type=jnp.float32
+            ).astype(jnp.bfloat16)
+            side = across(half_ref[pl.ds(rows, side_rows), :], below[...]).astype(jnp.bfloat16)
+            out[pl.ds(rows, top), pl.ds(0, width)] = side[:top]
+            out[pl.ds(rows, rest), pl.ds(width, width)] = side[top:]
+            if top > rest:
+                out[pl.ds(rows + rest, top - rest), pl.ds(width, width)] = jnp.zeros(
+                    (top - rest, width), jnp.bfloat16
+                )
+
+        while_arriving(next_one, depth, sources, targets, sems, work)
+
+    more = arriving(next_one, depth) if next_one else []
+    return pl.pallas_call(
+        body,
+        out_shape=[jax.ShapeDtypeStruct((rows + top, 2 * width), jnp.bfloat16)] + more,
+        in_specs=[VMEM] * 3 + [ANY] * (3 if next_one else 0),
+        out_specs=[VMEM] * (1 + len(more)),
+        scratch_shapes=[pltpu.SemaphoreType.DMA((3, 4))] if next_one else [],
+        compiler_params=pltpu.CompilerParams(vmem_limit_bytes=4 * 1024 * 1024),
+        cost_estimate=pl.CostEstimate(
+            flops=4 * depth * width * (rows + side_rows), bytes_accessed=10**6, transcendentals=0
+        ),
+        name="forward_half",
+    )(half, *weights, *(next_one[0] if next_one else ()))
+
+
 def forward(main, side, weights, place, width, dtype, next_one=None):
     rows, half = main.shape[0], side.shape[0] // 2
     depth = main.shape[1]
@@ -256,29 +319,16 @@
         out[pl.ds(rows, half), pl.ds(width, width)] = value[half:].astype(dtype)
 
     def body_ready(main_ref, side_ref, both, below, *refs):
-        copies = []
-        if next_one is not None:
-            *refs, next_both, next_below, sems = refs
-            *more, out = refs
-            units, depths = streams(
-                more, (next_both, next_below), sems, first_of(next_one[1]), next_one[2],
-                parts_of(depth, 128), parts_of(next_one[2], 32),
-            )
-            copies = units + [copy for pair in depths for copy in pair]
-        else:
-            (out,) = refs
-        for copy in copies:
-            copy.start()
-
-        @pl.when(lax.axis_index("narrow") >= 0)
-        def _():
+        sources, (out, *targets) = (refs[:3], refs[3:]) if next_one else ((), refs)
+        sems = targets.pop() if next_one else None
+
+        def work():
             out[pl.ds(0, rows), :] = jnp.dot(
                 main_ref[...], both[...], preferred_element_type=jnp.float32
             ).astype(dtype)
             put_side(out, across(side_ref[...], below[...]))
 
-        for copy in copies:
-            copy.wait()
+        while_arriving(next_one, depth, sources, targets, sems, work)
 
     def body(main_ref, side_ref, gate, up, down, out, both, below, total, sems):
         first = first_of(place)
@@ -308,10 +358,7 @@
         if next_one is not None:
             operands += next_one[0]
             specs += [ANY] * 3
-            out_shape += [
-                pltpu.VMEM((depth, 2 * next_one[2]), jnp.bfloat16),
-                pltpu.VMEM((next_one[2], depth), jnp.bfloat16),
-            ]
+            out_shape += arriving(next_one, depth)
             scratch = [pltpu.SemaphoreType.DMA((3, 4))]
     else:
         scratch = [
@@ -340,11 +387,24 @@
     rows = examples + references
     count = points.shape[0]
     lanes = 128 if width % 128 == 0 else width
-    piece = 16 if examples % 32 == 16 else examples // 2
+    middle = examples // 2
+    top = rounded(-(-middle // 2), 8)
+    pieces, left = [], middle
+    while left:
+        size = 16 if left == 16 or left >= 32 else left
+        pieces.append((middle - left, size))
+        left -= size
+    pieces += [(middle + first, size) for first, size in pieces]
+    arrays = [array for item in received for array in (item if isinstance(item, tuple) else (item,))]
     scale = 1.0 / (pairs * count)
 
     def body(points_ref, picks_ref, kept_ref, *refs):
-        got, out, base_gate, base_up = refs[:-3], refs[-3], refs[-2], refs[-1]
+        out, base_gate, base_up = refs[-3:]
+        refs = list(refs[:-3])
+        got = [
+            tuple(refs.pop(0) for _ in item) if isinstance(item, tuple) else refs.pop(0)
+            for item in received
+        ]
         picks = picks_ref[...]
         steps = [points_ref[m].astype(jnp.float32) * 0.125 for m in range(count)]
         steps_1 = sum(steps[1:], steps[0])
@@ -356,23 +416,41 @@
             else:
                 of = [pl.ds(pl.multiple_of(w * width + j * lanes, 128), lanes) for w in range(2)]
 
-            def total(start, size, w):
-                value = kept_ref[pl.ds(start, size), of[w]]
+            def of_references(ref, w):
+                if isinstance(ref, tuple):
+                    return jnp.concatenate([half[pl.ds(0, references // 2), of[w]] for half in ref])
+                return ref[pl.ds(0, references), of[w]]
+
+            def of_examples(ref, first, size, w):
+                if isinstance(ref, tuple):
+                    h = first // middle
+                    return ref[h][pl.ds(references // 2 + first - h * middle, size), of[w]]
+                return ref[pl.ds(references + first, size), of[w]]
+
+            def of_upstream(ref, h):
+                if isinstance(ref, tuple):
+                    return jnp.concatenate(
+                        [ref[h][pl.ds(rows // 2, top), of[0]], ref[h][pl.ds(rows // 2, middle - top), of[1]]]
+                    )
+                return ref[pl.ds(rows, middle), of[h]]
+
+            def total(take, *where):
+                value = take(kept_ref, *where)
                 for ref in got:
-                    value = value + ref[pl.ds(start, size), of[w]].astype(jnp.float32)
+                    value = value + take(ref, *where).astype(jnp.float32)
                 return value
 
             for w, target in enumerate((base_gate, base_up)):
-                value = total(0, references, w)
+                value = total(of_references, w)
                 high = value.astype(jnp.bfloat16)
                 low = (value - high.astype(jnp.float32)).astype(jnp.bfloat16)
                 target[...] = jnp.dot(picks, high, preferred_element_type=jnp.float32) + jnp.dot(
                     picks, low, preferred_element_type=jnp.float32
                 )
-            upstream = [total(rows, examples // 2, w) for w in range(2)]
-            for first in range(0, examples, piece):
-                gate = total(references + first, piece, 0) * 0.5
-                up = total(references + first, piece, 1)
+            upstream = [total(of_upstream, h) for h in range(2)]
+            for first, piece in pieces:
+                gate = total(of_examples, first, piece, 0) * 0.5
+                up = total(of_examples, first, piece, 1)
                 coef_gate = jnp.zeros_like(gate)
                 coef_up = jnp.zeros_like(gate)
                 for p in range(pairs):
@@ -395,7 +473,7 @@
                 base_up[pl.ds(first, piece), :] = coef_up * scale
             for w, source in enumerate((base_gate, base_up)):
                 for h in range(2):
-                    some = pl.ds(h * (examples // 2), examples // 2)
+                    some = pl.ds(h * middle, middle)
                     out[some, of[w]] = (upstream[h] * source[some, :]).astype(jnp.bfloat16)
             return 0
 
@@ -404,13 +482,13 @@
     return pl.pallas_call(
         body,
         out_shape=jax.ShapeDtypeStruct((examples, 2 * width), jnp.bfloat16),
-        in_specs=[SMEM, VMEM, VMEM] + [VMEM] * len(received),
+        in_specs=[SMEM, VMEM, VMEM] + [VMEM] * len(arrays),
         out_specs=VMEM,
         scratch_shapes=[pltpu.VMEM((pairs * examples, lanes), jnp.float32)] * 2,
         compiler_params=pltpu.CompilerParams(vmem_limit_bytes=4 * 1024 * 1024),
         cost_estimate=pl.CostEstimate(flops=5 * 10**9, bytes_accessed=10**6, transcendentals=0),
         name="coefficients",
-    )(points, picks, kept, *received)
+    )(points, picks, kept, *arrays)
 
 
 def backward(items, total, final, span=None):
@@ -562,31 +640,45 @@
     order = halvings(far)
     plane = [column[s] for s in order] + [beside[s] for s in order if near == 2]
     half = assemble(plane, whole, pieces, (r, e, k), depth)
+    blocks_of_weights = {}
+    early = ahead and pair == 2 and len(chunks) == 2
+    if ahead:
+        wanted = [(1, chunk) for chunk in chunks] + [(0, chunk) for chunk in chunks[1 if early else 0:]]
+        for s, chunk in wanted:
+            blocks_of_weights[s, chunk[0]] = fetch(*at_peer(s, *chunk), chunk[1])
     halves = [half]
     if pair == 2:
         halves.append(permute(half, "wide", dims, 2, 1))
+
+    parts = []
+    if early:
+        (offset, width), (next_offset, next_width) = chunks
+        weights = blocks_of_weights[1, offset]
+        count = half.shape[0] // (r + e + k) * k
+        kept_one = (*at_peer(0, offset, width), width)
+        (sent,) = forward_half(halves[0], count, weights, width)
+        received = [shift(sent, peers, 1)]
+        sent, both = forward_half(halves[1], count, weights, width, (*kept_one, True, False))
+        received.append(shift(sent, peers, 1))
+        parts.append((offset, width, [tuple(received)]))
     main, side = join(halves, (r, e, k))
-
-    blocks_of_weights = {}
-    if ahead:
-        for chunk in chunks:
-            blocks_of_weights[1, chunk[0]] = fetch(*at_peer(1, *chunk), chunk[1])
-
-    parts = []
-    for i, (offset, width) in enumerate(chunks):
-        received = []
-        for s in range(1, peers):
-            weights, place = at_peer(s, offset, width)
-            next_one = None
-            if ahead:
-                weights = blocks_of_weights[s, offset]
-                later = chunks[-1 - i]
-                next_one = (*at_peer(0, *later), later[1])
-            sent, *more = forward(main, side, weights, place, width, jnp.bfloat16, next_one)
-            if more:
-                blocks_of_weights[0, later[0]] = more
-            received.append(shift(sent, peers, s))
-        parts.append((offset, width, received))
+    if early:
+        sent, below = forward(
+            main, side, blocks_of_weights[1, next_offset], None, next_width, jnp.bfloat16,
+            (*kept_one, False, True),
+        )
+        parts.append((next_offset, next_width, [shift(sent, peers, 1)]))
+        blocks_of_weights[0, offset] = (both, below)
+    else:
+        for offset, width in chunks:
+            received = []
+            for s in range(1, peers):
+                weights, place = at_peer(s, offset, width)
+                if ahead:
+                    weights = blocks_of_weights[s, offset]
+                (sent,) = forward(main, side, weights, place, width, jnp.bfloat16)
+                received.append(shift(sent, peers, s))
+            parts.append((offset, width, received))
 
     jobs = []
     for offset, width, received in parts:

time: 98 us -> 100 us (1.020)
  Pallas kernels: 41 us -> 44.9 us
  waiting for transfers between devices: 28.2 us -> 26.1 us
    pallas_call x4 -> x3, Pallas kernels: 14.4 us -> 8.18 us  [forward(): pl.pallas_call(body_ready if ready else body, out_shape=out_shape, in_spe...]
    pallas_call x0 -> x2, Pallas kernels: none -> 6.15 us  [forward_half(): pl.pallas_call(body, out_shape=[jax.ShapeDtypeStruct((rows + top, 2 * wid...]
    pallas_call x2 -> x3, Pallas kernels: 8.66 us -> 12.5 us  [fetch(): pl.pallas_call(body, out_shape=(pltpu.VMEM((depth, 2 * width), jnp.bfloat...]
    ppermute x4 -> x5, waiting for transfers between devices: 4.54 us -> 2.8 us  [shift(): lax.ppermute(array, 'narrow', [(at, (at + amount) % size) for at in range...]
    ppermute x4 -> x5, starting transfers between devices: 5.34 us -> 6.08 us  [shift(): lax.ppermute(array, 'narrow', [(at, (at + amount) % size) for at in range...]
  transfers between devices with their start and end apart: 20 -> 21, of which waited for: 13 -> 11; matrix products, arithmetic and copies ran while one was open for 1% -> 1% of each run, Pallas kernels for 35% -> 42%
where the time goes in v4:
time: 100 us; the launch traced here: 99.9 us
  Pallas kernels  44.9 us (45%)
  starting transfers between devices  27 us (27%)
  waiting for transfers between devices  26.1 us (26%)
    ppermute x16, waiting for transfers between devices, permute(): return lax.ppermute(array, axis, pairs)  23.3 us
    ppermute x16, starting transfers between devices, permute(): return lax.ppermute(array, axis, pairs)  20.9 us
    pallas_call x3, Pallas kernels, fetch(): pl.pallas_call(body, out_shape=(pltpu.VMEM((depth, 2 * width), jnp.bfloat...  12.5 us
    pallas_call x4, Pallas kernels, backward(): pl.pallas_call(body, out_shape=out_shape, in_specs=specs, out_specs=out_s...  9.36 us
    pallas_call x3, Pallas kernels, forward(): pl.pallas_call(body_ready if ready else body, out_shape=out_shape, in_spe...  8.18 us
    pallas_call x2, Pallas kernels, coefficients(): pl.pallas_call(body, out_shape=jax.ShapeDtypeStruct((examples, 2 * width)...  6.64 us
    pallas_call x2, Pallas kernels, forward_half(): pl.pallas_call(body, out_shape=[jax.ShapeDtypeStruct((rows + top, 2 * wid...  6.15 us
    ppermute x5, starting transfers between devices, shift(): lax.ppermute(array, 'narrow', [(at, (at + amount) % size) for at in range...  6.08 us
  transfers between devices with their start and end apart: 21, of which 11 were waited for; matrix products, arithmetic and copies ran while one was open for 1% of the time, Pallas kernels for 42%

profile of v4, /device:TPU:0, one launch (start us, length us, event | category | flops | bytes accessed | tf_op | source)
XLA Modules:
  0.0 99.9 jit_solution(15545336428434827597)
XLA Ops:
  0.0 1.0 pack.1.refs_0_
  1.0 4.1 %collective-permute-start = (bf16[16,4608]{1,0:T(8,128)(2,1)S(1)}, bf16[16,4608]{1,0:T(8,128)(2,1)S(1)}, u32[]{:S(2)}, u32[]{:S(2)}) collective-permute-start(bf16[16,4608]{1,0:T(8,128)(2,1)S(1)} %pack.1.refs_0_), channel_id=1, source_target_pairs={{0,16},{2,18},{4,20},{6,22},{8,24},{10,26},{12,28},{14,30},{16,0},... | collective-permute-start | bytes 442376 | tf_op jit(solution)/shard_map/ppermute | solution.py:35
  5.1 1.6 %collective-permute-start.1 = (bf16[16,4608]{1,0:T(8,128)(2,1)S(1)}, bf16[16,4608]{1,0:T(8,128)(2,1)S(1)}, u32[]{:S(2)}, u32[]{:S(2)}) collective-permute-start(bf16[16,4608]{1,0:T(8,128)(2,1)S(1)} %pack.1.refs_0_), channel_id=1, source_target_pairs={{0,8},{2,10},{4,12},{6,14},{8,0},{10,2},{12,4},{14,6},{16,24},{18,... | collective-permute-start | bytes 442376 | tf_op jit(solution)/shard_map/ppermute | solution.py:35
  6.7 5.5 %collective-permute-done.refs_1_ = bf16[16,4608]{1,0:T(8,128)(2,1)S(1)} collective-permute-done((bf16[16,4608]{1,0:T(8,128)(2,1)S(1)}, bf16[16,4608]{1,0:T(8,128)(2,1)S(1)}, u32[]{:S(2)}, u32[]{:S(2)}) %collective-permute-start) | collective-permute-done | bytes 147488 | tf_op jit(solution)/shard_map/ppermute | solution.py:35
  12.2 0.6 collective-permute-start.2
  12.8 1.5 %collective-permute-start.3 = (bf16[16,4608]{1,0:T(8,128)(2,1)S(1)}, bf16[16,4608]{1,0:T(8,128)(2,1)S(1)}, u32[]{:S(2)}, u32[]{:S(2)}) collective-permute-start(bf16[16,4608]{1,0:T(8,128)(2,1)S(1)} %pack.1.refs_0_), channel_id=1, source_target_pairs={{0,4},{2,6},{4,0},{6,2},{8,12},{10,14},{12,8},{14,10},{16,20},{18,... | collective-permute-start | bytes 442376 | tf_op jit(solution)/shard_map/ppermute | solution.py:35
  14.4 0.5 collective-permute-start.4
  14.9 1.5 %collective-permute-start.5 = (bf16[16,4608]{1,0:T(8,128)(2,1)S(1)}, bf16[16,4608]{1,0:T(8,128)(2,1)S(1)}, u32[]{:S(2)}, u32[]{:S(2)}) collective-permute-start(bf16[16,4608]{1,0:T(8,128)(2,1)S(1)} %collective-permute-done.1.refs_2_), channel_id=1, source_target_pairs={{0,4},{2,6},{4,0},{6,2},{8,12},{10,14},{12,8},{14,10},{16,20},{18,... | collective-permute-start | bytes 442376 | tf_op jit(solution)/shard_map/ppermute | solution.py:35
  16.4 1.0 collective-permute-done.2.refs_3_
  17.4 1.6 %collective-permute-start.6 = (bf16[16,4608]{1,0:T(8,128)(2,1)S(1)}, bf16[16,4608]{1,0:T(8,128)(2,1)S(1)}, u32[]{:S(2)}, u32[]{:S(2)}) collective-permute-start(bf16[16,4608]{1,0:T(8,128)(2,1)S(1)} %collective-permute-done.2.refs_3_), channel_id=1, source_target_pairs={{0,4},{2,6},{4,0},{6,2},{8,12},{10,14},{12,8},{14,10},{16,20},{18,... | collective-permute-start | bytes 442376 | tf_op jit(solution)/shard_map/ppermute | solution.py:35
  18.9 0.8 copy.9.pair_ref
  19.9 2.8 %collective-permute-done.4.refs_5_ = bf16[16,4608]{1,0:T(8,128)(2,1)S(1)} collective-permute-done((bf16[16,4608]{1,0:T(8,128)(2,1)S(1)}, bf16[16,4608]{1,0:T(8,128)(2,1)S(1)}, u32[]{:S(2)}, u32[]{:S(2)}) %collective-permute-start.4) | collective-permute-done | bytes 147488 | tf_op jit(solution)/shard_map/ppermute | solution.py:35
  22.7 3.2 %collective-permute-done.5.refs_6_ = bf16[16,4608]{1,0:T(8,128)(2,1)S(1)} collective-permute-done((bf16[16,4608]{1,0:T(8,128)(2,1)S(1)}, bf16[16,4608]{1,0:T(8,128)(2,1)S(1)}, u32[]{:S(2)}, u32[]{:S(2)}) %collective-permute-start.5) | collective-permute-done | bytes 147488 | tf_op jit(solution)/shard_map/ppermute | solution.py:35
  25.9 1.9 %collective-permute-done.6.refs_7_ = bf16[16,4608]{1,0:T(8,128)(2,1)S(1)} collective-permute-done((bf16[16,4608]{1,0:T(8,128)(2,1)S(1)}, bf16[16,4608]{1,0:T(8,128)(2,1)S(1)}, u32[]{:S(2)}, u32[]{:S(2)}) %collective-permute-start.6) | collective-permute-done | bytes 147488 | tf_op jit(solution)/shard_map/ppermute | solution.py:35
  27.8 0.8 assemble.1.refs_0_.half_ref
  28.6 3.9 %fetch.4 = (bf16[4096,768]{1,0:T(8,128)(2,1)S(1)}, bf16[384,4096]{1,0:T(8,128)(2,1)S(1)}) custom-call(bf16[4096,1792]{1,0:T(8,128)(2,1)} %refs_0_.5, bf16[4096,1792]{1,0:T(8,128)(2,1)} %refs_1_.5, bf16[1792,4096]{1,0:T(8,128)(2,1)} %refs_2_.5), custom_call_target="tpu_custom_call" | custom-call | flops 4000000000 | bytes 9437184 | tf_op jit(solution)/shard_map/fetch/pallas_call | solution.py:231
  32.5 4.8 %fetch.5 = (bf16[4096,1024]{1,0:T(8,128)(2,1)S(1)}, bf16[512,4096]{1,0:T(8,128)(2,1)S(1)}) custom-call(bf16[4096,1792]{1,0:T(8,128)(2,1)} %refs_0_.5, bf16[4096,1792]{1,0:T(8,128)(2,1)} %refs_1_.5, bf16[1792,4096]{1,0:T(8,128)(2,1)} %refs_2_.5), custom_call_target="tpu_custom_call" | custom-call | flops 4000000000 | bytes 12582912 | tf_op jit(solution)/shard_map/fetch/pallas_call | solution.py:231
  37.3 3.9 %fetch.3 = (bf16[4096,768]{1,0:T(8,128)(2,1)S(1)}, bf16[384,4096]{1,0:T(8,128)(2,1)S(1)}) custom-call(bf16[4096,1792]{1,0:T(8,128)(2,1)} %refs_0_.5, bf16[4096,1792]{1,0:T(8,128)(2,1)} %refs_1_.5, bf16[1792,4096]{1,0:T(8,128)(2,1)} %refs_2_.5), custom_call_target="tpu_custom_call" | custom-call | flops 4000000000 | bytes 9437184 | tf_op jit(solution)/shard_map/fetch/pallas_call | solution.py:231
  41.2 2.5 %forward_half.3 = bf16[128,1024]{1,0:T(8,128)(2,1)S(1)} custom-call(bf16[144,4096]{1,0:T(8,128)(2,1)S(1)} %assemble.1.refs_0_.half_ref, bf16[4096,1024]{1,0:T(8,128)(2,1)S(1)} %get-tuple-element.28.both.refs_2_, bf16[512,4096]{1,0:T(8,128)(2,1)S(1)} %get-tuple-element.29.below), custom_call_target="tpu_custom_call" | custom-call | flops 1207959552 | bytes 1000000 | tf_op jit(solution)/shard_map/forward_half/pallas_call | solution.py:297
  43.7 1.6 %collective-permute-start.10 = (bf16[128,1024]{1,0:T(8,128)(2,1)S(1)}, bf16[128,1024]{1,0:T(8,128)(2,1)S(1)}, u32[]{:S(2)}, u32[]{:S(2)}) collective-permute-start(bf16[128,1024]{1,0:T(8,128)(2,1)S(1)} %forward_half.3), channel_id=1, source_target_pairs={{0,1},{1,0},{2,3},{3,2},{4,5},{5,4},{6,7},{7,6},{8,9},{9,8},{10,11... | collective-permute-start | bytes 786440 | tf_op jit(solution)/shard_map/ppermute | solution.py:39
  45.3 3.7 %forward_half.2 = (bf16[128,1024]{1,0:T(8,128)(2,1)S(1)}, bf16[4096,1024]{1,0:T(8,128)(2,1)S(1)}) custom-call(bf16[144,4096]{1,0:T(8,128)(2,1)S(1)} %collective-permute-done.7.refs_1_.half_ref, bf16[4096,1024]{1,0:T(8,128)(2,1)S(1)} %get-tuple-element.28.both.refs_2_, bf16[512,4096]{1,0:T(8,128)(2,1)S(1)} %get-tuple-element.29.below, ...), custom_call_target="tpu_custom_call" | custom-call | flops 1207959552 | bytes 1000000 | tf_op jit(solution)/shard_map/forward_half/pallas_call | solution.py:297
  49.0 0.4 collective-permute-start.11
  49.6 2.7 %forward.4 = (bf16[248,768]{1,0:T(8,128)(2,1)S(1)}, bf16[512,4096]{1,0:T(8,128)(2,1)S(1)}) custom-call(bf16[208,4096]{1,0:T(8,128)(2,1)S(1)} %get-tuple-element.21.main_ref, bf16[80,4096]{1,0:T(8,128)(2,1)S(1)} %get-tuple-element.22.side_ref, bf16[4096,768]{1,0:T(8,128)(2,1)S(1)} %get-tuple-element.25.both.refs_1_, ...), custom_call_target="tpu_custom_call" | custom-call | flops 1560281088 | bytes 9437184 | tf_op jit(solution)/shard_map/forward/pallas_call | solution.py:370
  52.3 1.7 %collective-permute-start.8 = (bf16[248,768]{1,0:T(8,128)(2,1)S(1)}, bf16[248,768]{1,0:T(8,128)(2,1)S(1)}, u32[]{:S(2)}, u32[]{:S(2)}) collective-permute-start(bf16[248,768]{1,0:T(8,128)(2,1)S(1)} %get-tuple-element.27), channel_id=1, source_target_pairs={{0,1},{1,0},{2,3},{3,2},{4,5},{5,4},{6,7},{7,6},{8,9},{9,8},{10,11... | collective-permute-start | bytes 1142792 | tf_op jit(solution)/shard_map/ppermute | solution.py:39
  54.0 2.4 %forward.3.kept_ref = f32[248,768]{1,0:T(8,128)S(1)} custom-call(bf16[208,4096]{1,0:T(8,128)(2,1)S(1)} %get-tuple-element.21.main_ref, bf16[80,4096]{1,0:T(8,128)(2,1)S(1)} %get-tuple-element.22.side_ref, bf16[4096,768]{1,0:T(8,128)(2,1)S(1)} %get-tuple-element.23.both.refs_3_, bf16[384,4096]{1,0:T(8,128)(2,1)S(1)} %get-tuple-element.24.below), custom_call_target="tpu_custom_call" | custom-call | flops 1560281088 | bytes 9437184 | tf_op jit(solution)/shard_map/forward/pallas_call | solution.py:370
  56.4 3.1 %forward.5.kept_ref = f32[248,1024]{1,0:T(8,128)S(1)} custom-call(bf16[208,4096]{1,0:T(8,128)(2,1)S(1)} %get-tuple-element.21.main_ref, bf16[80,4096]{1,0:T(8,128)(2,1)S(1)} %get-tuple-element.22.side_ref, bf16[4096,1024]{1,0:T(8,128)(2,1)S(1)} %get-tuple-element.30.both.refs_1_, bf16[512,4096]{1,0:T(8,128)(2,1)S(1)} %get-tuple-element.31.below), custom_call_target="tpu_custom_call" | custom-call | flops 2080374784 | bytes 12582912 | tf_op jit(solution)/shard_map/forward/pallas_call | solution.py:370
  59.6 3.7 %coefficients.3.refs_0_ = bf16[80,1024]{1,0:T(8,128)(2,1)S(1)} custom-call(s32[8]{0:T(128)S(1)} %copy-done, bf16[320,128]{1,0:T(8,128)(2,1)S(1)} %choices.1.picks_ref, f32[248,1024]{1,0:T(8,128)S(1)} %forward.5.kept_ref, bf16[128,1024]{1,0:T(8,128)(2,1)S(1)} %collective-permute-done.10.refs_0_, bf16[128,1024]{1,0:T(8,128)(2,1)S(1)} %collective-permute-done.11.refs_1_), custom_call_target="tpu_custom_call" | custom-call | flops 5000000000 | bytes 1000000 | tf_op jit(solution)/shard_map/coefficients/pallas_call | solution.py:482
  63.3 0.6 collective-permute-start.12
  63.9 2.8 %collective-permute-done.8.refs_0_ = bf16[248,768]{1,0:T(8,128)(2,1)S(1)} collective-permute-done((bf16[248,768]{1,0:T(8,128)(2,1)S(1)}, bf16[248,768]{1,0:T(8,128)(2,1)S(1)}, u32[]{:S(2)}, u32[]{:S(2)}) %collective-permute-start.8) | collective-permute-done | bytes 380960 | tf_op jit(solution)/shard_map/ppermute | solution.py:39
  66.7 2.9 %coefficients.2.refs_1_ = bf16[80,768]{1,0:T(8,128)(2,1)S(1)} custom-call(s32[8]{0:T(128)S(1)} %copy-done, bf16[320,128]{1,0:T(8,128)(2,1)S(1)} %choices.1.picks_ref, f32[248,768]{1,0:T(8,128)S(1)} %forward.3.kept_ref, bf16[248,768]{1,0:T(8,128)(2,1)S(1)} %collective-permute-done.8.refs_0_), custom_call_target="tpu_custom_call" | custom-call | flops 5000000000 | bytes 1000000 | tf_op jit(solution)/shard_map/coefficients/pallas_call | solution.py:482
  69.6 1.6 %collective-permute-start.9 = (bf16[80,768]{1,0:T(8,128)(2,1)S(1)}, bf16[80,768]{1,0:T(8,128)(2,1)S(1)}, u32[]{:S(2)}, u32[]{:S(2)}) collective-permute-start(bf16[80,768]{1,0:T(8,128)(2,1)S(1)} %coefficients.2.refs_1_), channel_id=1, source_target_pairs={{0,1},{1,0},{2,3},{3,2},{4,5},{5,4},{6,7},{7,6},{8,9},{9,8},{10,11... | collective-permute-start | bytes 368648 | tf_op jit(solution)/shard_map/ppermute | solution.py:39
  71.3 2.7 %backward.4.refs_4_ = f32[80,4096]{1,0:T(8,128)S(1)} custom-call(bf16[80,1024]{1,0:T(8,128)(2,1)S(1)} %coefficients.3.refs_0_, bf16[4096,1024]{1,0:T(8,128)(2,1)S(1)} %get-tuple-element.30.both.refs_1_), custom_call_target="tpu_custom_call" | custom-call | flops 671088640 | bytes 8388608 | tf_op jit(solution)/shard_map/backward/pallas_call | solution.py:541
  73.9 4.6 %backward.5.refs_2_ = f32[80,4096]{1,0:T(8,128)S(1)} custom-call(bf16[80,1024]{1,0:T(8,128)(2,1)S(1)} %collective-permute-done.12.refs_0_, bf16[80,768]{1,0:T(8,128)(2,1)S(1)} %coefficients.2.refs_1_, bf16[4096,1024]{1,0:T(8,128)(2,1)S(1)} %get-tuple-element.28.both.refs_2_, bf16[4096,768]{1,0:T(8,128)(2,1)S(1)} %get-tuple-element.23.both.refs_3_, ...), custom_call_target="tpu_custom_call" | custom-call | flops 1174405120 | bytes 8388608 | tf_op jit(solution)/shard_map/backward/pallas_call | solution.py:541
  78.5 1.1 %backward.6 = (bf16[40,2048]{1,0:T(8,128)(2,1)S(1)}, f32[40,2048]{1,0:T(8,128)S(1)}) custom-call(bf16[80,768]{1,0:T(8,128)(2,1)S(1)} %collective-permute-done.9.refs_0_, bf16[4096,768]{1,0:T(8,128)(2,1)S(1)} %get-tuple-element.25.both.refs_1_, f32[80,4096]{1,0:T(8,128)S(1)} %backward.5.refs_2_), custom_call_target="tpu_custom_call" | custom-call | flops 251658240 | bytes 3145728 | tf_op jit(solution)/shard_map/backward/pallas_call | solution.py:541
  79.7 1.1 %backward.7 = (bf16[40,2048]{1,0:T(8,128)(2,1)S(1)}, f32[40,2048]{1,0:T(8,128)S(1)}) custom-call(bf16[80,768]{1,0:T(8,128)(2,1)S(1)} %collective-permute-done.9.refs_0_, bf16[4096,768]{1,0:T(8,128)(2,1)S(1)} %get-tuple-element.25.both.refs_1_, f32[80,4096]{1,0:T(8,128)S(1)} %backward.5.refs_2_), custom_call_target="tpu_custom_call" | custom-call | flops 251658240 | bytes 3145728 | tf_op jit(solution)/shard_map/backward/pallas_call | solution.py:541
  80.7 0.6 collective-permute-start.17
  81.4 1.6 %collective-permute-start.14 = (bf16[20,2048]{1,0:T(8,128)(2,1)S(1)}, bf16[20,2048]{1,0:T(8,128)(2,1)S(1)}, u32[]{:S(2)}, u32[]{:S(2)}) collective-permute-start(bf16[20,2048]{1,0:T(8,128)(2,1)S(1)} %slice.91), channel_id=1, source_target_pairs={{0,4},{2,6},{4,0},{6,2},{8,12},{10,14},{12,8},{14,10},{16,20},{18,... | collective-permute-start | bytes 245768 | tf_op jit(solution)/shard_map/ppermute | solution.py:35
  83.1 0.4 collective-permute-start.18
  83.5 2.7 %collective-permute-done.14 = bf16[20,2048]{1,0:T(8,128)(2,1)S(1)} collective-permute-done((bf16[20,2048]{1,0:T(8,128)(2,1)S(1)}, bf16[20,2048]{1,0:T(8,128)(2,1)S(1)}, u32[]{:S(2)}, u32[]{:S(2)}) %collective-permute-start.14) | collective-permute-done | bytes 81952 | tf_op jit(solution)/shard_map/ppermute | solution.py:35
  86.2 0.4 collective-permute-start.15
  86.6 1.2 %collective-permute-done.18 = bf16[20,2048]{1,0:T(8,128)(2,1)S(1)} collective-permute-done((bf16[20,2048]{1,0:T(8,128)(2,1)S(1)}, bf16[20,2048]{1,0:T(8,128)(2,1)S(1)}, u32[]{:S(2)}, u32[]{:S(2)}) %collective-permute-start.18) | collective-permute-done | bytes 81952 | tf_op jit(solution)/shard_map/ppermute | solution.py:35
  87.8 1.4 %collective-permute-start.19 = (bf16[10,2048]{1,0:T(8,128)(2,1)S(1)}, bf16[10,2048]{1,0:T(8,128)(2,1)S(1)}, u32[]{:S(2)}, u32[]{:S(2)}) collective-permute-start(bf16[10,2048]{1,0:T(8,128)(2,1)S(1)} %slice.92), channel_id=1, source_target_pairs={{0,4},{2,6},{4,0},{6,2},{8,12},{10,14},{12,8},{14,10},{16,20},{18,... | collective-permute-start | bytes 122888 | tf_op jit(solution)/shard_map/ppermute | solution.py:35
  89.2 1.3 %collective-permute-done.15 = bf16[10,2048]{1,0:T(8,128)(2,1)S(1)} collective-permute-done((bf16[10,2048]{1,0:T(8,128)(2,1)S(1)}, bf16[10,2048]{1,0:T(8,128)(2,1)S(1)}, u32[]{:S(2)}, u32[]{:S(2)}) %collective-permute-start.15) | collective-permute-done | bytes 40992 | tf_op jit(solution)/shard_map/ppermute | solution.py:35
  90.6 3.8 %collective-permute-start.16 = (bf16[5,2048]{1,0:T(8,128)(2,1)S(1)}, bf16[5,2048]{1,0:T(8,128)(2,1)S(1)}, u32[]{:S(2)}, u32[]{:S(2)}) collective-permute-start(bf16[5,2048]{1,0:T(8,128)(2,1)S(1)} %slice.95), channel_id=1, source_target_pairs={{0,16},{2,18},{4,20},{6,22},{8,24},{10,26},{12,28},{14,30},{16,0},... | collective-permute-start | bytes 61448 | tf_op jit(solution)/shard_map/ppermute | solution.py:35
  94.4 1.2 %collective-permute-start.20 = (bf16[5,2048]{1,0:T(8,128)(2,1)S(1)}, bf16[5,2048]{1,0:T(8,128)(2,1)S(1)}, u32[]{:S(2)}, u32[]{:S(2)}) collective-permute-start(bf16[5,2048]{1,0:T(8,128)(2,1)S(1)} %slice.94), channel_id=1, source_target_pairs={{0,16},{2,18},{4,20},{6,22},{8,24},{10,26},{12,28},{14,30},{16,0},... | collective-permute-start | bytes 61448 | tf_op jit(solution)/shard_map/ppermute | solution.py:35
  95.6 0.9 collective-permute-done.16
  96.5 2.8 %collective-permute-done.20 = bf16[5,2048]{1,0:T(8,128)(2,1)S(1)} collective-permute-done((bf16[5,2048]{1,0:T(8,128)(2,1)S(1)}, bf16[5,2048]{1,0:T(8,128)(2,1)S(1)}, u32[]{:S(2)}, u32[]{:S(2)}) %collective-permute-start.20) | collective-permute-done | bytes 20512 | tf_op jit(solution)/shard_map/ppermute | solution.py:35
  99.3 0.6 pad_maximum_fusion.1
  (32 shorter events, 0.8 us)
Async XLA Ops:
  1.0 11.2 %collective-permute-start = (bf16[16,4608]{1,0:T(8,128)(2,1)S(1)}, bf16[16,4608]{1,0:T(8,128)(2,1)S(1)}, u32[]{:S(2)}, u32[]{:S(2)}) collective-permute-start(bf16[16,4608]{1,0:T(8,128)(2,1)S(1)} %pack.1.refs_0_), channel_id=1, source_target_pairs={{0,16},{2,18},{4,20},{6,22},{8,24},{10,26},{12,28},{14,30},{16,0},... | collective-permute-start | bytes 442376 | tf_op jit(solution)/shard_map/ppermute | solution.py:35
  5.1 9.8 %collective-permute-start.1 = (bf16[16,4608]{1,0:T(8,128)(2,1)S(1)}, bf16[16,4608]{1,0:T(8,128)(2,1)S(1)}, u32[]{:S(2)}, u32[]{:S(2)}) collective-permute-start(bf16[16,4608]{1,0:T(8,128)(2,1)S(1)} %pack.1.refs_0_), channel_id=1, source_target_pairs={{0,8},{2,10},{4,12},{6,14},{8,0},{10,2},{12,4},{14,6},{16,24},{18,... | collective-permute-start | bytes 442376 | tf_op jit(solution)/shard_map/ppermute | solution.py:35
  12.2 5.1 %collective-permute-start.2 = (bf16[16,4608]{1,0:T(8,128)(2,1)S(1)}, bf16[16,4608]{1,0:T(8,128)(2,1)S(1)}, u32[]{:S(2)}, u32[]{:S(2)}) collective-permute-start(bf16[16,4608]{1,0:T(8,128)(2,1)S(1)} %collective-permute-done.refs_1_), channel_id=1, source_target_pairs={{0,8},{2,10},{4,12},{6,14},{8,0},{10,2},{12,4},{14,6},{16,24},{18,... | collective-permute-start | bytes 442376 | tf_op jit(solution)/shard_map/ppermute | solution.py:35
  12.8 7.0 %collective-permute-start.3 = (bf16[16,4608]{1,0:T(8,128)(2,1)S(1)}, bf16[16,4608]{1,0:T(8,128)(2,1)S(1)}, u32[]{:S(2)}, u32[]{:S(2)}) collective-permute-start(bf16[16,4608]{1,0:T(8,128)(2,1)S(1)} %pack.1.refs_0_), channel_id=1, source_target_pairs={{0,4},{2,6},{4,0},{6,2},{8,12},{10,14},{12,8},{14,10},{16,20},{18,... | collective-permute-start | bytes 442376 | tf_op jit(solution)/shard_map/ppermute | solution.py:35
  14.4 8.4 %collective-permute-start.4 = (bf16[16,4608]{1,0:T(8,128)(2,1)S(1)}, bf16[16,4608]{1,0:T(8,128)(2,1)S(1)}, u32[]{:S(2)}, u32[]{:S(2)}) collective-permute-start(bf16[16,4608]{1,0:T(8,128)(2,1)S(1)} %collective-permute-done.refs_1_), channel_id=1, source_target_pairs={{0,4},{2,6},{4,0},{6,2},{8,12},{10,14},{12,8},{14,10},{16,20},{18,... | collective-permute-start | bytes 442376 | tf_op jit(solution)/shard_map/ppermute | solution.py:35
  14.9 11.0 %collective-permute-start.5 = (bf16[16,4608]{1,0:T(8,128)(2,1)S(1)}, bf16[16,4608]{1,0:T(8,128)(2,1)S(1)}, u32[]{:S(2)}, u32[]{:S(2)}) collective-permute-start(bf16[16,4608]{1,0:T(8,128)(2,1)S(1)} %collective-permute-done.1.refs_2_), channel_id=1, source_target_pairs={{0,4},{2,6},{4,0},{6,2},{8,12},{10,14},{12,8},{14,10},{16,20},{18,... | collective-permute-start | bytes 442376 | tf_op jit(solution)/shard_map/ppermute | solution.py:35
  17.4 10.4 %collective-permute-start.6 = (bf16[16,4608]{1,0:T(8,128)(2,1)S(1)}, bf16[16,4608]{1,0:T(8,128)(2,1)S(1)}, u32[]{:S(2)}, u32[]{:S(2)}) collective-permute-start(bf16[16,4608]{1,0:T(8,128)(2,1)S(1)} %collective-permute-done.2.refs_3_), channel_id=1, source_target_pairs={{0,4},{2,6},{4,0},{6,2},{8,12},{10,14},{12,8},{14,10},{16,20},{18,... | collective-permute-start | bytes 442376 | tf_op jit(solution)/shard_map/ppermute | solution.py:35
  28.6 16.8 %collective-permute-start.7 = (bf16[144,4096]{1,0:T(8,128)(2,1)S(1)}, bf16[144,4096]{1,0:T(8,128)(2,1)S(1)}, u32[]{:S(2)}, u32[]{:S(2)}) collective-permute-start(bf16[144,4096]{1,0:T(8,128)(2,1)S(1)} %assemble.1.refs_0_.half_ref), channel_id=1, source_target_pairs={{0,2},{2,0},{4,6},{6,4},{8,10},{10,8},{12,14},{14,12},{16,18},{18,... | collective-permute-start | bytes 3538952 | tf_op jit(solution)/shard_map/ppermute | solution.py:35
  43.7 15.8 %collective-permute-start.10 = (bf16[128,1024]{1,0:T(8,128)(2,1)S(1)}, bf16[128,1024]{1,0:T(8,128)(2,1)S(1)}, u32[]{:S(2)}, u32[]{:S(2)}) collective-permute-start(bf16[128,1024]{1,0:T(8,128)(2,1)S(1)} %forward_half.3), channel_id=1, source_target_pairs={{0,1},{1,0},{2,3},{3,2},{4,5},{5,4},{6,7},{7,6},{8,9},{9,8},{10,11... | collective-permute-start | bytes 786440 | tf_op jit(solution)/shard_map/ppermute | solution.py:39
  49.0 10.5 %collective-permute-start.11 = (bf16[128,1024]{1,0:T(8,128)(2,1)S(1)}, bf16[128,1024]{1,0:T(8,128)(2,1)S(1)}, u32[]{:S(2)}, u32[]{:S(2)}) collective-permute-start(bf16[128,1024]{1,0:T(8,128)(2,1)S(1)} %get-tuple-element.32), channel_id=1, source_target_pairs={{0,1},{1,0},{2,3},{3,2},{4,5},{5,4},{6,7},{7,6},{8,9},{9,8},{10,11... | collective-permute-start | bytes 786440 | tf_op jit(solution)/shard_map/ppermute | solution.py:39
  52.3 14.4 %collective-permute-start.8 = (bf16[248,768]{1,0:T(8,128)(2,1)S(1)}, bf16[248,768]{1,0:T(8,128)(2,1)S(1)}, u32[]{:S(2)}, u32[]{:S(2)}) collective-permute-start(bf16[248,768]{1,0:T(8,128)(2,1)S(1)} %get-tuple-element.27), channel_id=1, source_target_pairs={{0,1},{1,0},{2,3},{3,2},{4,5},{5,4},{6,7},{7,6},{8,9},{9,8},{10,11... | collective-permute-start | bytes 1142792 | tf_op jit(solution)/shard_map/ppermute | solution.py:39
  56.4 3.2 %copy-start = (s32[8]{0:T(128)S(1)}, s32[8]{0:T(128)}, u32[]{:S(2)}) copy-start(s32[8]{0:T(128)} %points_ref.3) | copy-start | bytes 100
  63.3 10.6 %collective-permute-start.12 = (bf16[80,1024]{1,0:T(8,128)(2,1)S(1)}, bf16[80,1024]{1,0:T(8,128)(2,1)S(1)}, u32[]{:S(2)}, u32[]{:S(2)}) collective-permute-start(bf16[80,1024]{1,0:T(8,128)(2,1)S(1)} %coefficients.3.refs_0_), channel_id=1, source_target_pairs={{0,1},{1,0},{2,3},{3,2},{4,5},{5,4},{6,7},{7,6},{8,9},{9,8},{10,11... | collective-permute-start | bytes 491528 | tf_op jit(solution)/shard_map/ppermute | solution.py:39
  69.6 8.9 %collective-permute-start.9 = (bf16[80,768]{1,0:T(8,128)(2,1)S(1)}, bf16[80,768]{1,0:T(8,128)(2,1)S(1)}, u32[]{:S(2)}, u32[]{:S(2)}) collective-permute-start(bf16[80,768]{1,0:T(8,128)(2,1)S(1)} %coefficients.2.refs_1_), channel_id=1, source_target_pairs={{0,1},{1,0},{2,3},{3,2},{4,5},{5,4},{6,7},{7,6},{8,9},{9,8},{10,11... | collective-permute-start | bytes 368648 | tf_op jit(solution)/shard_map/ppermute | solution.py:39
  79.6 1.7 %collective-permute-start.13 = (bf16[40,2048]{1,0:T(8,128)(2,1)S(1)}, bf16[40,2048]{1,0:T(8,128)(2,1)S(1)}, u32[]{:S(2)}, u32[]{:S(2)}) collective-permute-start(bf16[40,2048]{1,0:T(8,128)(2,1)S(1)} %get-tuple-element.34), channel_id=1, source_target_pairs={{0,2},{2,0},{4,6},{6,4},{8,10},{10,8},{12,14},{14,12},{16,18},{18,... | collective-permute-start | bytes 491528 | tf_op jit(solution)/shard_map/ppermute | solution.py:35
  80.7 2.2 %collective-permute-start.17 = (bf16[40,2048]{1,0:T(8,128)(2,1)S(1)}, bf16[40,2048]{1,0:T(8,128)(2,1)S(1)}, u32[]{:S(2)}, u32[]{:S(2)}) collective-permute-start(bf16[40,2048]{1,0:T(8,128)(2,1)S(1)} %get-tuple-element.36), channel_id=1, source_target_pairs={{0,2},{2,0},{4,6},{6,4},{8,10},{10,8},{12,14},{14,12},{16,18},{18,... | collective-permute-start | bytes 491528 | tf_op jit(solution)/shard_map/ppermute | solution.py:35
  81.4 4.8 %collective-permute-start.14 = (bf16[20,2048]{1,0:T(8,128)(2,1)S(1)}, bf16[20,2048]{1,0:T(8,128)(2,1)S(1)}, u32[]{:S(2)}, u32[]{:S(2)}) collective-permute-start(bf16[20,2048]{1,0:T(8,128)(2,1)S(1)} %slice.91), channel_id=1, source_target_pairs={{0,4},{2,6},{4,0},{6,2},{8,12},{10,14},{12,8},{14,10},{16,20},{18,... | collective-permute-start | bytes 245768 | tf_op jit(solution)/shard_map/ppermute | solution.py:35
  83.1 4.7 %collective-permute-start.18 = (bf16[20,2048]{1,0:T(8,128)(2,1)S(1)}, bf16[20,2048]{1,0:T(8,128)(2,1)S(1)}, u32[]{:S(2)}, u32[]{:S(2)}) collective-permute-start(bf16[20,2048]{1,0:T(8,128)(2,1)S(1)} %pad_maximum_fusion), channel_id=1, source_target_pairs={{0,8},{2,10},{4,12},{6,14},{8,0},{10,2},{12,4},{14,6},{16,24},{18,... | collective-permute-start | bytes 245768 | tf_op jit(solution)/shard_map/ppermute | solution.py:35
  86.2 4.3 %collective-permute-start.15 = (bf16[10,2048]{1,0:T(8,128)(2,1)S(1)}, bf16[10,2048]{1,0:T(8,128)(2,1)S(1)}, u32[]{:S(2)}, u32[]{:S(2)}) collective-permute-start(bf16[10,2048]{1,0:T(8,128)(2,1)S(1)} %slice.93), channel_id=1, source_target_pairs={{0,8},{2,10},{4,12},{6,14},{8,0},{10,2},{12,4},{14,6},{16,24},{18,... | collective-permute-start | bytes 122888 | tf_op jit(solution)/shard_map/ppermute | solution.py:35
  87.8 6.5 %collective-permute-start.19 = (bf16[10,2048]{1,0:T(8,128)(2,1)S(1)}, bf16[10,2048]{1,0:T(8,128)(2,1)S(1)}, u32[]{:S(2)}, u32[]{:S(2)}) collective-permute-start(bf16[10,2048]{1,0:T(8,128)(2,1)S(1)} %slice.92), channel_id=1, source_target_pairs={{0,4},{2,6},{4,0},{6,2},{8,12},{10,14},{12,8},{14,10},{16,20},{18,... | collective-permute-start | bytes 122888 | tf_op jit(solution)/shard_map/ppermute | solution.py:35
  90.6 5.9 %collective-permute-start.16 = (bf16[5,2048]{1,0:T(8,128)(2,1)S(1)}, bf16[5,2048]{1,0:T(8,128)(2,1)S(1)}, u32[]{:S(2)}, u32[]{:S(2)}) collective-permute-start(bf16[5,2048]{1,0:T(8,128)(2,1)S(1)} %slice.95), channel_id=1, source_target_pairs={{0,16},{2,18},{4,20},{6,22},{8,24},{10,26},{12,28},{14,30},{16,0},... | collective-permute-start | bytes 61448 | tf_op jit(solution)/shard_map/ppermute | solution.py:35
  94.4 4.9 %collective-permute-start.20 = (bf16[5,2048]{1,0:T(8,128)(2,1)S(1)}, bf16[5,2048]{1,0:T(8,128)(2,1)S(1)}, u32[]{:S(2)}, u32[]{:S(2)}) collective-permute-start(bf16[5,2048]{1,0:T(8,128)(2,1)S(1)} %slice.94), channel_id=1, source_target_pairs={{0,16},{2,18},{4,20},{6,22},{8,24},{10,26},{12,28},{14,30},{16,0},... | collective-permute-start | bytes 61448 | tf_op jit(solution)/shard_map/ppermute | solution.py:35

commit v5 on v4

--- a/solution.py
+++ b/solution.py
@@ -246,25 +246,43 @@
 
 
 def arriving(next_one, depth):
-    _, _, width, both, below = next_one
-    return [pltpu.VMEM((depth, 2 * width), jnp.bfloat16)] * both + [
+    _, _, width, span, below, _ = next_one
+    return [pltpu.VMEM((depth, 2 * width), jnp.bfloat16)] * (span is not None) + [
         pltpu.VMEM((width, depth), jnp.bfloat16)
     ] * below
 
 
-def while_arriving(next_one, depth, sources, targets, sems, work):
+def extras(next_one, depth, at):
     if next_one is None:
-        return work()
-    _, place, width, both, below = next_one
-    targets = list(targets)
-    buffers = (targets.pop(0) if both else None, targets.pop(0) if below else None)
+        return [], [], [], [], {}
+    weights, _, _, _, _, into = next_one
+    more = arriving(next_one, depth)
+    scratch = [pltpu.SemaphoreType.DMA((3, 4))]
+    if into is None:
+        return [*weights], [ANY] * 3, more, scratch, {}
+    return [*weights, into], [ANY] * 3 + [VMEM], more, scratch, {at + 3: 1}
+
+
+def while_arriving(next_one, refs, work):
+    if next_one is None:
+        return work(refs[0])
+    _, place, width, span, below, into = next_one
+    sources, (out, *targets, sems) = refs[:3], refs[3 + (into is not None):]
+    buffers = (targets.pop(0) if span else None, targets.pop(0) if below else None)
+    first, count = span or (0, 0)
     units, depths = streams(
-        sources, buffers, sems, first_of(place), width, parts_of(depth, 128), parts_of(width, 32)
+        sources,
+        buffers,
+        sems,
+        first_of(place),
+        width,
+        [(first + row, rows) for row, rows in parts_of(count, 128)] if span else [],
+        parts_of(width, 32),
     )
     copies = units + [copy for pair in depths for copy in pair]
     for copy in copies:
         copy.start()
-    pl.when(lax.axis_index("narrow") >= 0)(work)
+    pl.when(lax.axis_index("narrow") >= 0)(lambda: work(out))
     for copy in copies:
         copy.wait()
 
@@ -276,10 +294,7 @@
     rest = side_rows - top
 
     def body(half_ref, both, below, *refs):
-        sources, (out, *targets) = (refs[:3], refs[3:]) if next_one else ((), refs)
-        sems = targets.pop() if next_one else None
-
-        def work():
+        def work(out):
             out[pl.ds(0, rows), :] = jnp.dot(
                 half_ref[pl.ds(0, rows), :], both[...], preferred_element_type=jnp.float32
             ).astype(jnp.bfloat16)
@@ -291,21 +306,22 @@
                     (top - rest, width), jnp.bfloat16
                 )
 
-        while_arriving(next_one, depth, sources, targets, sems, work)
-
-    more = arriving(next_one, depth) if next_one else []
+        while_arriving(next_one, refs, work)
+
+    operands, specs, more, scratch, aliases = extras(next_one, depth, 3)
     return pl.pallas_call(
         body,
         out_shape=[jax.ShapeDtypeStruct((rows + top, 2 * width), jnp.bfloat16)] + more,
-        in_specs=[VMEM] * 3 + [ANY] * (3 if next_one else 0),
+        in_specs=[VMEM] * 3 + specs,
         out_specs=[VMEM] * (1 + len(more)),
-        scratch_shapes=[pltpu.SemaphoreType.DMA((3, 4))] if next_one else [],
+        scratch_shapes=scratch,
+        input_output_aliases=aliases,
         compiler_params=pltpu.CompilerParams(vmem_limit_bytes=4 * 1024 * 1024),
         cost_estimate=pl.CostEstimate(
             flops=4 * depth * width * (rows + side_rows), bytes_accessed=10**6, transcendentals=0
         ),
         name="forward_half",
-    )(half, *weights, *(next_one[0] if next_one else ()))
+    )(half, *weights, *operands)
 
 
 def forward(main, side, weights, place, width, dtype, next_one=None):
@@ -319,16 +335,13 @@
         out[pl.ds(rows, half), pl.ds(width, width)] = value[half:].astype(dtype)
 
     def body_ready(main_ref, side_ref, both, below, *refs):
-        sources, (out, *targets) = (refs[:3], refs[3:]) if next_one else ((), refs)
-        sems = targets.pop() if next_one else None
-
-        def work():
+        def work(out):
             out[pl.ds(0, rows), :] = jnp.dot(
                 main_ref[...], both[...], preferred_element_type=jnp.float32
             ).astype(dtype)
             put_side(out, across(side_ref[...], below[...]))
 
-        while_arriving(next_one, depth, sources, targets, sems, work)
+        while_arriving(next_one, refs, work)
 
     def body(main_ref, side_ref, gate, up, down, out, both, below, total, sems):
         first = first_of(place)
@@ -353,13 +366,12 @@
     out_shape = [jax.ShapeDtypeStruct((rows + half, 2 * width), dtype)]
     operands = [main, side, *weights]
     specs = [VMEM] * 2 + [VMEM if ready else ANY] * len(weights)
+    aliases = {}
     if ready:
-        scratch = []
-        if next_one is not None:
-            operands += next_one[0]
-            specs += [ANY] * 3
-            out_shape += arriving(next_one, depth)
-            scratch = [pltpu.SemaphoreType.DMA((3, 4))]
+        operands_more, specs_more, more, scratch, aliases = extras(next_one, depth, 4)
+        operands += operands_more
+        specs += specs_more
+        out_shape += more
     else:
         scratch = [
             pltpu.VMEM((depth, 2 * width), jnp.bfloat16),
@@ -373,6 +385,7 @@
         in_specs=specs,
         out_specs=[VMEM] * len(out_shape),
         scratch_shapes=scratch,
+        input_output_aliases=aliases,
         compiler_params=pltpu.CompilerParams(vmem_limit_bytes=(4 if ready else 20) * 1024 * 1024),
         cost_estimate=pl.CostEstimate(
             flops=4 * depth * width * (rows + half), bytes_accessed=6 * depth * width, transcendentals=0
@@ -383,7 +396,7 @@
 
 def coefficients(kept, received, picks, points, examples):
     width = kept.shape[1] // 2
-    pairs, references = picks.shape[0] // examples, picks.shape[1]
+    pairs, references = picks.shape[0] // examples, picks.shape[1] // 2
     rows = examples + references
     count = points.shape[0]
     lanes = 128 if width % 128 == 0 else width
@@ -410,16 +423,31 @@
         steps_1 = sum(steps[1:], steps[0])
         steps_2 = sum((t * t for t in steps[1:]), steps[0] * steps[0])
 
+        def total(take, *where):
+            value = take(kept_ref, *where)
+            for ref in got:
+                value = value + take(ref, *where).astype(jnp.float32)
+            return value
+
+        def of_references(ref, lanes_of):
+            if isinstance(ref, tuple):
+                return jnp.concatenate([half[pl.ds(0, references // 2), lanes_of] for half in ref])
+            return ref[pl.ds(0, references), lanes_of]
+
+        for w, target in enumerate((base_gate, base_up)):
+            value = total(of_references, pl.ds(w * width, width))
+            high = value.astype(jnp.bfloat16)
+            low = (value - high.astype(jnp.float32)).astype(jnp.bfloat16)
+            target[...] = jnp.dot(
+                picks, jnp.concatenate([high, low]), preferred_element_type=jnp.float32
+            )
+
         def block(j, _):
+            here = pl.ds(0, width) if lanes == width else pl.ds(pl.multiple_of(j * lanes, 128), lanes)
             if lanes == width:
                 of = [pl.ds(w * width, width) for w in range(2)]
             else:
                 of = [pl.ds(pl.multiple_of(w * width + j * lanes, 128), lanes) for w in range(2)]
-
-            def of_references(ref, w):
-                if isinstance(ref, tuple):
-                    return jnp.concatenate([half[pl.ds(0, references // 2), of[w]] for half in ref])
-                return ref[pl.ds(0, references), of[w]]
 
             def of_examples(ref, first, size, w):
                 if isinstance(ref, tuple):
@@ -434,19 +462,6 @@
                     )
                 return ref[pl.ds(rows, middle), of[h]]
 
-            def total(take, *where):
-                value = take(kept_ref, *where)
-                for ref in got:
-                    value = value + take(ref, *where).astype(jnp.float32)
-                return value
-
-            for w, target in enumerate((base_gate, base_up)):
-                value = total(of_references, w)
-                high = value.astype(jnp.bfloat16)
-                low = (value - high.astype(jnp.float32)).astype(jnp.bfloat16)
-                target[...] = jnp.dot(picks, high, preferred_element_type=jnp.float32) + jnp.dot(
-                    picks, low, preferred_element_type=jnp.float32
-                )
             upstream = [total(of_upstream, h) for h in range(2)]
             for first, piece in pieces:
                 gate = total(of_examples, first, piece, 0) * 0.5
@@ -454,7 +469,7 @@
                 coef_gate = jnp.zeros_like(gate)
                 coef_up = jnp.zeros_like(gate)
                 for p in range(pairs):
-                    start = base_gate[pl.ds(p * examples + first, piece), :] * 0.5
+                    start = base_gate[pl.ds(p * examples + first, piece), here] * 0.5
                     span = gate - start
                     flat = count + (count * start + steps_1 * span)
                     tilted = steps_1 + (steps_1 * start + steps_2 * span)
@@ -467,14 +482,14 @@
                         coef_up = coef_up + bent
                         flat = flat + turn
                         tilted = tilted + t * turn
-                    start_up = base_up[pl.ds(p * examples + first, piece), :]
+                    start_up = base_up[pl.ds(p * examples + first, piece), here]
                     coef_gate = coef_gate + (start_up * flat + (up - start_up) * tilted)
-                base_gate[pl.ds(first, piece), :] = coef_gate * (0.5 * scale)
-                base_up[pl.ds(first, piece), :] = coef_up * scale
+                base_gate[pl.ds(first, piece), here] = coef_gate * (0.5 * scale)
+                base_up[pl.ds(first, piece), here] = coef_up * scale
             for w, source in enumerate((base_gate, base_up)):
                 for h in range(2):
                     some = pl.ds(h * middle, middle)
-                    out[some, of[w]] = (upstream[h] * source[some, :]).astype(jnp.bfloat16)
+                    out[some, of[w]] = (upstream[h] * source[some, here]).astype(jnp.bfloat16)
             return 0
 
         lax.fori_loop(0, width // lanes, block, 0)
@@ -484,7 +499,7 @@
         out_shape=jax.ShapeDtypeStruct((examples, 2 * width), jnp.bfloat16),
         in_specs=[SMEM, VMEM, VMEM] + [VMEM] * len(arrays),
         out_specs=VMEM,
-        scratch_shapes=[pltpu.VMEM((pairs * examples, lanes), jnp.float32)] * 2,
+        scratch_shapes=[pltpu.VMEM((pairs * examples, width), jnp.float32)] * 2,
         compiler_params=pltpu.CompilerParams(vmem_limit_bytes=4 * 1024 * 1024),
         cost_estimate=pl.CostEstimate(flops=5 * 10**9, bytes_accessed=10**6, transcendentals=0),
         name="coefficients",
@@ -495,7 +510,7 @@
     grads, weights, place = items[0]
     rows, width, depth = grads.shape[0], grads.shape[1] // 2, weights[0].shape[0]
     low, columns = span or (0, depth)
-    by_depth = [(low + row, count) for row, count in parts_of(columns, 128)]
+    by_depth = [(low + row, count) for row, count in (parts_of(columns, 128) if len(weights) > 1 else [(0, columns)])]
     ready = len(weights) == 1
 
     def body(*refs):
@@ -570,13 +585,13 @@
             rows[pl.ds(q * e, e), :] = pair_ref[pl.ds(owner * e, e), :]
             name = jnp.where((col >= q * r) & (col < (q + 1) * r), owner * r + col - q * r, name)
         for p in range(pairs):
-            out[pl.ds(p * examples, examples), :] = (
-                (rows[:, pl.ds(p, 1)] == name).astype(jnp.float32).astype(jnp.bfloat16)
-            )
+            pick = (rows[:, pl.ds(p, 1)] == name).astype(jnp.float32).astype(jnp.bfloat16)
+            for h in range(2):
+                out[pl.ds(p * examples, examples), pl.ds(h * blocks * r, blocks * r)] = pick
 
     return pl.pallas_call(
         body,
-        out_shape=jax.ShapeDtypeStruct((pairs * examples, blocks * r), jnp.bfloat16),
+        out_shape=jax.ShapeDtypeStruct((pairs * examples, 2 * blocks * r), jnp.bfloat16),
         in_specs=[VMEM],
         out_specs=VMEM,
         scratch_shapes=[pltpu.VMEM((examples, pairs), jnp.int32)],
@@ -656,17 +671,17 @@
         weights = blocks_of_weights[1, offset]
         count = half.shape[0] // (r + e + k) * k
         kept_one = (*at_peer(0, offset, width), width)
-        (sent,) = forward_half(halves[0], count, weights, width)
+        sent, below = forward_half(halves[0], count, weights, width, (*kept_one, None, True, None))
         received = [shift(sent, peers, 1)]
-        sent, both = forward_half(halves[1], count, weights, width, (*kept_one, True, False))
+        upper = (*kept_one, (0, depth // 2), False, None)
+        sent, both = forward_half(halves[1], count, weights, width, upper)
         received.append(shift(sent, peers, 1))
         parts.append((offset, width, [tuple(received)]))
     main, side = join(halves, (r, e, k))
     if early:
-        sent, below = forward(
-            main, side, blocks_of_weights[1, next_offset], None, next_width, jnp.bfloat16,
-            (*kept_one, False, True),
-        )
+        lower = (*kept_one, (depth // 2, depth - depth // 2), False, both)
+        weights = blocks_of_weights[1, next_offset]
+        sent, both = forward(main, side, weights, None, next_width, jnp.bfloat16, lower)
         parts.append((next_offset, next_width, [shift(sent, peers, 1)]))
         blocks_of_weights[0, offset] = (both, below)
     else:

time: 100 us -> 99.8 us (level)
  Pallas kernels: 44.9 us -> 43 us
    pallas_call x2, Pallas kernels: 6.64 us -> 5.59 us  [coefficients(): pl.pallas_call(body, out_shape=jax.ShapeDtypeStruct((examples, 2 * width)...]
  transfers between devices with their start and end apart: 21 -> 21, of which waited for: 11 -> 11; matrix products, arithmetic and copies ran while one was open for 1% -> 1% of each run, Pallas kernels for 42% -> 40%
where the time goes in v5:
time: 99.8 us; the launch traced here: 99.7 us
  Pallas kernels  43 us (43%)
  starting transfers between devices  27.9 us (28%)
  waiting for transfers between devices  26.8 us (27%)
    ppermute x16, waiting for transfers between devices, permute(): return lax.ppermute(array, axis, pairs)  23.3 us
    ppermute x16, starting transfers between devices, permute(): return lax.ppermute(array, axis, pairs)  20.8 us
    pallas_call x3, Pallas kernels, fetch(): pl.pallas_call(body, out_shape=(pltpu.VMEM((depth, 2 * width), jnp.bfloat...  12.5 us
    pallas_call x4, Pallas kernels, backward(): pl.pallas_call(body, out_shape=out_shape, in_specs=specs, out_specs=out_s...  9.32 us
    pallas_call x3, Pallas kernels, forward(): pl.pallas_call(body_ready if ready else body, out_shape=out_shape, in_spe...  8.19 us
    ppermute x5, starting transfers between devices, shift(): lax.ppermute(array, 'narrow', [(at, (at + amount) % size) for at in range...  7.04 us
    pallas_call x2, Pallas kernels, coefficients(): pl.pallas_call(body, out_shape=jax.ShapeDtypeStruct((examples, 2 * width)...  5.59 us
    pallas_call x2, Pallas kernels, forward_half(): pl.pallas_call(body, out_shape=[jax.ShapeDtypeStruct((rows + top, 2 * wid...  5.35 us
  transfers between devices with their start and end apart: 21, of which 11 were waited for; matrix products, arithmetic and copies ran while one was open for 1% of the time, Pallas kernels for 40%

profile of v5, /device:TPU:0, one launch (start us, length us, event | category | flops | bytes accessed | tf_op | source)
XLA Modules:
  0.0 99.7 jit_solution(11582754212787488529)
XLA Ops:
  0.0 1.0 pack.1.refs_0_
  1.0 4.1 %collective-permute-start = (bf16[16,4608]{1,0:T(8,128)(2,1)S(1)}, bf16[16,4608]{1,0:T(8,128)(2,1)S(1)}, u32[]{:S(2)}, u32[]{:S(2)}) collective-permute-start(bf16[16,4608]{1,0:T(8,128)(2,1)S(1)} %pack.1.refs_0_), channel_id=1, source_target_pairs={{0,16},{2,18},{4,20},{6,22},{8,24},{10,26},{12,28},{14,30},{16,0},... | collective-permute-start | bytes 442376 | tf_op jit(solution)/shard_map/ppermute | solution.py:35
  5.1 1.6 %collective-permute-start.1 = (bf16[16,4608]{1,0:T(8,128)(2,1)S(1)}, bf16[16,4608]{1,0:T(8,128)(2,1)S(1)}, u32[]{:S(2)}, u32[]{:S(2)}) collective-permute-start(bf16[16,4608]{1,0:T(8,128)(2,1)S(1)} %pack.1.refs_0_), channel_id=1, source_target_pairs={{0,8},{2,10},{4,12},{6,14},{8,0},{10,2},{12,4},{14,6},{16,24},{18,... | collective-permute-start | bytes 442376 | tf_op jit(solution)/shard_map/ppermute | solution.py:35
  6.7 5.5 %collective-permute-done.refs_1_ = bf16[16,4608]{1,0:T(8,128)(2,1)S(1)} collective-permute-done((bf16[16,4608]{1,0:T(8,128)(2,1)S(1)}, bf16[16,4608]{1,0:T(8,128)(2,1)S(1)}, u32[]{:S(2)}, u32[]{:S(2)}) %collective-permute-start) | collective-permute-done | bytes 147488 | tf_op jit(solution)/shard_map/ppermute | solution.py:35
  12.2 0.6 collective-permute-start.2
  12.8 1.5 %collective-permute-start.3 = (bf16[16,4608]{1,0:T(8,128)(2,1)S(1)}, bf16[16,4608]{1,0:T(8,128)(2,1)S(1)}, u32[]{:S(2)}, u32[]{:S(2)}) collective-permute-start(bf16[16,4608]{1,0:T(8,128)(2,1)S(1)} %pack.1.refs_0_), channel_id=1, source_target_pairs={{0,4},{2,6},{4,0},{6,2},{8,12},{10,14},{12,8},{14,10},{16,20},{18,... | collective-permute-start | bytes 442376 | tf_op jit(solution)/shard_map/ppermute | solution.py:35
  14.4 0.5 collective-permute-start.4
  14.9 1.5 %collective-permute-start.5 = (bf16[16,4608]{1,0:T(8,128)(2,1)S(1)}, bf16[16,4608]{1,0:T(8,128)(2,1)S(1)}, u32[]{:S(2)}, u32[]{:S(2)}) collective-permute-start(bf16[16,4608]{1,0:T(8,128)(2,1)S(1)} %collective-permute-done.1.refs_2_), channel_id=1, source_target_pairs={{0,4},{2,6},{4,0},{6,2},{8,12},{10,14},{12,8},{14,10},{16,20},{18,... | collective-permute-start | bytes 442376 | tf_op jit(solution)/shard_map/ppermute | solution.py:35
  16.4 1.0 collective-permute-done.2.refs_3_
  17.4 1.6 %collective-permute-start.6 = (bf16[16,4608]{1,0:T(8,128)(2,1)S(1)}, bf16[16,4608]{1,0:T(8,128)(2,1)S(1)}, u32[]{:S(2)}, u32[]{:S(2)}) collective-permute-start(bf16[16,4608]{1,0:T(8,128)(2,1)S(1)} %collective-permute-done.2.refs_3_), channel_id=1, source_target_pairs={{0,4},{2,6},{4,0},{6,2},{8,12},{10,14},{12,8},{14,10},{16,20},{18,... | collective-permute-start | bytes 442376 | tf_op jit(solution)/shard_map/ppermute | solution.py:35
  18.9 0.8 copy.10.pair_ref
  19.9 2.8 %collective-permute-done.4.refs_5_ = bf16[16,4608]{1,0:T(8,128)(2,1)S(1)} collective-permute-done((bf16[16,4608]{1,0:T(8,128)(2,1)S(1)}, bf16[16,4608]{1,0:T(8,128)(2,1)S(1)}, u32[]{:S(2)}, u32[]{:S(2)}) %collective-permute-start.4) | collective-permute-done | bytes 147488 | tf_op jit(solution)/shard_map/ppermute | solution.py:35
  22.7 3.2 %collective-permute-done.5.refs_6_ = bf16[16,4608]{1,0:T(8,128)(2,1)S(1)} collective-permute-done((bf16[16,4608]{1,0:T(8,128)(2,1)S(1)}, bf16[16,4608]{1,0:T(8,128)(2,1)S(1)}, u32[]{:S(2)}, u32[]{:S(2)}) %collective-permute-start.5) | collective-permute-done | bytes 147488 | tf_op jit(solution)/shard_map/ppermute | solution.py:35
  25.9 1.9 %collective-permute-done.6.refs_7_ = bf16[16,4608]{1,0:T(8,128)(2,1)S(1)} collective-permute-done((bf16[16,4608]{1,0:T(8,128)(2,1)S(1)}, bf16[16,4608]{1,0:T(8,128)(2,1)S(1)}, u32[]{:S(2)}, u32[]{:S(2)}) %collective-permute-start.6) | collective-permute-done | bytes 147488 | tf_op jit(solution)/shard_map/ppermute | solution.py:35
  27.8 0.8 assemble.1.refs_0_.half_ref
  28.6 4.8 %fetch.5 = (bf16[4096,1024]{1,0:T(8,128)(2,1)S(1)}, bf16[512,4096]{1,0:T(8,128)(2,1)S(1)}) custom-call(bf16[4096,1792]{1,0:T(8,128)(2,1)} %refs_0_.7, bf16[4096,1792]{1,0:T(8,128)(2,1)} %refs_1_.7, bf16[1792,4096]{1,0:T(8,128)(2,1)} %refs_2_.7), custom_call_target="tpu_custom_call" | custom-call | flops 4000000000 | bytes 12582912 | tf_op jit(solution)/shard_map/fetch/pallas_call | solution.py:231
  33.4 3.9 %fetch.4 = (bf16[4096,768]{1,0:T(8,128)(2,1)S(1)}, bf16[384,4096]{1,0:T(8,128)(2,1)S(1)}) custom-call(bf16[4096,1792]{1,0:T(8,128)(2,1)} %refs_0_.7, bf16[4096,1792]{1,0:T(8,128)(2,1)} %refs_1_.7, bf16[1792,4096]{1,0:T(8,128)(2,1)} %refs_2_.7), custom_call_target="tpu_custom_call" | custom-call | flops 4000000000 | bytes 9437184 | tf_op jit(solution)/shard_map/fetch/pallas_call | solution.py:231
  37.3 3.9 %fetch.3 = (bf16[4096,768]{1,0:T(8,128)(2,1)S(1)}, bf16[384,4096]{1,0:T(8,128)(2,1)S(1)}) custom-call(bf16[4096,1792]{1,0:T(8,128)(2,1)} %refs_0_.7, bf16[4096,1792]{1,0:T(8,128)(2,1)} %refs_1_.7, bf16[1792,4096]{1,0:T(8,128)(2,1)} %refs_2_.7), custom_call_target="tpu_custom_call" | custom-call | flops 4000000000 | bytes 9437184 | tf_op jit(solution)/shard_map/fetch/pallas_call | solution.py:231
  41.2 2.7 %forward_half.3 = (bf16[128,1024]{1,0:T(8,128)(2,1)S(1)}, bf16[512,4096]{1,0:T(8,128)(2,1)S(1)}) custom-call(bf16[144,4096]{1,0:T(8,128)(2,1)S(1)} %assemble.1.refs_0_.half_ref, bf16[4096,1024]{1,0:T(8,128)(2,1)S(1)} %get-tuple-element.29.both.refs_2_, bf16[512,4096]{1,0:T(8,128)(2,1)S(1)} %get-tuple-element.30.below, bf16[4096,1792]{1,0:T(8,128)(2,1)} %refs_0_.7, ...), custom_call_target="tpu_custom_call" | custom-call | flops 1207959552 | bytes 1000000 | tf_op jit(solution)/shard_map/forward_half/pallas_call | solution.py:312
  43.9 1.6 %collective-permute-start.10 = (bf16[128,1024]{1,0:T(8,128)(2,1)S(1)}, bf16[128,1024]{1,0:T(8,128)(2,1)S(1)}, u32[]{:S(2)}, u32[]{:S(2)}) collective-permute-start(bf16[128,1024]{1,0:T(8,128)(2,1)S(1)} %get-tuple-element.35), channel_id=1, source_target_pairs={{0,1},{1,0},{2,3},{3,2},{4,5},{5,4},{6,7},{7,6},{8,9},{9,8},{10,11... | collective-permute-start | bytes 786440 | tf_op jit(solution)/shard_map/ppermute | solution.py:39
  45.5 2.7 %forward_half.2 = (bf16[128,1024]{1,0:T(8,128)(2,1)S(1)}, bf16[4096,1024]{1,0:T(8,128)(2,1)S(1)}) custom-call(bf16[144,4096]{1,0:T(8,128)(2,1)S(1)} %collective-permute-done.7.refs_1_.half_ref, bf16[4096,1024]{1,0:T(8,128)(2,1)S(1)} %get-tuple-element.29.both.refs_2_, bf16[512,4096]{1,0:T(8,128)(2,1)S(1)} %get-tuple-element.30.below, ...), custom_call_target="tpu_custom_call" | custom-call | flops 1207959552 | bytes 1000000 | tf_op jit(solution)/shard_map/forward_half/pallas_call | solution.py:312
  48.2 0.5 collective-permute-start.11
  48.9 2.7 %forward.4 = (bf16[248,768]{1,0:T(8,128)(2,1)S(1)}, bf16[4096,1024]{1,0:T(8,128)(2,1)S(1)}) custom-call(bf16[208,4096]{1,0:T(8,128)(2,1)S(1)} %get-tuple-element.23.main_ref, bf16[80,4096]{1,0:T(8,128)(2,1)S(1)} %get-tuple-element.24.side_ref, bf16[4096,768]{1,0:T(8,128)(2,1)S(1)} %get-tuple-element.27.both.refs_1_, ...), custom_call_target="tpu_custom_call", output_to_operand_aliasing={{1}: (7, {})} | custom-call | flops 1560281088 | bytes 9437184 | tf_op jit(solution)/shard_map/forward/pallas_call | solution.py:382
  51.6 1.6 %collective-permute-start.8 = (bf16[248,768]{1,0:T(8,128)(2,1)S(1)}, bf16[248,768]{1,0:T(8,128)(2,1)S(1)}, u32[]{:S(2)}, u32[]{:S(2)}) collective-permute-start(bf16[248,768]{1,0:T(8,128)(2,1)S(1)} %get-tuple-element.32), channel_id=1, source_target_pairs={{0,1},{1,0},{2,3},{3,2},{4,5},{5,4},{6,7},{7,6},{8,9},{9,8},{10,11... | collective-permute-start | bytes 1142792 | tf_op jit(solution)/shard_map/ppermute | solution.py:39
  53.2 2.4 %forward.3.kept_ref = f32[248,768]{1,0:T(8,128)S(1)} custom-call(bf16[208,4096]{1,0:T(8,128)(2,1)S(1)} %get-tuple-element.23.main_ref, bf16[80,4096]{1,0:T(8,128)(2,1)S(1)} %get-tuple-element.24.side_ref, bf16[4096,768]{1,0:T(8,128)(2,1)S(1)} %get-tuple-element.25.both.refs_3_, bf16[384,4096]{1,0:T(8,128)(2,1)S(1)} %get-tuple-element.26.below), custom_call_target="tpu_custom_call" | custom-call | flops 1560281088 | bytes 9437184 | tf_op jit(solution)/shard_map/forward/pallas_call | solution.py:382
  55.6 3.1 %forward.5.kept_ref = f32[248,1024]{1,0:T(8,128)S(1)} custom-call(bf16[208,4096]{1,0:T(8,128)(2,1)S(1)} %get-tuple-element.23.main_ref, bf16[80,4096]{1,0:T(8,128)(2,1)S(1)} %get-tuple-element.24.side_ref, bf16[4096,1024]{1,0:T(8,128)(2,1)S(1)} %get-tuple-element.33.both.refs_1_, bf16[512,4096]{1,0:T(8,128)(2,1)S(1)} %get-tuple-element.34.below), custom_call_target="tpu_custom_call" | custom-call | flops 2080374784 | bytes 12582912 | tf_op jit(solution)/shard_map/forward/pallas_call | solution.py:382
  58.8 3.1 %coefficients.3.refs_0_ = bf16[80,1024]{1,0:T(8,128)(2,1)S(1)} custom-call(s32[8]{0:T(128)S(1)} %copy-done, bf16[320,256]{1,0:T(8,128)(2,1)S(1)} %choices.1.picks_ref, f32[248,1024]{1,0:T(8,128)S(1)} %forward.5.kept_ref, bf16[128,1024]{1,0:T(8,128)(2,1)S(1)} %collective-permute-done.10.refs_0_, bf16[128,1024]{1,0:T(8,128)(2,1)S(1)} %collective-permute-done.11.refs_1_), custom_call_target="tpu_custom_call" | custom-call | flops 5000000000 | bytes 1000000 | tf_op jit(solution)/shard_map/coefficients/pallas_call | solution.py:497
  61.8 1.6 %collective-permute-start.12 = (bf16[80,1024]{1,0:T(8,128)(2,1)S(1)}, bf16[80,1024]{1,0:T(8,128)(2,1)S(1)}, u32[]{:S(2)}, u32[]{:S(2)}) collective-permute-start(bf16[80,1024]{1,0:T(8,128)(2,1)S(1)} %coefficients.3.refs_0_), channel_id=1, source_target_pairs={{0,1},{1,0},{2,3},{3,2},{4,5},{5,4},{6,7},{7,6},{8,9},{9,8},{10,11... | collective-permute-start | bytes 491528 | tf_op jit(solution)/shard_map/ppermute | solution.py:39
  63.5 3.4 %collective-permute-done.8.refs_0_ = bf16[248,768]{1,0:T(8,128)(2,1)S(1)} collective-permute-done((bf16[248,768]{1,0:T(8,128)(2,1)S(1)}, bf16[248,768]{1,0:T(8,128)(2,1)S(1)}, u32[]{:S(2)}, u32[]{:S(2)}) %collective-permute-start.8) | collective-permute-done | bytes 380960 | tf_op jit(solution)/shard_map/ppermute | solution.py:39
  66.9 2.5 %coefficients.2.refs_1_ = bf16[80,768]{1,0:T(8,128)(2,1)S(1)} custom-call(s32[8]{0:T(128)S(1)} %copy-done, bf16[320,256]{1,0:T(8,128)(2,1)S(1)} %choices.1.picks_ref, f32[248,768]{1,0:T(8,128)S(1)} %forward.3.kept_ref, bf16[248,768]{1,0:T(8,128)(2,1)S(1)} %collective-permute-done.8.refs_0_), custom_call_target="tpu_custom_call" | custom-call | flops 5000000000 | bytes 1000000 | tf_op jit(solution)/shard_map/coefficients/pallas_call | solution.py:497
  69.4 1.6 %collective-permute-start.9 = (bf16[80,768]{1,0:T(8,128)(2,1)S(1)}, bf16[80,768]{1,0:T(8,128)(2,1)S(1)}, u32[]{:S(2)}, u32[]{:S(2)}) collective-permute-start(bf16[80,768]{1,0:T(8,128)(2,1)S(1)} %coefficients.2.refs_1_), channel_id=1, source_target_pairs={{0,1},{1,0},{2,3},{3,2},{4,5},{5,4},{6,7},{7,6},{8,9},{9,8},{10,11... | collective-permute-start | bytes 368648 | tf_op jit(solution)/shard_map/ppermute | solution.py:39
  71.1 2.6 %backward.4.refs_4_ = f32[80,4096]{1,0:T(8,128)S(1)} custom-call(bf16[80,1024]{1,0:T(8,128)(2,1)S(1)} %coefficients.3.refs_0_, bf16[4096,1024]{1,0:T(8,128)(2,1)S(1)} %get-tuple-element.33.both.refs_1_), custom_call_target="tpu_custom_call" | custom-call | flops 671088640 | bytes 8388608 | tf_op jit(solution)/shard_map/backward/pallas_call | solution.py:556
  73.7 4.5 %backward.5.refs_2_ = f32[80,4096]{1,0:T(8,128)S(1)} custom-call(bf16[80,1024]{1,0:T(8,128)(2,1)S(1)} %collective-permute-done.12.refs_0_, bf16[80,768]{1,0:T(8,128)(2,1)S(1)} %coefficients.2.refs_1_, bf16[4096,1024]{1,0:T(8,128)(2,1)S(1)} %get-tuple-element.29.both.refs_2_, bf16[4096,768]{1,0:T(8,128)(2,1)S(1)} %get-tuple-element.25.both.refs_3_, ...), custom_call_target="tpu_custom_call" | custom-call | flops 1174405120 | bytes 8388608 | tf_op jit(solution)/shard_map/backward/pallas_call | solution.py:556
  78.3 1.1 %backward.6 = (bf16[40,2048]{1,0:T(8,128)(2,1)S(1)}, f32[40,2048]{1,0:T(8,128)S(1)}) custom-call(bf16[80,768]{1,0:T(8,128)(2,1)S(1)} %collective-permute-done.9.refs_0_, bf16[4096,768]{1,0:T(8,128)(2,1)S(1)} %get-tuple-element.27.both.refs_1_, f32[80,4096]{1,0:T(8,128)S(1)} %backward.5.refs_2_), custom_call_target="tpu_custom_call" | custom-call | flops 251658240 | bytes 3145728 | tf_op jit(solution)/shard_map/backward/pallas_call | solution.py:556
  79.4 1.1 %backward.7 = (bf16[40,2048]{1,0:T(8,128)(2,1)S(1)}, f32[40,2048]{1,0:T(8,128)S(1)}) custom-call(bf16[80,768]{1,0:T(8,128)(2,1)S(1)} %collective-permute-done.9.refs_0_, bf16[4096,768]{1,0:T(8,128)(2,1)S(1)} %get-tuple-element.27.both.refs_1_, f32[80,4096]{1,0:T(8,128)S(1)} %backward.5.refs_2_), custom_call_target="tpu_custom_call" | custom-call | flops 251658240 | bytes 3145728 | tf_op jit(solution)/shard_map/backward/pallas_call | solution.py:556
  80.5 0.6 collective-permute-start.17
  81.1 1.6 %collective-permute-start.14 = (bf16[20,2048]{1,0:T(8,128)(2,1)S(1)}, bf16[20,2048]{1,0:T(8,128)(2,1)S(1)}, u32[]{:S(2)}, u32[]{:S(2)}) collective-permute-start(bf16[20,2048]{1,0:T(8,128)(2,1)S(1)} %slice.91), channel_id=1, source_target_pairs={{0,4},{2,6},{4,0},{6,2},{8,12},{10,14},{12,8},{14,10},{16,20},{18,... | collective-permute-start | bytes 245768 | tf_op jit(solution)/shard_map/ppermute | solution.py:35
  82.8 0.3 collective-permute-start.18
  83.2 2.7 %collective-permute-done.14 = bf16[20,2048]{1,0:T(8,128)(2,1)S(1)} collective-permute-done((bf16[20,2048]{1,0:T(8,128)(2,1)S(1)}, bf16[20,2048]{1,0:T(8,128)(2,1)S(1)}, u32[]{:S(2)}, u32[]{:S(2)}) %collective-permute-start.14) | collective-permute-done | bytes 81952 | tf_op jit(solution)/shard_map/ppermute | solution.py:35
  85.9 0.4 collective-permute-start.15
  86.3 1.2 %collective-permute-done.18 = bf16[20,2048]{1,0:T(8,128)(2,1)S(1)} collective-permute-done((bf16[20,2048]{1,0:T(8,128)(2,1)S(1)}, bf16[20,2048]{1,0:T(8,128)(2,1)S(1)}, u32[]{:S(2)}, u32[]{:S(2)}) %collective-permute-start.18) | collective-permute-done | bytes 81952 | tf_op jit(solution)/shard_map/ppermute | solution.py:35
  87.6 1.4 %collective-permute-start.19 = (bf16[10,2048]{1,0:T(8,128)(2,1)S(1)}, bf16[10,2048]{1,0:T(8,128)(2,1)S(1)}, u32[]{:S(2)}, u32[]{:S(2)}) collective-permute-start(bf16[10,2048]{1,0:T(8,128)(2,1)S(1)} %slice.92), channel_id=1, source_target_pairs={{0,4},{2,6},{4,0},{6,2},{8,12},{10,14},{12,8},{14,10},{16,20},{18,... | collective-permute-start | bytes 122888 | tf_op jit(solution)/shard_map/ppermute | solution.py:35
  89.0 1.3 %collective-permute-done.15 = bf16[10,2048]{1,0:T(8,128)(2,1)S(1)} collective-permute-done((bf16[10,2048]{1,0:T(8,128)(2,1)S(1)}, bf16[10,2048]{1,0:T(8,128)(2,1)S(1)}, u32[]{:S(2)}, u32[]{:S(2)}) %collective-permute-start.15) | collective-permute-done | bytes 40992 | tf_op jit(solution)/shard_map/ppermute | solution.py:35
  90.3 3.8 %collective-permute-start.16 = (bf16[5,2048]{1,0:T(8,128)(2,1)S(1)}, bf16[5,2048]{1,0:T(8,128)(2,1)S(1)}, u32[]{:S(2)}, u32[]{:S(2)}) collective-permute-start(bf16[5,2048]{1,0:T(8,128)(2,1)S(1)} %slice.95), channel_id=1, source_target_pairs={{0,16},{2,18},{4,20},{6,22},{8,24},{10,26},{12,28},{14,30},{16,0},... | collective-permute-start | bytes 61448 | tf_op jit(solution)/shard_map/ppermute | solution.py:35
  94.1 1.2 %collective-permute-start.20 = (bf16[5,2048]{1,0:T(8,128)(2,1)S(1)}, bf16[5,2048]{1,0:T(8,128)(2,1)S(1)}, u32[]{:S(2)}, u32[]{:S(2)}) collective-permute-start(bf16[5,2048]{1,0:T(8,128)(2,1)S(1)} %slice.94), channel_id=1, source_target_pairs={{0,16},{2,18},{4,20},{6,22},{8,24},{10,26},{12,28},{14,30},{16,0},... | collective-permute-start | bytes 61448 | tf_op jit(solution)/shard_map/ppermute | solution.py:35
  95.4 0.9 collective-permute-done.16
  96.2 2.8 %collective-permute-done.20 = bf16[5,2048]{1,0:T(8,128)(2,1)S(1)} collective-permute-done((bf16[5,2048]{1,0:T(8,128)(2,1)S(1)}, bf16[5,2048]{1,0:T(8,128)(2,1)S(1)}, u32[]{:S(2)}, u32[]{:S(2)}) %collective-permute-start.20) | collective-permute-done | bytes 20512 | tf_op jit(solution)/shard_map/ppermute | solution.py:35
  99.0 0.6 pad_maximum_fusion.1
  (32 shorter events, 0.8 us)
Async XLA Ops:
  1.0 11.2 %collective-permute-start = (bf16[16,4608]{1,0:T(8,128)(2,1)S(1)}, bf16[16,4608]{1,0:T(8,128)(2,1)S(1)}, u32[]{:S(2)}, u32[]{:S(2)}) collective-permute-start(bf16[16,4608]{1,0:T(8,128)(2,1)S(1)} %pack.1.refs_0_), channel_id=1, source_target_pairs={{0,16},{2,18},{4,20},{6,22},{8,24},{10,26},{12,28},{14,30},{16,0},... | collective-permute-start | bytes 442376 | tf_op jit(solution)/shard_map/ppermute | solution.py:35
  5.1 9.8 %collective-permute-start.1 = (bf16[16,4608]{1,0:T(8,128)(2,1)S(1)}, bf16[16,4608]{1,0:T(8,128)(2,1)S(1)}, u32[]{:S(2)}, u32[]{:S(2)}) collective-permute-start(bf16[16,4608]{1,0:T(8,128)(2,1)S(1)} %pack.1.refs_0_), channel_id=1, source_target_pairs={{0,8},{2,10},{4,12},{6,14},{8,0},{10,2},{12,4},{14,6},{16,24},{18,... | collective-permute-start | bytes 442376 | tf_op jit(solution)/shard_map/ppermute | solution.py:35
  12.2 5.1 %collective-permute-start.2 = (bf16[16,4608]{1,0:T(8,128)(2,1)S(1)}, bf16[16,4608]{1,0:T(8,128)(2,1)S(1)}, u32[]{:S(2)}, u32[]{:S(2)}) collective-permute-start(bf16[16,4608]{1,0:T(8,128)(2,1)S(1)} %collective-permute-done.refs_1_), channel_id=1, source_target_pairs={{0,8},{2,10},{4,12},{6,14},{8,0},{10,2},{12,4},{14,6},{16,24},{18,... | collective-permute-start | bytes 442376 | tf_op jit(solution)/shard_map/ppermute | solution.py:35
  12.8 7.0 %collective-permute-start.3 = (bf16[16,4608]{1,0:T(8,128)(2,1)S(1)}, bf16[16,4608]{1,0:T(8,128)(2,1)S(1)}, u32[]{:S(2)}, u32[]{:S(2)}) collective-permute-start(bf16[16,4608]{1,0:T(8,128)(2,1)S(1)} %pack.1.refs_0_), channel_id=1, source_target_pairs={{0,4},{2,6},{4,0},{6,2},{8,12},{10,14},{12,8},{14,10},{16,20},{18,... | collective-permute-start | bytes 442376 | tf_op jit(solution)/shard_map/ppermute | solution.py:35
  14.4 8.4 %collective-permute-start.4 = (bf16[16,4608]{1,0:T(8,128)(2,1)S(1)}, bf16[16,4608]{1,0:T(8,128)(2,1)S(1)}, u32[]{:S(2)}, u32[]{:S(2)}) collective-permute-start(bf16[16,4608]{1,0:T(8,128)(2,1)S(1)} %collective-permute-done.refs_1_), channel_id=1, source_target_pairs={{0,4},{2,6},{4,0},{6,2},{8,12},{10,14},{12,8},{14,10},{16,20},{18,... | collective-permute-start | bytes 442376 | tf_op jit(solution)/shard_map/ppermute | solution.py:35
  14.9 11.0 %collective-permute-start.5 = (bf16[16,4608]{1,0:T(8,128)(2,1)S(1)}, bf16[16,4608]{1,0:T(8,128)(2,1)S(1)}, u32[]{:S(2)}, u32[]{:S(2)}) collective-permute-start(bf16[16,4608]{1,0:T(8,128)(2,1)S(1)} %collective-permute-done.1.refs_2_), channel_id=1, source_target_pairs={{0,4},{2,6},{4,0},{6,2},{8,12},{10,14},{12,8},{14,10},{16,20},{18,... | collective-permute-start | bytes 442376 | tf_op jit(solution)/shard_map/ppermute | solution.py:35
  17.4 10.4 %collective-permute-start.6 = (bf16[16,4608]{1,0:T(8,128)(2,1)S(1)}, bf16[16,4608]{1,0:T(8,128)(2,1)S(1)}, u32[]{:S(2)}, u32[]{:S(2)}) collective-permute-start(bf16[16,4608]{1,0:T(8,128)(2,1)S(1)} %collective-permute-done.2.refs_3_), channel_id=1, source_target_pairs={{0,4},{2,6},{4,0},{6,2},{8,12},{10,14},{12,8},{14,10},{16,20},{18,... | collective-permute-start | bytes 442376 | tf_op jit(solution)/shard_map/ppermute | solution.py:35
  28.6 17.0 %collective-permute-start.7 = (bf16[144,4096]{1,0:T(8,128)(2,1)S(1)}, bf16[144,4096]{1,0:T(8,128)(2,1)S(1)}, u32[]{:S(2)}, u32[]{:S(2)}) collective-permute-start(bf16[144,4096]{1,0:T(8,128)(2,1)S(1)} %assemble.1.refs_0_.half_ref), channel_id=1, source_target_pairs={{0,2},{2,0},{4,6},{6,4},{8,10},{10,8},{12,14},{14,12},{16,18},{18,... | collective-permute-start | bytes 3538952 | tf_op jit(solution)/shard_map/ppermute | solution.py:35
  43.9 14.8 %collective-permute-start.10 = (bf16[128,1024]{1,0:T(8,128)(2,1)S(1)}, bf16[128,1024]{1,0:T(8,128)(2,1)S(1)}, u32[]{:S(2)}, u32[]{:S(2)}) collective-permute-start(bf16[128,1024]{1,0:T(8,128)(2,1)S(1)} %get-tuple-element.35), channel_id=1, source_target_pairs={{0,1},{1,0},{2,3},{3,2},{4,5},{5,4},{6,7},{7,6},{8,9},{9,8},{10,11... | collective-permute-start | bytes 786440 | tf_op jit(solution)/shard_map/ppermute | solution.py:39
  48.2 10.6 %collective-permute-start.11 = (bf16[128,1024]{1,0:T(8,128)(2,1)S(1)}, bf16[128,1024]{1,0:T(8,128)(2,1)S(1)}, u32[]{:S(2)}, u32[]{:S(2)}) collective-permute-start(bf16[128,1024]{1,0:T(8,128)(2,1)S(1)} %get-tuple-element.36), channel_id=1, source_target_pairs={{0,1},{1,0},{2,3},{3,2},{4,5},{5,4},{6,7},{7,6},{8,9},{9,8},{10,11... | collective-permute-start | bytes 786440 | tf_op jit(solution)/shard_map/ppermute | solution.py:39
  51.6 15.3 %collective-permute-start.8 = (bf16[248,768]{1,0:T(8,128)(2,1)S(1)}, bf16[248,768]{1,0:T(8,128)(2,1)S(1)}, u32[]{:S(2)}, u32[]{:S(2)}) collective-permute-start(bf16[248,768]{1,0:T(8,128)(2,1)S(1)} %get-tuple-element.32), channel_id=1, source_target_pairs={{0,1},{1,0},{2,3},{3,2},{4,5},{5,4},{6,7},{7,6},{8,9},{9,8},{10,11... | collective-permute-start | bytes 1142792 | tf_op jit(solution)/shard_map/ppermute | solution.py:39
  55.6 3.2 %copy-start = (s32[8]{0:T(128)S(1)}, s32[8]{0:T(128)}, u32[]{:S(2)}) copy-start(s32[8]{0:T(128)} %points_ref.3) | copy-start | bytes 100
  61.8 11.9 %collective-permute-start.12 = (bf16[80,1024]{1,0:T(8,128)(2,1)S(1)}, bf16[80,1024]{1,0:T(8,128)(2,1)S(1)}, u32[]{:S(2)}, u32[]{:S(2)}) collective-permute-start(bf16[80,1024]{1,0:T(8,128)(2,1)S(1)} %coefficients.3.refs_0_), channel_id=1, source_target_pairs={{0,1},{1,0},{2,3},{3,2},{4,5},{5,4},{6,7},{7,6},{8,9},{9,8},{10,11... | collective-permute-start | bytes 491528 | tf_op jit(solution)/shard_map/ppermute | solution.py:39
  69.4 8.8 %collective-permute-start.9 = (bf16[80,768]{1,0:T(8,128)(2,1)S(1)}, bf16[80,768]{1,0:T(8,128)(2,1)S(1)}, u32[]{:S(2)}, u32[]{:S(2)}) collective-permute-start(bf16[80,768]{1,0:T(8,128)(2,1)S(1)} %coefficients.2.refs_1_), channel_id=1, source_target_pairs={{0,1},{1,0},{2,3},{3,2},{4,5},{5,4},{6,7},{7,6},{8,9},{9,8},{10,11... | collective-permute-start | bytes 368648 | tf_op jit(solution)/shard_map/ppermute | solution.py:39
  79.3 1.7 %collective-permute-start.13 = (bf16[40,2048]{1,0:T(8,128)(2,1)S(1)}, bf16[40,2048]{1,0:T(8,128)(2,1)S(1)}, u32[]{:S(2)}, u32[]{:S(2)}) collective-permute-start(bf16[40,2048]{1,0:T(8,128)(2,1)S(1)} %get-tuple-element.38), channel_id=1, source_target_pairs={{0,2},{2,0},{4,6},{6,4},{8,10},{10,8},{12,14},{14,12},{16,18},{18,... | collective-permute-start | bytes 491528 | tf_op jit(solution)/shard_map/ppermute | solution.py:35
  80.5 2.2 %collective-permute-start.17 = (bf16[40,2048]{1,0:T(8,128)(2,1)S(1)}, bf16[40,2048]{1,0:T(8,128)(2,1)S(1)}, u32[]{:S(2)}, u32[]{:S(2)}) collective-permute-start(bf16[40,2048]{1,0:T(8,128)(2,1)S(1)} %get-tuple-element.40), channel_id=1, source_target_pairs={{0,2},{2,0},{4,6},{6,4},{8,10},{10,8},{12,14},{14,12},{16,18},{18,... | collective-permute-start | bytes 491528 | tf_op jit(solution)/shard_map/ppermute | solution.py:35
  81.1 4.8 %collective-permute-start.14 = (bf16[20,2048]{1,0:T(8,128)(2,1)S(1)}, bf16[20,2048]{1,0:T(8,128)(2,1)S(1)}, u32[]{:S(2)}, u32[]{:S(2)}) collective-permute-start(bf16[20,2048]{1,0:T(8,128)(2,1)S(1)} %slice.91), channel_id=1, source_target_pairs={{0,4},{2,6},{4,0},{6,2},{8,12},{10,14},{12,8},{14,10},{16,20},{18,... | collective-permute-start | bytes 245768 | tf_op jit(solution)/shard_map/ppermute | solution.py:35
  82.8 4.7 %collective-permute-start.18 = (bf16[20,2048]{1,0:T(8,128)(2,1)S(1)}, bf16[20,2048]{1,0:T(8,128)(2,1)S(1)}, u32[]{:S(2)}, u32[]{:S(2)}) collective-permute-start(bf16[20,2048]{1,0:T(8,128)(2,1)S(1)} %pad_maximum_fusion), channel_id=1, source_target_pairs={{0,8},{2,10},{4,12},{6,14},{8,0},{10,2},{12,4},{14,6},{16,24},{18,... | collective-permute-start | bytes 245768 | tf_op jit(solution)/shard_map/ppermute | solution.py:35
  85.9 4.3 %collective-permute-start.15 = (bf16[10,2048]{1,0:T(8,128)(2,1)S(1)}, bf16[10,2048]{1,0:T(8,128)(2,1)S(1)}, u32[]{:S(2)}, u32[]{:S(2)}) collective-permute-start(bf16[10,2048]{1,0:T(8,128)(2,1)S(1)} %slice.93), channel_id=1, source_target_pairs={{0,8},{2,10},{4,12},{6,14},{8,0},{10,2},{12,4},{14,6},{16,24},{18,... | collective-permute-start | bytes 122888 | tf_op jit(solution)/shard_map/ppermute | solution.py:35
  87.6 6.5 %collective-permute-start.19 = (bf16[10,2048]{1,0:T(8,128)(2,1)S(1)}, bf16[10,2048]{1,0:T(8,128)(2,1)S(1)}, u32[]{:S(2)}, u32[]{:S(2)}) collective-permute-start(bf16[10,2048]{1,0:T(8,128)(2,1)S(1)} %slice.92), channel_id=1, source_target_pairs={{0,4},{2,6},{4,0},{6,2},{8,12},{10,14},{12,8},{14,10},{16,20},{18,... | collective-permute-start | bytes 122888 | tf_op jit(solution)/shard_map/ppermute | solution.py:35
  90.3 5.9 %collective-permute-start.16 = (bf16[5,2048]{1,0:T(8,128)(2,1)S(1)}, bf16[5,2048]{1,0:T(8,128)(2,1)S(1)}, u32[]{:S(2)}, u32[]{:S(2)}) collective-permute-start(bf16[5,2048]{1,0:T(8,128)(2,1)S(1)} %slice.95), channel_id=1, source_target_pairs={{0,16},{2,18},{4,20},{6,22},{8,24},{10,26},{12,28},{14,30},{16,0},... | collective-permute-start | bytes 61448 | tf_op jit(solution)/shard_map/ppermute | solution.py:35
  94.1 4.9 %collective-permute-start.20 = (bf16[5,2048]{1,0:T(8,128)(2,1)S(1)}, bf16[5,2048]{1,0:T(8,128)(2,1)S(1)}, u32[]{:S(2)}, u32[]{:S(2)}) collective-permute-start(bf16[5,2048]{1,0:T(8,128)(2,1)S(1)} %slice.94), channel_id=1, source_target_pairs={{0,16},{2,18},{4,20},{6,22},{8,24},{10,26},{12,28},{14,30},{16,0},... | collective-permute-start | bytes 61448 | tf_op jit(solution)/shard_map/ppermute | solution.py:35

commit v6 on v5

--- a/solution.py
+++ b/solution.py
@@ -287,41 +287,43 @@
         copy.wait()
 
 
-def forward_half(half, side_rows, weights, width, next_one=None):
+def forward_half(half, others, side_rows, weights, width, next_one=None):
     depth = half.shape[1]
     rows = half.shape[0] - side_rows
-    top = rounded(-(-side_rows // 2), 8)
-    rest = side_rows - top
-
-    def body(half_ref, both, below, *refs):
+    inputs = [half, weights[0]] + ([weights[1], *others] if others else [])
+    all_rows = rows + (side_rows if others else 0)
+
+    def body(half_ref, both, *refs):
+        refs = list(refs)
+        below = refs.pop(0) if others else None
+        side_refs = [refs.pop(0) for _ in others]
+
         def work(out):
             out[pl.ds(0, rows), :] = jnp.dot(
                 half_ref[pl.ds(0, rows), :], both[...], preferred_element_type=jnp.float32
             ).astype(jnp.bfloat16)
-            side = across(half_ref[pl.ds(rows, side_rows), :], below[...]).astype(jnp.bfloat16)
-            out[pl.ds(rows, top), pl.ds(0, width)] = side[:top]
-            out[pl.ds(rows, rest), pl.ds(width, width)] = side[top:]
-            if top > rest:
-                out[pl.ds(rows + rest, top - rest), pl.ds(width, width)] = jnp.zeros(
-                    (top - rest, width), jnp.bfloat16
-                )
+            if others:
+                side = jnp.concatenate([ref[pl.ds(rows, side_rows), :] for ref in side_refs])
+                value = across(side, below[...]).astype(jnp.bfloat16)
+                out[pl.ds(rows, side_rows), pl.ds(0, width)] = value[:side_rows]
+                out[pl.ds(rows, side_rows), pl.ds(width, width)] = value[side_rows:]
 
         while_arriving(next_one, refs, work)
 
-    operands, specs, more, scratch, aliases = extras(next_one, depth, 3)
+    operands, specs, more, scratch, aliases = extras(next_one, depth, len(inputs))
     return pl.pallas_call(
         body,
-        out_shape=[jax.ShapeDtypeStruct((rows + top, 2 * width), jnp.bfloat16)] + more,
-        in_specs=[VMEM] * 3 + specs,
+        out_shape=[jax.ShapeDtypeStruct((all_rows, 2 * width), jnp.bfloat16)] + more,
+        in_specs=[VMEM] * len(inputs) + specs,
         out_specs=[VMEM] * (1 + len(more)),
         scratch_shapes=scratch,
         input_output_aliases=aliases,
         compiler_params=pltpu.CompilerParams(vmem_limit_bytes=4 * 1024 * 1024),
         cost_estimate=pl.CostEstimate(
-            flops=4 * depth * width * (rows + side_rows), bytes_accessed=10**6, transcendentals=0
+            flops=4 * depth * width * all_rows, bytes_accessed=10**6, transcendentals=0
         ),
         name="forward_half",
-    )(half, *weights, *operands)
+    )(*inputs, *operands)
 
 
 def forward(main, side, weights, place, width, dtype, next_one=None):
@@ -401,7 +403,6 @@
     count = points.shape[0]
     lanes = 128 if width % 128 == 0 else width
     middle = examples // 2
-    top = rounded(-(-middle // 2), 8)
     pieces, left = [], middle
     while left:
         size = 16 if left == 16 or left >= 32 else left
@@ -456,11 +457,8 @@
                 return ref[pl.ds(references + first, size), of[w]]
 
             def of_upstream(ref, h):
-                if isinstance(ref, tuple):
-                    return jnp.concatenate(
-                        [ref[h][pl.ds(rows // 2, top), of[0]], ref[h][pl.ds(rows // 2, middle - top), of[1]]]
-                    )
-                return ref[pl.ds(rows, middle), of[h]]
+                ref, first = (ref[1], rows // 2) if isinstance(ref, tuple) else (ref, rows)
+                return ref[pl.ds(first, middle), of[h]]
 
             upstream = [total(of_upstream, h) for h in range(2)]
             for first, piece in pieces:
@@ -671,10 +669,10 @@
         weights = blocks_of_weights[1, offset]
         count = half.shape[0] // (r + e + k) * k
         kept_one = (*at_peer(0, offset, width), width)
-        sent, below = forward_half(halves[0], count, weights, width, (*kept_one, None, True, None))
+        (sent,) = forward_half(halves[0], [], count, weights, width)
         received = [shift(sent, peers, 1)]
         upper = (*kept_one, (0, depth // 2), False, None)
-        sent, both = forward_half(halves[1], count, weights, width, upper)
+        sent, both = forward_half(halves[1], halves, count, weights, width, upper)
         received.append(shift(sent, peers, 1))
         parts.append((offset, width, [tuple(received)]))
     main, side = join(halves, (r, e, k))
@@ -683,6 +681,10 @@
         weights = blocks_of_weights[1, next_offset]
         sent, both = forward(main, side, weights, None, next_width, jnp.bfloat16, lower)
         parts.append((next_offset, next_width, [shift(sent, peers, 1)]))
+        weights = blocks_of_weights[0, next_offset]
+        kept_last, below = forward(
+            main, side, weights, None, next_width, jnp.float32, (*kept_one, None, True, None)
+        )
         blocks_of_weights[0, offset] = (both, below)
     else:
         for offset, width in chunks:
@@ -696,11 +698,14 @@
             parts.append((offset, width, received))
 
     jobs = []
-    for offset, width, received in parts:
+    for i, (offset, width, received) in enumerate(parts):
         weights, place = at_peer(0, offset, width)
         if ahead:
             weights = blocks_of_weights[0, offset]
-        (kept,) = forward(main, side, weights, place, width, jnp.float32)
+        if early and i == 1:
+            kept = kept_last
+        else:
+            (kept,) = forward(main, side, weights, place, width, jnp.float32)
         grads = coefficients(kept, received, picks, points, blocks * e)
         jobs.append((grads, offset, width, 0))
         jobs += [(shift(grads, peers, s), offset, width, s) for s in range(1, peers)]

time: 99.8 us -> 98.2 us (0.984)
  Pallas kernels: 43 us -> 41.9 us
    pallas_call x2, Pallas kernels: 5.35 us -> 4.15 us  [forward_half(): pl.pallas_call(body, out_shape=[jax.ShapeDtypeStruct((all_rows, 2 * width...]
where the time goes in v6:
time: 98.2 us; the launch traced here: 98 us
  Pallas kernels  41.9 us (43%)
  starting transfers between devices  27.4 us (28%)
  waiting for transfers between devices  26.7 us (27%)
    ppermute x16, waiting for transfers between devices, permute(): return lax.ppermute(array, axis, pairs)  23.3 us
    ppermute x16, starting transfers between devices, permute(): return lax.ppermute(array, axis, pairs)  20.9 us
    pallas_call x3, Pallas kernels, fetch(): pl.pallas_call(body, out_shape=(pltpu.VMEM((depth, 2 * width), jnp.bfloat...  12.5 us
    pallas_call x4, Pallas kernels, backward(): pl.pallas_call(body, out_shape=out_shape, in_specs=specs, out_specs=out_s...  9.32 us
    pallas_call x3, Pallas kernels, forward(): pl.pallas_call(body_ready if ready else body, out_shape=out_shape, in_spe...  8.31 us
    ppermute x5, starting transfers between devices, shift(): lax.ppermute(array, 'narrow', [(at, (at + amount) % size) for at in range...  6.51 us
    pallas_call x2, Pallas kernels, coefficients(): pl.pallas_call(body, out_shape=jax.ShapeDtypeStruct((examples, 2 * width)...  5.58 us
    pallas_call x2, Pallas kernels, forward_half(): pl.pallas_call(body, out_shape=[jax.ShapeDtypeStruct((all_rows, 2 * width...  4.15 us
  transfers between devices with their start and end apart: 21, of which 11 were waited for; matrix products, arithmetic and copies ran while one was open for 1% of the time, Pallas kernels for 40%

profile of v6, /device:TPU:0, one launch (start us, length us, event | category | flops | bytes accessed | tf_op | source)
XLA Modules:
  0.0 98.0 jit_solution(4963282165203661053)
XLA Ops:
  0.0 1.0 pack.1.refs_0_
  1.0 4.1 %collective-permute-start = (bf16[16,4608]{1,0:T(8,128)(2,1)S(1)}, bf16[16,4608]{1,0:T(8,128)(2,1)S(1)}, u32[]{:S(2)}, u32[]{:S(2)}) collective-permute-start(bf16[16,4608]{1,0:T(8,128)(2,1)S(1)} %pack.1.refs_0_), channel_id=1, source_target_pairs={{0,16},{2,18},{4,20},{6,22},{8,24},{10,26},{12,28},{14,30},{16,0},... | collective-permute-start | bytes 442376 | tf_op jit(solution)/shard_map/ppermute | solution.py:35
  5.1 1.6 %collective-permute-start.1 = (bf16[16,4608]{1,0:T(8,128)(2,1)S(1)}, bf16[16,4608]{1,0:T(8,128)(2,1)S(1)}, u32[]{:S(2)}, u32[]{:S(2)}) collective-permute-start(bf16[16,4608]{1,0:T(8,128)(2,1)S(1)} %pack.1.refs_0_), channel_id=1, source_target_pairs={{0,8},{2,10},{4,12},{6,14},{8,0},{10,2},{12,4},{14,6},{16,24},{18,... | collective-permute-start | bytes 442376 | tf_op jit(solution)/shard_map/ppermute | solution.py:35
  6.7 5.5 %collective-permute-done.refs_1_ = bf16[16,4608]{1,0:T(8,128)(2,1)S(1)} collective-permute-done((bf16[16,4608]{1,0:T(8,128)(2,1)S(1)}, bf16[16,4608]{1,0:T(8,128)(2,1)S(1)}, u32[]{:S(2)}, u32[]{:S(2)}) %collective-permute-start) | collective-permute-done | bytes 147488 | tf_op jit(solution)/shard_map/ppermute | solution.py:35
  12.2 0.6 collective-permute-start.2
  12.8 1.5 %collective-permute-start.3 = (bf16[16,4608]{1,0:T(8,128)(2,1)S(1)}, bf16[16,4608]{1,0:T(8,128)(2,1)S(1)}, u32[]{:S(2)}, u32[]{:S(2)}) collective-permute-start(bf16[16,4608]{1,0:T(8,128)(2,1)S(1)} %pack.1.refs_0_), channel_id=1, source_target_pairs={{0,4},{2,6},{4,0},{6,2},{8,12},{10,14},{12,8},{14,10},{16,20},{18,... | collective-permute-start | bytes 442376 | tf_op jit(solution)/shard_map/ppermute | solution.py:35
  14.4 0.5 collective-permute-start.4
  14.9 1.5 %collective-permute-start.5 = (bf16[16,4608]{1,0:T(8,128)(2,1)S(1)}, bf16[16,4608]{1,0:T(8,128)(2,1)S(1)}, u32[]{:S(2)}, u32[]{:S(2)}) collective-permute-start(bf16[16,4608]{1,0:T(8,128)(2,1)S(1)} %collective-permute-done.1.refs_2_), channel_id=1, source_target_pairs={{0,4},{2,6},{4,0},{6,2},{8,12},{10,14},{12,8},{14,10},{16,20},{18,... | collective-permute-start | bytes 442376 | tf_op jit(solution)/shard_map/ppermute | solution.py:35
  16.4 1.0 collective-permute-done.2.refs_3_
  17.4 1.6 %collective-permute-start.6 = (bf16[16,4608]{1,0:T(8,128)(2,1)S(1)}, bf16[16,4608]{1,0:T(8,128)(2,1)S(1)}, u32[]{:S(2)}, u32[]{:S(2)}) collective-permute-start(bf16[16,4608]{1,0:T(8,128)(2,1)S(1)} %collective-permute-done.2.refs_3_), channel_id=1, source_target_pairs={{0,4},{2,6},{4,0},{6,2},{8,12},{10,14},{12,8},{14,10},{16,20},{18,... | collective-permute-start | bytes 442376 | tf_op jit(solution)/shard_map/ppermute | solution.py:35
  18.9 0.8 copy.10.pair_ref
  19.9 2.8 %collective-permute-done.4.refs_5_ = bf16[16,4608]{1,0:T(8,128)(2,1)S(1)} collective-permute-done((bf16[16,4608]{1,0:T(8,128)(2,1)S(1)}, bf16[16,4608]{1,0:T(8,128)(2,1)S(1)}, u32[]{:S(2)}, u32[]{:S(2)}) %collective-permute-start.4) | collective-permute-done | bytes 147488 | tf_op jit(solution)/shard_map/ppermute | solution.py:35
  22.7 3.2 %collective-permute-done.5.refs_6_ = bf16[16,4608]{1,0:T(8,128)(2,1)S(1)} collective-permute-done((bf16[16,4608]{1,0:T(8,128)(2,1)S(1)}, bf16[16,4608]{1,0:T(8,128)(2,1)S(1)}, u32[]{:S(2)}, u32[]{:S(2)}) %collective-permute-start.5) | collective-permute-done | bytes 147488 | tf_op jit(solution)/shard_map/ppermute | solution.py:35
  25.9 1.9 %collective-permute-done.6.refs_7_ = bf16[16,4608]{1,0:T(8,128)(2,1)S(1)} collective-permute-done((bf16[16,4608]{1,0:T(8,128)(2,1)S(1)}, bf16[16,4608]{1,0:T(8,128)(2,1)S(1)}, u32[]{:S(2)}, u32[]{:S(2)}) %collective-permute-start.6) | collective-permute-done | bytes 147488 | tf_op jit(solution)/shard_map/ppermute | solution.py:35
  27.8 0.8 assemble.1.refs_0_.refs_1_.half_ref
  28.6 4.8 %fetch.5 = (bf16[4096,1024]{1,0:T(8,128)(2,1)S(1)}, bf16[512,4096]{1,0:T(8,128)(2,1)S(1)}) custom-call(bf16[4096,1792]{1,0:T(8,128)(2,1)} %refs_0_.5, bf16[4096,1792]{1,0:T(8,128)(2,1)} %refs_1_.5, bf16[1792,4096]{1,0:T(8,128)(2,1)} %refs_2_.5), custom_call_target="tpu_custom_call" | custom-call | flops 4000000000 | bytes 12582912 | tf_op jit(solution)/shard_map/fetch/pallas_call | solution.py:231
  33.4 3.9 %fetch.4 = (bf16[4096,768]{1,0:T(8,128)(2,1)S(1)}, bf16[384,4096]{1,0:T(8,128)(2,1)S(1)}) custom-call(bf16[4096,1792]{1,0:T(8,128)(2,1)} %refs_0_.5, bf16[4096,1792]{1,0:T(8,128)(2,1)} %refs_1_.5, bf16[1792,4096]{1,0:T(8,128)(2,1)} %refs_2_.5), custom_call_target="tpu_custom_call" | custom-call | flops 4000000000 | bytes 9437184 | tf_op jit(solution)/shard_map/fetch/pallas_call | solution.py:231
  37.3 3.9 %fetch.3 = (bf16[4096,768]{1,0:T(8,128)(2,1)S(1)}, bf16[384,4096]{1,0:T(8,128)(2,1)S(1)}) custom-call(bf16[4096,1792]{1,0:T(8,128)(2,1)} %refs_0_.5, bf16[4096,1792]{1,0:T(8,128)(2,1)} %refs_1_.5, bf16[1792,4096]{1,0:T(8,128)(2,1)} %refs_2_.5), custom_call_target="tpu_custom_call" | custom-call | flops 4000000000 | bytes 9437184 | tf_op jit(solution)/shard_map/fetch/pallas_call | solution.py:231
  41.2 1.4 %forward_half.3 = bf16[104,1024]{1,0:T(8,128)(2,1)S(1)} custom-call(bf16[144,4096]{1,0:T(8,128)(2,1)S(1)} %assemble.1.refs_0_.refs_1_.half_ref, bf16[4096,1024]{1,0:T(8,128)(2,1)S(1)} %get-tuple-element.30.both.refs_2_), custom_call_target="tpu_custom_call" | custom-call | flops 872415232 | bytes 1000000 | tf_op jit(solution)/shard_map/forward_half/pallas_call | solution.py:314
  42.6 1.6 %collective-permute-start.10 = (bf16[104,1024]{1,0:T(8,128)(2,1)S(1)}, bf16[104,1024]{1,0:T(8,128)(2,1)S(1)}, u32[]{:S(2)}, u32[]{:S(2)}) collective-permute-start(bf16[104,1024]{1,0:T(8,128)(2,1)S(1)} %forward_half.3), channel_id=1, source_target_pairs={{0,1},{1,0},{2,3},{3,2},{4,5},{5,4},{6,7},{7,6},{8,9},{9,8},{10,11... | collective-permute-start | bytes 638984 | tf_op jit(solution)/shard_map/ppermute | solution.py:39
  44.2 2.7 %forward_half.2 = (bf16[144,1024]{1,0:T(8,128)(2,1)S(1)}, bf16[4096,1024]{1,0:T(8,128)(2,1)S(1)}) custom-call(bf16[144,4096]{1,0:T(8,128)(2,1)S(1)} %collective-permute-done.7.refs_1_.half_ref.refs_2_, bf16[4096,1024]{1,0:T(8,128)(2,1)S(1)} %get-tuple-element.30.both.refs_2_, bf16[512,4096]{1,0:T(8,128)(2,1)S(1)} %get-tuple-element.31.refs_0_, ...), custom_call_target="tpu_custom_call" | custom-call | flops 1207959552 | bytes 1000000 | tf_op jit(solution)/shard_map/forward_half/pallas_call | solution.py:314
  47.0 0.5 collective-permute-start.11
  47.7 2.5 %forward.4 = (bf16[248,768]{1,0:T(8,128)(2,1)S(1)}, bf16[4096,1024]{1,0:T(8,128)(2,1)S(1)}) custom-call(bf16[208,4096]{1,0:T(8,128)(2,1)S(1)} %get-tuple-element.23.main_ref, bf16[80,4096]{1,0:T(8,128)(2,1)S(1)} %get-tuple-element.24.side_ref, bf16[4096,768]{1,0:T(8,128)(2,1)S(1)} %get-tuple-element.28.both.refs_1_, ...), custom_call_target="tpu_custom_call", output_to_operand_aliasing={{1}: (7, {})} | custom-call | flops 1560281088 | bytes 9437184 | tf_op jit(solution)/shard_map/forward/pallas_call | solution.py:384
  50.2 1.6 %collective-permute-start.8 = (bf16[248,768]{1,0:T(8,128)(2,1)S(1)}, bf16[248,768]{1,0:T(8,128)(2,1)S(1)}, u32[]{:S(2)}, u32[]{:S(2)}) collective-permute-start(bf16[248,768]{1,0:T(8,128)(2,1)S(1)} %get-tuple-element.33), channel_id=1, source_target_pairs={{0,1},{1,0},{2,3},{3,2},{4,5},{5,4},{6,7},{7,6},{8,9},{9,8},{10,11... | collective-permute-start | bytes 1142792 | tf_op jit(solution)/shard_map/ppermute | solution.py:39
  51.8 2.6 %forward.3 = (f32[248,768]{1,0:T(8,128)S(1)}, bf16[512,4096]{1,0:T(8,128)(2,1)S(1)}) custom-call(bf16[208,4096]{1,0:T(8,128)(2,1)S(1)} %get-tuple-element.23.main_ref, bf16[80,4096]{1,0:T(8,128)(2,1)S(1)} %get-tuple-element.24.side_ref, bf16[4096,768]{1,0:T(8,128)(2,1)S(1)} %get-tuple-element.25.both.refs_3_, bf16[384,4096]{1,0:T(8,128)(2,1)S(1)} %get-tuple-element.26.below, ...), custom_call_target="tpu_custom_call" | custom-call | flops 1560281088 | bytes 9437184 | tf_op jit(solution)/shard_map/forward/pallas_call | solution.py:384
  54.5 3.1 %forward.5.kept_ref = f32[248,1024]{1,0:T(8,128)S(1)} custom-call(bf16[208,4096]{1,0:T(8,128)(2,1)S(1)} %get-tuple-element.23.main_ref, bf16[80,4096]{1,0:T(8,128)(2,1)S(1)} %get-tuple-element.24.side_ref, bf16[4096,1024]{1,0:T(8,128)(2,1)S(1)} %get-tuple-element.34.both.refs_1_, bf16[512,4096]{1,0:T(8,128)(2,1)S(1)} %get-tuple-element.35.below), custom_call_target="tpu_custom_call" | custom-call | flops 2080374784 | bytes 12582912 | tf_op jit(solution)/shard_map/forward/pallas_call | solution.py:384
  57.7 3.1 %coefficients.3.refs_0_ = bf16[80,1024]{1,0:T(8,128)(2,1)S(1)} custom-call(s32[8]{0:T(128)S(1)} %copy-done, bf16[320,256]{1,0:T(8,128)(2,1)S(1)} %choices.1.picks_ref, f32[248,1024]{1,0:T(8,128)S(1)} %forward.5.kept_ref, bf16[104,1024]{1,0:T(8,128)(2,1)S(1)} %collective-permute-done.10.refs_0_, bf16[144,1024]{1,0:T(8,128)(2,1)S(1)} %collective-permute-done.11.refs_1_), custom_call_target="tpu_custom_call" | custom-call | flops 5000000000 | bytes 1000000 | tf_op jit(solution)/shard_map/coefficients/pallas_call | solution.py:495
  60.8 1.1 %collective-permute-start.12 = (bf16[80,1024]{1,0:T(8,128)(2,1)S(1)}, bf16[80,1024]{1,0:T(8,128)(2,1)S(1)}, u32[]{:S(2)}, u32[]{:S(2)}) collective-permute-start(bf16[80,1024]{1,0:T(8,128)(2,1)S(1)} %coefficients.3.refs_0_), channel_id=1, source_target_pairs={{0,1},{1,0},{2,3},{3,2},{4,5},{5,4},{6,7},{7,6},{8,9},{9,8},{10,11... | collective-permute-start | bytes 491528 | tf_op jit(solution)/shard_map/ppermute | solution.py:39
  61.8 3.4 %collective-permute-done.8.refs_0_ = bf16[248,768]{1,0:T(8,128)(2,1)S(1)} collective-permute-done((bf16[248,768]{1,0:T(8,128)(2,1)S(1)}, bf16[248,768]{1,0:T(8,128)(2,1)S(1)}, u32[]{:S(2)}, u32[]{:S(2)}) %collective-permute-start.8) | collective-permute-done | bytes 380960 | tf_op jit(solution)/shard_map/ppermute | solution.py:39
  65.3 2.5 %coefficients.2.refs_1_ = bf16[80,768]{1,0:T(8,128)(2,1)S(1)} custom-call(s32[8]{0:T(128)S(1)} %copy-done, bf16[320,256]{1,0:T(8,128)(2,1)S(1)} %choices.1.picks_ref, f32[248,768]{1,0:T(8,128)S(1)} %get-tuple-element.27.kept_ref, bf16[248,768]{1,0:T(8,128)(2,1)S(1)} %collective-permute-done.8.refs_0_), custom_call_target="tpu_custom_call" | custom-call | flops 5000000000 | bytes 1000000 | tf_op jit(solution)/shard_map/coefficients/pallas_call | solution.py:495
  67.8 1.7 %collective-permute-start.9 = (bf16[80,768]{1,0:T(8,128)(2,1)S(1)}, bf16[80,768]{1,0:T(8,128)(2,1)S(1)}, u32[]{:S(2)}, u32[]{:S(2)}) collective-permute-start(bf16[80,768]{1,0:T(8,128)(2,1)S(1)} %coefficients.2.refs_1_), channel_id=1, source_target_pairs={{0,1},{1,0},{2,3},{3,2},{4,5},{5,4},{6,7},{7,6},{8,9},{9,8},{10,11... | collective-permute-start | bytes 368648 | tf_op jit(solution)/shard_map/ppermute | solution.py:39
  69.4 2.6 %backward.4.refs_4_ = f32[80,4096]{1,0:T(8,128)S(1)} custom-call(bf16[80,1024]{1,0:T(8,128)(2,1)S(1)} %coefficients.3.refs_0_, bf16[4096,1024]{1,0:T(8,128)(2,1)S(1)} %get-tuple-element.34.both.refs_1_), custom_call_target="tpu_custom_call" | custom-call | flops 671088640 | bytes 8388608 | tf_op jit(solution)/shard_map/backward/pallas_call | solution.py:554
  72.1 4.5 %backward.5.refs_2_ = f32[80,4096]{1,0:T(8,128)S(1)} custom-call(bf16[80,1024]{1,0:T(8,128)(2,1)S(1)} %collective-permute-done.12.refs_0_, bf16[80,768]{1,0:T(8,128)(2,1)S(1)} %coefficients.2.refs_1_, bf16[4096,1024]{1,0:T(8,128)(2,1)S(1)} %get-tuple-element.30.both.refs_2_, bf16[4096,768]{1,0:T(8,128)(2,1)S(1)} %get-tuple-element.25.both.refs_3_, ...), custom_call_target="tpu_custom_call" | custom-call | flops 1174405120 | bytes 8388608 | tf_op jit(solution)/shard_map/backward/pallas_call | solution.py:554
  76.6 1.1 %backward.6 = (bf16[40,2048]{1,0:T(8,128)(2,1)S(1)}, f32[40,2048]{1,0:T(8,128)S(1)}) custom-call(bf16[80,768]{1,0:T(8,128)(2,1)S(1)} %collective-permute-done.9.refs_0_, bf16[4096,768]{1,0:T(8,128)(2,1)S(1)} %get-tuple-element.28.both.refs_1_, f32[80,4096]{1,0:T(8,128)S(1)} %backward.5.refs_2_), custom_call_target="tpu_custom_call" | custom-call | flops 251658240 | bytes 3145728 | tf_op jit(solution)/shard_map/backward/pallas_call | solution.py:554
  77.8 1.1 %backward.7 = (bf16[40,2048]{1,0:T(8,128)(2,1)S(1)}, f32[40,2048]{1,0:T(8,128)S(1)}) custom-call(bf16[80,768]{1,0:T(8,128)(2,1)S(1)} %collective-permute-done.9.refs_0_, bf16[4096,768]{1,0:T(8,128)(2,1)S(1)} %get-tuple-element.28.both.refs_1_, f32[80,4096]{1,0:T(8,128)S(1)} %backward.5.refs_2_), custom_call_target="tpu_custom_call" | custom-call | flops 251658240 | bytes 3145728 | tf_op jit(solution)/shard_map/backward/pallas_call | solution.py:554
  78.8 0.6 collective-permute-start.17
  79.5 1.6 %collective-permute-start.14 = (bf16[20,2048]{1,0:T(8,128)(2,1)S(1)}, bf16[20,2048]{1,0:T(8,128)(2,1)S(1)}, u32[]{:S(2)}, u32[]{:S(2)}) collective-permute-start(bf16[20,2048]{1,0:T(8,128)(2,1)S(1)} %slice.91), channel_id=1, source_target_pairs={{0,4},{2,6},{4,0},{6,2},{8,12},{10,14},{12,8},{14,10},{16,20},{18,... | collective-permute-start | bytes 245768 | tf_op jit(solution)/shard_map/ppermute | solution.py:35
  81.2 0.4 collective-permute-start.18
  81.6 2.7 %collective-permute-done.14 = bf16[20,2048]{1,0:T(8,128)(2,1)S(1)} collective-permute-done((bf16[20,2048]{1,0:T(8,128)(2,1)S(1)}, bf16[20,2048]{1,0:T(8,128)(2,1)S(1)}, u32[]{:S(2)}, u32[]{:S(2)}) %collective-permute-start.14) | collective-permute-done | bytes 81952 | tf_op jit(solution)/shard_map/ppermute | solution.py:35
  84.3 0.4 collective-permute-start.15
  84.7 1.2 %collective-permute-done.18 = bf16[20,2048]{1,0:T(8,128)(2,1)S(1)} collective-permute-done((bf16[20,2048]{1,0:T(8,128)(2,1)S(1)}, bf16[20,2048]{1,0:T(8,128)(2,1)S(1)}, u32[]{:S(2)}, u32[]{:S(2)}) %collective-permute-start.18) | collective-permute-done | bytes 81952 | tf_op jit(solution)/shard_map/ppermute | solution.py:35
  85.9 1.4 %collective-permute-start.19 = (bf16[10,2048]{1,0:T(8,128)(2,1)S(1)}, bf16[10,2048]{1,0:T(8,128)(2,1)S(1)}, u32[]{:S(2)}, u32[]{:S(2)}) collective-permute-start(bf16[10,2048]{1,0:T(8,128)(2,1)S(1)} %slice.92), channel_id=1, source_target_pairs={{0,4},{2,6},{4,0},{6,2},{8,12},{10,14},{12,8},{14,10},{16,20},{18,... | collective-permute-start | bytes 122888 | tf_op jit(solution)/shard_map/ppermute | solution.py:35
  87.3 1.3 %collective-permute-done.15 = bf16[10,2048]{1,0:T(8,128)(2,1)S(1)} collective-permute-done((bf16[10,2048]{1,0:T(8,128)(2,1)S(1)}, bf16[10,2048]{1,0:T(8,128)(2,1)S(1)}, u32[]{:S(2)}, u32[]{:S(2)}) %collective-permute-start.15) | collective-permute-done | bytes 40992 | tf_op jit(solution)/shard_map/ppermute | solution.py:35
  88.7 3.8 %collective-permute-start.16 = (bf16[5,2048]{1,0:T(8,128)(2,1)S(1)}, bf16[5,2048]{1,0:T(8,128)(2,1)S(1)}, u32[]{:S(2)}, u32[]{:S(2)}) collective-permute-start(bf16[5,2048]{1,0:T(8,128)(2,1)S(1)} %slice.95), channel_id=1, source_target_pairs={{0,16},{2,18},{4,20},{6,22},{8,24},{10,26},{12,28},{14,30},{16,0},... | collective-permute-start | bytes 61448 | tf_op jit(solution)/shard_map/ppermute | solution.py:35
  92.5 1.3 %collective-permute-start.20 = (bf16[5,2048]{1,0:T(8,128)(2,1)S(1)}, bf16[5,2048]{1,0:T(8,128)(2,1)S(1)}, u32[]{:S(2)}, u32[]{:S(2)}) collective-permute-start(bf16[5,2048]{1,0:T(8,128)(2,1)S(1)} %slice.94), channel_id=1, source_target_pairs={{0,16},{2,18},{4,20},{6,22},{8,24},{10,26},{12,28},{14,30},{16,0},... | collective-permute-start | bytes 61448 | tf_op jit(solution)/shard_map/ppermute | solution.py:35
  93.7 0.9 collective-permute-done.16
  94.6 2.8 %collective-permute-done.20 = bf16[5,2048]{1,0:T(8,128)(2,1)S(1)} collective-permute-done((bf16[5,2048]{1,0:T(8,128)(2,1)S(1)}, bf16[5,2048]{1,0:T(8,128)(2,1)S(1)}, u32[]{:S(2)}, u32[]{:S(2)}) %collective-permute-start.20) | collective-permute-done | bytes 20512 | tf_op jit(solution)/shard_map/ppermute | solution.py:35
  97.4 0.6 pad_maximum_fusion.1
  (32 shorter events, 0.8 us)
Async XLA Ops:
  1.0 11.2 %collective-permute-start = (bf16[16,4608]{1,0:T(8,128)(2,1)S(1)}, bf16[16,4608]{1,0:T(8,128)(2,1)S(1)}, u32[]{:S(2)}, u32[]{:S(2)}) collective-permute-start(bf16[16,4608]{1,0:T(8,128)(2,1)S(1)} %pack.1.refs_0_), channel_id=1, source_target_pairs={{0,16},{2,18},{4,20},{6,22},{8,24},{10,26},{12,28},{14,30},{16,0},... | collective-permute-start | bytes 442376 | tf_op jit(solution)/shard_map/ppermute | solution.py:35
  5.1 9.8 %collective-permute-start.1 = (bf16[16,4608]{1,0:T(8,128)(2,1)S(1)}, bf16[16,4608]{1,0:T(8,128)(2,1)S(1)}, u32[]{:S(2)}, u32[]{:S(2)}) collective-permute-start(bf16[16,4608]{1,0:T(8,128)(2,1)S(1)} %pack.1.refs_0_), channel_id=1, source_target_pairs={{0,8},{2,10},{4,12},{6,14},{8,0},{10,2},{12,4},{14,6},{16,24},{18,... | collective-permute-start | bytes 442376 | tf_op jit(solution)/shard_map/ppermute | solution.py:35
  12.2 5.1 %collective-permute-start.2 = (bf16[16,4608]{1,0:T(8,128)(2,1)S(1)}, bf16[16,4608]{1,0:T(8,128)(2,1)S(1)}, u32[]{:S(2)}, u32[]{:S(2)}) collective-permute-start(bf16[16,4608]{1,0:T(8,128)(2,1)S(1)} %collective-permute-done.refs_1_), channel_id=1, source_target_pairs={{0,8},{2,10},{4,12},{6,14},{8,0},{10,2},{12,4},{14,6},{16,24},{18,... | collective-permute-start | bytes 442376 | tf_op jit(solution)/shard_map/ppermute | solution.py:35
  12.8 7.0 %collective-permute-start.3 = (bf16[16,4608]{1,0:T(8,128)(2,1)S(1)}, bf16[16,4608]{1,0:T(8,128)(2,1)S(1)}, u32[]{:S(2)}, u32[]{:S(2)}) collective-permute-start(bf16[16,4608]{1,0:T(8,128)(2,1)S(1)} %pack.1.refs_0_), channel_id=1, source_target_pairs={{0,4},{2,6},{4,0},{6,2},{8,12},{10,14},{12,8},{14,10},{16,20},{18,... | collective-permute-start | bytes 442376 | tf_op jit(solution)/shard_map/ppermute | solution.py:35
  14.4 8.4 %collective-permute-start.4 = (bf16[16,4608]{1,0:T(8,128)(2,1)S(1)}, bf16[16,4608]{1,0:T(8,128)(2,1)S(1)}, u32[]{:S(2)}, u32[]{:S(2)}) collective-permute-start(bf16[16,4608]{1,0:T(8,128)(2,1)S(1)} %collective-permute-done.refs_1_), channel_id=1, source_target_pairs={{0,4},{2,6},{4,0},{6,2},{8,12},{10,14},{12,8},{14,10},{16,20},{18,... | collective-permute-start | bytes 442376 | tf_op jit(solution)/shard_map/ppermute | solution.py:35
  14.9 11.0 %collective-permute-start.5 = (bf16[16,4608]{1,0:T(8,128)(2,1)S(1)}, bf16[16,4608]{1,0:T(8,128)(2,1)S(1)}, u32[]{:S(2)}, u32[]{:S(2)}) collective-permute-start(bf16[16,4608]{1,0:T(8,128)(2,1)S(1)} %collective-permute-done.1.refs_2_), channel_id=1, source_target_pairs={{0,4},{2,6},{4,0},{6,2},{8,12},{10,14},{12,8},{14,10},{16,20},{18,... | collective-permute-start | bytes 442376 | tf_op jit(solution)/shard_map/ppermute | solution.py:35
  17.4 10.4 %collective-permute-start.6 = (bf16[16,4608]{1,0:T(8,128)(2,1)S(1)}, bf16[16,4608]{1,0:T(8,128)(2,1)S(1)}, u32[]{:S(2)}, u32[]{:S(2)}) collective-permute-start(bf16[16,4608]{1,0:T(8,128)(2,1)S(1)} %collective-permute-done.2.refs_3_), channel_id=1, source_target_pairs={{0,4},{2,6},{4,0},{6,2},{8,12},{10,14},{12,8},{14,10},{16,20},{18,... | collective-permute-start | bytes 442376 | tf_op jit(solution)/shard_map/ppermute | solution.py:35
  28.6 15.7 %collective-permute-start.7 = (bf16[144,4096]{1,0:T(8,128)(2,1)S(1)}, bf16[144,4096]{1,0:T(8,128)(2,1)S(1)}, u32[]{:S(2)}, u32[]{:S(2)}) collective-permute-start(bf16[144,4096]{1,0:T(8,128)(2,1)S(1)} %assemble.1.refs_0_.refs_1_.half_ref), channel_id=1, source_target_pairs={{0,2},{2,0},{4,6},{6,4},{8,10},{10,8},{12,14},{14,12},{16,18},{18,... | collective-permute-start | bytes 3538952 | tf_op jit(solution)/shard_map/ppermute | solution.py:35
  42.6 15.0 %collective-permute-start.10 = (bf16[104,1024]{1,0:T(8,128)(2,1)S(1)}, bf16[104,1024]{1,0:T(8,128)(2,1)S(1)}, u32[]{:S(2)}, u32[]{:S(2)}) collective-permute-start(bf16[104,1024]{1,0:T(8,128)(2,1)S(1)} %forward_half.3), channel_id=1, source_target_pairs={{0,1},{1,0},{2,3},{3,2},{4,5},{5,4},{6,7},{7,6},{8,9},{9,8},{10,11... | collective-permute-start | bytes 638984 | tf_op jit(solution)/shard_map/ppermute | solution.py:39
  47.0 10.7 %collective-permute-start.11 = (bf16[144,1024]{1,0:T(8,128)(2,1)S(1)}, bf16[144,1024]{1,0:T(8,128)(2,1)S(1)}, u32[]{:S(2)}, u32[]{:S(2)}) collective-permute-start(bf16[144,1024]{1,0:T(8,128)(2,1)S(1)} %get-tuple-element.36), channel_id=1, source_target_pairs={{0,1},{1,0},{2,3},{3,2},{4,5},{5,4},{6,7},{7,6},{8,9},{9,8},{10,11... | collective-permute-start | bytes 884744 | tf_op jit(solution)/shard_map/ppermute | solution.py:39
  50.2 15.1 %collective-permute-start.8 = (bf16[248,768]{1,0:T(8,128)(2,1)S(1)}, bf16[248,768]{1,0:T(8,128)(2,1)S(1)}, u32[]{:S(2)}, u32[]{:S(2)}) collective-permute-start(bf16[248,768]{1,0:T(8,128)(2,1)S(1)} %get-tuple-element.33), channel_id=1, source_target_pairs={{0,1},{1,0},{2,3},{3,2},{4,5},{5,4},{6,7},{7,6},{8,9},{9,8},{10,11... | collective-permute-start | bytes 1142792 | tf_op jit(solution)/shard_map/ppermute | solution.py:39
  54.5 3.2 %copy-start = (s32[8]{0:T(128)S(1)}, s32[8]{0:T(128)}, u32[]{:S(2)}) copy-start(s32[8]{0:T(128)} %points_ref.3) | copy-start | bytes 100
  60.8 11.3 %collective-permute-start.12 = (bf16[80,1024]{1,0:T(8,128)(2,1)S(1)}, bf16[80,1024]{1,0:T(8,128)(2,1)S(1)}, u32[]{:S(2)}, u32[]{:S(2)}) collective-permute-start(bf16[80,1024]{1,0:T(8,128)(2,1)S(1)} %coefficients.3.refs_0_), channel_id=1, source_target_pairs={{0,1},{1,0},{2,3},{3,2},{4,5},{5,4},{6,7},{7,6},{8,9},{9,8},{10,11... | collective-permute-start | bytes 491528 | tf_op jit(solution)/shard_map/ppermute | solution.py:39
  67.8 8.8 %collective-permute-start.9 = (bf16[80,768]{1,0:T(8,128)(2,1)S(1)}, bf16[80,768]{1,0:T(8,128)(2,1)S(1)}, u32[]{:S(2)}, u32[]{:S(2)}) collective-permute-start(bf16[80,768]{1,0:T(8,128)(2,1)S(1)} %coefficients.2.refs_1_), channel_id=1, source_target_pairs={{0,1},{1,0},{2,3},{3,2},{4,5},{5,4},{6,7},{7,6},{8,9},{9,8},{10,11... | collective-permute-start | bytes 368648 | tf_op jit(solution)/shard_map/ppermute | solution.py:39
  77.7 1.7 %collective-permute-start.13 = (bf16[40,2048]{1,0:T(8,128)(2,1)S(1)}, bf16[40,2048]{1,0:T(8,128)(2,1)S(1)}, u32[]{:S(2)}, u32[]{:S(2)}) collective-permute-start(bf16[40,2048]{1,0:T(8,128)(2,1)S(1)} %get-tuple-element.38), channel_id=1, source_target_pairs={{0,2},{2,0},{4,6},{6,4},{8,10},{10,8},{12,14},{14,12},{16,18},{18,... | collective-permute-start | bytes 491528 | tf_op jit(solution)/shard_map/ppermute | solution.py:35
  78.8 2.2 %collective-permute-start.17 = (bf16[40,2048]{1,0:T(8,128)(2,1)S(1)}, bf16[40,2048]{1,0:T(8,128)(2,1)S(1)}, u32[]{:S(2)}, u32[]{:S(2)}) collective-permute-start(bf16[40,2048]{1,0:T(8,128)(2,1)S(1)} %get-tuple-element.40), channel_id=1, source_target_pairs={{0,2},{2,0},{4,6},{6,4},{8,10},{10,8},{12,14},{14,12},{16,18},{18,... | collective-permute-start | bytes 491528 | tf_op jit(solution)/shard_map/ppermute | solution.py:35
  79.5 4.8 %collective-permute-start.14 = (bf16[20,2048]{1,0:T(8,128)(2,1)S(1)}, bf16[20,2048]{1,0:T(8,128)(2,1)S(1)}, u32[]{:S(2)}, u32[]{:S(2)}) collective-permute-start(bf16[20,2048]{1,0:T(8,128)(2,1)S(1)} %slice.91), channel_id=1, source_target_pairs={{0,4},{2,6},{4,0},{6,2},{8,12},{10,14},{12,8},{14,10},{16,20},{18,... | collective-permute-start | bytes 245768 | tf_op jit(solution)/shard_map/ppermute | solution.py:35
  81.2 4.7 %collective-permute-start.18 = (bf16[20,2048]{1,0:T(8,128)(2,1)S(1)}, bf16[20,2048]{1,0:T(8,128)(2,1)S(1)}, u32[]{:S(2)}, u32[]{:S(2)}) collective-permute-start(bf16[20,2048]{1,0:T(8,128)(2,1)S(1)} %pad_maximum_fusion), channel_id=1, source_target_pairs={{0,8},{2,10},{4,12},{6,14},{8,0},{10,2},{12,4},{14,6},{16,24},{18,... | collective-permute-start | bytes 245768 | tf_op jit(solution)/shard_map/ppermute | solution.py:35
  84.3 4.3 %collective-permute-start.15 = (bf16[10,2048]{1,0:T(8,128)(2,1)S(1)}, bf16[10,2048]{1,0:T(8,128)(2,1)S(1)}, u32[]{:S(2)}, u32[]{:S(2)}) collective-permute-start(bf16[10,2048]{1,0:T(8,128)(2,1)S(1)} %slice.93), channel_id=1, source_target_pairs={{0,8},{2,10},{4,12},{6,14},{8,0},{10,2},{12,4},{14,6},{16,24},{18,... | collective-permute-start | bytes 122888 | tf_op jit(solution)/shard_map/ppermute | solution.py:35
  85.9 6.5 %collective-permute-start.19 = (bf16[10,2048]{1,0:T(8,128)(2,1)S(1)}, bf16[10,2048]{1,0:T(8,128)(2,1)S(1)}, u32[]{:S(2)}, u32[]{:S(2)}) collective-permute-start(bf16[10,2048]{1,0:T(8,128)(2,1)S(1)} %slice.92), channel_id=1, source_target_pairs={{0,4},{2,6},{4,0},{6,2},{8,12},{10,14},{12,8},{14,10},{16,20},{18,... | collective-permute-start | bytes 122888 | tf_op jit(solution)/shard_map/ppermute | solution.py:35
  88.7 5.9 %collective-permute-start.16 = (bf16[5,2048]{1,0:T(8,128)(2,1)S(1)}, bf16[5,2048]{1,0:T(8,128)(2,1)S(1)}, u32[]{:S(2)}, u32[]{:S(2)}) collective-permute-start(bf16[5,2048]{1,0:T(8,128)(2,1)S(1)} %slice.95), channel_id=1, source_target_pairs={{0,16},{2,18},{4,20},{6,22},{8,24},{10,26},{12,28},{14,30},{16,0},... | collective-permute-start | bytes 61448 | tf_op jit(solution)/shard_map/ppermute | solution.py:35
  92.5 4.9 %collective-permute-start.20 = (bf16[5,2048]{1,0:T(8,128)(2,1)S(1)}, bf16[5,2048]{1,0:T(8,128)(2,1)S(1)}, u32[]{:S(2)}, u32[]{:S(2)}) collective-permute-start(bf16[5,2048]{1,0:T(8,128)(2,1)S(1)} %slice.94), channel_id=1, source_target_pairs={{0,16},{2,18},{4,20},{6,22},{8,24},{10,26},{12,28},{14,30},{16,0},... | collective-permute-start | bytes 61448 | tf_op jit(solution)/shard_map/ppermute | solution.py:35

commit v7 on v6

--- a/solution.py
+++ b/solution.py
@@ -572,7 +572,8 @@
     blocks = far * near * pair
     examples, pairs = pair_ref.shape
 
-    def body(pair_ref, out, rows):
+    def body(pair_ref, out, rows, table):
+        table[pl.ds(0, examples), :] = pair_ref[...]
         at = lax.axis_index("wide")
         z, y, c = at // (near * pair), at // pair % near, at % pair
         col = lax.broadcasted_iota(jnp.int32, (examples, blocks * r), 1)
@@ -580,7 +581,7 @@
         for q in range(blocks):
             s, b, p = halvings(far)[q % far], q // far % near, q // (far * near)
             owner = ((z ^ s) * near + (y ^ b)) * pair + (c ^ p)
-            rows[pl.ds(q * e, e), :] = pair_ref[pl.ds(owner * e, e), :]
+            rows[pl.ds(q * e, e), :] = table[pl.ds(owner * e, e), :]
             name = jnp.where((col >= q * r) & (col < (q + 1) * r), owner * r + col - q * r, name)
         for p in range(pairs):
             pick = (rows[:, pl.ds(p, 1)] == name).astype(jnp.float32).astype(jnp.bfloat16)
@@ -592,7 +593,10 @@
         out_shape=jax.ShapeDtypeStruct((pairs * examples, 2 * blocks * r), jnp.bfloat16),
         in_specs=[VMEM],
         out_specs=VMEM,
-        scratch_shapes=[pltpu.VMEM((examples, pairs), jnp.int32)],
+        scratch_shapes=[
+            pltpu.VMEM((examples, pairs), jnp.int32),
+            pltpu.VMEM((rounded(examples, 8) + 8, pairs), jnp.int32),
+        ],
         compiler_params=pltpu.CompilerParams(vmem_limit_bytes=2 * 1024 * 1024),
         cost_estimate=pl.CostEstimate(flops=10**9, bytes_accessed=10**6, transcendentals=0),
         name="choices",
@@ -721,7 +725,8 @@
     total = None
     for group in groups[:-1]:
         total = backward(group, total, False)
-    spans = [(0, depth // 2), (depth // 2, depth // 2)] if depth % 256 == 0 else [(0, depth)]
+    cut = depth // 2 if depth % 1024 else depth // 8 * 5
+    spans = [(0, cut), (cut, depth - cut)] if depth % 256 == 0 else [(0, depth)]
     last = [backward(groups[-1], total, pair == 2, span) for span in spans]
 
     results = []
@@ -744,8 +749,8 @@
 
             got = permute(half(1).astype(jnp.bfloat16), "wide", dims, *step)
             value = half(0) + got.astype(jnp.float32)
-        results.append(value.astype(jnp.bfloat16))
-    return results[0] if len(results) == 1 else jnp.concatenate(results, axis=1)
+        results.append(value)
+    return jnp.concatenate(results, axis=1).astype(jnp.bfloat16)
 
 
 def solution(mesh):

time: 98.2 us -> 98.3 us (level)
  starting transfers between devices: 27.4 us -> 29.6 us
  waiting for transfers between devices: 26.7 us -> 24.6 us
    ppermute x16, starting transfers between devices: 20.9 us -> 23.1 us  [permute(): return lax.ppermute(array, axis, pairs)]
    ppermute x16, waiting for transfers between devices: 23.3 us -> 21.1 us  [permute(): return lax.ppermute(array, axis, pairs)]
where the time goes in v7:
time: 98.3 us; the launch traced here: 98.1 us
  Pallas kernels  41.9 us (43%)
  starting transfers between devices  29.6 us (30%)
  waiting for transfers between devices  24.6 us (25%)
    ppermute x16, starting transfers between devices, permute(): return lax.ppermute(array, axis, pairs)  23.1 us
    ppermute x16, waiting for transfers between devices, permute(): return lax.ppermute(array, axis, pairs)  21.1 us
    pallas_call x3, Pallas kernels, fetch(): pl.pallas_call(body, out_shape=(pltpu.VMEM((depth, 2 * width), jnp.bfloat...  12.5 us
    pallas_call x4, Pallas kernels, backward(): pl.pallas_call(body, out_shape=out_shape, in_specs=specs, out_specs=out_s...  9.31 us
    pallas_call x3, Pallas kernels, forward(): pl.pallas_call(body_ready if ready else body, out_shape=out_shape, in_spe...  8.31 us
    ppermute x5, starting transfers between devices, shift(): lax.ppermute(array, 'narrow', [(at, (at + amount) % size) for at in range...  6.51 us
    pallas_call x2, Pallas kernels, coefficients(): pl.pallas_call(body, out_shape=jax.ShapeDtypeStruct((examples, 2 * width)...  5.56 us
    pallas_call x2, Pallas kernels, forward_half(): pl.pallas_call(body, out_shape=[jax.ShapeDtypeStruct((all_rows, 2 * width...  4.15 us
  transfers between devices with their start and end apart: 21, of which 11 were waited for; matrix products, arithmetic and copies ran while one was open for 1% of the time, Pallas kernels for 40%

profile of v7, /device:TPU:0, one launch (start us, length us, event | category | flops | bytes accessed | tf_op | source)
XLA Modules:
  0.0 98.1 jit_solution(4917548109751032658)
XLA Ops:
  0.0 1.0 pack.1.refs_0_
  1.0 4.1 %collective-permute-start = (bf16[16,4608]{1,0:T(8,128)(2,1)S(1)}, bf16[16,4608]{1,0:T(8,128)(2,1)S(1)}, u32[]{:S(2)}, u32[]{:S(2)}) collective-permute-start(bf16[16,4608]{1,0:T(8,128)(2,1)S(1)} %pack.1.refs_0_), channel_id=1, source_target_pairs={{0,16},{2,18},{4,20},{6,22},{8,24},{10,26},{12,28},{14,30},{16,0},... | collective-permute-start | bytes 442376 | tf_op jit(solution)/shard_map/ppermute | solution.py:35
  5.1 1.6 %collective-permute-start.1 = (bf16[16,4608]{1,0:T(8,128)(2,1)S(1)}, bf16[16,4608]{1,0:T(8,128)(2,1)S(1)}, u32[]{:S(2)}, u32[]{:S(2)}) collective-permute-start(bf16[16,4608]{1,0:T(8,128)(2,1)S(1)} %pack.1.refs_0_), channel_id=1, source_target_pairs={{0,8},{2,10},{4,12},{6,14},{8,0},{10,2},{12,4},{14,6},{16,24},{18,... | collective-permute-start | bytes 442376 | tf_op jit(solution)/shard_map/ppermute | solution.py:35
  6.7 5.5 %collective-permute-done.refs_1_ = bf16[16,4608]{1,0:T(8,128)(2,1)S(1)} collective-permute-done((bf16[16,4608]{1,0:T(8,128)(2,1)S(1)}, bf16[16,4608]{1,0:T(8,128)(2,1)S(1)}, u32[]{:S(2)}, u32[]{:S(2)}) %collective-permute-start) | collective-permute-done | bytes 147488 | tf_op jit(solution)/shard_map/ppermute | solution.py:35
  12.2 0.6 collective-permute-start.2
  12.8 1.5 %collective-permute-start.3 = (bf16[16,4608]{1,0:T(8,128)(2,1)S(1)}, bf16[16,4608]{1,0:T(8,128)(2,1)S(1)}, u32[]{:S(2)}, u32[]{:S(2)}) collective-permute-start(bf16[16,4608]{1,0:T(8,128)(2,1)S(1)} %pack.1.refs_0_), channel_id=1, source_target_pairs={{0,4},{2,6},{4,0},{6,2},{8,12},{10,14},{12,8},{14,10},{16,20},{18,... | collective-permute-start | bytes 442376 | tf_op jit(solution)/shard_map/ppermute | solution.py:35
  14.4 0.5 collective-permute-start.4
  14.9 1.5 %collective-permute-start.5 = (bf16[16,4608]{1,0:T(8,128)(2,1)S(1)}, bf16[16,4608]{1,0:T(8,128)(2,1)S(1)}, u32[]{:S(2)}, u32[]{:S(2)}) collective-permute-start(bf16[16,4608]{1,0:T(8,128)(2,1)S(1)} %collective-permute-done.1.refs_2_), channel_id=1, source_target_pairs={{0,4},{2,6},{4,0},{6,2},{8,12},{10,14},{12,8},{14,10},{16,20},{18,... | collective-permute-start | bytes 442376 | tf_op jit(solution)/shard_map/ppermute | solution.py:35
  16.4 1.0 collective-permute-done.2.refs_3_
  17.4 1.6 %collective-permute-start.6 = (bf16[16,4608]{1,0:T(8,128)(2,1)S(1)}, bf16[16,4608]{1,0:T(8,128)(2,1)S(1)}, u32[]{:S(2)}, u32[]{:S(2)}) collective-permute-start(bf16[16,4608]{1,0:T(8,128)(2,1)S(1)} %collective-permute-done.2.refs_3_), channel_id=1, source_target_pairs={{0,4},{2,6},{4,0},{6,2},{8,12},{10,14},{12,8},{14,10},{16,20},{18,... | collective-permute-start | bytes 442376 | tf_op jit(solution)/shard_map/ppermute | solution.py:35
  18.9 0.8 copy.10.pair_ref
  19.9 2.8 %collective-permute-done.4.refs_5_ = bf16[16,4608]{1,0:T(8,128)(2,1)S(1)} collective-permute-done((bf16[16,4608]{1,0:T(8,128)(2,1)S(1)}, bf16[16,4608]{1,0:T(8,128)(2,1)S(1)}, u32[]{:S(2)}, u32[]{:S(2)}) %collective-permute-start.4) | collective-permute-done | bytes 147488 | tf_op jit(solution)/shard_map/ppermute | solution.py:35
  22.7 3.2 %collective-permute-done.5.refs_6_ = bf16[16,4608]{1,0:T(8,128)(2,1)S(1)} collective-permute-done((bf16[16,4608]{1,0:T(8,128)(2,1)S(1)}, bf16[16,4608]{1,0:T(8,128)(2,1)S(1)}, u32[]{:S(2)}, u32[]{:S(2)}) %collective-permute-start.5) | collective-permute-done | bytes 147488 | tf_op jit(solution)/shard_map/ppermute | solution.py:35
  25.9 1.9 %collective-permute-done.6.refs_7_ = bf16[16,4608]{1,0:T(8,128)(2,1)S(1)} collective-permute-done((bf16[16,4608]{1,0:T(8,128)(2,1)S(1)}, bf16[16,4608]{1,0:T(8,128)(2,1)S(1)}, u32[]{:S(2)}, u32[]{:S(2)}) %collective-permute-start.6) | collective-permute-done | bytes 147488 | tf_op jit(solution)/shard_map/ppermute | solution.py:35
  27.8 0.8 assemble.1.refs_0_.refs_1_.half_ref
  28.6 4.8 %fetch.5 = (bf16[4096,1024]{1,0:T(8,128)(2,1)S(1)}, bf16[512,4096]{1,0:T(8,128)(2,1)S(1)}) custom-call(bf16[4096,1792]{1,0:T(8,128)(2,1)} %refs_0_.5, bf16[4096,1792]{1,0:T(8,128)(2,1)} %refs_1_.5, bf16[1792,4096]{1,0:T(8,128)(2,1)} %refs_2_.5), custom_call_target="tpu_custom_call" | custom-call | flops 4000000000 | bytes 12582912 | tf_op jit(solution)/shard_map/fetch/pallas_call | solution.py:231
  33.4 3.9 %fetch.4 = (bf16[4096,768]{1,0:T(8,128)(2,1)S(1)}, bf16[384,4096]{1,0:T(8,128)(2,1)S(1)}) custom-call(bf16[4096,1792]{1,0:T(8,128)(2,1)} %refs_0_.5, bf16[4096,1792]{1,0:T(8,128)(2,1)} %refs_1_.5, bf16[1792,4096]{1,0:T(8,128)(2,1)} %refs_2_.5), custom_call_target="tpu_custom_call" | custom-call | flops 4000000000 | bytes 9437184 | tf_op jit(solution)/shard_map/fetch/pallas_call | solution.py:231
  37.3 3.9 %fetch.3 = (bf16[4096,768]{1,0:T(8,128)(2,1)S(1)}, bf16[384,4096]{1,0:T(8,128)(2,1)S(1)}) custom-call(bf16[4096,1792]{1,0:T(8,128)(2,1)} %refs_0_.5, bf16[4096,1792]{1,0:T(8,128)(2,1)} %refs_1_.5, bf16[1792,4096]{1,0:T(8,128)(2,1)} %refs_2_.5), custom_call_target="tpu_custom_call" | custom-call | flops 4000000000 | bytes 9437184 | tf_op jit(solution)/shard_map/fetch/pallas_call | solution.py:231
  41.2 1.4 %forward_half.3 = bf16[104,1024]{1,0:T(8,128)(2,1)S(1)} custom-call(bf16[144,4096]{1,0:T(8,128)(2,1)S(1)} %assemble.1.refs_0_.refs_1_.half_ref, bf16[4096,1024]{1,0:T(8,128)(2,1)S(1)} %get-tuple-element.30.both.refs_2_), custom_call_target="tpu_custom_call" | custom-call | flops 872415232 | bytes 1000000 | tf_op jit(solution)/shard_map/forward_half/pallas_call | solution.py:314
  42.6 1.6 %collective-permute-start.10 = (bf16[104,1024]{1,0:T(8,128)(2,1)S(1)}, bf16[104,1024]{1,0:T(8,128)(2,1)S(1)}, u32[]{:S(2)}, u32[]{:S(2)}) collective-permute-start(bf16[104,1024]{1,0:T(8,128)(2,1)S(1)} %forward_half.3), channel_id=1, source_target_pairs={{0,1},{1,0},{2,3},{3,2},{4,5},{5,4},{6,7},{7,6},{8,9},{9,8},{10,11... | collective-permute-start | bytes 638984 | tf_op jit(solution)/shard_map/ppermute | solution.py:39
  44.2 2.7 %forward_half.2 = (bf16[144,1024]{1,0:T(8,128)(2,1)S(1)}, bf16[4096,1024]{1,0:T(8,128)(2,1)S(1)}) custom-call(bf16[144,4096]{1,0:T(8,128)(2,1)S(1)} %collective-permute-done.7.refs_1_.half_ref.refs_2_, bf16[4096,1024]{1,0:T(8,128)(2,1)S(1)} %get-tuple-element.30.both.refs_2_, bf16[512,4096]{1,0:T(8,128)(2,1)S(1)} %get-tuple-element.31.refs_0_, ...), custom_call_target="tpu_custom_call" | custom-call | flops 1207959552 | bytes 1000000 | tf_op jit(solution)/shard_map/forward_half/pallas_call | solution.py:314
  47.0 0.5 collective-permute-start.11
  47.7 2.5 %forward.4 = (bf16[248,768]{1,0:T(8,128)(2,1)S(1)}, bf16[4096,1024]{1,0:T(8,128)(2,1)S(1)}) custom-call(bf16[208,4096]{1,0:T(8,128)(2,1)S(1)} %get-tuple-element.23.main_ref, bf16[80,4096]{1,0:T(8,128)(2,1)S(1)} %get-tuple-element.24.side_ref, bf16[4096,768]{1,0:T(8,128)(2,1)S(1)} %get-tuple-element.28.both.refs_1_, ...), custom_call_target="tpu_custom_call", output_to_operand_aliasing={{1}: (7, {})} | custom-call | flops 1560281088 | bytes 9437184 | tf_op jit(solution)/shard_map/forward/pallas_call | solution.py:384
  50.2 1.6 %collective-permute-start.8 = (bf16[248,768]{1,0:T(8,128)(2,1)S(1)}, bf16[248,768]{1,0:T(8,128)(2,1)S(1)}, u32[]{:S(2)}, u32[]{:S(2)}) collective-permute-start(bf16[248,768]{1,0:T(8,128)(2,1)S(1)} %get-tuple-element.33), channel_id=1, source_target_pairs={{0,1},{1,0},{2,3},{3,2},{4,5},{5,4},{6,7},{7,6},{8,9},{9,8},{10,11... | collective-permute-start | bytes 1142792 | tf_op jit(solution)/shard_map/ppermute | solution.py:39
  51.8 2.6 %forward.3 = (f32[248,768]{1,0:T(8,128)S(1)}, bf16[512,4096]{1,0:T(8,128)(2,1)S(1)}) custom-call(bf16[208,4096]{1,0:T(8,128)(2,1)S(1)} %get-tuple-element.23.main_ref, bf16[80,4096]{1,0:T(8,128)(2,1)S(1)} %get-tuple-element.24.side_ref, bf16[4096,768]{1,0:T(8,128)(2,1)S(1)} %get-tuple-element.25.both.refs_3_, bf16[384,4096]{1,0:T(8,128)(2,1)S(1)} %get-tuple-element.26.below, ...), custom_call_target="tpu_custom_call" | custom-call | flops 1560281088 | bytes 9437184 | tf_op jit(solution)/shard_map/forward/pallas_call | solution.py:384
  54.5 3.1 %forward.5.kept_ref = f32[248,1024]{1,0:T(8,128)S(1)} custom-call(bf16[208,4096]{1,0:T(8,128)(2,1)S(1)} %get-tuple-element.23.main_ref, bf16[80,4096]{1,0:T(8,128)(2,1)S(1)} %get-tuple-element.24.side_ref, bf16[4096,1024]{1,0:T(8,128)(2,1)S(1)} %get-tuple-element.34.both.refs_1_, bf16[512,4096]{1,0:T(8,128)(2,1)S(1)} %get-tuple-element.35.below), custom_call_target="tpu_custom_call" | custom-call | flops 2080374784 | bytes 12582912 | tf_op jit(solution)/shard_map/forward/pallas_call | solution.py:384
  57.7 3.1 %coefficients.3.refs_0_ = bf16[80,1024]{1,0:T(8,128)(2,1)S(1)} custom-call(s32[8]{0:T(128)S(1)} %copy-done, bf16[320,256]{1,0:T(8,128)(2,1)S(1)} %choices.1.picks_ref, f32[248,1024]{1,0:T(8,128)S(1)} %forward.5.kept_ref, bf16[104,1024]{1,0:T(8,128)(2,1)S(1)} %collective-permute-done.10.refs_0_, bf16[144,1024]{1,0:T(8,128)(2,1)S(1)} %collective-permute-done.11.refs_1_), custom_call_target="tpu_custom_call" | custom-call | flops 5000000000 | bytes 1000000 | tf_op jit(solution)/shard_map/coefficients/pallas_call | solution.py:495
  60.8 1.1 %collective-permute-start.12 = (bf16[80,1024]{1,0:T(8,128)(2,1)S(1)}, bf16[80,1024]{1,0:T(8,128)(2,1)S(1)}, u32[]{:S(2)}, u32[]{:S(2)}) collective-permute-start(bf16[80,1024]{1,0:T(8,128)(2,1)S(1)} %coefficients.3.refs_0_), channel_id=1, source_target_pairs={{0,1},{1,0},{2,3},{3,2},{4,5},{5,4},{6,7},{7,6},{8,9},{9,8},{10,11... | collective-permute-start | bytes 491528 | tf_op jit(solution)/shard_map/ppermute | solution.py:39
  61.8 3.4 %collective-permute-done.8.refs_0_ = bf16[248,768]{1,0:T(8,128)(2,1)S(1)} collective-permute-done((bf16[248,768]{1,0:T(8,128)(2,1)S(1)}, bf16[248,768]{1,0:T(8,128)(2,1)S(1)}, u32[]{:S(2)}, u32[]{:S(2)}) %collective-permute-start.8) | collective-permute-done | bytes 380960 | tf_op jit(solution)/shard_map/ppermute | solution.py:39
  65.3 2.5 %coefficients.2.refs_1_ = bf16[80,768]{1,0:T(8,128)(2,1)S(1)} custom-call(s32[8]{0:T(128)S(1)} %copy-done, bf16[320,256]{1,0:T(8,128)(2,1)S(1)} %choices.1.picks_ref, f32[248,768]{1,0:T(8,128)S(1)} %get-tuple-element.27.kept_ref, bf16[248,768]{1,0:T(8,128)(2,1)S(1)} %collective-permute-done.8.refs_0_), custom_call_target="tpu_custom_call" | custom-call | flops 5000000000 | bytes 1000000 | tf_op jit(solution)/shard_map/coefficients/pallas_call | solution.py:495
  67.8 1.7 %collective-permute-start.9 = (bf16[80,768]{1,0:T(8,128)(2,1)S(1)}, bf16[80,768]{1,0:T(8,128)(2,1)S(1)}, u32[]{:S(2)}, u32[]{:S(2)}) collective-permute-start(bf16[80,768]{1,0:T(8,128)(2,1)S(1)} %coefficients.2.refs_1_), channel_id=1, source_target_pairs={{0,1},{1,0},{2,3},{3,2},{4,5},{5,4},{6,7},{7,6},{8,9},{9,8},{10,11... | collective-permute-start | bytes 368648 | tf_op jit(solution)/shard_map/ppermute | solution.py:39
  69.4 2.6 %backward.4.refs_4_ = f32[80,4096]{1,0:T(8,128)S(1)} custom-call(bf16[80,1024]{1,0:T(8,128)(2,1)S(1)} %coefficients.3.refs_0_, bf16[4096,1024]{1,0:T(8,128)(2,1)S(1)} %get-tuple-element.34.both.refs_1_), custom_call_target="tpu_custom_call" | custom-call | flops 671088640 | bytes 8388608 | tf_op jit(solution)/shard_map/backward/pallas_call | solution.py:554
  72.1 4.5 %backward.5.refs_2_ = f32[80,4096]{1,0:T(8,128)S(1)} custom-call(bf16[80,1024]{1,0:T(8,128)(2,1)S(1)} %collective-permute-done.12.refs_0_, bf16[80,768]{1,0:T(8,128)(2,1)S(1)} %coefficients.2.refs_1_, bf16[4096,1024]{1,0:T(8,128)(2,1)S(1)} %get-tuple-element.30.both.refs_2_, bf16[4096,768]{1,0:T(8,128)(2,1)S(1)} %get-tuple-element.25.both.refs_3_, ...), custom_call_target="tpu_custom_call" | custom-call | flops 1174405120 | bytes 8388608 | tf_op jit(solution)/shard_map/backward/pallas_call | solution.py:554
  76.6 0.8 backward.7
  77.5 1.3 %backward.6 = (bf16[40,2560]{1,0:T(8,128)(2,1)S(1)}, f32[40,2560]{1,0:T(8,128)S(1)}) custom-call(bf16[80,768]{1,0:T(8,128)(2,1)S(1)} %collective-permute-done.9.refs_0_, bf16[4096,768]{1,0:T(8,128)(2,1)S(1)} %get-tuple-element.28.both.refs_1_, f32[80,4096]{1,0:T(8,128)S(1)} %backward.5.refs_2_), custom_call_target="tpu_custom_call" | custom-call | flops 314572800 | bytes 3932160 | tf_op jit(solution)/shard_map/backward/pallas_call | solution.py:554
  78.8 0.6 collective-permute-start.13
  79.5 0.4 collective-permute-start.18
  79.9 0.6 collective-permute-done.13
  80.5 1.6 %collective-permute-start.14 = (bf16[20,2560]{1,0:T(8,128)(2,1)S(1)}, bf16[20,2560]{1,0:T(8,128)(2,1)S(1)}, u32[]{:S(2)}, u32[]{:S(2)}) collective-permute-start(bf16[20,2560]{1,0:T(8,128)(2,1)S(1)} %slice.91), channel_id=1, source_target_pairs={{0,4},{2,6},{4,0},{6,2},{8,12},{10,14},{12,8},{14,10},{16,20},{18,... | collective-permute-start | bytes 307208 | tf_op jit(solution)/shard_map/ppermute | solution.py:35
  82.1 1.8 %collective-permute-done.18 = bf16[20,1536]{1,0:T(8,128)(2,1)S(1)} collective-permute-done((bf16[20,1536]{1,0:T(8,128)(2,1)S(1)}, bf16[20,1536]{1,0:T(8,128)(2,1)S(1)}, u32[]{:S(2)}, u32[]{:S(2)}) %collective-permute-start.18) | collective-permute-done | bytes 61472 | tf_op jit(solution)/shard_map/ppermute | solution.py:35
  84.0 1.6 %collective-permute-start.19 = (bf16[10,1536]{1,0:T(8,128)(2,1)S(1)}, bf16[10,1536]{1,0:T(8,128)(2,1)S(1)}, u32[]{:S(2)}, u32[]{:S(2)}) collective-permute-start(bf16[10,1536]{1,0:T(8,128)(2,1)S(1)} %slice.93), channel_id=1, source_target_pairs={{0,4},{2,6},{4,0},{6,2},{8,12},{10,14},{12,8},{14,10},{16,20},{18,... | collective-permute-start | bytes 92168 | tf_op jit(solution)/shard_map/ppermute | solution.py:35
  85.6 1.2 %collective-permute-done.14 = bf16[20,2560]{1,0:T(8,128)(2,1)S(1)} collective-permute-done((bf16[20,2560]{1,0:T(8,128)(2,1)S(1)}, bf16[20,2560]{1,0:T(8,128)(2,1)S(1)}, u32[]{:S(2)}, u32[]{:S(2)}) %collective-permute-start.14) | collective-permute-done | bytes 102432 | tf_op jit(solution)/shard_map/ppermute | solution.py:35
  86.8 0.6 collective-permute-start.15
  87.4 0.7 collective-permute-done.19
  88.1 3.5 %collective-permute-start.20 = (bf16[5,1536]{1,0:T(8,128)(2,1)S(1)}, bf16[5,1536]{1,0:T(8,128)(2,1)S(1)}, u32[]{:S(2)}, u32[]{:S(2)}) collective-permute-start(bf16[5,1536]{1,0:T(8,128)(2,1)S(1)} %slice.95), channel_id=1, source_target_pairs={{0,16},{2,18},{4,20},{6,22},{8,24},{10,26},{12,28},{14,30},{16,0},... | collective-permute-start | bytes 46088 | tf_op jit(solution)/shard_map/ppermute | solution.py:35
  91.6 3.4 %collective-permute-start.16 = (bf16[5,2560]{1,0:T(8,128)(2,1)S(1)}, bf16[5,2560]{1,0:T(8,128)(2,1)S(1)}, u32[]{:S(2)}, u32[]{:S(2)}) collective-permute-start(bf16[5,2560]{1,0:T(8,128)(2,1)S(1)} %slice.94), channel_id=1, source_target_pairs={{0,16},{2,18},{4,20},{6,22},{8,24},{10,26},{12,28},{14,30},{16,0},... | collective-permute-start | bytes 76808 | tf_op jit(solution)/shard_map/ppermute | solution.py:35
  95.1 2.3 %collective-permute-done.16 = bf16[5,2560]{1,0:T(8,128)(2,1)S(1)} collective-permute-done((bf16[5,2560]{1,0:T(8,128)(2,1)S(1)}, bf16[5,2560]{1,0:T(8,128)(2,1)S(1)}, u32[]{:S(2)}, u32[]{:S(2)}) %collective-permute-start.16) | collective-permute-done | bytes 25632 | tf_op jit(solution)/shard_map/ppermute | solution.py:35
  97.4 0.6 pad_maximum_fusion.1
  (32 shorter events, 0.8 us)
Async XLA Ops:
  1.0 11.2 %collective-permute-start = (bf16[16,4608]{1,0:T(8,128)(2,1)S(1)}, bf16[16,4608]{1,0:T(8,128)(2,1)S(1)}, u32[]{:S(2)}, u32[]{:S(2)}) collective-permute-start(bf16[16,4608]{1,0:T(8,128)(2,1)S(1)} %pack.1.refs_0_), channel_id=1, source_target_pairs={{0,16},{2,18},{4,20},{6,22},{8,24},{10,26},{12,28},{14,30},{16,0},... | collective-permute-start | bytes 442376 | tf_op jit(solution)/shard_map/ppermute | solution.py:35
  5.1 9.8 %collective-permute-start.1 = (bf16[16,4608]{1,0:T(8,128)(2,1)S(1)}, bf16[16,4608]{1,0:T(8,128)(2,1)S(1)}, u32[]{:S(2)}, u32[]{:S(2)}) collective-permute-start(bf16[16,4608]{1,0:T(8,128)(2,1)S(1)} %pack.1.refs_0_), channel_id=1, source_target_pairs={{0,8},{2,10},{4,12},{6,14},{8,0},{10,2},{12,4},{14,6},{16,24},{18,... | collective-permute-start | bytes 442376 | tf_op jit(solution)/shard_map/ppermute | solution.py:35
  12.2 5.1 %collective-permute-start.2 = (bf16[16,4608]{1,0:T(8,128)(2,1)S(1)}, bf16[16,4608]{1,0:T(8,128)(2,1)S(1)}, u32[]{:S(2)}, u32[]{:S(2)}) collective-permute-start(bf16[16,4608]{1,0:T(8,128)(2,1)S(1)} %collective-permute-done.refs_1_), channel_id=1, source_target_pairs={{0,8},{2,10},{4,12},{6,14},{8,0},{10,2},{12,4},{14,6},{16,24},{18,... | collective-permute-start | bytes 442376 | tf_op jit(solution)/shard_map/ppermute | solution.py:35
  12.8 7.0 %collective-permute-start.3 = (bf16[16,4608]{1,0:T(8,128)(2,1)S(1)}, bf16[16,4608]{1,0:T(8,128)(2,1)S(1)}, u32[]{:S(2)}, u32[]{:S(2)}) collective-permute-start(bf16[16,4608]{1,0:T(8,128)(2,1)S(1)} %pack.1.refs_0_), channel_id=1, source_target_pairs={{0,4},{2,6},{4,0},{6,2},{8,12},{10,14},{12,8},{14,10},{16,20},{18,... | collective-permute-start | bytes 442376 | tf_op jit(solution)/shard_map/ppermute | solution.py:35
  14.4 8.4 %collective-permute-start.4 = (bf16[16,4608]{1,0:T(8,128)(2,1)S(1)}, bf16[16,4608]{1,0:T(8,128)(2,1)S(1)}, u32[]{:S(2)}, u32[]{:S(2)}) collective-permute-start(bf16[16,4608]{1,0:T(8,128)(2,1)S(1)} %collective-permute-done.refs_1_), channel_id=1, source_target_pairs={{0,4},{2,6},{4,0},{6,2},{8,12},{10,14},{12,8},{14,10},{16,20},{18,... | collective-permute-start | bytes 442376 | tf_op jit(solution)/shard_map/ppermute | solution.py:35
  14.9 11.0 %collective-permute-start.5 = (bf16[16,4608]{1,0:T(8,128)(2,1)S(1)}, bf16[16,4608]{1,0:T(8,128)(2,1)S(1)}, u32[]{:S(2)}, u32[]{:S(2)}) collective-permute-start(bf16[16,4608]{1,0:T(8,128)(2,1)S(1)} %collective-permute-done.1.refs_2_), channel_id=1, source_target_pairs={{0,4},{2,6},{4,0},{6,2},{8,12},{10,14},{12,8},{14,10},{16,20},{18,... | collective-permute-start | bytes 442376 | tf_op jit(solution)/shard_map/ppermute | solution.py:35
  17.4 10.4 %collective-permute-start.6 = (bf16[16,4608]{1,0:T(8,128)(2,1)S(1)}, bf16[16,4608]{1,0:T(8,128)(2,1)S(1)}, u32[]{:S(2)}, u32[]{:S(2)}) collective-permute-start(bf16[16,4608]{1,0:T(8,128)(2,1)S(1)} %collective-permute-done.2.refs_3_), channel_id=1, source_target_pairs={{0,4},{2,6},{4,0},{6,2},{8,12},{10,14},{12,8},{14,10},{16,20},{18,... | collective-permute-start | bytes 442376 | tf_op jit(solution)/shard_map/ppermute | solution.py:35
  28.6 15.7 %collective-permute-start.7 = (bf16[144,4096]{1,0:T(8,128)(2,1)S(1)}, bf16[144,4096]{1,0:T(8,128)(2,1)S(1)}, u32[]{:S(2)}, u32[]{:S(2)}) collective-permute-start(bf16[144,4096]{1,0:T(8,128)(2,1)S(1)} %assemble.1.refs_0_.refs_1_.half_ref), channel_id=1, source_target_pairs={{0,2},{2,0},{4,6},{6,4},{8,10},{10,8},{12,14},{14,12},{16,18},{18,... | collective-permute-start | bytes 3538952 | tf_op jit(solution)/shard_map/ppermute | solution.py:35
  42.6 15.0 %collective-permute-start.10 = (bf16[104,1024]{1,0:T(8,128)(2,1)S(1)}, bf16[104,1024]{1,0:T(8,128)(2,1)S(1)}, u32[]{:S(2)}, u32[]{:S(2)}) collective-permute-start(bf16[104,1024]{1,0:T(8,128)(2,1)S(1)} %forward_half.3), channel_id=1, source_target_pairs={{0,1},{1,0},{2,3},{3,2},{4,5},{5,4},{6,7},{7,6},{8,9},{9,8},{10,11... | collective-permute-start | bytes 638984 | tf_op jit(solution)/shard_map/ppermute | solution.py:39
  47.0 10.7 %collective-permute-start.11 = (bf16[144,1024]{1,0:T(8,128)(2,1)S(1)}, bf16[144,1024]{1,0:T(8,128)(2,1)S(1)}, u32[]{:S(2)}, u32[]{:S(2)}) collective-permute-start(bf16[144,1024]{1,0:T(8,128)(2,1)S(1)} %get-tuple-element.36), channel_id=1, source_target_pairs={{0,1},{1,0},{2,3},{3,2},{4,5},{5,4},{6,7},{7,6},{8,9},{9,8},{10,11... | collective-permute-start | bytes 884744 | tf_op jit(solution)/shard_map/ppermute | solution.py:39
  50.2 15.1 %collective-permute-start.8 = (bf16[248,768]{1,0:T(8,128)(2,1)S(1)}, bf16[248,768]{1,0:T(8,128)(2,1)S(1)}, u32[]{:S(2)}, u32[]{:S(2)}) collective-permute-start(bf16[248,768]{1,0:T(8,128)(2,1)S(1)} %get-tuple-element.33), channel_id=1, source_target_pairs={{0,1},{1,0},{2,3},{3,2},{4,5},{5,4},{6,7},{7,6},{8,9},{9,8},{10,11... | collective-permute-start | bytes 1142792 | tf_op jit(solution)/shard_map/ppermute | solution.py:39
  54.5 3.2 %copy-start = (s32[8]{0:T(128)S(1)}, s32[8]{0:T(128)}, u32[]{:S(2)}) copy-start(s32[8]{0:T(128)} %points_ref.3) | copy-start | bytes 100
  60.8 11.3 %collective-permute-start.12 = (bf16[80,1024]{1,0:T(8,128)(2,1)S(1)}, bf16[80,1024]{1,0:T(8,128)(2,1)S(1)}, u32[]{:S(2)}, u32[]{:S(2)}) collective-permute-start(bf16[80,1024]{1,0:T(8,128)(2,1)S(1)} %coefficients.3.refs_0_), channel_id=1, source_target_pairs={{0,1},{1,0},{2,3},{3,2},{4,5},{5,4},{6,7},{7,6},{8,9},{9,8},{10,11... | collective-permute-start | bytes 491528 | tf_op jit(solution)/shard_map/ppermute | solution.py:39
  67.8 8.8 %collective-permute-start.9 = (bf16[80,768]{1,0:T(8,128)(2,1)S(1)}, bf16[80,768]{1,0:T(8,128)(2,1)S(1)}, u32[]{:S(2)}, u32[]{:S(2)}) collective-permute-start(bf16[80,768]{1,0:T(8,128)(2,1)S(1)} %coefficients.2.refs_1_), channel_id=1, source_target_pairs={{0,1},{1,0},{2,3},{3,2},{4,5},{5,4},{6,7},{7,6},{8,9},{9,8},{10,11... | collective-permute-start | bytes 368648 | tf_op jit(solution)/shard_map/ppermute | solution.py:39
  77.4 1.9 %collective-permute-start.17 = (bf16[40,1536]{1,0:T(8,128)(2,1)S(1)}, bf16[40,1536]{1,0:T(8,128)(2,1)S(1)}, u32[]{:S(2)}, u32[]{:S(2)}) collective-permute-start(bf16[40,1536]{1,0:T(8,128)(2,1)S(1)} %get-tuple-element.40), channel_id=1, source_target_pairs={{0,2},{2,0},{4,6},{6,4},{8,10},{10,8},{12,14},{14,12},{16,18},{18,... | collective-permute-start | bytes 368648 | tf_op jit(solution)/shard_map/ppermute | solution.py:35
  78.8 1.6 %collective-permute-start.13 = (bf16[40,2560]{1,0:T(8,128)(2,1)S(1)}, bf16[40,2560]{1,0:T(8,128)(2,1)S(1)}, u32[]{:S(2)}, u32[]{:S(2)}) collective-permute-start(bf16[40,2560]{1,0:T(8,128)(2,1)S(1)} %get-tuple-element.38), channel_id=1, source_target_pairs={{0,2},{2,0},{4,6},{6,4},{8,10},{10,8},{12,14},{14,12},{16,18},{18,... | collective-permute-start | bytes 614408 | tf_op jit(solution)/shard_map/ppermute | solution.py:35
  79.5 4.4 %collective-permute-start.18 = (bf16[20,1536]{1,0:T(8,128)(2,1)S(1)}, bf16[20,1536]{1,0:T(8,128)(2,1)S(1)}, u32[]{:S(2)}, u32[]{:S(2)}) collective-permute-start(bf16[20,1536]{1,0:T(8,128)(2,1)S(1)} %pad_maximum_fusion), channel_id=1, source_target_pairs={{0,8},{2,10},{4,12},{6,14},{8,0},{10,2},{12,4},{14,6},{16,24},{18,... | collective-permute-start | bytes 184328 | tf_op jit(solution)/shard_map/ppermute | solution.py:35
  80.5 6.2 %collective-permute-start.14 = (bf16[20,2560]{1,0:T(8,128)(2,1)S(1)}, bf16[20,2560]{1,0:T(8,128)(2,1)S(1)}, u32[]{:S(2)}, u32[]{:S(2)}) collective-permute-start(bf16[20,2560]{1,0:T(8,128)(2,1)S(1)} %slice.91), channel_id=1, source_target_pairs={{0,4},{2,6},{4,0},{6,2},{8,12},{10,14},{12,8},{14,10},{16,20},{18,... | collective-permute-start | bytes 307208 | tf_op jit(solution)/shard_map/ppermute | solution.py:35
  84.0 4.2 %collective-permute-start.19 = (bf16[10,1536]{1,0:T(8,128)(2,1)S(1)}, bf16[10,1536]{1,0:T(8,128)(2,1)S(1)}, u32[]{:S(2)}, u32[]{:S(2)}) collective-permute-start(bf16[10,1536]{1,0:T(8,128)(2,1)S(1)} %slice.93), channel_id=1, source_target_pairs={{0,4},{2,6},{4,0},{6,2},{8,12},{10,14},{12,8},{14,10},{16,20},{18,... | collective-permute-start | bytes 92168 | tf_op jit(solution)/shard_map/ppermute | solution.py:35
  86.8 4.8 %collective-permute-start.15 = (bf16[10,2560]{1,0:T(8,128)(2,1)S(1)}, bf16[10,2560]{1,0:T(8,128)(2,1)S(1)}, u32[]{:S(2)}, u32[]{:S(2)}) collective-permute-start(bf16[10,2560]{1,0:T(8,128)(2,1)S(1)} %slice.92), channel_id=1, source_target_pairs={{0,8},{2,10},{4,12},{6,14},{8,0},{10,2},{12,4},{14,6},{16,24},{18,... | collective-permute-start | bytes 153608 | tf_op jit(solution)/shard_map/ppermute | solution.py:35
  88.1 6.9 %collective-permute-start.20 = (bf16[5,1536]{1,0:T(8,128)(2,1)S(1)}, bf16[5,1536]{1,0:T(8,128)(2,1)S(1)}, u32[]{:S(2)}, u32[]{:S(2)}) collective-permute-start(bf16[5,1536]{1,0:T(8,128)(2,1)S(1)} %slice.95), channel_id=1, source_target_pairs={{0,16},{2,18},{4,20},{6,22},{8,24},{10,26},{12,28},{14,30},{16,0},... | collective-permute-start | bytes 46088 | tf_op jit(solution)/shard_map/ppermute | solution.py:35
  91.6 5.8 %collective-permute-start.16 = (bf16[5,2560]{1,0:T(8,128)(2,1)S(1)}, bf16[5,2560]{1,0:T(8,128)(2,1)S(1)}, u32[]{:S(2)}, u32[]{:S(2)}) collective-permute-start(bf16[5,2560]{1,0:T(8,128)(2,1)S(1)} %slice.94), channel_id=1, source_target_pairs={{0,16},{2,18},{4,20},{6,22},{8,24},{10,26},{12,28},{14,30},{16,0},... | collective-permute-start | bytes 76808 | tf_op jit(solution)/shard_map/ppermute | solution.py:35

commit v8 on v7

--- a/solution.py
+++ b/solution.py
@@ -572,8 +572,12 @@
     blocks = far * near * pair
     examples, pairs = pair_ref.shape
 
-    def body(pair_ref, out, rows, table):
-        table[pl.ds(0, examples), :] = pair_ref[...]
+    long = rounded(examples + 8, 128)
+
+    def body(turned, out, rows, wide, table):
+        wide[...] = jnp.zeros_like(wide)
+        wide[pl.ds(0, pairs), pl.ds(0, examples)] = turned[...]
+        table[...] = wide[...].T
         at = lax.axis_index("wide")
         z, y, c = at // (near * pair), at // pair % near, at % pair
         col = lax.broadcasted_iota(jnp.int32, (examples, blocks * r), 1)
@@ -581,7 +585,7 @@
         for q in range(blocks):
             s, b, p = halvings(far)[q % far], q // far % near, q // (far * near)
             owner = ((z ^ s) * near + (y ^ b)) * pair + (c ^ p)
-            rows[pl.ds(q * e, e), :] = table[pl.ds(owner * e, e), :]
+            rows[pl.ds(q * e, e), :] = table[pl.ds(owner * e, e), pl.ds(0, pairs)]
             name = jnp.where((col >= q * r) & (col < (q + 1) * r), owner * r + col - q * r, name)
         for p in range(pairs):
             pick = (rows[:, pl.ds(p, 1)] == name).astype(jnp.float32).astype(jnp.bfloat16)
@@ -595,12 +599,13 @@
         out_specs=VMEM,
         scratch_shapes=[
             pltpu.VMEM((examples, pairs), jnp.int32),
-            pltpu.VMEM((rounded(examples, 8) + 8, pairs), jnp.int32),
+            pltpu.VMEM((128, long), jnp.int32),
+            pltpu.VMEM((long, 128), jnp.int32),
         ],
         compiler_params=pltpu.CompilerParams(vmem_limit_bytes=2 * 1024 * 1024),
         cost_estimate=pl.CostEstimate(flops=10**9, bytes_accessed=10**6, transcendentals=0),
         name="choices",
-    )(pair_ref)
+    )(pair_ref.T)
 
 
 def chunks_of(width):
@@ -725,8 +730,7 @@
     total = None
     for group in groups[:-1]:
         total = backward(group, total, False)
-    cut = depth // 2 if depth % 1024 else depth // 8 * 5
-    spans = [(0, cut), (cut, depth - cut)] if depth % 256 == 0 else [(0, depth)]
+    spans = [(0, depth // 2), (depth // 2, depth // 2)] if depth % 256 == 0 else [(0, depth)]
     last = [backward(groups[-1], total, pair == 2, span) for span in spans]
 
     results = []

time: 98.3 us -> 98.2 us (level)
  starting transfers between devices: 29.6 us -> 27.4 us
  waiting for transfers between devices: 24.6 us -> 26.7 us
    ppermute x16, starting transfers between devices: 23.1 us -> 20.9 us  [permute(): return lax.ppermute(array, axis, pairs)]
    ppermute x16, waiting for transfers between devices: 21.1 us -> 23.3 us  [permute(): return lax.ppermute(array, axis, pairs)]
  transfers between devices with their start and end apart: 21 -> 21, of which waited for: 11 -> 11; matrix products, arithmetic and copies ran while one was open for 1% -> 0% of each run, Pallas kernels for 40% -> 40%
where the time goes in v8:
time: 98.2 us; the launch traced here: 98 us
  Pallas kernels  42 us (43%)
  starting transfers between devices  27.4 us (28%)
  waiting for transfers between devices  26.7 us (27%)
    ppermute x16, waiting for transfers between devices, permute(): return lax.ppermute(array, axis, pairs)  23.3 us
    ppermute x16, starting transfers between devices, permute(): return lax.ppermute(array, axis, pairs)  20.9 us
    pallas_call x3, Pallas kernels, fetch(): pl.pallas_call(body, out_shape=(pltpu.VMEM((depth, 2 * width), jnp.bfloat...  12.5 us
    pallas_call x4, Pallas kernels, backward(): pl.pallas_call(body, out_shape=out_shape, in_specs=specs, out_specs=out_s...  9.32 us
    pallas_call x3, Pallas kernels, forward(): pl.pallas_call(body_ready if ready else body, out_shape=out_shape, in_spe...  8.31 us
    ppermute x5, starting transfers between devices, shift(): lax.ppermute(array, 'narrow', [(at, (at + amount) % size) for at in range...  6.51 us
    pallas_call x2, Pallas kernels, coefficients(): pl.pallas_call(body, out_shape=jax.ShapeDtypeStruct((examples, 2 * width)...  5.58 us
    pallas_call x2, Pallas kernels, forward_half(): pl.pallas_call(body, out_shape=[jax.ShapeDtypeStruct((all_rows, 2 * width...  4.15 us
  transfers between devices with their start and end apart: 21, of which 11 were waited for; matrix products, arithmetic and copies ran while one was open for 0% of the time, Pallas kernels for 40%

profile of v8, /device:TPU:0, one launch (start us, length us, event | category | flops | bytes accessed | tf_op | source)
XLA Modules:
  0.0 98.0 jit_solution(12259075782836435388)
XLA Ops:
  0.0 1.0 pack.1.refs_0_
  1.0 4.1 %collective-permute-start = (bf16[16,4608]{1,0:T(8,128)(2,1)S(1)}, bf16[16,4608]{1,0:T(8,128)(2,1)S(1)}, u32[]{:S(2)}, u32[]{:S(2)}) collective-permute-start(bf16[16,4608]{1,0:T(8,128)(2,1)S(1)} %pack.1.refs_0_), channel_id=1, source_target_pairs={{0,16},{2,18},{4,20},{6,22},{8,24},{10,26},{12,28},{14,30},{16,0},... | collective-permute-start | bytes 442376 | tf_op jit(solution)/shard_map/ppermute | solution.py:35
  5.1 1.6 %collective-permute-start.1 = (bf16[16,4608]{1,0:T(8,128)(2,1)S(1)}, bf16[16,4608]{1,0:T(8,128)(2,1)S(1)}, u32[]{:S(2)}, u32[]{:S(2)}) collective-permute-start(bf16[16,4608]{1,0:T(8,128)(2,1)S(1)} %pack.1.refs_0_), channel_id=1, source_target_pairs={{0,8},{2,10},{4,12},{6,14},{8,0},{10,2},{12,4},{14,6},{16,24},{18,... | collective-permute-start | bytes 442376 | tf_op jit(solution)/shard_map/ppermute | solution.py:35
  6.7 5.5 %collective-permute-done.refs_1_ = bf16[16,4608]{1,0:T(8,128)(2,1)S(1)} collective-permute-done((bf16[16,4608]{1,0:T(8,128)(2,1)S(1)}, bf16[16,4608]{1,0:T(8,128)(2,1)S(1)}, u32[]{:S(2)}, u32[]{:S(2)}) %collective-permute-start) | collective-permute-done | bytes 147488 | tf_op jit(solution)/shard_map/ppermute | solution.py:35
  12.2 0.6 collective-permute-start.2
  12.8 1.5 %collective-permute-start.3 = (bf16[16,4608]{1,0:T(8,128)(2,1)S(1)}, bf16[16,4608]{1,0:T(8,128)(2,1)S(1)}, u32[]{:S(2)}, u32[]{:S(2)}) collective-permute-start(bf16[16,4608]{1,0:T(8,128)(2,1)S(1)} %pack.1.refs_0_), channel_id=1, source_target_pairs={{0,4},{2,6},{4,0},{6,2},{8,12},{10,14},{12,8},{14,10},{16,20},{18,... | collective-permute-start | bytes 442376 | tf_op jit(solution)/shard_map/ppermute | solution.py:35
  14.4 0.5 collective-permute-start.4
  14.9 1.5 %collective-permute-start.5 = (bf16[16,4608]{1,0:T(8,128)(2,1)S(1)}, bf16[16,4608]{1,0:T(8,128)(2,1)S(1)}, u32[]{:S(2)}, u32[]{:S(2)}) collective-permute-start(bf16[16,4608]{1,0:T(8,128)(2,1)S(1)} %collective-permute-done.1.refs_2_), channel_id=1, source_target_pairs={{0,4},{2,6},{4,0},{6,2},{8,12},{10,14},{12,8},{14,10},{16,20},{18,... | collective-permute-start | bytes 442376 | tf_op jit(solution)/shard_map/ppermute | solution.py:35
  16.4 1.0 collective-permute-done.2.refs_3_
  17.4 1.6 %collective-permute-start.6 = (bf16[16,4608]{1,0:T(8,128)(2,1)S(1)}, bf16[16,4608]{1,0:T(8,128)(2,1)S(1)}, u32[]{:S(2)}, u32[]{:S(2)}) collective-permute-start(bf16[16,4608]{1,0:T(8,128)(2,1)S(1)} %collective-permute-done.2.refs_3_), channel_id=1, source_target_pairs={{0,4},{2,6},{4,0},{6,2},{8,12},{10,14},{12,8},{14,10},{16,20},{18,... | collective-permute-start | bytes 442376 | tf_op jit(solution)/shard_map/ppermute | solution.py:35
  18.9 0.7 copy-done
  19.9 2.8 %collective-permute-done.4.refs_5_ = bf16[16,4608]{1,0:T(8,128)(2,1)S(1)} collective-permute-done((bf16[16,4608]{1,0:T(8,128)(2,1)S(1)}, bf16[16,4608]{1,0:T(8,128)(2,1)S(1)}, u32[]{:S(2)}, u32[]{:S(2)}) %collective-permute-start.4) | collective-permute-done | bytes 147488 | tf_op jit(solution)/shard_map/ppermute | solution.py:35
  22.7 3.2 %collective-permute-done.5.refs_6_ = bf16[16,4608]{1,0:T(8,128)(2,1)S(1)} collective-permute-done((bf16[16,4608]{1,0:T(8,128)(2,1)S(1)}, bf16[16,4608]{1,0:T(8,128)(2,1)S(1)}, u32[]{:S(2)}, u32[]{:S(2)}) %collective-permute-start.5) | collective-permute-done | bytes 147488 | tf_op jit(solution)/shard_map/ppermute | solution.py:35
  25.9 1.9 %collective-permute-done.6.refs_7_ = bf16[16,4608]{1,0:T(8,128)(2,1)S(1)} collective-permute-done((bf16[16,4608]{1,0:T(8,128)(2,1)S(1)}, bf16[16,4608]{1,0:T(8,128)(2,1)S(1)}, u32[]{:S(2)}, u32[]{:S(2)}) %collective-permute-start.6) | collective-permute-done | bytes 147488 | tf_op jit(solution)/shard_map/ppermute | solution.py:35
  27.8 0.8 assemble.1.refs_0_.refs_1_.half_ref
  28.6 4.8 %fetch.5 = (bf16[4096,1024]{1,0:T(8,128)(2,1)S(1)}, bf16[512,4096]{1,0:T(8,128)(2,1)S(1)}) custom-call(bf16[4096,1792]{1,0:T(8,128)(2,1)} %refs_0_.5, bf16[4096,1792]{1,0:T(8,128)(2,1)} %refs_1_.5, bf16[1792,4096]{1,0:T(8,128)(2,1)} %refs_2_.5), custom_call_target="tpu_custom_call" | custom-call | flops 4000000000 | bytes 12582912 | tf_op jit(solution)/shard_map/fetch/pallas_call | solution.py:231
  33.4 3.9 %fetch.4 = (bf16[4096,768]{1,0:T(8,128)(2,1)S(1)}, bf16[384,4096]{1,0:T(8,128)(2,1)S(1)}) custom-call(bf16[4096,1792]{1,0:T(8,128)(2,1)} %refs_0_.5, bf16[4096,1792]{1,0:T(8,128)(2,1)} %refs_1_.5, bf16[1792,4096]{1,0:T(8,128)(2,1)} %refs_2_.5), custom_call_target="tpu_custom_call" | custom-call | flops 4000000000 | bytes 9437184 | tf_op jit(solution)/shard_map/fetch/pallas_call | solution.py:231
  37.3 3.9 %fetch.3 = (bf16[4096,768]{1,0:T(8,128)(2,1)S(1)}, bf16[384,4096]{1,0:T(8,128)(2,1)S(1)}) custom-call(bf16[4096,1792]{1,0:T(8,128)(2,1)} %refs_0_.5, bf16[4096,1792]{1,0:T(8,128)(2,1)} %refs_1_.5, bf16[1792,4096]{1,0:T(8,128)(2,1)} %refs_2_.5), custom_call_target="tpu_custom_call" | custom-call | flops 4000000000 | bytes 9437184 | tf_op jit(solution)/shard_map/fetch/pallas_call | solution.py:231
  41.2 1.4 %forward_half.3 = bf16[104,1024]{1,0:T(8,128)(2,1)S(1)} custom-call(bf16[144,4096]{1,0:T(8,128)(2,1)S(1)} %assemble.1.refs_0_.refs_1_.half_ref, bf16[4096,1024]{1,0:T(8,128)(2,1)S(1)} %get-tuple-element.30.both.refs_2_), custom_call_target="tpu_custom_call" | custom-call | flops 872415232 | bytes 1000000 | tf_op jit(solution)/shard_map/forward_half/pallas_call | solution.py:314
  42.6 1.6 %collective-permute-start.10 = (bf16[104,1024]{1,0:T(8,128)(2,1)S(1)}, bf16[104,1024]{1,0:T(8,128)(2,1)S(1)}, u32[]{:S(2)}, u32[]{:S(2)}) collective-permute-start(bf16[104,1024]{1,0:T(8,128)(2,1)S(1)} %forward_half.3), channel_id=1, source_target_pairs={{0,1},{1,0},{2,3},{3,2},{4,5},{5,4},{6,7},{7,6},{8,9},{9,8},{10,11... | collective-permute-start | bytes 638984 | tf_op jit(solution)/shard_map/ppermute | solution.py:39
  44.2 2.7 %forward_half.2 = (bf16[144,1024]{1,0:T(8,128)(2,1)S(1)}, bf16[4096,1024]{1,0:T(8,128)(2,1)S(1)}) custom-call(bf16[144,4096]{1,0:T(8,128)(2,1)S(1)} %collective-permute-done.7.refs_1_.half_ref.refs_2_, bf16[4096,1024]{1,0:T(8,128)(2,1)S(1)} %get-tuple-element.30.both.refs_2_, bf16[512,4096]{1,0:T(8,128)(2,1)S(1)} %get-tuple-element.31.refs_0_, ...), custom_call_target="tpu_custom_call" | custom-call | flops 1207959552 | bytes 1000000 | tf_op jit(solution)/shard_map/forward_half/pallas_call | solution.py:314
  47.0 0.5 collective-permute-start.11
  47.7 2.5 %forward.4 = (bf16[248,768]{1,0:T(8,128)(2,1)S(1)}, bf16[4096,1024]{1,0:T(8,128)(2,1)S(1)}) custom-call(bf16[208,4096]{1,0:T(8,128)(2,1)S(1)} %get-tuple-element.23.main_ref, bf16[80,4096]{1,0:T(8,128)(2,1)S(1)} %get-tuple-element.24.side_ref, bf16[4096,768]{1,0:T(8,128)(2,1)S(1)} %get-tuple-element.28.both.refs_1_, ...), custom_call_target="tpu_custom_call", output_to_operand_aliasing={{1}: (7, {})} | custom-call | flops 1560281088 | bytes 9437184 | tf_op jit(solution)/shard_map/forward/pallas_call | solution.py:384
  50.2 1.6 %collective-permute-start.8 = (bf16[248,768]{1,0:T(8,128)(2,1)S(1)}, bf16[248,768]{1,0:T(8,128)(2,1)S(1)}, u32[]{:S(2)}, u32[]{:S(2)}) collective-permute-start(bf16[248,768]{1,0:T(8,128)(2,1)S(1)} %get-tuple-element.33), channel_id=1, source_target_pairs={{0,1},{1,0},{2,3},{3,2},{4,5},{5,4},{6,7},{7,6},{8,9},{9,8},{10,11... | collective-permute-start | bytes 1142792 | tf_op jit(solution)/shard_map/ppermute | solution.py:39
  51.8 2.6 %forward.3 = (f32[248,768]{1,0:T(8,128)S(1)}, bf16[512,4096]{1,0:T(8,128)(2,1)S(1)}) custom-call(bf16[208,4096]{1,0:T(8,128)(2,1)S(1)} %get-tuple-element.23.main_ref, bf16[80,4096]{1,0:T(8,128)(2,1)S(1)} %get-tuple-element.24.side_ref, bf16[4096,768]{1,0:T(8,128)(2,1)S(1)} %get-tuple-element.25.both.refs_3_, bf16[384,4096]{1,0:T(8,128)(2,1)S(1)} %get-tuple-element.26.below, ...), custom_call_target="tpu_custom_call" | custom-call | flops 1560281088 | bytes 9437184 | tf_op jit(solution)/shard_map/forward/pallas_call | solution.py:384
  54.5 3.1 %forward.5.kept_ref = f32[248,1024]{1,0:T(8,128)S(1)} custom-call(bf16[208,4096]{1,0:T(8,128)(2,1)S(1)} %get-tuple-element.23.main_ref, bf16[80,4096]{1,0:T(8,128)(2,1)S(1)} %get-tuple-element.24.side_ref, bf16[4096,1024]{1,0:T(8,128)(2,1)S(1)} %get-tuple-element.34.both.refs_1_, bf16[512,4096]{1,0:T(8,128)(2,1)S(1)} %get-tuple-element.35.below), custom_call_target="tpu_custom_call" | custom-call | flops 2080374784 | bytes 12582912 | tf_op jit(solution)/shard_map/forward/pallas_call | solution.py:384
  57.7 3.1 %coefficients.3.refs_0_ = bf16[80,1024]{1,0:T(8,128)(2,1)S(1)} custom-call(s32[8]{0:T(128)S(1)} %copy-done.1, bf16[320,256]{1,0:T(8,128)(2,1)S(1)} %choices.1.picks_ref, f32[248,1024]{1,0:T(8,128)S(1)} %forward.5.kept_ref, bf16[104,1024]{1,0:T(8,128)(2,1)S(1)} %collective-permute-done.10.refs_0_, bf16[144,1024]{1,0:T(8,128)(2,1)S(1)} %collective-permute-done.11.refs_1_), custom_call_target="tpu_custom_call" | custom-call | flops 5000000000 | bytes 1000000 | tf_op jit(solution)/shard_map/coefficients/pallas_call | solution.py:495
  60.8 1.1 %collective-permute-start.12 = (bf16[80,1024]{1,0:T(8,128)(2,1)S(1)}, bf16[80,1024]{1,0:T(8,128)(2,1)S(1)}, u32[]{:S(2)}, u32[]{:S(2)}) collective-permute-start(bf16[80,1024]{1,0:T(8,128)(2,1)S(1)} %coefficients.3.refs_0_), channel_id=1, source_target_pairs={{0,1},{1,0},{2,3},{3,2},{4,5},{5,4},{6,7},{7,6},{8,9},{9,8},{10,11... | collective-permute-start | bytes 491528 | tf_op jit(solution)/shard_map/ppermute | solution.py:39
  61.8 3.4 %collective-permute-done.8.refs_0_ = bf16[248,768]{1,0:T(8,128)(2,1)S(1)} collective-permute-done((bf16[248,768]{1,0:T(8,128)(2,1)S(1)}, bf16[248,768]{1,0:T(8,128)(2,1)S(1)}, u32[]{:S(2)}, u32[]{:S(2)}) %collective-permute-start.8) | collective-permute-done | bytes 380960 | tf_op jit(solution)/shard_map/ppermute | solution.py:39
  65.3 2.5 %coefficients.2.refs_1_ = bf16[80,768]{1,0:T(8,128)(2,1)S(1)} custom-call(s32[8]{0:T(128)S(1)} %copy-done.1, bf16[320,256]{1,0:T(8,128)(2,1)S(1)} %choices.1.picks_ref, f32[248,768]{1,0:T(8,128)S(1)} %get-tuple-element.27.kept_ref, bf16[248,768]{1,0:T(8,128)(2,1)S(1)} %collective-permute-done.8.refs_0_), custom_call_target="tpu_custom_call" | custom-call | flops 5000000000 | bytes 1000000 | tf_op jit(solution)/shard_map/coefficients/pallas_call | solution.py:495
  67.8 1.7 %collective-permute-start.9 = (bf16[80,768]{1,0:T(8,128)(2,1)S(1)}, bf16[80,768]{1,0:T(8,128)(2,1)S(1)}, u32[]{:S(2)}, u32[]{:S(2)}) collective-permute-start(bf16[80,768]{1,0:T(8,128)(2,1)S(1)} %coefficients.2.refs_1_), channel_id=1, source_target_pairs={{0,1},{1,0},{2,3},{3,2},{4,5},{5,4},{6,7},{7,6},{8,9},{9,8},{10,11... | collective-permute-start | bytes 368648 | tf_op jit(solution)/shard_map/ppermute | solution.py:39
  69.4 2.6 %backward.4.refs_4_ = f32[80,4096]{1,0:T(8,128)S(1)} custom-call(bf16[80,1024]{1,0:T(8,128)(2,1)S(1)} %coefficients.3.refs_0_, bf16[4096,1024]{1,0:T(8,128)(2,1)S(1)} %get-tuple-element.34.both.refs_1_), custom_call_target="tpu_custom_call" | custom-call | flops 671088640 | bytes 8388608 | tf_op jit(solution)/shard_map/backward/pallas_call | solution.py:554
  72.1 4.5 %backward.5.refs_2_ = f32[80,4096]{1,0:T(8,128)S(1)} custom-call(bf16[80,1024]{1,0:T(8,128)(2,1)S(1)} %collective-permute-done.12.refs_0_, bf16[80,768]{1,0:T(8,128)(2,1)S(1)} %coefficients.2.refs_1_, bf16[4096,1024]{1,0:T(8,128)(2,1)S(1)} %get-tuple-element.30.both.refs_2_, bf16[4096,768]{1,0:T(8,128)(2,1)S(1)} %get-tuple-element.25.both.refs_3_, ...), custom_call_target="tpu_custom_call" | custom-call | flops 1174405120 | bytes 8388608 | tf_op jit(solution)/shard_map/backward/pallas_call | solution.py:554
  76.6 1.1 %backward.6 = (bf16[40,2048]{1,0:T(8,128)(2,1)S(1)}, f32[40,2048]{1,0:T(8,128)S(1)}) custom-call(bf16[80,768]{1,0:T(8,128)(2,1)S(1)} %collective-permute-done.9.refs_0_, bf16[4096,768]{1,0:T(8,128)(2,1)S(1)} %get-tuple-element.28.both.refs_1_, f32[80,4096]{1,0:T(8,128)S(1)} %backward.5.refs_2_), custom_call_target="tpu_custom_call" | custom-call | flops 251658240 | bytes 3145728 | tf_op jit(solution)/shard_map/backward/pallas_call | solution.py:554
  77.8 1.1 %backward.7 = (bf16[40,2048]{1,0:T(8,128)(2,1)S(1)}, f32[40,2048]{1,0:T(8,128)S(1)}) custom-call(bf16[80,768]{1,0:T(8,128)(2,1)S(1)} %collective-permute-done.9.refs_0_, bf16[4096,768]{1,0:T(8,128)(2,1)S(1)} %get-tuple-element.28.both.refs_1_, f32[80,4096]{1,0:T(8,128)S(1)} %backward.5.refs_2_), custom_call_target="tpu_custom_call" | custom-call | flops 251658240 | bytes 3145728 | tf_op jit(solution)/shard_map/backward/pallas_call | solution.py:554
  78.8 0.6 collective-permute-start.17
  79.5 1.6 %collective-permute-start.14 = (bf16[20,2048]{1,0:T(8,128)(2,1)S(1)}, bf16[20,2048]{1,0:T(8,128)(2,1)S(1)}, u32[]{:S(2)}, u32[]{:S(2)}) collective-permute-start(bf16[20,2048]{1,0:T(8,128)(2,1)S(1)} %slice.91), channel_id=1, source_target_pairs={{0,4},{2,6},{4,0},{6,2},{8,12},{10,14},{12,8},{14,10},{16,20},{18,... | collective-permute-start | bytes 245768 | tf_op jit(solution)/shard_map/ppermute | solution.py:35
  81.2 0.4 collective-permute-start.18
  81.6 2.7 %collective-permute-done.14 = bf16[20,2048]{1,0:T(8,128)(2,1)S(1)} collective-permute-done((bf16[20,2048]{1,0:T(8,128)(2,1)S(1)}, bf16[20,2048]{1,0:T(8,128)(2,1)S(1)}, u32[]{:S(2)}, u32[]{:S(2)}) %collective-permute-start.14) | collective-permute-done | bytes 81952 | tf_op jit(solution)/shard_map/ppermute | solution.py:35
  84.3 0.4 collective-permute-start.15
  84.7 1.2 %collective-permute-done.18 = bf16[20,2048]{1,0:T(8,128)(2,1)S(1)} collective-permute-done((bf16[20,2048]{1,0:T(8,128)(2,1)S(1)}, bf16[20,2048]{1,0:T(8,128)(2,1)S(1)}, u32[]{:S(2)}, u32[]{:S(2)}) %collective-permute-start.18) | collective-permute-done | bytes 81952 | tf_op jit(solution)/shard_map/ppermute | solution.py:35
  85.9 1.4 %collective-permute-start.19 = (bf16[10,2048]{1,0:T(8,128)(2,1)S(1)}, bf16[10,2048]{1,0:T(8,128)(2,1)S(1)}, u32[]{:S(2)}, u32[]{:S(2)}) collective-permute-start(bf16[10,2048]{1,0:T(8,128)(2,1)S(1)} %slice.92), channel_id=1, source_target_pairs={{0,4},{2,6},{4,0},{6,2},{8,12},{10,14},{12,8},{14,10},{16,20},{18,... | collective-permute-start | bytes 122888 | tf_op jit(solution)/shard_map/ppermute | solution.py:35
  87.3 1.3 %collective-permute-done.15 = bf16[10,2048]{1,0:T(8,128)(2,1)S(1)} collective-permute-done((bf16[10,2048]{1,0:T(8,128)(2,1)S(1)}, bf16[10,2048]{1,0:T(8,128)(2,1)S(1)}, u32[]{:S(2)}, u32[]{:S(2)}) %collective-permute-start.15) | collective-permute-done | bytes 40992 | tf_op jit(solution)/shard_map/ppermute | solution.py:35
  88.7 3.8 %collective-permute-start.16 = (bf16[5,2048]{1,0:T(8,128)(2,1)S(1)}, bf16[5,2048]{1,0:T(8,128)(2,1)S(1)}, u32[]{:S(2)}, u32[]{:S(2)}) collective-permute-start(bf16[5,2048]{1,0:T(8,128)(2,1)S(1)} %slice.95), channel_id=1, source_target_pairs={{0,16},{2,18},{4,20},{6,22},{8,24},{10,26},{12,28},{14,30},{16,0},... | collective-permute-start | bytes 61448 | tf_op jit(solution)/shard_map/ppermute | solution.py:35
  92.5 1.3 %collective-permute-start.20 = (bf16[5,2048]{1,0:T(8,128)(2,1)S(1)}, bf16[5,2048]{1,0:T(8,128)(2,1)S(1)}, u32[]{:S(2)}, u32[]{:S(2)}) collective-permute-start(bf16[5,2048]{1,0:T(8,128)(2,1)S(1)} %slice.94), channel_id=1, source_target_pairs={{0,16},{2,18},{4,20},{6,22},{8,24},{10,26},{12,28},{14,30},{16,0},... | collective-permute-start | bytes 61448 | tf_op jit(solution)/shard_map/ppermute | solution.py:35
  93.7 0.9 collective-permute-done.16
  94.6 2.8 %collective-permute-done.20 = bf16[5,2048]{1,0:T(8,128)(2,1)S(1)} collective-permute-done((bf16[5,2048]{1,0:T(8,128)(2,1)S(1)}, bf16[5,2048]{1,0:T(8,128)(2,1)S(1)}, u32[]{:S(2)}, u32[]{:S(2)}) %collective-permute-start.20) | collective-permute-done | bytes 20512 | tf_op jit(solution)/shard_map/ppermute | solution.py:35
  97.4 0.6 pad_maximum_fusion.1
  (33 shorter events, 0.9 us)
Async XLA Ops:
  1.0 11.2 %collective-permute-start = (bf16[16,4608]{1,0:T(8,128)(2,1)S(1)}, bf16[16,4608]{1,0:T(8,128)(2,1)S(1)}, u32[]{:S(2)}, u32[]{:S(2)}) collective-permute-start(bf16[16,4608]{1,0:T(8,128)(2,1)S(1)} %pack.1.refs_0_), channel_id=1, source_target_pairs={{0,16},{2,18},{4,20},{6,22},{8,24},{10,26},{12,28},{14,30},{16,0},... | collective-permute-start | bytes 442376 | tf_op jit(solution)/shard_map/ppermute | solution.py:35
  5.1 9.8 %collective-permute-start.1 = (bf16[16,4608]{1,0:T(8,128)(2,1)S(1)}, bf16[16,4608]{1,0:T(8,128)(2,1)S(1)}, u32[]{:S(2)}, u32[]{:S(2)}) collective-permute-start(bf16[16,4608]{1,0:T(8,128)(2,1)S(1)} %pack.1.refs_0_), channel_id=1, source_target_pairs={{0,8},{2,10},{4,12},{6,14},{8,0},{10,2},{12,4},{14,6},{16,24},{18,... | collective-permute-start | bytes 442376 | tf_op jit(solution)/shard_map/ppermute | solution.py:35
  12.2 5.1 %collective-permute-start.2 = (bf16[16,4608]{1,0:T(8,128)(2,1)S(1)}, bf16[16,4608]{1,0:T(8,128)(2,1)S(1)}, u32[]{:S(2)}, u32[]{:S(2)}) collective-permute-start(bf16[16,4608]{1,0:T(8,128)(2,1)S(1)} %collective-permute-done.refs_1_), channel_id=1, source_target_pairs={{0,8},{2,10},{4,12},{6,14},{8,0},{10,2},{12,4},{14,6},{16,24},{18,... | collective-permute-start | bytes 442376 | tf_op jit(solution)/shard_map/ppermute | solution.py:35
  12.8 7.0 %collective-permute-start.3 = (bf16[16,4608]{1,0:T(8,128)(2,1)S(1)}, bf16[16,4608]{1,0:T(8,128)(2,1)S(1)}, u32[]{:S(2)}, u32[]{:S(2)}) collective-permute-start(bf16[16,4608]{1,0:T(8,128)(2,1)S(1)} %pack.1.refs_0_), channel_id=1, source_target_pairs={{0,4},{2,6},{4,0},{6,2},{8,12},{10,14},{12,8},{14,10},{16,20},{18,... | collective-permute-start | bytes 442376 | tf_op jit(solution)/shard_map/ppermute | solution.py:35
  14.4 8.4 %collective-permute-start.4 = (bf16[16,4608]{1,0:T(8,128)(2,1)S(1)}, bf16[16,4608]{1,0:T(8,128)(2,1)S(1)}, u32[]{:S(2)}, u32[]{:S(2)}) collective-permute-start(bf16[16,4608]{1,0:T(8,128)(2,1)S(1)} %collective-permute-done.refs_1_), channel_id=1, source_target_pairs={{0,4},{2,6},{4,0},{6,2},{8,12},{10,14},{12,8},{14,10},{16,20},{18,... | collective-permute-start | bytes 442376 | tf_op jit(solution)/shard_map/ppermute | solution.py:35
  14.9 11.0 %collective-permute-start.5 = (bf16[16,4608]{1,0:T(8,128)(2,1)S(1)}, bf16[16,4608]{1,0:T(8,128)(2,1)S(1)}, u32[]{:S(2)}, u32[]{:S(2)}) collective-permute-start(bf16[16,4608]{1,0:T(8,128)(2,1)S(1)} %collective-permute-done.1.refs_2_), channel_id=1, source_target_pairs={{0,4},{2,6},{4,0},{6,2},{8,12},{10,14},{12,8},{14,10},{16,20},{18,... | collective-permute-start | bytes 442376 | tf_op jit(solution)/shard_map/ppermute | solution.py:35
  17.4 10.4 %collective-permute-start.6 = (bf16[16,4608]{1,0:T(8,128)(2,1)S(1)}, bf16[16,4608]{1,0:T(8,128)(2,1)S(1)}, u32[]{:S(2)}, u32[]{:S(2)}) collective-permute-start(bf16[16,4608]{1,0:T(8,128)(2,1)S(1)} %collective-permute-done.2.refs_3_), channel_id=1, source_target_pairs={{0,4},{2,6},{4,0},{6,2},{8,12},{10,14},{12,8},{14,10},{16,20},{18,... | collective-permute-start | bytes 442376 | tf_op jit(solution)/shard_map/ppermute | solution.py:35
  18.9 0.7 copy-start
  28.6 15.7 %collective-permute-start.7 = (bf16[144,4096]{1,0:T(8,128)(2,1)S(1)}, bf16[144,4096]{1,0:T(8,128)(2,1)S(1)}, u32[]{:S(2)}, u32[]{:S(2)}) collective-permute-start(bf16[144,4096]{1,0:T(8,128)(2,1)S(1)} %assemble.1.refs_0_.refs_1_.half_ref), channel_id=1, source_target_pairs={{0,2},{2,0},{4,6},{6,4},{8,10},{10,8},{12,14},{14,12},{16,18},{18,... | collective-permute-start | bytes 3538952 | tf_op jit(solution)/shard_map/ppermute | solution.py:35
  42.6 15.0 %collective-permute-start.10 = (bf16[104,1024]{1,0:T(8,128)(2,1)S(1)}, bf16[104,1024]{1,0:T(8,128)(2,1)S(1)}, u32[]{:S(2)}, u32[]{:S(2)}) collective-permute-start(bf16[104,1024]{1,0:T(8,128)(2,1)S(1)} %forward_half.3), channel_id=1, source_target_pairs={{0,1},{1,0},{2,3},{3,2},{4,5},{5,4},{6,7},{7,6},{8,9},{9,8},{10,11... | collective-permute-start | bytes 638984 | tf_op jit(solution)/shard_map/ppermute | solution.py:39
  47.0 10.7 %collective-permute-start.11 = (bf16[144,1024]{1,0:T(8,128)(2,1)S(1)}, bf16[144,1024]{1,0:T(8,128)(2,1)S(1)}, u32[]{:S(2)}, u32[]{:S(2)}) collective-permute-start(bf16[144,1024]{1,0:T(8,128)(2,1)S(1)} %get-tuple-element.36), channel_id=1, source_target_pairs={{0,1},{1,0},{2,3},{3,2},{4,5},{5,4},{6,7},{7,6},{8,9},{9,8},{10,11... | collective-permute-start | bytes 884744 | tf_op jit(solution)/shard_map/ppermute | solution.py:39
  50.2 15.1 %collective-permute-start.8 = (bf16[248,768]{1,0:T(8,128)(2,1)S(1)}, bf16[248,768]{1,0:T(8,128)(2,1)S(1)}, u32[]{:S(2)}, u32[]{:S(2)}) collective-permute-start(bf16[248,768]{1,0:T(8,128)(2,1)S(1)} %get-tuple-element.33), channel_id=1, source_target_pairs={{0,1},{1,0},{2,3},{3,2},{4,5},{5,4},{6,7},{7,6},{8,9},{9,8},{10,11... | collective-permute-start | bytes 1142792 | tf_op jit(solution)/shard_map/ppermute | solution.py:39
  54.5 3.2 %copy-start.1 = (s32[8]{0:T(128)S(1)}, s32[8]{0:T(128)}, u32[]{:S(2)}) copy-start(s32[8]{0:T(128)} %points_ref.3) | copy-start | bytes 100
  60.8 11.3 %collective-permute-start.12 = (bf16[80,1024]{1,0:T(8,128)(2,1)S(1)}, bf16[80,1024]{1,0:T(8,128)(2,1)S(1)}, u32[]{:S(2)}, u32[]{:S(2)}) collective-permute-start(bf16[80,1024]{1,0:T(8,128)(2,1)S(1)} %coefficients.3.refs_0_), channel_id=1, source_target_pairs={{0,1},{1,0},{2,3},{3,2},{4,5},{5,4},{6,7},{7,6},{8,9},{9,8},{10,11... | collective-permute-start | bytes 491528 | tf_op jit(solution)/shard_map/ppermute | solution.py:39
  67.8 8.8 %collective-permute-start.9 = (bf16[80,768]{1,0:T(8,128)(2,1)S(1)}, bf16[80,768]{1,0:T(8,128)(2,1)S(1)}, u32[]{:S(2)}, u32[]{:S(2)}) collective-permute-start(bf16[80,768]{1,0:T(8,128)(2,1)S(1)} %coefficients.2.refs_1_), channel_id=1, source_target_pairs={{0,1},{1,0},{2,3},{3,2},{4,5},{5,4},{6,7},{7,6},{8,9},{9,8},{10,11... | collective-permute-start | bytes 368648 | tf_op jit(solution)/shard_map/ppermute | solution.py:39
  77.7 1.7 %collective-permute-start.13 = (bf16[40,2048]{1,0:T(8,128)(2,1)S(1)}, bf16[40,2048]{1,0:T(8,128)(2,1)S(1)}, u32[]{:S(2)}, u32[]{:S(2)}) collective-permute-start(bf16[40,2048]{1,0:T(8,128)(2,1)S(1)} %get-tuple-element.38), channel_id=1, source_target_pairs={{0,2},{2,0},{4,6},{6,4},{8,10},{10,8},{12,14},{14,12},{16,18},{18,... | collective-permute-start | bytes 491528 | tf_op jit(solution)/shard_map/ppermute | solution.py:35
  78.8 2.2 %collective-permute-start.17 = (bf16[40,2048]{1,0:T(8,128)(2,1)S(1)}, bf16[40,2048]{1,0:T(8,128)(2,1)S(1)}, u32[]{:S(2)}, u32[]{:S(2)}) collective-permute-start(bf16[40,2048]{1,0:T(8,128)(2,1)S(1)} %get-tuple-element.40), channel_id=1, source_target_pairs={{0,2},{2,0},{4,6},{6,4},{8,10},{10,8},{12,14},{14,12},{16,18},{18,... | collective-permute-start | bytes 491528 | tf_op jit(solution)/shard_map/ppermute | solution.py:35
  79.5 4.8 %collective-permute-start.14 = (bf16[20,2048]{1,0:T(8,128)(2,1)S(1)}, bf16[20,2048]{1,0:T(8,128)(2,1)S(1)}, u32[]{:S(2)}, u32[]{:S(2)}) collective-permute-start(bf16[20,2048]{1,0:T(8,128)(2,1)S(1)} %slice.91), channel_id=1, source_target_pairs={{0,4},{2,6},{4,0},{6,2},{8,12},{10,14},{12,8},{14,10},{16,20},{18,... | collective-permute-start | bytes 245768 | tf_op jit(solution)/shard_map/ppermute | solution.py:35
  81.2 4.7 %collective-permute-start.18 = (bf16[20,2048]{1,0:T(8,128)(2,1)S(1)}, bf16[20,2048]{1,0:T(8,128)(2,1)S(1)}, u32[]{:S(2)}, u32[]{:S(2)}) collective-permute-start(bf16[20,2048]{1,0:T(8,128)(2,1)S(1)} %pad_maximum_fusion), channel_id=1, source_target_pairs={{0,8},{2,10},{4,12},{6,14},{8,0},{10,2},{12,4},{14,6},{16,24},{18,... | collective-permute-start | bytes 245768 | tf_op jit(solution)/shard_map/ppermute | solution.py:35
  84.3 4.3 %collective-permute-start.15 = (bf16[10,2048]{1,0:T(8,128)(2,1)S(1)}, bf16[10,2048]{1,0:T(8,128)(2,1)S(1)}, u32[]{:S(2)}, u32[]{:S(2)}) collective-permute-start(bf16[10,2048]{1,0:T(8,128)(2,1)S(1)} %slice.93), channel_id=1, source_target_pairs={{0,8},{2,10},{4,12},{6,14},{8,0},{10,2},{12,4},{14,6},{16,24},{18,... | collective-permute-start | bytes 122888 | tf_op jit(solution)/shard_map/ppermute | solution.py:35
  85.9 6.5 %collective-permute-start.19 = (bf16[10,2048]{1,0:T(8,128)(2,1)S(1)}, bf16[10,2048]{1,0:T(8,128)(2,1)S(1)}, u32[]{:S(2)}, u32[]{:S(2)}) collective-permute-start(bf16[10,2048]{1,0:T(8,128)(2,1)S(1)} %slice.92), channel_id=1, source_target_pairs={{0,4},{2,6},{4,0},{6,2},{8,12},{10,14},{12,8},{14,10},{16,20},{18,... | collective-permute-start | bytes 122888 | tf_op jit(solution)/shard_map/ppermute | solution.py:35
  88.7 5.9 %collective-permute-start.16 = (bf16[5,2048]{1,0:T(8,128)(2,1)S(1)}, bf16[5,2048]{1,0:T(8,128)(2,1)S(1)}, u32[]{:S(2)}, u32[]{:S(2)}) collective-permute-start(bf16[5,2048]{1,0:T(8,128)(2,1)S(1)} %slice.95), channel_id=1, source_target_pairs={{0,16},{2,18},{4,20},{6,22},{8,24},{10,26},{12,28},{14,30},{16,0},... | collective-permute-start | bytes 61448 | tf_op jit(solution)/shard_map/ppermute | solution.py:35
  92.5 4.9 %collective-permute-start.20 = (bf16[5,2048]{1,0:T(8,128)(2,1)S(1)}, bf16[5,2048]{1,0:T(8,128)(2,1)S(1)}, u32[]{:S(2)}, u32[]{:S(2)}) collective-permute-start(bf16[5,2048]{1,0:T(8,128)(2,1)S(1)} %slice.94), channel_id=1, source_target_pairs={{0,16},{2,18},{4,20},{6,22},{8,24},{10,26},{12,28},{14,30},{16,0},... | collective-permute-start | bytes 61448 | tf_op jit(solution)/shard_map/ppermute | solution.py:35
